TPU v7x, 32 devices: a whole 2x2x4 slice. The times are simulated.
32 devices in a mesh: dp: 8 (over z, y), head: 4 (over x, core).
Axes of the slice: x: 2, y: 2, z: 4, core: 2. Of those that a mesh axis runs over, the one named last changes fastest.
Arguments:
- tokens: bfloat16 [32768, 768], P(('dp', 'head')), may hold values from -6 to 6
- seq_lengths: int32 [64, 32], P('dp'), may hold values from 0 to 512, as said below
- qkv_weight: bfloat16 [2, 3, 768, 768], P(None, None, None, 'head'), may hold values from -0.21875 to 0.21875
- qv_bias: float32 [2, 2, 768], P(None, None, 'head'), may hold values from -3 to 3
- out_weight: bfloat16 [2, 768, 768], replicated, may hold values from -0.875 to 0.875
- out_bias: float32 [2, 768], replicated, may hold values from -3 to 3
- norm1_gain: float32 [2, 768], replicated, may hold values from 0.25 to 1.75
- norm1_shift: float32 [2, 768], replicated, may hold values from -3 to 3
- up_weight: bfloat16 [2, 768, 3072], replicated, may hold values from -0.21875 to 0.21875
- up_bias: float32 [2, 3072], replicated, may hold values from -3 to 3
- down_weight: bfloat16 [2, 3072, 768], replicated, may hold values from -0.109375 to 0.109375
- down_bias: float32 [2, 768], replicated, may hold values from -3 to 3
- norm2_gain: float32 [2, 768], replicated, may hold values from 0.25 to 1.75
- norm2_shift: float32 [2, 768], replicated, may hold values from -3 to 3
- out_grad: bfloat16 [32768, 768], P(('dp', 'head')), may hold values from -6 to 6
Outputs:
- out_state: bfloat16 [32768, 768], P(('dp', 'head'))
- input_grad: bfloat16 [32768, 768], P(('dp', 'head'))
- qkv_weight_grad: float32 [2, 3, 768, 768], P(None, None, 'dp', 'head')
- qv_bias_grad: float32 [2, 2, 768], replicated
- out_weight_grad: float32 [2, 768, 768], P(None, 'dp', 'head')
- out_bias_grad: float32 [2, 768], replicated
- norm1_gain_grad: float32 [2, 768], replicated
- norm1_shift_grad: float32 [2, 768], replicated
- up_weight_grad: float32 [2, 768, 3072], P(None, 'dp', 'head')
- up_bias_grad: float32 [2, 3072], replicated
- down_weight_grad: float32 [2, 3072, 768], P(None, 'head', 'dp')
- down_bias_grad: float32 [2, 768], replicated
- norm2_gain_grad: float32 [2, 768], replicated
- norm2_shift_grad: float32 [2, 768], replicated
Inputs may be any that keep to these rules, and one draw needn't show every extreme that they name: `seq_lengths`: each slot's row sums to 512; nonzero entries come first and zero entries mark no sequence; some slot holds a single sequence of 512 rows.
All inputs are finite; a program needn't handle non-finite values.
Results may differ from a plain program's by a relative error of at most 0.025.
Values may be sent and summed in bfloat16 or wider, within the bound.
No kernel may reach another device: no remote copies, remote signals or barrier semaphores. Data moves between devices by JAX's collectives and lax.ppermute only.
A program may use at most 256 MiB of HBM per device.

v0:
```python
import jax
import jax.numpy as jnp
from jax import lax
from jax.sharding import PartitionSpec as P

HD = 64


EPSILON = 1e-06


def norm_rows(values, gain, shift):
    centre = jnp.mean(values, axis=-1, keepdims=True)
    centred = values - centre
    spread = jnp.mean(centred * centred, axis=-1, keepdims=True)
    return centred * lax.rsqrt(spread + EPSILON) * gain + shift


def exact_gelu(values):
    return jax.nn.gelu(values, approximate=False)


def segment_ids(lengths, slot_rows):
    boundary = jnp.cumsum(lengths, axis=1)
    position = jnp.arange(slot_rows, dtype=jnp.int32)
    return jnp.sum((position[None, :, None] >= boundary[:, None, :]).astype(jnp.int32), axis=2)


def slot_scores(queries, keys_in, segments):
    scaling = queries.shape[-1] ** (-0.5)
    scores = (
        jnp.einsum("qhd,khd->hqk", queries, keys_in, preferred_element_type=jnp.float32) * scaling
    )
    inside = (segments[:, None] == segments[None, :])[None]
    return (scores, inside)


def slot_forward(packed):
    queries, keys_in, values_in, segments = packed
    scores, inside = slot_scores(queries, keys_in, segments)
    scores = jnp.where(inside, scores, -1e30)
    peak_score = jnp.max(scores, axis=-1, keepdims=True)
    weights = jnp.exp(scores - peak_score)
    denominator = jnp.sum(weights, axis=-1, keepdims=True)
    probability = (weights / denominator).astype(jnp.bfloat16)
    context = jnp.einsum("hqk,khd->qhd", probability, values_in, preferred_element_type=jnp.float32)
    return (context.astype(jnp.bfloat16), (peak_score + jnp.log(denominator))[..., 0])


def slot_backward(packed):
    queries, keys_in, values_in, grad_context, log_total, segments = packed
    scaling = queries.shape[-1] ** (-0.5)
    scores, inside = slot_scores(queries, keys_in, segments)
    probability = jnp.where(inside, jnp.exp(scores - log_total[..., None]), 0.0)
    grad_prob = jnp.einsum(
        "qhd,khd->hqk", grad_context, values_in, preferred_element_type=jnp.float32
    )
    shares = jnp.sum(probability * grad_prob, axis=-1, keepdims=True)
    grad_score = (probability * (grad_prob - shares)).astype(jnp.bfloat16)
    grad_query = (
        jnp.einsum("hqk,khd->qhd", grad_score, keys_in, preferred_element_type=jnp.float32)
        * scaling
    )
    grad_key = (
        jnp.einsum("hqk,qhd->khd", grad_score, queries, preferred_element_type=jnp.float32)
        * scaling
    )
    grad_value = jnp.einsum(
        "hqk,qhd->khd",
        probability.astype(jnp.bfloat16),
        grad_context,
        preferred_element_type=jnp.float32,
    )
    return (
        grad_query.astype(jnp.bfloat16),
        grad_key.astype(jnp.bfloat16),
        grad_value.astype(jnp.bfloat16),
    )


def on_device(
    tokens,
    seq_lengths,
    qkv_weight,
    qv_bias,
    out_weight,
    out_bias,
    norm1_gain,
    norm1_shift,
    up_weight,
    up_bias,
    down_weight,
    down_bias,
    norm2_gain,
    norm2_shift,
    out_grad,
):
    heads_count = lax.axis_size("head")
    head_index = lax.axis_index("head")
    local_rows, model_width = tokens.shape
    group_rows = local_rows * heads_count
    slots_here = seq_lengths.shape[0]
    slot_rows = group_rows // slots_here
    segments = segment_ids(seq_lengths, slot_rows)
    head_width = qkv_weight.shape[-1]
    local_heads = head_width // HD
    layers = qkv_weight.shape[0]
    qkv_shape = (slots_here, slot_rows, 3, local_heads, HD)
    hidden_state = tokens.astype(jnp.float32)
    kept_values = []
    for layer_index in range(layers):
        gathered = lax.all_gather(hidden_state.astype(jnp.bfloat16), "head", axis=0, tiled=True)
        projected = jnp.einsum(
            "rd,cde->rce", gathered, qkv_weight[layer_index], preferred_element_type=jnp.float32
        )
        bias_rows = jnp.stack(
            [
                qv_bias[layer_index, 0],
                jnp.zeros_like(qv_bias[layer_index, 0]),
                qv_bias[layer_index, 1],
            ]
        )
        projected = (projected + bias_rows[None]).astype(jnp.bfloat16)
        shaped = projected.reshape(qkv_shape)
        context, log_total = lax.map(
            slot_forward, (shaped[:, :, 0], shaped[:, :, 1], shaped[:, :, 2], segments)
        )
        context = context.reshape(group_rows, head_width)
        token_context = lax.all_to_all(context, "head", split_axis=0, concat_axis=1, tiled=True)
        attended = (
            jnp.dot(token_context, out_weight[layer_index], preferred_element_type=jnp.float32)
            + out_bias[layer_index]
        )
        first_sum = hidden_state + attended
        normed = norm_rows(first_sum, norm1_gain[layer_index], norm1_shift[layer_index])
        normed_low = normed.astype(jnp.bfloat16)
        ffn_rows = normed_low
        up_part = up_weight[layer_index]
        up_shift = up_bias[layer_index]
        down_part = down_weight[layer_index]
        before_gelu = jnp.dot(ffn_rows, up_part, preferred_element_type=jnp.float32) + up_shift
        activated = exact_gelu(before_gelu).astype(jnp.bfloat16)
        branch = jnp.dot(activated, down_part, preferred_element_type=jnp.float32)
        second_sum = normed + branch + down_bias[layer_index]
        hidden_state = norm_rows(second_sum, norm2_gain[layer_index], norm2_shift[layer_index])
        kept_values.append(
            (
                gathered,
                projected,
                log_total,
                token_context,
                first_sum,
                ffn_rows,
                up_part,
                down_part,
                before_gelu,
                activated,
                second_sum,
            )
        )
    out_state = hidden_state.astype(jnp.bfloat16)
    grad_state = out_grad.astype(jnp.float32)
    ffn_list, proj_list, attn_list, small_list, shift_list = ([], [], [], [], [])
    for layer_index in reversed(range(layers)):
        (
            gathered,
            projected,
            log_total,
            token_context,
            first_sum,
            ffn_rows,
            up_part,
            down_part,
            before_gelu,
            activated,
            second_sum,
        ) = kept_values[layer_index]
        pull_second = jax.vjp(
            norm_rows, second_sum, norm2_gain[layer_index], norm2_shift[layer_index]
        )[1]
        grad_second, grad_gain2, grad_shift2 = pull_second(grad_state)
        grad_branch = grad_second.astype(jnp.bfloat16)
        grad_down_shift = jnp.sum(grad_branch.astype(jnp.float32), axis=0)
        grad_down = jnp.einsum(
            "rd,rf->df", grad_branch, activated, preferred_element_type=jnp.float32
        )
        grad_act = jnp.einsum(
            "rd,fd->rf", grad_branch, down_part, preferred_element_type=jnp.float32
        )
        pull_gelu = jax.vjp(exact_gelu, before_gelu)[1]
        grad_pre = pull_gelu(grad_act)[0].astype(jnp.bfloat16)
        grad_up_shift = jnp.sum(grad_pre.astype(jnp.float32), axis=0)
        grad_up = jnp.einsum("rd,rf->df", ffn_rows, grad_pre, preferred_element_type=jnp.float32)
        grad_normed_low = jnp.einsum(
            "rf,df->rd", grad_pre, up_part, preferred_element_type=jnp.float32
        )
        grad_normed = grad_second + grad_normed_low
        pull_first = jax.vjp(
            norm_rows, first_sum, norm1_gain[layer_index], norm1_shift[layer_index]
        )[1]
        grad_first, grad_gain1, grad_shift1 = pull_first(grad_normed)
        grad_attended = grad_first.astype(jnp.bfloat16)
        grad_out_shift = jnp.sum(grad_attended.astype(jnp.float32), axis=0)
        grad_out = jnp.einsum(
            "rd,re->de", token_context, grad_attended, preferred_element_type=jnp.float32
        )
        grad_mixed = jnp.einsum(
            "re,de->rd", grad_attended, out_weight[layer_index], preferred_element_type=jnp.float32
        ).astype(jnp.bfloat16)
        grad_context = lax.all_to_all(grad_mixed, "head", split_axis=1, concat_axis=0, tiled=True)
        shaped = projected.reshape(qkv_shape)
        grad_query, grad_key, grad_value = lax.map(
            slot_backward,
            (
                shaped[:, :, 0],
                shaped[:, :, 1],
                shaped[:, :, 2],
                grad_context.reshape(slots_here, slot_rows, local_heads, HD),
                log_total,
                segments,
            ),
        )
        grad_proj = jnp.stack([grad_query, grad_key, grad_value], axis=2).reshape(
            group_rows, 3, head_width
        )
        grad_qkv = jnp.einsum(
            "rd,rce->cde", gathered, grad_proj, preferred_element_type=jnp.float32
        )
        bias_local = jnp.sum(grad_proj.astype(jnp.float32), axis=0)
        qv_local = jnp.stack([bias_local[0], bias_local[2]])
        qv_full = lax.dynamic_update_slice_in_dim(
            jnp.zeros((2, model_width), jnp.float32), qv_local, head_index * head_width, 1
        )
        layer_weights = qkv_weight[layer_index]
        grad_state = grad_first + lax.psum_scatter(
            jnp.einsum(
                "rce,cde->rd", grad_proj, layer_weights, preferred_element_type=jnp.float32
            ).astype(jnp.bfloat16),
            "head",
            scatter_dimension=0,
            tiled=True,
        ).astype(jnp.float32)
        ffn_list.append(jnp.stack([grad_up, grad_down]))
        proj_list.append(grad_out)
        attn_list.append(grad_qkv)
        small_list.append(
            jnp.concatenate(
                [
                    qv_full,
                    jnp.stack(
                        [
                            grad_out_shift,
                            grad_gain1,
                            grad_shift1,
                            grad_down_shift,
                            grad_gain2,
                            grad_shift2,
                        ]
                    ),
                ],
                axis=0,
            )
        )
        shift_list.append(grad_up_shift)
    input_grad = grad_state.astype(jnp.bfloat16)
    ffn_stack = jnp.stack(ffn_list[::-1])
    proj_stack = jnp.stack(proj_list[::-1])
    attn_stack = jnp.stack(attn_list[::-1])
    small_stack = jnp.stack(small_list[::-1])
    shift_stack = jnp.stack(shift_list[::-1])
    ffn_data, proj_data, attn_data = (
        lax.psum_scatter(
            ffn_stack.astype(jnp.bfloat16), "dp", scatter_dimension=2, tiled=True
        ).astype(jnp.float32),
        lax.psum_scatter(
            proj_stack.astype(jnp.bfloat16), "dp", scatter_dimension=1, tiled=True
        ).astype(jnp.float32),
        lax.psum_scatter(
            attn_stack.astype(jnp.bfloat16), "dp", scatter_dimension=2, tiled=True
        ).astype(jnp.float32),
    )
    ffn_head, proj_head = (
        lax.psum_scatter(
            ffn_data.astype(jnp.bfloat16), "head", scatter_dimension=3, tiled=True
        ).astype(jnp.float32),
        lax.psum_scatter(
            proj_data.astype(jnp.bfloat16), "head", scatter_dimension=2, tiled=True
        ).astype(jnp.float32),
    )
    small_sum, shift_sum = lax.psum((small_stack, shift_stack), ("dp", "head"))
    down_weight_grad = jnp.transpose(ffn_head[:, 1], (0, 2, 1))
    return (
        out_state,
        input_grad,
        attn_data,
        small_sum[:, 0:2],
        proj_head,
        small_sum[:, 2],
        small_sum[:, 3],
        small_sum[:, 4],
        ffn_head[:, 0],
        shift_sum,
        down_weight_grad,
        small_sum[:, 5],
        small_sum[:, 6],
        small_sum[:, 7],
    )


def solution(mesh):
    in_specs = (
        P(("dp", "head"), None),
        P("dp", None),
        P(None, None, None, "head"),
        P(None, None, "head"),
        P(),
        P(),
        P(),
        P(),
        P(),
        P(),
        P(),
        P(),
        P(),
        P(),
        P(("dp", "head"), None),
    )
    out_specs = (
        P(("dp", "head"), None),
        P(("dp", "head"), None),
        P(None, None, "dp", "head"),
        P(),
        P(None, "dp", "head"),
        P(),
        P(),
        P(),
        P(None, "dp", "head"),
        P(),
        P(None, "head", "dp"),
        P(),
        P(),
        P(),
    )
    return jax.shard_map(
        on_device, mesh=mesh, in_specs=in_specs, out_specs=out_specs, check_vma=False
    )
```

profile of v0, /device:TPU:0, one launch (start us, length us, event | category | flops | bytes accessed | tf_op | source)
XLA Modules:
  0.0 1406.1 jit_solution(3311266776964060774)
XLA Ops:
  12.9 45.8 %all-gather.3.cloned.1.call-done = bf16[4096,768]{1,0:T(8,128)(2,1)} async-done(((bf16[1024,768]{1,0:T(8,128)(2,1)}), bf16[4096,768]{1,0:T(8,128)(2,1)}) %all-gather.3.cloned.1.call-update) | async-done | bytes 6291472 | tf_op jit(solution)/shard_map/all_gather | solution.py:112
  73.9 35.4 %while.52 = (s32[]{:T(128)}, bf16[8,512,3,64]{1,3,2,0:T(8,128)(2,1)}, f32[8,3,512]{2,1,0:T(4,128)S(1)}, bf16[8,512,3,64]{1,3,2,0:T(8,128)(2,1)}, s32[8,512]{1,0:...) while((s32[]{:T(128)}, ...), condition=%wide.region_5.6_spmd, body=%wide.region_2.5_spmd.sunk | while | flops 211122688 | bytes 11335773 | solution.py:125
  113.8 13.7 all_to_all.52
  139.1 15.2 %all-to-all-done = bf16[4,1024,192]{1,2,0:T(8,128)(2,1)S(1)} async-done(((bf16[4,1024,192]{1,2,0:T(8,128)(2,1)}), bf16[4,1024,192]{1,2,0:T(8,128)(2,1)S(1)}, u32[]{:S(2)}, u32[]{:S(2)}) %all-to-all-start) | async-done | bytes 1572896 | tf_op jit(solution)/shard_map/all_to_all | solution.py:129
  158.9 38.8 %multiply_convert_fusion.3 = (bf16[1024,3072]{1,0:T(8,128)(2,1)}, f32[1024,3072]{1,0:T(8,128)}, f32[1024,3072]{1,0:T(8,128)}) fusion(f32[3072]{0:T(1024)S(1)} %bitcast.494, bf16[2,768,3072]{2,1,0:T(8,128)(2,1)} %param.31, f32[1024,768]{0,1:T(8,128)S(1)} %get-tuple-element.478, f32[768]{0:T(1024)S(1)} %get-tuple-element.347, ...), kind=kOutput, calls=%fused_computation.148 | convolution fusion | flops 5043388416 | bytes 39348224 | tf_op jit(solution)/shard_map/dot_general | solution.py:141
  208.6 46.5 %all-gather.5.cloned.1.call-done = bf16[4096,768]{0,1:T(8,128)(2,1)} async-done(((bf16[1024,768]{0,1:T(8,128)(2,1)}), bf16[4096,768]{0,1:T(8,128)(2,1)}) %all-gather.5.cloned.1.call-update) | async-done | bytes 6291472 | tf_op jit(solution)/shard_map/all_gather | solution.py:112
  273.1 43.5 %while.53 = (s32[]{:T(128)}, bf16[8,512,3,64]{1,3,2,0:T(8,128)(2,1)}, f32[8,3,512]{2,1,0:T(4,128)S(1)}, bf16[8,512,3,64]{1,3,2,0:T(8,128)(2,1)}, s32[8,512]{1,0:...) while((s32[]{:T(128)}, ...), condition=%wide.region_13.14_spmd, body=%wide.region_10.13_spmd.sunk | while | flops 211122688 | bytes 11335773 | solution.py:125
  334.3 17.5 %all-to-all-done.1 = bf16[4,1024,192]{1,2,0:T(8,128)(2,1)} async-done(((bf16[4,1024,192]{1,2,0:T(8,128)(2,1)}), bf16[4,1024,192]{1,2,0:T(8,128)(2,1)}, u32[]{:S(2)}, u32[]{:S(2)}) %all-to-all-start.1) | async-done | bytes 1572896 | tf_op jit(solution)/shard_map/all_to_all | solution.py:129
  356.5 38.4 %multiply_convert_fusion.2 = (bf16[1024,3072]{1,0:T(8,128)(2,1)}, f32[1024,3072]{1,0:T(8,128)}, f32[1024,3072]{1,0:T(8,128)}) fusion(f32[3072]{0:T(1024)S(1)} %bitcast.497, bf16[2,768,3072]{2,1,0:T(8,128)(2,1)} %param.31, f32[1024,768]{0,1:T(8,128)S(1)} %get-tuple-element.483, f32[768]{0:T(1024)S(1)} %copy-done.73, f32[768]{0:T(1024)S(1)} %copy-done.52, ...), kind=kOutput, calls=%fused_computation.135 | convolution fusion | flops 5043388416 | bytes 39348224 | tf_op jit(solution)/shard_map/dot_general | solution.py:141
  411.1 18.2 %convert_reduce_fusion = (f32[3072]{0:T(1024)}, bf16[1024,3072]{1,0:T(8,128)(2,1)}) fusion(f32[1024,3072]{1,0:T(8,128)} %get-tuple-element.435, bf16[1024,768]{0,1:T(8,128)(2,1)S(1)} %get-tuple-element.425, bf16[2,3072,768]{2,1,0:T(8,128)(2,1)} %param.33, f32[1024,3072]{1,0:T(8,128)} %get-tuple-element.484, f32[3072]{0:T(1024)S(1)} %bitcast.498), kind=kOutput, calls=%fused_computation.131 | convolution fusion | flops 4885312512 | bytes 37773312 | tf_op jit(solution)/shard_map/rd,fd->rf/dot_general | solution.py:187
  429.4 11.7 multiply_reduce_fusion.2
  451.5 20.0 %all-to-all-done.2 = bf16[1024,4,192]{0,2,1:T(8,128)(2,1)S(1)} async-done(((bf16[1024,4,192]{0,2,1:T(8,128)(2,1)}), bf16[1024,4,192]{0,2,1:T(8,128)(2,1)S(1)}, u32[]{:S(2)}, u32[]{:S(2)}) %all-to-all-start.2) | async-done | bytes 1572896 | tf_op jit(solution)/shard_map/all_to_all | solution.py:210
  479.6 88.1 %while.54 = (s32[]{:T(128)}, bf16[8,512,3,64]{1,3,2,0:T(8,128)(2,1)S(1)}, bf16[8,512,3,64]{1,3,2,0:T(8,128)(2,1)}, bf16[8,512,3,64]{1,3,2,0:T(8,128)(2,1)}, bf16...) while((s32[]{:T(128)}, ...), condition=%wide.region_24.25_spmd, body=%wide.region_22.24_spmd.sunk | while | flops 511146496 | bytes 26125428 | solution.py:212
  598.8 11.7 fusion.140
  610.5 41.4 %reduce-scatter.12.cloned.1.call-done = bf16[1024,768]{0,1:T(8,128)(2,1)} async-done(((bf16[4096,768]{0,1:T(8,128)(2,1)}), bf16[1024,768]{0,1:T(8,128)(2,1)}) %reduce-scatter.12.cloned.1.call-update) | async-done | bytes 1572880 | tf_op jit(solution)/shard_map/reduce_scatter | solution.py:235
  659.1 18.5 %convert_reduce_fusion.1 = (f32[3072]{0:T(1024)S(1)}, bf16[1024,3072]{1,0:T(8,128)(2,1)}) fusion(f32[1024,3072]{1,0:T(8,128)} %get-tuple-element.437, bf16[1024,768]{0,1:T(8,128)(2,1)} %get-tuple-element.421, bf16[2,3072,768]{2,1,0:T(8,128)(2,1)} %param.33, f32[1024,3072]{1,0:T(8,128)} %get-tuple-element.479, f32[3072]{0:T(1024)S(1)} %bitcast.495), kind=kOutput, calls=%fused_computation.132 | convolution fusion | flops 4885312512 | bytes 37773312 | tf_op jit(solution)/shard_map/rd,fd->rf/dot_general | solution.py:187
  738.1 16.7 %pad_maximum_fusion = bf16[2,2,768,3072]{3,2,1,0:T(8,128)(2,1)} fusion(bf16[1,2,768,3072]{3,2,1,0:T(8,128)(2,1)} %maximum_bitcast_fusion.1, bf16[1,2,768,3072]{3,2,1,0:T(8,128)(2,1)} %maximum_bitcast_fusion), kind=kLoop, calls=%fused_computation.126 | loop fusion | flops 9437184 | bytes 37748736 | tf_op jit(solution)/shard_map/stack | solution.py:266
  802.2 101.9 %while.55 = (s32[]{:T(128)}, bf16[8,512,3,64]{1,3,2,0:T(8,128)(2,1)}, bf16[8,512,3,64]{1,3,2,0:T(8,128)(2,1)}, bf16[8,512,3,64]{1,3,2,0:T(8,128)(2,1)}, bf16[8,5...) while((s32[]{:T(128)}, ...), condition=%wide.region_32.33_spmd, body=%wide.region_30.32_spmd.sunk | while | flops 511146496 | bytes 26125428 | solution.py:212
  966.8 112.1 %reduce-scatter.18.cloned.1.call-done = bf16[2,2,96,3072]{3,2,1,0:T(8,128)(2,1)} async-done(((bf16[2,2,768,3072]{3,2,1,0:T(8,128)(2,1)}), bf16[2,2,96,3072]{3,2,1,0:T(8,128)(2,1)}) %reduce-scatter.18.cloned.1.call-update) | async-done | bytes 2359312 | tf_op jit(solution)/shard_map/reduce_scatter | solution.py:272
  1081.6 122.8 %all-reduce.3.cloned.1.call-done = (f32[2,8,768]{2,0,1:T(2,128)}, f32[2,3072]{1,0:T(2,128)}) async-done(((f32[2,8,768]{2,0,1:T(2,128)}, f32[2,3072]{1,0:T(2,128)}), (f32[2,8,768]{2,0,1:T(2,128)}, f32[2,3072]{1,0:T(2,128)})) %all-reduce.3.cloned.1.call-update) | async-done | bytes 73744 | tf_op jit(solution)/shard_map/psum | solution.py:290
  1207.1 69.8 %reduce-scatter.22.cloned.1.call-done = bf16[96,1152]{1,0:T(8,128)(2,1)} async-done(((bf16[768,1152]{1,0:T(8,128)(2,1)}), bf16[96,1152]{1,0:T(8,128)(2,1)}) %reduce-scatter.22.cloned.1.call-update) | async-done | bytes 221200
  1281.1 18.6 %reduce-scatter.24.cloned.1.call-done = bf16[192,192]{1,0:T(8,128)(2,1)} async-done(((bf16[768,192]{1,0:T(8,128)(2,1)}), bf16[192,192]{1,0:T(8,128)(2,1)}) %reduce-scatter.24.cloned.1.call-update) | async-done | bytes 73744
  1301.4 59.1 %reduce-scatter.14.cloned.1.call-done = bf16[1024,768]{0,1:T(8,128)(2,1)} async-done(((bf16[4096,768]{0,1:T(8,128)(2,1)}), bf16[1024,768]{0,1:T(8,128)(2,1)}) %reduce-scatter.14.cloned.1.call-update) | async-done | bytes 1572880 | tf_op jit(solution)/shard_map/reduce_scatter | solution.py:235
  1366.3 29.9 %reduce-scatter.20.cloned.1.call-done = bf16[2,2,96,768]{3,2,1,0:T(8,128)(2,1)} async-done(((bf16[2,2,96,3072]{3,2,1,0:T(8,128)(2,1)}), bf16[2,2,96,768]{3,2,1,0:T(8,128)(2,1)}) %reduce-scatter.20.cloned.1.call-update) | async-done | bytes 589840 | tf_op jit(solution)/shard_map/reduce_scatter | solution.py:283
  (599 shorter events, 623.1 us)
Async XLA Ops:
  7.2 51.5 %all-gather.3.cloned.1.call-start = ((), (), s32[]{:S(2)}) async-start(), calls=%async_computation.11 | async-start | bytes 7864320 | tf_op jit(solution)/shard_map/all_gather | solution.py:112
  130.6 23.8 %all-to-all-start = ((bf16[4,1024,192]{1,2,0:T(8,128)(2,1)}), bf16[4,1024,192]{1,2,0:T(8,128)(2,1)S(1)}, u32[]{:S(2)}, u32[]{:S(2)}) async-start(bf16[4,1024,192]{1,2,0:T(8,128)(2,1)} %copy.160), calls=%async_computation | async-start | bytes 3145728 | tf_op jit(solution)/shard_map/all_to_all | solution.py:129
  134.3 120.8 %all-gather.5.cloned.1.call-start = ((), (), s32[]{:S(2)}) async-start(), calls=%async_computation.12 | async-start | bytes 7864320 | tf_op jit(solution)/shard_map/all_gather | solution.py:112
  137.9 59.8 %copy-start.50 = (f32[768]{0:T(1024)}, f32[768]{0:T(1024)S(1)}, u32[]{:S(2)}) copy-start(f32[768]{0:T(1024)S(1)} %get-tuple-element.495) | copy-start | bytes 9220
  137.9 59.8 %copy-start.71 = (f32[768]{0:T(1024)}, f32[768]{0:T(1024)S(1)}, u32[]{:S(2)}) copy-start(f32[768]{0:T(1024)S(1)} %get-tuple-element.347) | copy-start | bytes 9220
  138.5 213.3 %copy-start.35 = (f32[768]{0:T(1024)}, f32[768]{0:T(1024)S(1)}, u32[]{:S(2)}) copy-start(f32[768]{0:T(1024)S(1)} %get-tuple-element.497) | copy-start | bytes 9220
  206.4 145.4 %copy-start = (f32[1024,768]{0,1:T(8,128)}, f32[1024,768]{0,1:T(8,128)S(1)}, u32[]{:S(2)}) copy-start(f32[1024,768]{0,1:T(8,128)S(1)} %get-tuple-element.481) | copy-start | bytes 9437188
  206.4 145.4 %copy-start.33 = (f32[1024]{0:T(1024)}, f32[1024]{0:T(1024)S(1)}, u32[]{:S(2)}) copy-start(f32[1024]{0:T(1024)S(1)} %broadcast_multiply_fusion.2) | copy-start | bytes 12292
  206.8 145.0 %copy-start.37 = (f32[1024]{0:T(1024)}, f32[1024]{0:T(1024)S(1)}, u32[]{:S(2)}) copy-start(f32[1024]{0:T(1024)S(1)} %fusion.190) | copy-start | bytes 12292
  327.0 24.8 %all-to-all-start.1 = ((bf16[4,1024,192]{1,2,0:T(8,128)(2,1)}), bf16[4,1024,192]{1,2,0:T(8,128)(2,1)}, u32[]{:S(2)}, u32[]{:S(2)}) async-start(bf16[4,1024,192]{1,2,0:T(8,128)(2,1)} %copy.166), calls=%async_computation.1 | async-start | bytes 3145728 | tf_op jit(solution)/shard_map/all_to_all | solution.py:129
  447.9 23.6 %all-to-all-start.2 = ((bf16[1024,4,192]{0,2,1:T(8,128)(2,1)}), bf16[1024,4,192]{0,2,1:T(8,128)(2,1)S(1)}, u32[]{:S(2)}, u32[]{:S(2)}) async-start(bf16[1024,4,192]{0,2,1:T(8,128)(2,1)} %bitcast.68), calls=%async_computation.2 | async-start | bytes 3145728 | tf_op jit(solution)/shard_map/all_to_all | solution.py:210
  451.4 200.5 %reduce-scatter.12.cloned.1.call-start = ((), (), s32[]{:S(2)}) async-start(), calls=%async_computation.13 | async-start | bytes 7864320 | tf_op jit(solution)/shard_map/reduce_scatter | solution.py:235
  593.4 361.3 %reduce-scatter.16.cloned.1.call-start = ((), (), s32[]{:S(2)}) async-start(), calls=%async_computation.15 | async-start | bytes 2654208 | tf_op jit(solution)/shard_map/reduce_scatter | solution.py:275
  598.8 53.1 %copy-start.1 = (f32[1024,768]{0,1:T(8,128)S(1)}, f32[1024,768]{0,1:T(8,128)}, u32[]{:S(2)}) copy-start(f32[1024,768]{0,1:T(8,128)} %copy-done) | copy-start | bytes 9437188
  598.8 53.1 %copy-start.34 = (f32[1024]{0:T(1024)S(1)}, f32[1024]{0:T(1024)}, u32[]{:S(2)}) copy-start(f32[1024]{0:T(1024)} %copy-done.33) | copy-start | bytes 12292
  598.8 53.1 %copy-start.36 = (f32[768]{0:T(1024)S(1)}, f32[768]{0:T(1024)}, u32[]{:S(2)}) copy-start(f32[768]{0:T(1024)} %copy-done.35) | copy-start | bytes 9220
  598.8 53.1 %copy-start.38 = (f32[1024]{0:T(1024)S(1)}, f32[1024]{0:T(1024)}, u32[]{:S(2)}) copy-start(f32[1024]{0:T(1024)} %copy-done.37) | copy-start | bytes 12292
  693.2 385.8 %reduce-scatter.18.cloned.1.call-start = ((), (), s32[]{:S(2)}) async-start(), calls=%async_computation.16 | async-start | bytes 21233664 | tf_op jit(solution)/shard_map/reduce_scatter | solution.py:272
  763.2 24.5 %all-to-all-start.3 = ((bf16[1024,4,192]{0,2,1:T(8,128)(2,1)}), bf16[1024,4,192]{0,2,1:T(8,128)(2,1)}, u32[]{:S(2)}, u32[]{:S(2)}) async-start(bf16[1024,4,192]{0,2,1:T(8,128)(2,1)} %bitcast.483), calls=%async_computation.4 | async-start | bytes 3145728 | tf_op jit(solution)/shard_map/all_to_all | solution.py:210
  767.6 436.8 %all-reduce.3.cloned.1.call-start = ((), (), s32[]{:S(2)}) async-start(), calls=%async_computation.20 | async-start | bytes 147456 | tf_op jit(solution)/shard_map/psum | solution.py:290
  932.0 344.8 %reduce-scatter.22.cloned.1.call-start = ((), (), s32[]{:S(2)}) async-start(), calls=%async_computation.18 | async-start | bytes 1990656
  954.6 345.0 %reduce-scatter.24.cloned.1.call-start = ((), (), s32[]{:S(2)}) async-start(), calls=%async_computation.19 | async-start | bytes 491520
  957.0 403.6 %reduce-scatter.14.cloned.1.call-start = ((), (), s32[]{:S(2)}) async-start(), calls=%async_computation.14 | async-start | bytes 7864320 | tf_op jit(solution)/shard_map/reduce_scatter | solution.py:235
  966.8 429.4 %reduce-scatter.20.cloned.1.call-start = ((), (), s32[]{:S(2)}) async-start(), calls=%async_computation.17 | async-start | bytes 2949120 | tf_op jit(solution)/shard_map/reduce_scatter | solution.py:283
  (75 other events, 1029.3 us)
Sparse Core Ops, SparseCore 0:
  9.6 49.0 all-gather.2
  208.7 46.3 all-gather.4
  593.5 58.3 reduce-scatter.11
  693.3 69.0 reduce-scatter.15
  766.6 312.3 reduce-scatter.17
  1086.6 117.7 all-reduce.2
  1208.2 68.5 reduce-scatter.21
  1279.9 19.7 reduce-scatter.23
  1302.2 58.3 reduce-scatter.13
  1363.1 33.0 reduce-scatter.19
where the time goes:
time: 1420 us; the launch traced here: 1410 us
  waiting for transfers between devices  610 us (43%)
  matrix products  475 us (33%)
  local copies, waits for them, and re-layouts  185 us (13%)
  other arithmetic  102 us (7%)
  starting transfers between devices  17.2 us (1%)
  between operations  15.7 us (1%)
    psum x1, waiting for transfers between devices, on_device(): small_sum, shift_sum = lax.psum((small_stack, shift_stack), ('dp', 'head'))  123 us
    reduce_scatter x1, waiting for transfers between devices, on_device(): lax.psum_scatter(ffn_stack.astype(jnp.bfloat16), 'dp', scatter_dimension=...  112 us
    reduce_scatter x2, waiting for transfers between devices, on_device(): lax.psum_scatter(jnp.einsum('rce,cde->rd', grad_proj, layer_weights, pref...  101 us
    all_gather x2, waiting for transfers between devices, on_device(): lax.all_gather(hidden_state.astype(jnp.bfloat16), 'head', axis=0, tiled=T...  92.3 us
    unnamed x12, waiting for transfers between devices  89.2 us
    dot_general x2, matrix products, on_device(): jnp.dot(ffn_rows, up_part, preferred_element_type=jnp.float32) + up_shift  77.2 us
    unnamed x195, local copies, waits for them, and re-layouts  57.6 us
    dot_general x32, matrix products, slot_scores(): jnp.einsum('qhd,khd->hqk', queries, keys_in, preferred_element_type=jnp.f...  55.1 us
  transfers between devices with their start and end apart: 14, of which 13 were waited for; matrix products, arithmetic and copies ran while one was open for 21% of the time, Pallas kernels for 0%

commit v1 on v0

v1 whole, which is shorter than its diff:
```python
import jax
import jax.numpy as jnp
from jax import lax
from jax.sharding import PartitionSpec as P

HD = 64


EPSILON = 1e-06


def norm_rows(values, gain, shift):
    centre = jnp.mean(values, axis=-1, keepdims=True)
    centred = values - centre
    spread = jnp.mean(centred * centred, axis=-1, keepdims=True)
    return centred * lax.rsqrt(spread + EPSILON) * gain + shift


def exact_gelu(values):
    return jax.nn.gelu(values, approximate=False)


def segment_ids(lengths, slot_rows):
    order = jnp.arange(lengths.shape[1], dtype=jnp.int32)
    upto = order[:, None] <= order[None, :]
    boundary = jnp.sum(jnp.where(upto[None], lengths[:, :, None], 0), axis=1)
    position = jnp.arange(slot_rows, dtype=jnp.int32)
    return jnp.sum((position[None, :, None] >= boundary[:, None, :]).astype(jnp.int32), axis=2)


def slot_scores(queries, keys_in, segments):
    scaling = queries.shape[-1] ** (-0.5)
    scores = (
        jnp.einsum("qhd,khd->hqk", queries, keys_in, preferred_element_type=jnp.float32) * scaling
    )
    inside = (segments[:, None] == segments[None, :])[None]
    return (scores, inside)


def slot_forward(packed):
    queries, keys_in, values_in, segments = packed
    scores, inside = slot_scores(queries, keys_in, segments)
    scores = jnp.where(inside, scores, -1e30)
    peak_score = jnp.max(scores, axis=-1, keepdims=True)
    weights = jnp.exp(scores - peak_score)
    denominator = jnp.sum(weights, axis=-1, keepdims=True)
    probability = (weights / denominator).astype(jnp.bfloat16)
    context = jnp.einsum("hqk,khd->qhd", probability, values_in, preferred_element_type=jnp.float32)
    return (context.astype(jnp.bfloat16), (peak_score + jnp.log(denominator))[..., 0])


def slot_backward(packed):
    queries, keys_in, values_in, grad_context, log_total, segments = packed
    scaling = queries.shape[-1] ** (-0.5)
    scores, inside = slot_scores(queries, keys_in, segments)
    probability = jnp.where(inside, jnp.exp(scores - log_total[..., None]), 0.0)
    grad_prob = jnp.einsum(
        "qhd,khd->hqk", grad_context, values_in, preferred_element_type=jnp.float32
    )
    shares = jnp.sum(probability * grad_prob, axis=-1, keepdims=True)
    grad_score = (probability * (grad_prob - shares)).astype(jnp.bfloat16)
    grad_query = (
        jnp.einsum("hqk,khd->qhd", grad_score, keys_in, preferred_element_type=jnp.float32)
        * scaling
    )
    grad_key = (
        jnp.einsum("hqk,qhd->khd", grad_score, queries, preferred_element_type=jnp.float32)
        * scaling
    )
    grad_value = jnp.einsum(
        "hqk,qhd->khd",
        probability.astype(jnp.bfloat16),
        grad_context,
        preferred_element_type=jnp.float32,
    )
    return (
        grad_query.astype(jnp.bfloat16),
        grad_key.astype(jnp.bfloat16),
        grad_value.astype(jnp.bfloat16),
    )


def chunked(grad, dp_count, head_count):
    rows, columns = grad.shape
    split = grad.reshape(dp_count, rows // dp_count, head_count, columns // head_count)
    return jnp.transpose(split, (0, 2, 1, 3)).reshape(dp_count * head_count, -1, rows)


def on_device(
    tokens,
    seq_lengths,
    qkv_weight,
    qv_bias,
    out_weight,
    out_bias,
    norm1_gain,
    norm1_shift,
    up_weight,
    up_bias,
    down_weight,
    down_bias,
    norm2_gain,
    norm2_shift,
    out_grad,
):
    head_count = lax.axis_size("head")
    dp_count = lax.axis_size("dp")
    head_index = lax.axis_index("head")
    local_rows, model_width = tokens.shape
    slots_group = seq_lengths.shape[0]
    slot_rows = local_rows * head_count // slots_group
    slots = local_rows // slot_rows
    lengths = lax.dynamic_slice_in_dim(seq_lengths, head_index * slots, slots, 0)
    segments = segment_ids(lengths, slot_rows)
    layers = qkv_weight.shape[0]
    heads = model_width // HD
    full_bias = lax.all_gather(qv_bias, "head", axis=2, tiled=True)
    full_qkv = [
        lax.all_gather(qkv_weight[layer], "head", axis=2, tiled=True) for layer in range(layers)
    ]
    hidden_state = tokens.astype(jnp.float32)
    kept = []
    for layer in range(layers):
        rounded = hidden_state.astype(jnp.bfloat16)
        weights = full_qkv[layer]

        def project(which, bias):
            made = jnp.dot(rounded, weights[which], preferred_element_type=jnp.float32)
            if bias is not None:
                made = made + bias
            return made.astype(jnp.bfloat16).reshape(slots, slot_rows, heads, HD)

        queries = project(0, full_bias[layer, 0])
        keys_in = project(1, None)
        values_in = project(2, full_bias[layer, 1])
        context, log_total = lax.map(slot_forward, (queries, keys_in, values_in, segments))
        context = context.reshape(local_rows, model_width)
        attended = (
            jnp.dot(context, out_weight[layer], preferred_element_type=jnp.float32)
            + out_bias[layer]
        )
        first_sum = hidden_state + attended
        normed = norm_rows(first_sum, norm1_gain[layer], norm1_shift[layer])
        normed_low = normed.astype(jnp.bfloat16)
        before_gelu = (
            jnp.dot(normed_low, up_weight[layer], preferred_element_type=jnp.float32)
            + up_bias[layer]
        )
        activated = exact_gelu(before_gelu).astype(jnp.bfloat16)
        branch = jnp.dot(activated, down_weight[layer], preferred_element_type=jnp.float32)
        second_sum = normed + branch + down_bias[layer]
        hidden_state = norm_rows(second_sum, norm2_gain[layer], norm2_shift[layer])
        kept.append(
            (
                rounded,
                queries,
                keys_in,
                values_in,
                log_total,
                context,
                first_sum,
                normed_low,
                before_gelu,
                activated,
                second_sum,
            )
        )
    out_state = hidden_state.astype(jnp.bfloat16)
    grad_state = out_grad.astype(jnp.float32)
    summed = [None] * layers
    small = [None] * layers
    shifts = [None] * layers
    for layer in reversed(range(layers)):
        (
            rounded,
            queries,
            keys_in,
            values_in,
            log_total,
            context,
            first_sum,
            normed_low,
            before_gelu,
            activated,
            second_sum,
        ) = kept[layer]
        pull_second = jax.vjp(norm_rows, second_sum, norm2_gain[layer], norm2_shift[layer])[1]
        grad_second, grad_gain2, grad_shift2 = pull_second(grad_state)
        grad_branch = grad_second.astype(jnp.bfloat16)
        grad_down_shift = jnp.sum(grad_branch.astype(jnp.float32), axis=0)
        grad_down = jnp.einsum(
            "rd,rf->df", grad_branch, activated, preferred_element_type=jnp.float32
        )
        grad_act = jnp.einsum(
            "rd,fd->rf", grad_branch, down_weight[layer], preferred_element_type=jnp.float32
        )
        pull_gelu = jax.vjp(exact_gelu, before_gelu)[1]
        grad_pre = pull_gelu(grad_act)[0].astype(jnp.bfloat16)
        grad_up_shift = jnp.sum(grad_pre.astype(jnp.float32), axis=0)
        grad_up = jnp.einsum("rd,rf->df", normed_low, grad_pre, preferred_element_type=jnp.float32)
        grad_normed = grad_second + jnp.einsum(
            "rf,df->rd", grad_pre, up_weight[layer], preferred_element_type=jnp.float32
        )
        pull_first = jax.vjp(norm_rows, first_sum, norm1_gain[layer], norm1_shift[layer])[1]
        grad_first, grad_gain1, grad_shift1 = pull_first(grad_normed)
        grad_attended = grad_first.astype(jnp.bfloat16)
        grad_out_shift = jnp.sum(grad_attended.astype(jnp.float32), axis=0)
        grad_out = jnp.einsum("rd,re->de", context, grad_attended, preferred_element_type=jnp.float32)
        grad_context = jnp.einsum(
            "re,de->rd", grad_attended, out_weight[layer], preferred_element_type=jnp.float32
        ).astype(jnp.bfloat16)
        parts = lax.map(
            slot_backward,
            (
                queries,
                keys_in,
                values_in,
                grad_context.reshape(slots, slot_rows, heads, HD),
                log_total,
                segments,
            ),
        )
        parts = [part.reshape(local_rows, model_width) for part in parts]
        grad_qkv = [
            jnp.einsum("rd,re->de", rounded, part, preferred_element_type=jnp.float32)
            for part in parts
        ]
        grad_state = grad_first
        for which in range(3):
            grad_state = grad_state + jnp.einsum(
                "re,de->rd",
                parts[which],
                full_qkv[layer][which],
                preferred_element_type=jnp.float32,
            )
        packed = jnp.concatenate(
            [
                chunked(grad.astype(jnp.bfloat16), dp_count, head_count)
                for grad in (grad_up, grad_down, *grad_qkv, grad_out)
            ],
            axis=1,
        )
        summed[layer] = lax.psum_scatter(
            packed, ("dp", "head"), scatter_dimension=0, tiled=True
        )[0].astype(jnp.float32)
        small[layer] = jnp.stack(
            [
                jnp.sum(parts[0].astype(jnp.float32), axis=0),
                jnp.sum(parts[2].astype(jnp.float32), axis=0),
                grad_out_shift,
                grad_gain1,
                grad_shift1,
                grad_down_shift,
                grad_gain2,
                grad_shift2,
            ]
        )
        shifts[layer] = grad_up_shift
    input_grad = grad_state.astype(jnp.bfloat16)
    small_sum, shift_sum = lax.psum((jnp.stack(small), jnp.stack(shifts)), ("dp", "head"))
    sums = jnp.stack(summed)
    dp_rows = model_width // dp_count
    head_width = model_width // head_count
    ffn_width = up_weight.shape[2] // head_count
    tall = dp_rows * ffn_width // model_width
    short = dp_rows * head_width // model_width
    up_sum = sums[:, :tall].reshape(layers, dp_rows, ffn_width)
    down_sum = sums[:, tall : 2 * tall].reshape(layers, dp_rows, ffn_width)
    wide = sums[:, 2 * tall :].reshape(layers, 4, dp_rows, head_width)
    return (
        out_state,
        input_grad,
        wide[:, :3],
        small_sum[:, 0:2],
        wide[:, 3],
        small_sum[:, 2],
        small_sum[:, 3],
        small_sum[:, 4],
        up_sum,
        shift_sum,
        jnp.transpose(down_sum, (0, 2, 1)),
        small_sum[:, 5],
        small_sum[:, 6],
        small_sum[:, 7],
    )


def solution(mesh):
    in_specs = (
        P(("dp", "head"), None),
        P("dp", None),
        P(None, None, None, "head"),
        P(None, None, "head"),
        P(),
        P(),
        P(),
        P(),
        P(),
        P(),
        P(),
        P(),
        P(),
        P(),
        P(("dp", "head"), None),
    )
    out_specs = (
        P(("dp", "head"), None),
        P(("dp", "head"), None),
        P(None, None, "dp", "head"),
        P(),
        P(None, "dp", "head"),
        P(),
        P(),
        P(),
        P(None, "dp", "head"),
        P(),
        P(None, "head", "dp"),
        P(),
        P(),
        P(),
    )
    return jax.shard_map(
        on_device, mesh=mesh, in_specs=in_specs, out_specs=out_specs, check_vma=False
    )
```

time: 1420 us -> 1060 us (0.75)
  waiting for transfers between devices: 610 us -> 324 us
  matrix products: 475 us -> 349 us
  local copies, waits for them, and re-layouts: 185 us -> 291 us
  other arithmetic: 102 us -> 61.2 us
  starting transfers between devices: 17.2 us -> 0.2 us
    psum x1, waiting for transfers between devices: 123 us -> 0.01 us  [on_device(): lax.psum((jnp.stack(small), jnp.stack(shifts)), ('dp', 'head'))]
    reshape x2 -> x29, local copies, waits for them, and re-layouts: 5.61 us -> 109 us  [the longest x12 64.6 us: chunked(): grad.reshape(dp_count, rows // dp_count, head_count, columns // head_count)]
    unnamed x12 -> x5, waiting for transfers between devices: 89.2 us -> 0.76 us
    all_gather x2, waiting for transfers between devices: 92.3 us -> 4.75 us  [on_device(): lax.all_gather(qkv_weight[layer], 'head', axis=2, tiled=True)]
    reduce_scatter x5 -> x2, waiting for transfers between devices: 243 us -> 319 us  [on_device(): lax.psum_scatter(packed, ('dp', 'head'), scatter_dimension=0, tiled=True)[0]]
    all_to_all x4 -> x0, waiting for transfers between devices: 62.8 us -> none  [the longest x2 32.8 us: on_device(): lax.all_to_all(context, 'head', split_axis=0, concat_axis=1, tiled=True)]
    dot_general x32 -> x8, matrix products: 55.1 us -> 15.8 us  [slot_scores(): jnp.einsum('qhd,khd->hqk', queries, keys_in, preferred_element_type=jnp.f...]
    transpose x1 -> x13, local copies, waits for them, and re-layouts: 1.09 us -> 37.9 us  [the longest x12 36.8 us: chunked(): jnp.transpose(split, (0, 2, 1, 3)).reshape(dp_count * head_count, -1, rows)]
  transfers between devices with their start and end apart: 14 -> 5, of which waited for: 13 -> 3; matrix products, arithmetic and copies ran while one was open for 21% -> 24% of each run, Pallas kernels for 0% -> 0%
where the time goes in v1:
time: 1060 us; the launch traced here: 1050 us
  matrix products  349 us (33%)
  waiting for transfers between devices  324 us (31%)
  local copies, waits for them, and re-layouts  291 us (27%)
  other arithmetic  61.2 us (6%)
  between operations  16.1 us (2%)
    reduce_scatter x2, waiting for transfers between devices, on_device(): lax.psum_scatter(packed, ('dp', 'head'), scatter_dimension=0, tiled=True)[0]  319 us
    dot_general x2, matrix products, on_device(): jnp.dot(normed_low, up_weight[layer], preferred_element_type=jnp.float32)  77.9 us
    reshape x12, local copies, waits for them, and re-layouts, chunked(): grad.reshape(dp_count, rows // dp_count, head_count, columns // head_count)  64.6 us
    unnamed x321, local copies, waits for them, and re-layouts  58.9 us
    dot_general x2, matrix products, on_device(): jnp.einsum('rd,fd->rf', grad_branch, down_weight[layer], preferred_elemen...  37.2 us
    transpose x12, local copies, waits for them, and re-layouts, chunked(): jnp.transpose(split, (0, 2, 1, 3)).reshape(dp_count * head_count, -1, rows)  36.8 us
    reshape x8, local copies, waits for them, and re-layouts, chunked(): jnp.transpose(split, (0, 2, 1, 3)).reshape(dp_count * head_count, -1, rows)  30.2 us
    convert_element_type x4, other arithmetic, slot_backward(): grad_score = (probability * (grad_prob - shares)).astype(jnp.bfloat16)  26.9 us
  transfers between devices with their start and end apart: 5, of which 3 were waited for; matrix products, arithmetic and copies ran while one was open for 24% of the time, Pallas kernels for 0%

profile of v1, /device:TPU:0, one launch (start us, length us, event | category | flops | bytes accessed | tf_op | source)
XLA Modules:
  0.0 1053.8 jit_solution(1845226687353587301)
XLA Ops:
  13.1 10.0 all_gather.10
  23.2 10.7 %slice_reduce_fusion = (f32[768]{0:T(1024)}, f32[768]{0:T(1024)}, f32[768]{0:T(1024)S(1)}, f32[768]{0:T(1024)S(1)}) fusion(f32[2,2,768]{1,0,2:T(2,128)S(1)} %all_gather.10), kind=kLoop, calls=%fused_computation.277 | loop fusion | bytes 24576 | tf_op jit(solution)/shard_map/slice | solution.py:133
  74.1 20.9 %while.52 = (s32[]{:T(128)}, bf16[2,512,12,64]{1,3,2,0:T(8,128)(2,1)}, f32[2,12,512]{2,1,0:T(8,128)S(1)}, bf16[2,512,12,64]{1,3,2,0:T(8,128)(2,1)}, s32[2,512]{1...) while((s32[]{:T(128)}, ...), condition=%wide.region_5.6_spmd, body=%wide.region_2.5_spmd.sunk | while | flops 843704320 | bytes 42172516 | solution.py:136
  102.5 38.9 %multiply_convert_fusion.7 = (bf16[1024,3072]{1,0:T(8,128)(2,1)}, f32[1024,3072]{1,0:T(8,128)}, f32[1024,3072]{1,0:T(8,128)}) fusion(f32[3072]{0:T(1024)S(1)} %bitcast.510, bf16[2,768,3072]{2,1,0:T(8,128)(2,1)} %param.31, f32[1024,768]{0,1:T(8,128)S(1)} %get-tuple-element.591, f32[768]{0:T(1024)S(1)} %get-tuple-element.475, ...), kind=kOutput, calls=%fused_computation.149 | convolution fusion | flops 5043388416 | bytes 39348224 | tf_op jit(solution)/shard_map/dot_general | solution.py:146
  141.5 8.8 fusion.195
  182.3 20.7 %while.53 = (s32[]{:T(128)}, bf16[2,512,12,64]{1,3,2,0:T(8,128)(2,1)}, f32[2,12,512]{2,1,0:T(8,128)S(1)}, bf16[2,512,12,64]{1,3,2,0:T(8,128)(2,1)}, s32[2,512]{1...) while((s32[]{:T(128)}, ...), condition=%wide.region_13.14_spmd, body=%wide.region_10.13_spmd.sunk | while | flops 843704320 | bytes 42172516 | solution.py:136
  210.7 39.0 %multiply_convert_fusion.6 = (bf16[1024,3072]{1,0:T(8,128)(2,1)}, f32[1024,3072]{1,0:T(8,128)}, f32[1024,3072]{1,0:T(8,128)}) fusion(f32[3072]{0:T(1024)S(1)} %bitcast.513, bf16[2,768,3072]{2,1,0:T(8,128)(2,1)} %param.31, f32[1024,768]{0,1:T(8,128)S(1)} %get-tuple-element.596, f32[768]{0:T(1024)S(1)} %copy-done.134, f32[768]{0:T(1024)S(1)} %copy-done.102, ...), kind=kOutput, calls=%fused_computation.136 | convolution fusion | flops 5043388416 | bytes 39348224 | tf_op jit(solution)/shard_map/dot_general | solution.py:146
  249.8 8.8 fusion.197
  265.9 18.1 %convert_reduce_fusion = (f32[3072]{0:T(1024)}, bf16[1024,3072]{1,0:T(8,128)(2,1)}) fusion(f32[1024,3072]{1,0:T(8,128)} %get-tuple-element.563, bf16[1024,768]{0,1:T(8,128)(2,1)S(1)} %get-tuple-element.553, bf16[2,3072,768]{2,1,0:T(8,128)(2,1)} %param.33, f32[1024,3072]{1,0:T(8,128)} %get-tuple-element.597, f32[3072]{0:T(1024)S(1)} %bitcast.514), kind=kOutput, calls=%fused_computation.132 | convolution fusion | flops 4885312512 | bytes 37773312 | tf_op jit(solution)/shard_map/rd,fd->rf/dot_general | solution.py:194
  284.0 11.7 %multiply_reduce_fusion.2 = (f32[768]{0:T(1024)}, f32[1024]{0:T(1024)S(1)}, f32[768]{0:T(1024)}, f32[1024,768]{0,1:T(8,128)S(1)}) fusion(f32[1024,768]{0,1:T(8,128)} %copy-done.28, f32[1024]{0:T(1024)S(1)} %fusion.180, f32[1024]{0:T(1024)S(1)} %broadcast_multiply_fusion.1, f32[768]{0:T(1024)S(1)} %copy-done.102, ...), kind=kOutput, calls=%fused_computation.202 | convolution fusion | flops 4845204480 | bytes 22061056 | tf_op jit(solution)/shard_map/rf,df->rd/dot_general | solution.py:201
  309.3 47.2 %while.54 = (s32[]{:T(128)}, bf16[2,512,12,64]{1,3,2,0:T(8,128)(2,1)}, bf16[2,512,12,64]{1,3,2,0:T(8,128)(2,1)}, bf16[2,512,12,64]{1,3,2,0:T(8,128)(2,1)}, bf16[...) while((s32[]{:T(128)}, ...), condition=%wide.region_24.25_spmd, body=%wide.region_22.24_spmd.sunk | while | flops 2062673920 | bytes 141233456 | solution.py:212
  388.2 19.1 %convert_reduce_fusion.1 = (f32[3072]{0:T(1024)}, bf16[1024,3072]{1,0:T(8,128)(2,1)}) fusion(f32[1024,3072]{1,0:T(8,128)} %get-tuple-element.565, bf16[1024,768]{0,1:T(8,128)(2,1)} %copy-done.67, bf16[2,3072,768]{2,1,0:T(8,128)(2,1)} %param.33, f32[1024,3072]{1,0:T(8,128)} %get-tuple-element.592, f32[3072]{0:T(1024)S(1)} %bitcast.511), kind=kOutput, calls=%fused_computation.133 | convolution fusion | flops 4885312512 | bytes 37773312 | tf_op jit(solution)/shard_map/rd,fd->rf/dot_general | solution.py:194
  407.4 10.5 multiply_reduce_fusion.4
  417.9 7.1 convolution_convert_fusion.3
  439.7 46.9 %while.55 = (s32[]{:T(128)}, bf16[2,512,12,64]{1,3,2,0:T(8,128)(2,1)}, bf16[2,512,12,64]{1,3,2,0:T(8,128)(2,1)}, bf16[2,512,12,64]{1,3,2,0:T(8,128)(2,1)}, bf16[...) while((s32[]{:T(128)}, ...), condition=%wide.region_31.32_spmd, body=%wide.region_29.31_spmd.sunk | while | flops 2062673920 | bytes 141233456 | solution.py:212
  452.3 6.7 multiply_convert_fusion.11
  495.2 9.9 reshape.507
  510.4 9.7 reshape.505
  595.8 9.9 convolution_convert_fusion
  605.7 9.8 reshape.519
  621.0 9.8 convolution_convert_fusion.1
  630.9 9.8 reshape.517
  723.4 151.3 %reduce-scatter.3.cloned.1.call-done = bf16[1,288,768]{2,1,0:T(8,128)(2,1)} async-done(((bf16[32,288,768]{2,1,0:T(8,128)(2,1)}), bf16[1,288,768]{2,1,0:T(8,128)(2,1)}) %reduce-scatter.3.cloned.1.call-update) | async-done | bytes 442384 | tf_op jit(solution)/shard_map/reduce_scatter | solution.py:243
  874.6 167.5 %reduce-scatter.5.cloned.1.call-done = bf16[1,288,768]{2,1,0:T(8,128)(2,1)} async-done(((bf16[32,288,768]{2,1,0:T(8,128)(2,1)}), bf16[1,288,768]{2,1,0:T(8,128)(2,1)}) %reduce-scatter.5.cloned.1.call-update) | async-done | bytes 442384 | tf_op jit(solution)/shard_map/reduce_scatter | solution.py:243
  (613 shorter events, 468.7 us)
Async XLA Ops:
  7.2 36.5 %all-gather.5.cloned.1.call-start = ((), (), s32[]{:S(2)}) async-start(), calls=%async_computation.4 | async-start | bytes 4423680 | tf_op jit(solution)/shard_map/all_gather | solution.py:119
  10.1 142.5 %all-gather.7.cloned.1.call-start = ((), (), s32[]{:S(2)}) async-start(), calls=%async_computation.5 | async-start | bytes 4423680 | tf_op jit(solution)/shard_map/all_gather | solution.py:119
  10.8 709.8 %all-reduce.3.cloned.1.call-start = ((), (), s32[]{:S(2)}) async-start(), calls=%async_computation.6 | async-start | bytes 147456 | tf_op jit(solution)/shard_map/psum | solution.py:260
  39.0 102.4 %copy-start.104 = (f32[768]{0:T(1024)}, f32[768]{0:T(1024)S(1)}, u32[]{:S(2)}) copy-start(f32[768]{0:T(1024)S(1)} %get-tuple-element.607) | copy-start | bytes 9220
  39.0 102.4 %copy-start.136 = (f32[768]{0:T(1024)}, f32[768]{0:T(1024)S(1)}, u32[]{:S(2)}) copy-start(f32[768]{0:T(1024)S(1)} %get-tuple-element.475) | copy-start | bytes 9220
  99.8 41.7 %slice-start.2 = ((s8[9437184]{0:T(1024)(128)(4,1)}), s8[1048576]{0:T(1024)(128)(4,1)S(1)}, s32[]{:S(2)}) async-start(s8[9437184]{0:T(1024)(128)(4,1)} %bitcast.516), calls=%async_computation.9 | async-start | bytes 2097152
  101.5 40.0 %copy-start.31 = (f32[1024,768]{0,1:T(8,128)}, f32[1024,768]{0,1:T(8,128)S(1)}, u32[]{:S(2)}) copy-start(f32[1024,768]{0,1:T(8,128)S(1)} %get-tuple-element.591) | copy-start | bytes 9437188
  101.5 39.9 %copy-start.88 = (f32[1024]{0:T(1024)}, f32[1024]{0:T(1024)S(1)}, u32[]{:S(2)}) copy-start(f32[1024]{0:T(1024)S(1)} %broadcast_multiply_fusion.3) | copy-start | bytes 12292
  102.5 39.0 %copy-start.115 = (f32[1024]{0:T(1024)}, f32[1024]{0:T(1024)S(1)}, u32[]{:S(2)}) copy-start(f32[1024]{0:T(1024)S(1)} %fusion.178) | copy-start | bytes 12292
  102.5 39.0 %copy-start.140 = (f32[768]{0:T(1024)S(1)}, f32[768]{0:T(1024)}, u32[]{:S(2)}) copy-start(f32[768]{0:T(1024)} %get-tuple-element.471) | copy-start | bytes 9220
  102.5 39.0 %slice-start.3 = ((s8[9437184]{0:T(1024)(128)(4,1)}), s8[4194304]{0:T(1024)(128)(4,1)S(1)}, s32[]{:S(2)}) async-start(s8[9437184]{0:T(1024)(128)(4,1)} %bitcast.516), calls=%async_computation.10 | async-start | bytes 8388608
  102.5 39.0 %slice-start.4 = ((s8[9437184]{0:T(1024)(128)(4,1)}), s8[4194304]{0:T(1024)(128)(4,1)S(1)}, s32[]{:S(2)}) async-start(s8[9437184]{0:T(1024)(128)(4,1)} %bitcast.516), calls=%async_computation.11 | async-start | bytes 8388608
  150.3 57.4 %copy-start.77 = (f32[1024]{0:T(1024)}, f32[1024]{0:T(1024)S(1)}, u32[]{:S(2)}) copy-start(f32[1024]{0:T(1024)S(1)} %broadcast_multiply_fusion.2) | copy-start | bytes 12292
  150.8 57.0 %copy-start.82 = (f32[1024]{0:T(1024)}, f32[1024]{0:T(1024)S(1)}, u32[]{:S(2)}) copy-start(f32[1024]{0:T(1024)S(1)} %fusion.179) | copy-start | bytes 12292
  207.8 42.0 %slice-start.5 = ((s8[9437184]{0:T(1024)(128)(4,1)}), s8[4194304]{0:T(1024)(128)(4,1)S(1)}, s32[]{:S(2)}) async-start(s8[9437184]{0:T(1024)(128)(4,1)} %bitcast.518), calls=%async_computation.12 | async-start | bytes 8388608
  209.9 39.8 %copy-start.28 = (f32[1024,768]{0,1:T(8,128)}, f32[1024,768]{0,1:T(8,128)S(1)}, u32[]{:S(2)}) copy-start(f32[1024,768]{0,1:T(8,128)S(1)} %get-tuple-element.596) | copy-start | bytes 9437188
  210.0 85.8 %copy-start.86 = (f32[1024]{0:T(1024)}, f32[1024]{0:T(1024)S(1)}, u32[]{:S(2)}) copy-start(f32[1024]{0:T(1024)S(1)} %broadcast_multiply_fusion.1) | copy-start | bytes 12292
  210.4 39.4 %copy-start.94 = (f32[1024]{0:T(1024)}, f32[1024]{0:T(1024)S(1)}, u32[]{:S(2)}) copy-start(f32[1024]{0:T(1024)S(1)} %multiply_reduce_fusion.9) | copy-start | bytes 12292
  210.4 85.4 %copy-start.113 = (f32[1024]{0:T(1024)}, f32[1024]{0:T(1024)S(1)}, u32[]{:S(2)}) copy-start(f32[1024]{0:T(1024)S(1)} %fusion.180) | copy-start | bytes 12292
  210.7 39.0 %copy-start.138 = (f32[768]{0:T(1024)S(1)}, f32[768]{0:T(1024)}, u32[]{:S(2)}) copy-start(f32[768]{0:T(1024)} %get-tuple-element.470) | copy-start | bytes 9220
  210.7 39.1 %slice-start.6 = ((s8[9437184]{0:T(1024)(128)(4,1)}), s8[4194304]{0:T(1024)(128)(4,1)S(1)}, s32[]{:S(2)}) async-start(s8[9437184]{0:T(1024)(128)(4,1)} %bitcast.518), calls=%async_computation.13 | async-start | bytes 8388608
  210.7 39.1 %slice-start.7 = ((s8[9437184]{0:T(1024)(128)(4,1)}), s8[1048576]{0:T(1024)(128)(4,1)S(1)}, s32[]{:S(2)}) async-start(s8[9437184]{0:T(1024)(128)(4,1)} %bitcast.518), calls=%async_computation.14 | async-start | bytes 2097152
  585.0 289.7 %reduce-scatter.3.cloned.1.call-start = ((), (), s32[]{:S(2)}) async-start(), calls=%async_computation.2 | async-start | bytes 14598144 | tf_op jit(solution)/shard_map/reduce_scatter | solution.py:243
  594.4 447.7 %reduce-scatter.5.cloned.1.call-start = ((), (), s32[]{:S(2)}) async-start(), calls=%async_computation.3 | async-start | bytes 14598144 | tf_op jit(solution)/shard_map/reduce_scatter | solution.py:243
  (153 other events, 679.6 us)
Sparse Core Ops, SparseCore 0:
  10.2 33.4 all-gather.4
  45.3 30.7 all-gather.6
  585.1 118.6 all-reduce.2
  709.6 164.9 reduce-scatter.2
  880.5 161.5 reduce-scatter.4

commit v2 on v1

v2 whole, which is shorter than its diff:
```python
import functools

import jax
import jax.numpy as jnp
from jax import lax
from jax.experimental import pallas as pl
from jax.experimental.pallas import tpu as pltpu
from jax.sharding import PartitionSpec as P

HD = 64
EPSILON = 1e-06
GROUP = 256
LOW = jnp.bfloat16
WIDE = jnp.float32
VMEM_BYTES = 56 << 20
ROOT_HALF = 0.7071067811865476
INV_ROOT_TAU = 0.3989422804014327


def row_stats(values):
    centre = jnp.mean(values, axis=-1, keepdims=True)
    centred = values - centre
    spread = jnp.mean(centred * centred, axis=-1, keepdims=True)
    inverse = lax.rsqrt(spread + EPSILON)
    return centred * inverse, inverse


def dot_nn(left, right):
    return jnp.dot(left, right, preferred_element_type=WIDE)


def dot_nt(left, right):
    return lax.dot_general(left, right, (((1,), (1,)), ((), ())), preferred_element_type=WIDE)


def dot_tn(left, right):
    return lax.dot_general(left, right, (((0,), (0,)), ((), ())), preferred_element_type=WIDE)


def ffn_forward_kernel(
    o_ref, x_ref, wo_ref, wu_ref, wd_ref, bu_ref, small_ref,
    u1_ref, hr_ref, gr_ref, gp_ref, u2_ref, *outs, chunk,
):
    attended = dot_nn(o_ref[...], wo_ref[...])
    u1 = x_ref[...].astype(WIDE) + attended + small_ref[0:1]
    u1_ref[...] = u1
    xhat, _ = row_stats(u1)
    normed = xhat * small_ref[1:2] + small_ref[2:3]
    hr = normed.astype(LOW)
    hr_ref[...] = hr
    total = normed + small_ref[3:4]
    for start in range(0, wu_ref.shape[1], chunk):
        at = slice(start, start + chunk)
        z = dot_nn(hr, wu_ref[:, at]) + bu_ref[:, at]
        g, slope = gelu_pair(z)
        gr = g.astype(LOW)
        gr_ref[:, at] = gr
        gp_ref[:, at] = slope.astype(LOW)
        total = total + dot_nn(gr, wd_ref[at, :])
    u2_ref[...] = total
    xhat, _ = row_stats(total)
    made = xhat * small_ref[4:5] + small_ref[5:6]
    for out in outs:
        out[...] = made.astype(out.dtype)


def whole(array):
    return pl.BlockSpec(array.shape, lambda *ids: (0,) * array.ndim, pipeline_mode=pl.Buffered(1))


def params():
    return pltpu.CompilerParams(vmem_limit_bytes=VMEM_BYTES)


def rows_spec(tile, width):
    return pl.BlockSpec((tile, width), lambda i: (i, 0))


def ffn_forward(o, x, wo, wu, wd, bu, small, out_types, tile=256, chunk=512):
    rows, width = o.shape
    hidden = wu.shape[1]
    made = lambda w, t: jax.ShapeDtypeStruct((rows, w), t)
    outs = [made(width, WIDE), made(width, LOW), made(hidden, LOW), made(hidden, LOW), made(width, WIDE)]
    outs += [made(width, t) for t in out_types]
    return pl.pallas_call(
        functools.partial(ffn_forward_kernel, chunk=chunk),
        grid=(rows // tile,),
        in_specs=[rows_spec(tile, width), rows_spec(tile, width), whole(wo), whole(wu), whole(wd), whole(bu), whole(small)],
        out_specs=[rows_spec(tile, s.shape[1]) for s in outs],
        out_shape=outs,
        compiler_params=params(),
        name="ffn_forward",
    )(o, x, wo, wu, wd, bu, small)


def norm_backward(upstream, xhat, inverse, gain):
    scaled = upstream * gain
    first = jnp.mean(scaled, axis=-1, keepdims=True)
    second = jnp.mean(scaled * xhat, axis=-1, keepdims=True)
    return (scaled - first - xhat * second) * inverse


def column_sum(values):
    return jnp.sum(values, axis=0, keepdims=True)


def ffn_backward_kernel(
    gx_ref, u2_ref, u1_ref, gp_ref, wd_ref, wu_ref, wo_ref, gain_ref,
    df_ref, dz_ref, da_ref, do_ref, du_ref, sums_ref, zsum_ref, *, chunk,
):
    @pl.when(pl.program_id(0) == 0)
    def _():
        sums_ref[...] = jnp.zeros_like(sums_ref)
        zsum_ref[...] = jnp.zeros_like(zsum_ref)

    gx = gx_ref[...].astype(WIDE)
    xhat, inverse = row_stats(u2_ref[...])
    sums_ref[0:1] += column_sum(gx * xhat)
    sums_ref[1:2] += column_sum(gx)
    gv = norm_backward(gx, xhat, inverse, gain_ref[1:2])
    df = gv.astype(LOW)
    df_ref[...] = df
    sums_ref[2:3] += column_sum(df.astype(WIDE))
    total = gv
    for start in range(0, wu_ref.shape[1], chunk):
        at = slice(start, start + chunk)
        dg = dot_nt(df, wd_ref[at, :])
        dz = (dg * gp_ref[:, at].astype(WIDE)).astype(LOW)
        dz_ref[:, at] = dz
        zsum_ref[:, at] += column_sum(dz.astype(WIDE))
        total = total + dot_nt(dz, wu_ref[:, at])
    xhat, inverse = row_stats(u1_ref[...])
    sums_ref[3:4] += column_sum(total * xhat)
    sums_ref[4:5] += column_sum(total)
    du = norm_backward(total, xhat, inverse, gain_ref[0:1])
    du_ref[...] = du
    da = du.astype(LOW)
    da_ref[...] = da
    sums_ref[5:6] += column_sum(da.astype(WIDE))
    do_ref[...] = dot_nt(da, wo_ref[...]).astype(LOW)


def ffn_backward(gx, u2, u1, gp, wd, wu, wo, gains, tile=256, chunk=512):
    rows, width = gx.shape
    hidden = wu.shape[1]
    made = lambda w, t: jax.ShapeDtypeStruct((rows, w), t)
    outs = [made(width, LOW), made(hidden, LOW), made(width, LOW), made(width, LOW), made(width, WIDE)]
    sums = [jax.ShapeDtypeStruct((8, width), WIDE), jax.ShapeDtypeStruct((1, hidden), WIDE)]
    keep = lambda s: pl.BlockSpec(s.shape, lambda i: (0, 0))
    return pl.pallas_call(
        functools.partial(ffn_backward_kernel, chunk=chunk),
        grid=(rows // tile,),
        in_specs=[rows_spec(tile, width)] * 3 + [rows_spec(tile, hidden)] + [whole(wd), whole(wu), whole(wo), whole(gains)],
        out_specs=[rows_spec(tile, s.shape[1]) for s in outs] + [keep(s) for s in sums],
        out_shape=outs + sums,
        compiler_params=params(),
        name="ffn_backward",
    )(gx, u2, u1, gp, wd, wu, wo, gains)


def weight_grad_kernel(a_ref, b_ref, out_ref, t_ref):
    @pl.when(pl.program_id(0) == 0)
    def _():
        t_ref[...] = a_ref[...].T

    out_ref[...] = dot_nn(t_ref[...], b_ref[...]).astype(LOW)


def weight_grad(a, b, width):
    rows, depth = a.shape
    count = b.shape[1] // width
    return pl.pallas_call(
        weight_grad_kernel,
        grid=(count,),
        in_specs=[whole(a), pl.BlockSpec((rows, width), lambda i: (0, i))],
        out_specs=pl.BlockSpec((None, depth, width), lambda i: (i, 0, 0)),
        out_shape=jax.ShapeDtypeStruct((count, depth, width), LOW),
        scratch_shapes=[pltpu.VMEM((depth, rows), LOW)],
        compiler_params=params(),
        name="weight_grad",
    )(a, b)


def gelu_pair(z):
    cdf = 0.5 + 0.5 * lax.erf(z * ROOT_HALF)
    return z * cdf, cdf + z * (jnp.exp(z * z * -0.5) * INV_ROOT_TAU)


def head_lanes(group):
    return lax.broadcasted_iota(jnp.int32, (1, group), 1) // HD


def pick(mask, values):
    return jnp.where(mask, values, jnp.zeros_like(values))


def attention_forward_kernel(
    x_ref, w_ref, b_ref, bias_ref, q_ref, k_ref, v_ref, p_ref, o_ref, s_ref, *, tile
):
    rows, group = q_ref.shape
    x = x_ref[...]
    q = ((dot_nn(x, w_ref[0]) + b_ref[0]).astype(LOW) * HD**-0.5).astype(LOW)
    k = dot_nn(x, w_ref[1]).astype(LOW)
    v = (dot_nn(x, w_ref[2]) + b_ref[1]).astype(LOW)
    q_ref[...] = q
    k_ref[...] = k
    v_ref[...] = v
    lanes = head_lanes(group)
    total = None
    for head in range(group // HD):
        mask = lanes == head
        s_ref[head] = dot_nt(pick(mask, q), k)
        for start in range(0, rows, tile):
            at = slice(start, start + tile)
            s = s_ref[head, at] + bias_ref[at]
            e = jnp.exp(s - jnp.max(s, axis=1, keepdims=True))
            p_ref[head, at] = (e * (1.0 / jnp.sum(e, axis=1, keepdims=True))).astype(LOW)
        part = dot_nn(p_ref[head], pick(mask, v))
        total = part if total is None else total + part
    o_ref[...] = total.astype(LOW)


def attention_forward(x, w, qv_bias, bias, tile=64):
    rows, width = x.shape
    slots, slot_rows, _ = bias.shape
    groups = width // GROUP
    per = GROUP // HD
    row = pl.BlockSpec((slot_rows, GROUP), lambda s, g: (s, g))
    made = jax.ShapeDtypeStruct((rows, width), LOW)
    probs = jax.ShapeDtypeStruct((slots * groups * per, slot_rows, slot_rows), LOW)
    return pl.pallas_call(
        functools.partial(attention_forward_kernel, tile=tile),
        grid=(slots, groups),
        in_specs=[
            pl.BlockSpec((slot_rows, width), lambda s, g: (s, 0)),
            pl.BlockSpec((3, width, GROUP), lambda s, g: (0, 0, g)),
            pl.BlockSpec((2, 1, GROUP), lambda s, g: (0, 0, g)),
            pl.BlockSpec((None, slot_rows, slot_rows), lambda s, g: (s, 0, 0)),
        ],
        out_specs=[row, row, row, pl.BlockSpec((per, slot_rows, slot_rows), lambda s, g: (s * groups + g, 0, 0)), row],
        out_shape=[made, made, made, probs, made],
        scratch_shapes=[pltpu.VMEM((per, slot_rows, slot_rows), WIDE)],
        compiler_params=params(),
        name="attention_forward",
    )(x, w, qv_bias, bias)


def attention_backward_kernel(
    q_ref, k_ref, v_ref, do_ref, p_ref, dq_ref, dk_ref, dv_ref, sums_ref, t_ref, ds_ref, *, tile
):
    rows, group = q_ref.shape
    lanes = head_lanes(group)
    dq = dk = dv = None
    for head in range(group // HD):
        mask = lanes == head
        do = pick(mask, do_ref[...])
        t_ref[head] = dot_nt(do, v_ref[...])
        for start in range(0, rows, tile):
            at = slice(start, start + tile)
            p = p_ref[head, at].astype(WIDE)
            dp = t_ref[head, at]
            share = jnp.sum(p * dp, axis=1, keepdims=True)
            ds_ref[head, at] = (p * (dp - share)).astype(LOW)
        parts = (
            dot_nn(ds_ref[head], pick(mask, k_ref[...])),
            dot_tn(ds_ref[head], pick(mask, q_ref[...])),
            dot_tn(p_ref[head], do),
        )
        dq, dk, dv = parts if dq is None else (dq + parts[0], dk + parts[1], dv + parts[2])
    dq = (dq * HD**-0.5).astype(LOW)
    dv = dv.astype(LOW)
    dq_ref[...] = dq
    dk_ref[...] = dk.astype(LOW)
    dv_ref[...] = dv

    @pl.when(pl.program_id(1) == 0)
    def _():
        sums_ref[...] = jnp.zeros_like(sums_ref)

    sums_ref[0:1] += column_sum(dq.astype(WIDE))
    sums_ref[1:2] += column_sum(dv.astype(WIDE))


def attention_backward(q, k, v, do, p, tile=64):
    rows, width = q.shape
    slot_rows = p.shape[1]
    slots = rows // slot_rows
    groups = width // GROUP
    per = GROUP // HD
    row = pl.BlockSpec((slot_rows, GROUP), lambda g, s: (s, g))
    made = jax.ShapeDtypeStruct((rows, width), LOW)
    return pl.pallas_call(
        functools.partial(attention_backward_kernel, tile=tile),
        grid=(groups, slots),
        in_specs=[row] * 4 + [pl.BlockSpec((per, slot_rows, slot_rows), lambda g, s: (s * groups + g, 0, 0))],
        out_specs=[row] * 3 + [pl.BlockSpec((8, GROUP), lambda g, s: (0, g))],
        out_shape=[made] * 3 + [jax.ShapeDtypeStruct((8, width), WIDE)],
        scratch_shapes=[pltpu.VMEM((per, slot_rows, slot_rows), WIDE), pltpu.VMEM((per, slot_rows, slot_rows), LOW)],
        compiler_params=params(),
        name="attention_backward",
    )(q, k, v, do, p)


def mask_kernel(base_ref, lengths_ref, bias_ref):
    slots, rows, _ = bias_ref.shape
    count = lengths_ref.shape[1]
    across = lax.broadcasted_iota(jnp.int32, (8, rows), 1)
    down = lax.broadcasted_iota(jnp.int32, (rows, 128), 0)
    for slot in range(slots):
        reach = jnp.int32(0)
        seg_across = jnp.zeros((8, rows), jnp.int32)
        seg_down = jnp.zeros((rows, 128), jnp.int32)
        for k in range(count):
            reach = reach + lengths_ref[base_ref[0] + slot, k]
            seg_across += (across >= reach).astype(jnp.int32)
            seg_down += (down >= reach).astype(jnp.int32)
        inside = seg_down[:, 0:1] == seg_across[0:1, :]
        bias_ref[slot] = jnp.where(inside, 0.0, -1e30)


def mask_bias(lengths, base, slots, slot_rows):
    smem = pl.BlockSpec(memory_space=pltpu.SMEM)
    return pl.pallas_call(
        mask_kernel,
        in_specs=[smem, smem],
        out_shape=jax.ShapeDtypeStruct((slots, slot_rows, slot_rows), WIDE),
        compiler_params=params(),
        name="mask_bias",
    )(base, lengths)


def qkv_grads(x, o, dq, dk, dv, da, heads):
    rows, depth = x.shape
    part = depth // heads

    def kernel(x_ref, o_ref, dq_ref, dk_ref, dv_ref, da_ref, out_ref, xt_ref, ot_ref):
        @pl.when(pl.program_id(0) == 0)
        def _():
            xt_ref[...] = x_ref[...].T
            ot_ref[...] = o_ref[...].T

        for head in range(heads):

            @pl.when(pl.program_id(0) == head)
            def _():
                at = slice(head * part, (head + 1) * part)
                joined = jnp.concatenate([dq_ref[:, at], dk_ref[:, at], dv_ref[:, at]], axis=1)
                first = dot_nn(xt_ref[...], joined)
                second = dot_nn(ot_ref[...], da_ref[:, at])
                out_ref[...] = jnp.concatenate([first, second], axis=1).astype(LOW)

    return pl.pallas_call(
        kernel,
        grid=(heads,),
        in_specs=[whole(v) for v in (x, o, dq, dk, dv, da)],
        out_specs=pl.BlockSpec((None, depth, 4 * part), lambda i: (i, 0, 0)),
        out_shape=jax.ShapeDtypeStruct((heads, depth, 4 * part), LOW),
        scratch_shapes=[pltpu.VMEM((depth, rows), LOW)] * 2,
        compiler_params=params(),
        name="qkv_grads",
    )(x, o, dq, dk, dv, da)


def input_grad_kernel(du_ref, dq_ref, dk_ref, dv_ref, w_ref, out_ref):
    total = du_ref[...]
    for which, part in enumerate((dq_ref, dk_ref, dv_ref)):
        total = total + dot_nt(part[...], w_ref[which])
    out_ref[...] = total.astype(out_ref.dtype)


def input_grad(du, dq, dk, dv, w, out_type, tile=256):
    rows, width = du.shape
    return pl.pallas_call(
        input_grad_kernel,
        grid=(rows // tile,),
        in_specs=[rows_spec(tile, width)] * 4 + [whole(w)],
        out_specs=rows_spec(tile, width),
        out_shape=jax.ShapeDtypeStruct((rows, width), out_type),
        compiler_params=params(),
        name="input_grad",
    )(du, dq, dk, dv, w)


def bits_of(axis):
    size = lax.axis_size(axis)
    return [1 << bit for bit in range(size.bit_length() - 1)]


def swap(value, axis, bit):
    size = lax.axis_size(axis)
    return lax.ppermute(value, axis, [(i, i ^ bit) for i in range(size)])


def my_bit(axis, bit):
    return (lax.axis_index(axis) // bit) % 2


def gather_over(value, axis):
    blocks = [value]
    for bit in bits_of(axis):
        blocks = blocks + [swap(block, axis, bit) for block in blocks]
    mine = lax.axis_index(axis)
    stacked = jnp.stack(blocks)
    return [
        lax.dynamic_index_in_dim(stacked, block ^ mine, 0, keepdims=False)
        for block in range(len(blocks))
    ]


def sum_everywhere(value, axes):
    for axis in axes:
        for bit in bits_of(axis):
            value = value + swap(value, axis, bit)
    return value


def sum_and_scatter(value, order):
    head_count, dp_count = lax.axis_size("head"), lax.axis_size("dp")
    head_bits, dp_bits = bits_of("head")[::-1], bits_of("dp")[::-1]
    names = [("head", bit) for bit in head_bits] + [("dp", bit) for bit in dp_bits]
    rows = value.shape[1] // dp_count
    value = value.reshape([2] * len(names) + [rows, value.shape[2]])
    for step, (axis, bit) in enumerate(order):
        at = names.index((axis, bit))
        names.pop(at)
        mine = my_bit(axis, bit)
        kept = lax.dynamic_index_in_dim(value, mine, at, keepdims=False)
        sent = lax.dynamic_index_in_dim(value, 1 - mine, at, keepdims=False)
        value = kept.astype(WIDE) + swap(sent, axis, bit).astype(WIDE)
        if step < len(order) - 1:
            value = value.astype(LOW)
    return value


def stage_orders():
    head = [("head", bit) for bit in bits_of("head")]
    dp = [("dp", bit) for bit in bits_of("dp")]
    return head + dp, head[:1] + dp[:1] + head[1:] + dp[1:]


def on_device(
    tokens,
    seq_lengths,
    qkv_weight,
    qv_bias,
    out_weight,
    out_bias,
    norm1_gain,
    norm1_shift,
    up_weight,
    up_bias,
    down_weight,
    down_bias,
    norm2_gain,
    norm2_shift,
    out_grad,
):
    head_count = lax.axis_size("head")
    dp_count = lax.axis_size("dp")
    head_index = lax.axis_index("head")
    local_rows, width = tokens.shape
    slot_rows = local_rows * head_count // seq_lengths.shape[0]
    slots = local_rows // slot_rows
    layers = qkv_weight.shape[0]
    hidden = up_weight.shape[2]
    first_bias = jnp.concatenate(gather_over(qv_bias, "head"), axis=2)
    full_qkv = [jnp.concatenate(gather_over(qkv_weight[0], "head"), axis=2)]
    for layer in range(1, layers):
        full_qkv.append(lax.all_gather(qkv_weight[layer], "head", axis=2, tiled=True))
    base = (head_index * slots).astype(jnp.int32).reshape(1)
    bias = mask_bias(seq_lengths, base, slots, slot_rows)
    rounded, residual = tokens, tokens
    kept = []
    for layer in range(layers):
        q, k, v, probs, context = attention_forward(
            rounded, full_qkv[layer], first_bias[layer][:, None], bias
        )
        small = jnp.stack(
            [
                out_bias[layer],
                norm1_gain[layer],
                norm1_shift[layer],
                down_bias[layer],
                norm2_gain[layer],
                norm2_shift[layer],
            ]
        )
        last = layer == layers - 1
        u1, hr, gr, slope, u2, *made = ffn_forward(
            context,
            residual,
            out_weight[layer],
            up_weight[layer],
            down_weight[layer],
            up_bias[layer][None],
            small,
            (LOW,) if last else (LOW, WIDE),
            chunk=width,
        )
        kept.append((rounded, q, k, v, probs, context, u1, hr, gr, slope, u2))
        rounded, residual = made[0], made[-1]
    out_state = rounded
    grad_state = out_grad
    orders = stage_orders()
    summed = [None] * layers
    small_sums = [None] * layers
    hidden_sums = [None] * layers
    for layer in reversed(range(layers)):
        rounded, q, k, v, probs, context, u1, hr, gr, slope, u2 = kept[layer]
        gains = jnp.stack([norm1_gain[layer], norm2_gain[layer]])
        df, dz, da, do, du, sums, hidden_sums[layer] = ffn_backward(
            grad_state,
            u2,
            u1,
            slope,
            down_weight[layer],
            up_weight[layer],
            out_weight[layer],
            gains,
            chunk=width,
        )
        down_sum = sum_and_scatter(weight_grad(df, gr, hidden // head_count), orders[0])
        up_sum = sum_and_scatter(weight_grad(hr, dz, hidden // head_count), orders[1])
        dq, dk, dv, qv_sums = attention_backward(q, k, v, do, probs)
        wide_sum = sum_and_scatter(
            qkv_grads(rounded, context, dq, dk, dv, da, head_count), orders[0]
        )
        grad_state = input_grad(du, dq, dk, dv, full_qkv[layer], WIDE if layer else LOW)
        summed[layer] = (up_sum, down_sum, wide_sum)
        small_sums[layer] = jnp.concatenate([sums[:6], qv_sums[:2]])
    small_sum, hidden_sum = (
        sum_everywhere(jnp.stack(part), ("head", "dp")) for part in (small_sums, hidden_sums)
    )
    part = width // head_count
    wide = [layer_sums[2].reshape(-1, 4, part).transpose(1, 0, 2) for layer_sums in summed]
    return (
        out_state,
        grad_state,
        jnp.stack([w[:3] for w in wide]),
        small_sum[:, 6:8],
        jnp.stack([w[3] for w in wide]),
        small_sum[:, 5],
        small_sum[:, 3],
        small_sum[:, 4],
        jnp.stack([layer_sums[0] for layer_sums in summed]),
        hidden_sum[:, 0],
        jnp.stack([layer_sums[1].T for layer_sums in summed]),
        small_sum[:, 2],
        small_sum[:, 0],
        small_sum[:, 1],
    )


def solution(mesh):
    in_specs = (
        P(("dp", "head"), None),
        P("dp", None),
        P(None, None, None, "head"),
        P(None, None, "head"),
        P(),
        P(),
        P(),
        P(),
        P(),
        P(),
        P(),
        P(),
        P(),
        P(),
        P(("dp", "head"), None),
    )
    out_specs = (
        P(("dp", "head"), None),
        P(("dp", "head"), None),
        P(None, None, "dp", "head"),
        P(),
        P(None, "dp", "head"),
        P(),
        P(),
        P(),
        P(None, "dp", "head"),
        P(),
        P(None, "head", "dp"),
        P(),
        P(),
        P(),
    )
    return jax.shard_map(
        on_device, mesh=mesh, in_specs=in_specs, out_specs=out_specs, check_vma=False
    )
```

time: 1060 us -> 621 us (0.59)
  matrix products: 349 us -> 0 us
  Pallas kernels: 0 us -> 267 us
  local copies, waits for them, and re-layouts: 291 us -> 75.3 us
  waiting for transfers between devices: 324 us -> 187 us
  starting transfers between devices: 0.2 us -> 46.5 us
  other arithmetic: 61.2 us -> 24.4 us
    dot_general x64 -> x0, matrix products: 349 us -> none  [the longest x2 77.9 us: on_device(): jnp.dot(normed_low, up_weight[layer], preferred_element_type=jnp.float32)]
    reduce_scatter x2 -> x0, waiting for transfers between devices: 319 us -> none  [on_device(): lax.psum_scatter(packed, ('dp', 'head'), scatter_dimension=0, tiled=True)[0]]
    pallas_call x0 -> x17, Pallas kernels: none -> 267 us  [the longest x2 47.4 us: attention_backward(): pl.pallas_call(functools.partial(attention_backward_kernel, tile=tile), g...]
    ppermute x0 -> x46, waiting for transfers between devices: none -> 187 us  [swap(): return lax.ppermute(value, axis, [(i, i ^ bit) for i in range(size)])]
    reshape x37 -> x2, local copies, waits for them, and re-layouts: 109 us -> 0.57 us  [on_device(): layer_sums[2].reshape(-1, 4, part).transpose(1, 0, 2)]
    unnamed x321 -> x52, local copies, waits for them, and re-layouts: 58.9 us -> 6.21 us
    ppermute x0 -> x46, starting transfers between devices: none -> 46.5 us  [swap(): return lax.ppermute(value, axis, [(i, i ^ bit) for i in range(size)])]
    while x64 -> x0, local copies, waits for them, and re-layouts: 39.9 us -> none  [the longest x8 18.4 us: on_device(): lax.map(slot_forward, (queries, keys_in, values_in, segments))]
  transfers between devices with their start and end apart: 5 -> 47, of which waited for: 3 -> 18; matrix products, arithmetic and copies ran while one was open for 24% -> 14% of each run, Pallas kernels for 0% -> 22%
where the time goes in v2:
time: 621 us; the launch traced here: 615 us
  Pallas kernels  267 us (43%)
  waiting for transfers between devices  187 us (30%)
  local copies, waits for them, and re-layouts  75.3 us (12%)
  starting transfers between devices  46.5 us (7%)
  other arithmetic  24.4 us (4%)
  between operations  15.6 us (3%)
    ppermute x46, waiting for transfers between devices, swap(): return lax.ppermute(value, axis, [(i, i ^ bit) for i in range(size)])  187 us
    pallas_call x2, Pallas kernels, attention_backward(): pl.pallas_call(functools.partial(attention_backward_kernel, tile=tile), g...  47.4 us
    ppermute x46, starting transfers between devices, swap(): return lax.ppermute(value, axis, [(i, i ^ bit) for i in range(size)])  46.5 us
    pallas_call x2, Pallas kernels, ffn_forward(): pl.pallas_call(functools.partial(ffn_forward_kernel, chunk=chunk), grid=(...  45.7 us
    pallas_call x2, Pallas kernels, ffn_backward(): pl.pallas_call(functools.partial(ffn_backward_kernel, chunk=chunk), grid=...  44 us
    pallas_call x2, Pallas kernels, attention_forward(): pl.pallas_call(functools.partial(attention_forward_kernel, tile=tile), gr...  43 us
    pallas_call x4, Pallas kernels, weight_grad(): pl.pallas_call(weight_grad_kernel, grid=(count,), in_specs=[whole(a), pl....  38.5 us
    pallas_call x2, Pallas kernels, qkv_grads(): pl.pallas_call(kernel, grid=(heads,), in_specs=[whole(v) for v in (x, o,...  25.8 us
  transfers between devices with their start and end apart: 47, of which 18 were waited for; matrix products, arithmetic and copies ran while one was open for 14% of the time, Pallas kernels for 22%

profile of v2, /device:TPU:0, one launch (start us, length us, event | category | flops | bytes accessed | tf_op | source)
XLA Modules:
  0.0 615.3 jit_solution(5817143041868170314)
XLA Ops:
  15.7 9.1 %slice_bitcast_fusion = (bf16[3072,768]{1,0:T(8,128)(2,1)}, bf16[3072,768]{1,0:T(8,128)(2,1)}) fusion(bf16[2,3072,768]{2,1,0:T(8,128)(2,1)} %param.25), kind=kLoop, calls=%fused_computation.12 | loop fusion | bytes 18874368 | tf_op jit(solution)/shard_map/squeeze | solution.py:494
  46.7 25.4 %collective-permute-done.2 = bf16[3,768,192]{1,2,0:T(8,128)(2,1)S(1)} collective-permute-done((bf16[3,768,192]{1,2,0:T(8,128)(2,1)}, bf16[3,768,192]{1,2,0:T(8,128)(2,1)S(1)}, u32[]{:S(2)}, u32[]{:S(2)}) %collective-permute-start.2) | collective-permute-done | bytes 884768 | tf_op jit(solution)/shard_map/ppermute | solution.py:391
  85.2 21.4 %attention_forward.2 = (bf16[1024,768]{1,0:T(8,128)(2,1)}, bf16[1024,768]{1,0:T(8,128)(2,1)}, bf16[1024,768]{1,0:T(8,128)(2,1)}, bf16[24,512,512]{2,1,0:T(8,128)(2,1)}, bf16[1024,768]{1,0:T(8,128)(2,1)}) custom-call(bf16[1024,768]{1,0:T(8,128)(2,1)} %x_ref.5, bf16[3,768,768]{2,1,0:T(8,128)(2,1)} %pad_maximum_fusion.1.w_ref, ...), custom_call_target="tpu_custom_call" | custom-call | tf_op jit(solution)/shard_map/attention_forward/pallas_call | solution.py:231
  106.5 22.9 %ffn_forward.2 = (f32[1024,768]{1,0:T(8,128)}, bf16[1024,768]{1,0:T(8,128)(2,1)}, bf16[1024,3072]{1,0:T(8,128)(2,1)}, bf16[1024,3072]{1,0:T(8,128)(2,1)}, f32[10...) custom-call(bf16[1024,768]{1,0:T(8,128)(2,1)} %get-tuple-element.59.o_ref, bf16[1024,768]{1,0:T(8,128)(2,1)} %x_ref.5, ...), custom_call_target="tpu_custom_call" | custom-call | tf_op jit(solution)/shard_map/ffn_forward/pallas_call | solution.py:85
  135.5 21.6 %attention_forward.3 = (bf16[1024,768]{1,0:T(8,128)(2,1)}, bf16[1024,768]{1,0:T(8,128)(2,1)}, bf16[1024,768]{1,0:T(8,128)(2,1)}, bf16[24,512,512]{2,1,0:T(8,128)(2,1)}, bf16[1024,768]{1,0:T(8,128)(2,1)}) custom-call(bf16[1024,768]{1,0:T(8,128)(2,1)} %get-tuple-element.60.x_ref, bf16[3,768,768]{2,1,0:T(8,128)(2,1)} %bitcast.259, ...), custom_call_target="tpu_custom_call" | custom-call | tf_op jit(solution)/shard_map/attention_forward/pallas_call | solution.py:231
  157.1 22.8 %ffn_forward.3 = (f32[1024,768]{1,0:T(8,128)}, bf16[1024,768]{1,0:T(8,128)(2,1)}, bf16[1024,3072]{1,0:T(8,128)(2,1)}, bf16[1024,3072]{1,0:T(8,128)(2,1)}, f32[10...) custom-call(bf16[1024,768]{1,0:T(8,128)(2,1)} %get-tuple-element.61.o_ref, f32[1024,768]{1,0:T(8,128)} %get-tuple-element.62.x_ref, ...), custom_call_target="tpu_custom_call" | custom-call | tf_op jit(solution)/shard_map/ffn_forward/pallas_call | solution.py:85
  180.0 21.9 %ffn_backward.2 = (bf16[1024,768]{1,0:T(8,128)(2,1)}, bf16[1024,3072]{1,0:T(8,128)(2,1)}, bf16[1024,768]{1,0:T(8,128)(2,1)}, bf16[1024,768]{1,0:T(8,128)(2,1)}, ...) custom-call(bf16[1024,768]{1,0:T(8,128)(2,1)} %gx_ref.1, f32[1024,768]{1,0:T(8,128)} %get-tuple-element.64.u2_ref, ...), custom_call_target="tpu_custom_call" | custom-call | tf_op jit(solution)/shard_map/ffn_backward/pallas_call | solution.py:150
  201.9 23.9 %attention_backward.2 = (bf16[1024,768]{1,0:T(8,128)(2,1)}, bf16[1024,768]{1,0:T(8,128)(2,1)}, bf16[1024,768]{1,0:T(8,128)(2,1)}, f32[8,768]{1,0:T(8,128)}) custom-call(bf16[1024,768]{1,0:T(8,128)(2,1)} %get-tuple-element.68.q_ref, bf16[1024,768]{1,0:T(8,128)(2,1)} %get-tuple-element.69.k_ref, bf16[1024,768]{1,0:T(8,128)(2,1)} %get-tuple-element.70.v_ref, ...), custom_call_target="tpu_custom_call" | custom-call | tf_op jit(solution)/shard_map/attention_backward/pallas_call | solution.py:292
  225.8 8.9 %input_grad.2.gx_ref = f32[1024,768]{1,0:T(8,128)} custom-call(f32[1024,768]{1,0:T(8,128)} %get-tuple-element.67.du_ref, bf16[1024,768]{1,0:T(8,128)(2,1)} %get-tuple-element.73.dq_ref, bf16[1024,768]{1,0:T(8,128)(2,1)} %get-tuple-element.74.dk_ref, bf16[1024,768]{1,0:T(8,128)(2,1)} %get-tuple-element.75.dv_ref, bf16[3,768,768]{2,1,0:T(8,128)(2,1)} %bitcast.260), custom_call_target="tpu_custom_call" | custom-call | tf_op jit(solution)/shard_map/input_grad/pallas_call | solution.py:373
  234.8 22.0 %ffn_backward.3 = (bf16[1024,768]{1,0:T(8,128)(2,1)}, bf16[1024,3072]{1,0:T(8,128)(2,1)}, bf16[1024,768]{1,0:T(8,128)(2,1)}, bf16[1024,768]{1,0:T(8,128)(2,1)}, ...) custom-call(f32[1024,768]{1,0:T(8,128)} %input_grad.2.gx_ref, f32[1024,768]{1,0:T(8,128)} %get-tuple-element.76.u2_ref, ...), custom_call_target="tpu_custom_call" | custom-call | tf_op jit(solution)/shard_map/ffn_backward/pallas_call | solution.py:150
  256.8 9.6 %weight_grad.6 = bf16[4,768,768]{2,1,0:T(8,128)(2,1)} custom-call(bf16[1024,768]{1,0:T(8,128)(2,1)} %get-tuple-element.100.a_ref, bf16[1024,3072]{1,0:T(8,128)(2,1)} %get-tuple-element.101.b_ref), custom_call_target="tpu_custom_call" | custom-call | tf_op jit(solution)/shard_map/weight_grad/pallas_call | solution.py:172
  270.6 9.6 %weight_grad.7 = bf16[4,768,768]{2,1,0:T(8,128)(2,1)} custom-call(bf16[1024,768]{1,0:T(8,128)(2,1)} %get-tuple-element.102.a_ref, bf16[1024,3072]{1,0:T(8,128)(2,1)} %get-tuple-element.103.b_ref), custom_call_target="tpu_custom_call" | custom-call | tf_op jit(solution)/shard_map/weight_grad/pallas_call | solution.py:172
  285.1 9.8 %weight_grad.4 = bf16[4,768,768]{2,1,0:T(8,128)(2,1)} custom-call(bf16[1024,768]{1,0:T(8,128)(2,1)} %get-tuple-element.94.a_ref, bf16[1024,3072]{1,0:T(8,128)(2,1)} %get-tuple-element.95.b_ref), custom_call_target="tpu_custom_call" | custom-call | tf_op jit(solution)/shard_map/weight_grad/pallas_call | solution.py:172
  299.6 23.5 %attention_backward.3 = (bf16[1024,768]{1,0:T(8,128)(2,1)}, bf16[1024,768]{1,0:T(8,128)(2,1)}, bf16[1024,768]{1,0:T(8,128)(2,1)}, f32[8,768]{1,0:T(8,128)}) custom-call(bf16[1024,768]{1,0:T(8,128)(2,1)} %get-tuple-element.80.q_ref, bf16[1024,768]{1,0:T(8,128)(2,1)} %get-tuple-element.81.k_ref, bf16[1024,768]{1,0:T(8,128)(2,1)} %get-tuple-element.82.v_ref, ...), custom_call_target="tpu_custom_call" | custom-call | tf_op jit(solution)/shard_map/attention_backward/pallas_call | solution.py:292
  324.8 9.6 %weight_grad.5 = bf16[4,768,768]{2,1,0:T(8,128)(2,1)} custom-call(bf16[1024,768]{1,0:T(8,128)(2,1)} %get-tuple-element.96.a_ref, bf16[1024,3072]{1,0:T(8,128)(2,1)} %get-tuple-element.97.b_ref), custom_call_target="tpu_custom_call" | custom-call | tf_op jit(solution)/shard_map/weight_grad/pallas_call | solution.py:172
  345.1 12.9 %qkv_grads.2 = bf16[4,768,768]{2,1,0:T(8,128)(2,1)} custom-call(bf16[1024,768]{1,0:T(8,128)(2,1)} %x_ref.5, bf16[1024,768]{1,0:T(8,128)(2,1)} %get-tuple-element.59.o_ref, bf16[1024,768]{1,0:T(8,128)(2,1)} %get-tuple-element.85.dq_ref, bf16[1024,768]{1,0:T(8,128)(2,1)} %get-tuple-element.86.dk_ref, bf16[1024,768]{1,0:T(8,128)(2,1)} %get-tuple-element.87.dv_ref, ...), custom_call_target="tpu_custom_call" | custom-call | tf_op jit(solution)/shard_map/qkv_grads/pallas_call | solution.py:352
  365.1 12.9 %qkv_grads.3 = bf16[4,768,768]{2,1,0:T(8,128)(2,1)} custom-call(bf16[1024,768]{1,0:T(8,128)(2,1)} %get-tuple-element.60.x_ref, bf16[1024,768]{1,0:T(8,128)(2,1)} %get-tuple-element.61.o_ref, bf16[1024,768]{1,0:T(8,128)(2,1)} %get-tuple-element.73.dq_ref, bf16[1024,768]{1,0:T(8,128)(2,1)} %get-tuple-element.74.dk_ref, ...), custom_call_target="tpu_custom_call" | custom-call | tf_op jit(solution)/shard_map/qkv_grads/pallas_call | solution.py:352
  427.0 14.4 %collective-permute-done.37 = bf16[2,2,2,96,768]{4,3,0,1,2:T(8,128)(2,1)S(1)} collective-permute-done((bf16[2,2,2,96,768]{4,3,0,1,2:T(8,128)(2,1)S(1)}, bf16[2,2,2,96,768]{4,3,0,1,2:T(8,128)(2,1)S(1)}, u32[]{:S(2)}, u32[]{:S(2)}) %collective-permute-start.37) | collective-permute-done | bytes 1179680 | tf_op jit(solution)/shard_map/ppermute | solution.py:391
  443.5 23.2 %collective-permute-done.42 = bf16[2,2,2,96,768]{4,3,0,1,2:T(8,128)(2,1)S(1)} collective-permute-done((bf16[2,2,2,96,768]{4,3,0,1,2:T(8,128)(2,1)S(1)}, bf16[2,2,2,96,768]{4,3,0,1,2:T(8,128)(2,1)S(1)}, u32[]{:S(2)}, u32[]{:S(2)}) %collective-permute-start.42) | collective-permute-done | bytes 1179680 | tf_op jit(solution)/shard_map/ppermute | solution.py:391
  475.9 16.0 %collective-permute-done.7 = bf16[2,2,2,96,768]{4,3,0,1,2:T(8,128)(2,1)S(1)} collective-permute-done((bf16[2,2,2,96,768]{4,3,0,1,2:T(8,128)(2,1)S(1)}, bf16[2,2,2,96,768]{4,3,0,1,2:T(8,128)(2,1)S(1)}, u32[]{:S(2)}, u32[]{:S(2)}) %collective-permute-start.7) | collective-permute-done | bytes 1179680 | tf_op jit(solution)/shard_map/ppermute | solution.py:391
  494.1 23.2 %collective-permute-done.12 = bf16[2,2,2,96,768]{4,3,0,1,2:T(8,128)(2,1)S(1)} collective-permute-done((bf16[2,2,2,96,768]{4,3,0,1,2:T(8,128)(2,1)S(1)}, bf16[2,2,2,96,768]{4,3,0,1,2:T(8,128)(2,1)S(1)}, u32[]{:S(2)}, u32[]{:S(2)}) %collective-permute-start.12) | collective-permute-done | bytes 1179680 | tf_op jit(solution)/shard_map/ppermute | solution.py:391
  531.7 9.9 %collective-permute-done.28 = bf16[2,2,96,768]{3,2,0,1:T(8,128)(2,1)S(1)} collective-permute-done((bf16[2,2,96,768]{3,2,0,1:T(8,128)(2,1)S(1)}, bf16[2,2,96,768]{3,2,0,1:T(8,128)(2,1)S(1)}, u32[]{:S(2)}, u32[]{:S(2)}) %collective-permute-start.28) | collective-permute-done | bytes 589856 | tf_op jit(solution)/shard_map/ppermute | solution.py:391
  556.7 9.0 %collective-permute-done.29 = bf16[2,96,768]{2,1,0:T(8,128)(2,1)S(1)} collective-permute-done((bf16[2,96,768]{2,1,0:T(8,128)(2,1)S(1)}, bf16[2,96,768]{2,1,0:T(8,128)(2,1)S(1)}, u32[]{:S(2)}, u32[]{:S(2)}) %collective-permute-start.29) | collective-permute-done | bytes 294944 | tf_op jit(solution)/shard_map/ppermute | solution.py:391
  577.9 14.8 %collective-permute-done.10 = bf16[96,768]{1,0:T(8,128)(2,1)S(1)} collective-permute-done((bf16[96,768]{1,0:T(8,128)(2,1)S(1)}, bf16[96,768]{1,0:T(8,128)(2,1)S(1)}, u32[]{:S(2)}, u32[]{:S(2)}) %collective-permute-start.10) | collective-permute-done | bytes 147488 | tf_op jit(solution)/shard_map/ppermute | solution.py:391
  (261 shorter events, 201.5 us)
Async XLA Ops:
  7.3 122.2 %all-gather.3.cloned.1.call-start = ((), (), s32[]{:S(2)}) async-start(), calls=%async_computation | async-start | bytes 4423680 | tf_op jit(solution)/shard_map/all_gather | solution.py:469
  10.5 32.9 %collective-permute-start = (bf16[3,768,192]{1,2,0:T(8,128)(2,1)}, bf16[3,768,192]{1,2,0:T(8,128)(2,1)}, u32[]{:S(2)}, u32[]{:S(2)}) collective-permute-start(bf16[3,768,192]{1,2,0:T(8,128)(2,1)} %get-tuple-element.155), channel_id=1, source_target_pairs={{0,1},{1,0},{2,3},{3,2},{4,5},{5,4},{6,7},{7,6},{8,9},{9,8},{10,11... | collective-permute-start | bytes 2654216 | tf_op jit(solution)/shard_map/ppermute | solution.py:391
  11.0 35.7 %collective-permute-start.1 = (bf16[3,768,192]{1,2,0:T(8,128)(2,1)}, bf16[3,768,192]{1,2,0:T(8,128)(2,1)}, u32[]{:S(2)}, u32[]{:S(2)}) collective-permute-start(bf16[3,768,192]{1,2,0:T(8,128)(2,1)} %get-tuple-element.155), channel_id=1, source_target_pairs={{0,2},{1,3},{2,0},{3,1},{4,6},{5,7},{6,4},{7,5},{8,10},{9,11},{10,... | collective-permute-start | bytes 2654216 | tf_op jit(solution)/shard_map/ppermute | solution.py:391
  13.7 29.6 %collective-permute-start.4 = (f32[2,2,192]{2,1,0:T(2,128)S(1)}, f32[2,2,192]{2,1,0:T(2,128)S(1)}, u32[]{:S(2)}, u32[]{:S(2)}) collective-permute-start(f32[2,2,192]{2,1,0:T(2,128)S(1)} %copy-done.18), channel_id=1, source_target_pairs={{0,2},{1,3},{2,0},{3,1},{4,6},{5,7},{6,4},{7,5},{8,10},{9,11},{10,... | collective-permute-start | bytes 9224 | tf_op jit(solution)/shard_map/ppermute | solution.py:391
  43.4 28.7 %collective-permute-start.2 = (bf16[3,768,192]{1,2,0:T(8,128)(2,1)}, bf16[3,768,192]{1,2,0:T(8,128)(2,1)S(1)}, u32[]{:S(2)}, u32[]{:S(2)}) collective-permute-start(bf16[3,768,192]{1,2,0:T(8,128)(2,1)} %collective-permute-done), channel_id=1, source_target_pairs={{0,2},{1,3},{2,0},{3,1},{4,6},{5,7},{6,4},{7,5},{8,10},{9,11},{10,... | collective-permute-start | bytes 2654216 | tf_op jit(solution)/shard_map/ppermute | solution.py:391
  270.6 138.9 %collective-permute-start.36 = (bf16[2,2,2,2,96,768]{5,4,1,2,3,0:T(8,128)(2,1)}, bf16[2,2,2,2,96,768]{5,4,1,2,3,0:T(8,128)(2,1)}, u32[]{:S(2)}, u32[]{:S(2)}) collective-permute-start(bf16[2,2,2,2,96,768]{5,4,1,2,3,0:T(8,128)(2,1)} %bitcast.246), channel_id=1, source_target_pairs={{0,1},{1,0},{2,3},{3,2},{4,5},{5,4},{6,7},{7,6},{8,9},{9,8},{10,11... | collective-permute-start | bytes 7077896 | tf_op jit(solution)/shard_map/ppermute | solution.py:391
  284.5 128.0 %collective-permute-start.41 = (bf16[2,2,2,2,96,768]{5,4,1,2,3,0:T(8,128)(2,1)}, bf16[2,2,2,2,96,768]{5,4,1,2,3,0:T(8,128)(2,1)}, u32[]{:S(2)}, u32[]{:S(2)}) collective-permute-start(bf16[2,2,2,2,96,768]{5,4,1,2,3,0:T(8,128)(2,1)} %bitcast.245), channel_id=1, source_target_pairs={{0,1},{1,0},{2,3},{3,2},{4,5},{5,4},{6,7},{7,6},{8,9},{9,8},{10,11... | collective-permute-start | bytes 7077896 | tf_op jit(solution)/shard_map/ppermute | solution.py:391
  285.0 49.3 %collective-permute-start.31 = (f32[2,1,3072]{2,0,1:T(2,128)S(1)}, f32[2,1,3072]{2,0,1:T(2,128)S(1)}, u32[]{:S(2)}, u32[]{:S(2)}) collective-permute-start(f32[2,1,3072]{2,0,1:T(2,128)S(1)} %pad_maximum_fusion.7), channel_id=1, source_target_pairs={{0,1},{1,0},{2,3},{3,2},{4,5},{5,4},{6,7},{7,6},{8,9},{9,8},{10,11... | collective-permute-start | bytes 73736 | tf_op jit(solution)/shard_map/ppermute | solution.py:391
  299.1 117.6 %collective-permute-start.21 = (bf16[2,2,2,2,96,768]{5,4,1,2,0,3:T(8,128)(2,1)}, bf16[2,2,2,2,96,768]{5,4,1,2,0,3:T(8,128)(2,1)}, u32[]{:S(2)}, u32[]{:S(2)}) collective-permute-start(bf16[2,2,2,2,96,768]{5,4,1,2,0,3:T(8,128)(2,1)} %bitcast.248), channel_id=1, source_target_pairs={{0,1},{1,0},{2,3},{3,2},{4,5},{5,4},{6,7},{7,6},{8,9},{9,8},{10,11... | collective-permute-start | bytes 7077896 | tf_op jit(solution)/shard_map/ppermute | solution.py:391
  412.5 28.9 %collective-permute-start.37 = (bf16[2,2,2,96,768]{4,3,0,1,2:T(8,128)(2,1)S(1)}, bf16[2,2,2,96,768]{4,3,0,1,2:T(8,128)(2,1)S(1)}, u32[]{:S(2)}, u32[]{:S(2)}) collective-permute-start(bf16[2,2,2,96,768]{4,3,0,1,2:T(8,128)(2,1)S(1)} %dynamic-slice_bitcast_fusion.1), channel_id=1, source_target_pairs={{0,2},{1,3},{2,0},{3,1},{4,6},{5,7},{6,4},{7,5},{8,10},{9,11},{10,... | collective-permute-start | bytes 3538952 | tf_op jit(solution)/shard_map/ppermute | solution.py:391
  416.8 49.9 %collective-permute-start.42 = (bf16[2,2,2,96,768]{4,3,0,1,2:T(8,128)(2,1)S(1)}, bf16[2,2,2,96,768]{4,3,0,1,2:T(8,128)(2,1)S(1)}, u32[]{:S(2)}, u32[]{:S(2)}) collective-permute-start(bf16[2,2,2,96,768]{4,3,0,1,2:T(8,128)(2,1)S(1)} %dynamic-slice_bitcast_fusion), channel_id=1, source_target_pairs={{0,2},{1,3},{2,0},{3,1},{4,6},{5,7},{6,4},{7,5},{8,10},{9,11},{10,... | collective-permute-start | bytes 3538952 | tf_op jit(solution)/shard_map/ppermute | solution.py:391
  419.6 48.9 %collective-permute-start.22 = (bf16[2,2,2,96,768]{4,3,1,2,0:T(8,128)(2,1)S(1)}, bf16[2,2,2,96,768]{4,3,1,2,0:T(8,128)(2,1)S(1)}, u32[]{:S(2)}, u32[]{:S(2)}) collective-permute-start(bf16[2,2,2,96,768]{4,3,1,2,0:T(8,128)(2,1)S(1)} %dynamic-slice_bitcast_fusion.3), channel_id=1, source_target_pairs={{0,4},{4,0},{8,12},{12,8},{16,20},{20,16},{24,28},{28,24},{1,5},{5... | collective-permute-start | bytes 3538952 | tf_op jit(solution)/shard_map/ppermute | solution.py:391
  422.0 51.9 %collective-permute-start.27 = (bf16[2,2,2,96,768]{4,3,1,2,0:T(8,128)(2,1)S(1)}, bf16[2,2,2,96,768]{4,3,1,2,0:T(8,128)(2,1)S(1)}, u32[]{:S(2)}, u32[]{:S(2)}) collective-permute-start(bf16[2,2,2,96,768]{4,3,1,2,0:T(8,128)(2,1)S(1)} %dynamic-slice_bitcast_fusion.2), channel_id=1, source_target_pairs={{0,4},{4,0},{8,12},{12,8},{16,20},{20,16},{24,28},{28,24},{1,5},{5... | collective-permute-start | bytes 3538952 | tf_op jit(solution)/shard_map/ppermute | solution.py:391
  424.3 67.6 %collective-permute-start.7 = (bf16[2,2,2,96,768]{4,3,0,1,2:T(8,128)(2,1)S(1)}, bf16[2,2,2,96,768]{4,3,0,1,2:T(8,128)(2,1)S(1)}, u32[]{:S(2)}, u32[]{:S(2)}) collective-permute-start(bf16[2,2,2,96,768]{4,3,0,1,2:T(8,128)(2,1)S(1)} %dynamic-slice_bitcast_fusion.5), channel_id=1, source_target_pairs={{0,2},{1,3},{2,0},{3,1},{4,6},{5,7},{6,4},{7,5},{8,10},{9,11},{10,... | collective-permute-start | bytes 3538952 | tf_op jit(solution)/shard_map/ppermute | solution.py:391
  441.4 75.8 %collective-permute-start.12 = (bf16[2,2,2,96,768]{4,3,0,1,2:T(8,128)(2,1)S(1)}, bf16[2,2,2,96,768]{4,3,0,1,2:T(8,128)(2,1)S(1)}, u32[]{:S(2)}, u32[]{:S(2)}) collective-permute-start(bf16[2,2,2,96,768]{4,3,0,1,2:T(8,128)(2,1)S(1)} %dynamic-slice_bitcast_fusion.4), channel_id=1, source_target_pairs={{0,2},{1,3},{2,0},{3,1},{4,6},{5,7},{6,4},{7,5},{8,10},{9,11},{10,... | collective-permute-start | bytes 3538952 | tf_op jit(solution)/shard_map/ppermute | solution.py:391
  466.7 52.4 %collective-permute-start.38 = (bf16[2,2,96,768]{3,2,0,1:T(8,128)(2,1)S(1)}, bf16[2,2,96,768]{3,2,0,1:T(8,128)(2,1)S(1)}, u32[]{:S(2)}, u32[]{:S(2)}) collective-permute-start(bf16[2,2,96,768]{3,2,0,1:T(8,128)(2,1)S(1)} %dynamic-slice_bitcast_fusion.7), channel_id=1, source_target_pairs={{0,4},{4,0},{8,12},{12,8},{16,20},{20,16},{24,28},{28,24},{1,5},{5... | collective-permute-start | bytes 1769480 | tf_op jit(solution)/shard_map/ppermute | solution.py:391
  468.5 51.4 %collective-permute-start.43 = (bf16[2,2,96,768]{3,2,0,1:T(8,128)(2,1)S(1)}, bf16[2,2,96,768]{3,2,0,1:T(8,128)(2,1)S(1)}, u32[]{:S(2)}, u32[]{:S(2)}) collective-permute-start(bf16[2,2,96,768]{3,2,0,1:T(8,128)(2,1)S(1)} %dynamic-slice_bitcast_fusion.6), channel_id=1, source_target_pairs={{0,4},{4,0},{8,12},{12,8},{16,20},{20,16},{24,28},{28,24},{1,5},{5... | collective-permute-start | bytes 1769480 | tf_op jit(solution)/shard_map/ppermute | solution.py:391
  473.8 56.0 %collective-permute-start.23 = (bf16[2,2,96,768]{3,2,0,1:T(8,128)(2,1)S(1)}, bf16[2,2,96,768]{3,2,0,1:T(8,128)(2,1)S(1)}, u32[]{:S(2)}, u32[]{:S(2)}) collective-permute-start(bf16[2,2,96,768]{3,2,0,1:T(8,128)(2,1)S(1)} %dynamic-slice_bitcast_fusion.9), channel_id=1, source_target_pairs={{0,2},{1,3},{2,0},{3,1},{4,6},{5,7},{6,4},{7,5},{8,10},{9,11},{10,... | collective-permute-start | bytes 1769480 | tf_op jit(solution)/shard_map/ppermute | solution.py:391
  491.9 49.6 %collective-permute-start.28 = (bf16[2,2,96,768]{3,2,0,1:T(8,128)(2,1)S(1)}, bf16[2,2,96,768]{3,2,0,1:T(8,128)(2,1)S(1)}, u32[]{:S(2)}, u32[]{:S(2)}) collective-permute-start(bf16[2,2,96,768]{3,2,0,1:T(8,128)(2,1)S(1)} %dynamic-slice_bitcast_fusion.8), channel_id=1, source_target_pairs={{0,2},{1,3},{2,0},{3,1},{4,6},{5,7},{6,4},{7,5},{8,10},{9,11},{10,... | collective-permute-start | bytes 1769480 | tf_op jit(solution)/shard_map/ppermute | solution.py:391
  545.9 30.9 %collective-permute-start.14 = (bf16[2,96,768]{2,1,0:T(8,128)(2,1)S(1)}, bf16[2,96,768]{2,1,0:T(8,128)(2,1)S(1)}, u32[]{:S(2)}, u32[]{:S(2)}) collective-permute-start(bf16[2,96,768]{2,1,0:T(8,128)(2,1)S(1)} %dynamic-slice_bitcast_fusion.16), channel_id=1, source_target_pairs={{0,8},{4,12},{8,0},{12,4},{16,24},{20,28},{24,16},{28,20},{1,9},{5... | collective-permute-start | bytes 884744 | tf_op jit(solution)/shard_map/ppermute | solution.py:391
  546.6 56.3 %collective-permute-start.40 = (bf16[96,768]{1,0:T(8,128)(2,1)S(1)}, bf16[96,768]{1,0:T(8,128)(2,1)S(1)}, u32[]{:S(2)}, u32[]{:S(2)}) collective-permute-start(bf16[96,768]{1,0:T(8,128)(2,1)S(1)} %dynamic-slice_bitcast_fusion.19), channel_id=1, source_target_pairs={{0,16},{4,20},{8,24},{12,28},{16,0},{20,4},{24,8},{28,12},{1,17},{... | collective-permute-start | bytes 442376 | tf_op jit(solution)/shard_map/ppermute | solution.py:391
  556.3 46.7 %collective-permute-start.45 = (bf16[96,768]{1,0:T(8,128)(2,1)S(1)}, bf16[96,768]{1,0:T(8,128)(2,1)}, u32[]{:S(2)}, u32[]{:S(2)}) collective-permute-start(bf16[96,768]{1,0:T(8,128)(2,1)S(1)} %dynamic-slice_bitcast_fusion.18), channel_id=1, source_target_pairs={{0,16},{4,20},{8,24},{12,28},{16,0},{20,4},{24,8},{28,12},{1,17},{... | collective-permute-start | bytes 442376 | tf_op jit(solution)/shard_map/ppermute | solution.py:391
  565.7 38.6 %collective-permute-start.25 = (bf16[96,768]{1,0:T(8,128)(2,1)S(1)}, bf16[96,768]{1,0:T(8,128)(2,1)S(1)}, u32[]{:S(2)}, u32[]{:S(2)}) collective-permute-start(bf16[96,768]{1,0:T(8,128)(2,1)S(1)} %dynamic-slice_bitcast_fusion.21), channel_id=1, source_target_pairs={{0,16},{4,20},{8,24},{12,28},{16,0},{20,4},{24,8},{28,12},{1,17},{... | collective-permute-start | bytes 442376 | tf_op jit(solution)/shard_map/ppermute | solution.py:391
  572.4 34.6 %collective-permute-start.30 = (bf16[96,768]{1,0:T(8,128)(2,1)S(1)}, bf16[96,768]{1,0:T(8,128)(2,1)S(1)}, u32[]{:S(2)}, u32[]{:S(2)}) collective-permute-start(bf16[96,768]{1,0:T(8,128)(2,1)S(1)} %dynamic-slice_bitcast_fusion.20), channel_id=1, source_target_pairs={{0,16},{4,20},{8,24},{12,28},{16,0},{20,4},{24,8},{28,12},{1,17},{... | collective-permute-start | bytes 442376 | tf_op jit(solution)/shard_map/ppermute | solution.py:391
  (45 other events, 608.1 us)
Sparse Core Ops, SparseCore 0:
  14.1 47.0 all-gather.2

commit v3 on v2

--- a/solution.py
+++ b/solution.py
@@ -158,27 +158,140 @@
     )(gx, u2, u1, gp, wd, wu, wo, gains)
 
 
-def weight_grad_kernel(a_ref, b_ref, out_ref, t_ref):
-    @pl.when(pl.program_id(0) == 0)
+def reversed_bits(value, count):
+    made = 0
+    for bit in range(count):
+        made |= (value >> bit & 1) << (count - 1 - bit)
+    return made
+
+
+def put_chunks(out_ref, made, dp_count):
+    rows = made.shape[0] // dp_count
+    rest = dp_count.bit_length() - 2
+    for dp in range(dp_count):
+        chunk = made[dp * rows : (dp + 1) * rows]
+        out_ref[dp & 1, reversed_bits(dp >> 1, rest)] = chunk
+
+
+def chunk_spec(dp_count, rows, columns, dp_first, pick_block):
+    rest = dp_count // 2
+    if dp_first:
+        shape = (2, None, rest, rows, columns)
+        return pl.BlockSpec(shape, lambda i, *refs: (0, pick_block(i), 0, 0, 0))
+    return pl.BlockSpec((None, 2, rest, rows, columns), lambda i, *refs: (pick_block(i), 0, 0, 0, 0))
+
+
+def first_two(i):
+    return jnp.minimum(i, 1)
+
+
+def last_two(i):
+    return jnp.maximum(i - 2, 0)
+
+
+def weight_grad_kernel(bit_ref, a_ref, b_ref, send_ref, keep_ref, t_ref, *, dp_count):
+    step = pl.program_id(0)
+
+    @pl.when(step == 0)
     def _():
         t_ref[...] = a_ref[...].T
 
-    out_ref[...] = dot_nn(t_ref[...], b_ref[...]).astype(LOW)
-
-
-def weight_grad(a, b, width):
+    made = dot_nn(t_ref[...], b_ref[...]).astype(LOW)
+
+    @pl.when(step < 2)
+    def _():
+        put_chunks(send_ref, made, dp_count)
+
+    @pl.when(step >= 2)
+    def _():
+        put_chunks(keep_ref, made, dp_count)
+
+
+def weight_grad(a, b, core, dp_count, dp_first):
     rows, depth = a.shape
-    count = b.shape[1] // width
-    return pl.pallas_call(
-        weight_grad_kernel,
-        grid=(count,),
-        in_specs=[whole(a), pl.BlockSpec((rows, width), lambda i: (0, i))],
-        out_specs=pl.BlockSpec((None, depth, width), lambda i: (i, 0, 0)),
-        out_shape=jax.ShapeDtypeStruct((count, depth, width), LOW),
-        scratch_shapes=[pltpu.VMEM((depth, rows), LOW)],
+    width = b.shape[1] // 4
+    chunk = depth // dp_count
+    made = jax.ShapeDtypeStruct((2, 2, dp_count // 2, chunk, width), LOW)
+
+    def block(i, core_ref):
+        other = 1 - core_ref[0]
+        return (0, jnp.where(i < 2, 2 * i + other, 2 * (i - 2) + core_ref[0]))
+
+    return pl.pallas_call(
+        functools.partial(weight_grad_kernel, dp_count=dp_count),
+        grid_spec=pltpu.PrefetchScalarGridSpec(
+            num_scalar_prefetch=1,
+            grid=(4,),
+            in_specs=[whole(a), pl.BlockSpec((rows, width), block)],
+            out_specs=[
+                chunk_spec(dp_count, chunk, width, dp_first, first_two),
+                chunk_spec(dp_count, chunk, width, dp_first, last_two),
+            ],
+            scratch_shapes=[pltpu.VMEM((depth, rows), LOW)],
+        ),
+        out_shape=[made, made],
         compiler_params=params(),
         name="weight_grad",
-    )(a, b)
+    )(core, a, b)
+
+
+def add_split_kernel(bits_ref, *refs, parts, merged):
+    ins, outs = refs[: 2 * parts], refs[2 * parts :]
+    phase = pl.program_id(0)
+    for part in range(parts):
+        made = (ins[2 * part][...].astype(WIDE) + ins[2 * part + 1][...].astype(WIDE)).astype(LOW)
+        send, keep = (outs[0].at[part], outs[1].at[part]) if merged else outs[2 * part : 2 * part + 2]
+
+        @pl.when(phase == 0)
+        def _():
+            send[...] = made
+
+        @pl.when(phase == 1)
+        def _():
+            keep[...] = made
+
+
+def add_split(pairs, bits, merged=False):
+    parts = len(pairs)
+    shape = pairs[0][0].shape
+    half = shape[0] // 2
+    steps = 2 if half % 2 == 0 and half > 2 else 1
+    block = half // steps
+    tail = shape[1:]
+    zeros = (0,) * len(tail)
+
+    def source(part):
+        def index(phase, i, bits_ref):
+            mine = bits_ref[part]
+            return (jnp.where(phase == 0, 1 - mine, mine) * steps + i, *zeros)
+
+        return index
+
+    send_at = lambda phase, i: jnp.where(phase == 0, i, steps - 1)
+    keep_at = lambda phase, i: jnp.where(phase == 0, 0, i)
+    ins = [pl.BlockSpec((block, *tail), source(part)) for part in range(parts) for _ in range(2)]
+    if merged:
+        outs = [
+            pl.BlockSpec((parts, block, *tail), lambda phase, i, r, at=at: (0, at(phase, i), *zeros))
+            for at in (send_at, keep_at)
+        ]
+        out_shape = [jax.ShapeDtypeStruct((parts, half, *tail), LOW)] * 2
+    else:
+        outs = [
+            pl.BlockSpec((block, *tail), lambda phase, i, r, at=at: (at(phase, i), *zeros))
+            for _ in range(parts)
+            for at in (send_at, keep_at)
+        ]
+        out_shape = [jax.ShapeDtypeStruct((half, *tail), LOW)] * (2 * parts)
+    return pl.pallas_call(
+        functools.partial(add_split_kernel, parts=parts, merged=merged),
+        grid_spec=pltpu.PrefetchScalarGridSpec(
+            num_scalar_prefetch=1, grid=(2, steps), in_specs=ins, out_specs=outs
+        ),
+        out_shape=out_shape,
+        compiler_params=params(),
+        name="add_split",
+    )(bits, *[value for pair in pairs for value in pair])
 
 
 def gelu_pair(z):
@@ -329,36 +442,62 @@
     )(base, lengths)
 
 
-def qkv_grads(x, o, dq, dk, dv, da, heads):
+def qkv_grads(x, o, dq, dk, dv, da, core, dp_count):
     rows, depth = x.shape
-    part = depth // heads
-
-    def kernel(x_ref, o_ref, dq_ref, dk_ref, dv_ref, da_ref, out_ref, xt_ref, ot_ref):
-        @pl.when(pl.program_id(0) == 0)
+    part = depth // 4
+    chunk = depth // dp_count
+
+    def kernel(core_ref, x_ref, o_ref, dq_ref, dk_ref, dv_ref, da_ref, *refs):
+        outs, (xt_ref, ot_ref) = refs[:4], refs[4:]
+        step = pl.program_id(0)
+
+        @pl.when(step == 0)
         def _():
             xt_ref[...] = x_ref[...].T
             ot_ref[...] = o_ref[...].T
 
-        for head in range(heads):
-
-            @pl.when(pl.program_id(0) == head)
+        flip = jnp.where(step < 2, 1 - core_ref[0], core_ref[0])
+        wanted = 2 * (step % 2) + flip
+        for head in range(4):
+
+            @pl.when(wanted == head)
             def _():
                 at = slice(head * part, (head + 1) * part)
                 joined = jnp.concatenate([dq_ref[:, at], dk_ref[:, at], dv_ref[:, at]], axis=1)
                 first = dot_nn(xt_ref[...], joined)
                 second = dot_nn(ot_ref[...], da_ref[:, at])
-                out_ref[...] = jnp.concatenate([first, second], axis=1).astype(LOW)
-
+                made = jnp.concatenate([first, second], axis=1).astype(LOW)
+                for where_to, chosen in ((outs[0], step < 2), (outs[1], step >= 2)):
+
+                    @pl.when(chosen)
+                    def _():
+                        put_chunks(where_to, made[:, : 2 * part], dp_count)
+
+                for where_to, chosen in ((outs[2], step < 2), (outs[3], step >= 2)):
+
+                    @pl.when(chosen)
+                    def _():
+                        put_chunks(where_to, made[:, 2 * part :], dp_count)
+
+    made = jax.ShapeDtypeStruct((2, 2, dp_count // 2, chunk, 2 * part), LOW)
+    specs = [
+        chunk_spec(dp_count, chunk, 2 * part, dp_first, at)
+        for dp_first in (False, True)
+        for at in (first_two, last_two)
+    ]
     return pl.pallas_call(
         kernel,
-        grid=(heads,),
-        in_specs=[whole(v) for v in (x, o, dq, dk, dv, da)],
-        out_specs=pl.BlockSpec((None, depth, 4 * part), lambda i: (i, 0, 0)),
-        out_shape=jax.ShapeDtypeStruct((heads, depth, 4 * part), LOW),
-        scratch_shapes=[pltpu.VMEM((depth, rows), LOW)] * 2,
+        grid_spec=pltpu.PrefetchScalarGridSpec(
+            num_scalar_prefetch=1,
+            grid=(4,),
+            in_specs=[whole(v) for v in (x, o, dq, dk, dv, da)],
+            out_specs=specs,
+            scratch_shapes=[pltpu.VMEM((depth, rows), LOW)] * 2,
+        ),
+        out_shape=[made] * 4,
         compiler_params=params(),
         name="qkv_grads",
-    )(x, o, dq, dk, dv, da)
+    )(core, x, o, dq, dk, dv, da)
 
 
 def input_grad_kernel(du_ref, dq_ref, dk_ref, dv_ref, w_ref, out_ref):
@@ -414,28 +553,51 @@
     return value
 
 
-def sum_and_scatter(value, order):
-    head_count, dp_count = lax.axis_size("head"), lax.axis_size("dp")
-    head_bits, dp_bits = bits_of("head")[::-1], bits_of("dp")[::-1]
-    names = [("head", bit) for bit in head_bits] + [("dp", bit) for bit in dp_bits]
-    rows = value.shape[1] // dp_count
-    value = value.reshape([2] * len(names) + [rows, value.shape[2]])
-    for step, (axis, bit) in enumerate(order):
-        at = names.index((axis, bit))
-        names.pop(at)
-        mine = my_bit(axis, bit)
-        kept = lax.dynamic_index_in_dim(value, mine, at, keepdims=False)
-        sent = lax.dynamic_index_in_dim(value, 1 - mine, at, keepdims=False)
-        value = kept.astype(WIDE) + swap(sent, axis, bit).astype(WIDE)
-        if step < len(order) - 1:
-            value = value.astype(LOW)
-    return value
-
-
-def stage_orders():
-    head = [("head", bit) for bit in bits_of("head")]
-    dp = [("dp", bit) for bit in bits_of("dp")]
-    return head + dp, head[:1] + dp[:1] + head[1:] + dp[1:]
+class Summing:
+    def __init__(self, sends, keeps):
+        head, dp = bits_of("head"), bits_of("dp")
+        self.first = ("head", head[0])
+        self.stages = [
+            (("head", head[1]), ("dp", dp[0])),
+            (("dp", dp[0]), ("head", head[1])),
+        ] + [(("dp", bit),) * 2 for bit in dp[1:]]
+        self.at = 0
+        self.merged = False
+        self.kept = list(keeps)
+        self.got = [swap(send, *self.first) for send in sends]
+
+    def pairs(self):
+        kept, got = self.kept, self.got
+        if self.merged:
+            kept, got = [kept[0][0], kept[0][1]], [got[0][0], got[0][1]]
+        return [
+            (k.reshape(-1, *k.shape[-2:]), g.reshape(-1, *g.shape[-2:])) for k, g in zip(kept, got)
+        ]
+
+    def step(self, after):
+        stage = self.stages[self.at]
+        merge = self.at >= 2
+        bits = jnp.stack([my_bit(*one) for one in stage]).astype(jnp.int32)
+        pairs, _ = lax.optimization_barrier((self.pairs(), after))
+        outs = add_split(pairs, bits, merged=merge)
+        if merge:
+            self.got, self.kept = [swap(outs[0], *stage[0])], [outs[1]]
+        else:
+            self.got = [swap(outs[0], *stage[0]), swap(outs[2], *stage[1])]
+            self.kept = [outs[1], outs[3]]
+        self.merged = merge
+        self.at += 1
+        return outs[-1]
+
+    def finish(self):
+        while self.at < len(self.stages):
+            self.step(self.kept[0])
+        return (self.kept[0].astype(WIDE) + self.got[0].astype(WIDE))[:, 0]
+
+
+def ordered(after, *values):
+    values, _ = lax.optimization_barrier((values, after))
+    return values
 
 
 def on_device(
@@ -501,10 +663,18 @@
         rounded, residual = made[0], made[-1]
     out_state = rounded
     grad_state = out_grad
-    orders = stage_orders()
-    summed = [None] * layers
+    core = my_bit("head", bits_of("head")[0]).astype(jnp.int32).reshape(1)
     small_sums = [None] * layers
     hidden_sums = [None] * layers
+    ffn_groups, wide_groups = [None] * layers, [None] * layers
+    running = []
+
+    def advance(after):
+        for group in running:
+            if group.at < len(group.stages):
+                after = group.step(after)
+        return after
+
     for layer in reversed(range(layers)):
         rounded, q, k, v, probs, context, u1, hr, gr, slope, u2 = kept[layer]
         gains = jnp.stack([norm1_gain[layer], norm2_gain[layer]])
@@ -519,32 +689,51 @@
             gains,
             chunk=width,
         )
-        down_sum = sum_and_scatter(weight_grad(df, gr, hidden // head_count), orders[0])
-        up_sum = sum_and_scatter(weight_grad(hr, dz, hidden // head_count), orders[1])
+        token = advance(do)
+        (dz, hr) = ordered(token, dz, hr)
+        up_send, up_keep = weight_grad(hr, dz, core, dp_count, True)
+        (df, gr) = ordered(up_keep, df, gr)
+        down_send, down_keep = weight_grad(df, gr, core, dp_count, False)
+        ffn_groups[layer] = Summing((down_send, up_send), (down_keep, up_keep))
+        token = advance(down_keep)
+        (do, q) = ordered(token, do, q)
         dq, dk, dv, qv_sums = attention_backward(q, k, v, do, probs)
-        wide_sum = sum_and_scatter(
-            qkv_grads(rounded, context, dq, dk, dv, da, head_count), orders[0]
-        )
+        running.append(ffn_groups[layer])
+        token = advance(dv)
+        (dq, rounded) = ordered(token, dq, rounded)
+        a_send, a_keep, b_send, b_keep = qkv_grads(rounded, context, dq, dk, dv, da, core, dp_count)
+        wide_groups[layer] = Summing((a_send, b_send), (a_keep, b_keep))
+        (dq, du) = ordered(b_keep, dq, du)
         grad_state = input_grad(du, dq, dk, dv, full_qkv[layer], WIDE if layer else LOW)
-        summed[layer] = (up_sum, down_sum, wide_sum)
+        running.append(wide_groups[layer])
+        token = advance(grad_state)
+        if layer:
+            (grad_state,) = ordered(token, grad_state)
         small_sums[layer] = jnp.concatenate([sums[:6], qv_sums[:2]])
     small_sum, hidden_sum = (
         sum_everywhere(jnp.stack(part), ("head", "dp")) for part in (small_sums, hidden_sums)
     )
+    while any(group.at < len(group.stages) for group in running):
+        token = advance(token)
+    ffn_sums = [group.finish() for group in ffn_groups]
+    wide_sums = [group.finish() for group in wide_groups]
     part = width // head_count
-    wide = [layer_sums[2].reshape(-1, 4, part).transpose(1, 0, 2) for layer_sums in summed]
+    wide = [
+        [both[half, :, at * part : (at + 1) * part] for half in range(2) for at in range(2)]
+        for both in wide_sums
+    ]
     return (
         out_state,
         grad_state,
-        jnp.stack([w[:3] for w in wide]),
+        jnp.stack([jnp.stack(w[:3]) for w in wide]),
         small_sum[:, 6:8],
         jnp.stack([w[3] for w in wide]),
         small_sum[:, 5],
         small_sum[:, 3],
         small_sum[:, 4],
-        jnp.stack([layer_sums[0] for layer_sums in summed]),
+        jnp.stack([both[1] for both in ffn_sums]),
         hidden_sum[:, 0],
-        jnp.stack([layer_sums[1].T for layer_sums in summed]),
+        jnp.stack([both[0].T for both in ffn_sums]),
         small_sum[:, 2],
         small_sum[:, 0],
         small_sum[:, 1],

time: 621 us -> 575 us (0.926)
  waiting for transfers between devices: 187 us -> 90.4 us
  Pallas kernels: 267 us -> 345 us
  local copies, waits for them, and re-layouts: 75.3 us -> 62.4 us
  other arithmetic: 24.4 us -> 12.8 us
    ppermute x46 -> x48, waiting for transfers between devices: 187 us -> 90.4 us  [swap(): return lax.ppermute(value, axis, [(i, i ^ bit) for i in range(size)])]
    pallas_call x6 -> x22, Pallas kernels: 64.2 us -> 143 us  [the longest x16 72.2 us: add_split(): pl.pallas_call(functools.partial(add_split_kernel, parts=parts, merged=me...]
    dynamic_slice x12 -> x0, local copies, waits for them, and re-layouts: 31.7 us -> none  [the longest x6 22.2 us: sum_and_scatter(): kept = lax.dynamic_index_in_dim(value, mine, at, keepdims=False)]
    convert_element_type x24 -> x0, other arithmetic: 12.3 us -> none  [sum_and_scatter(): value = value.astype(LOW)]
    unnamed x52 -> x106, local copies, waits for them, and re-layouts: 6.21 us -> 18.1 us
    squeeze x24 -> x8, local copies, waits for them, and re-layouts: 1.09 us -> 7.32 us  [pairs(): kept, got = ([kept[0][0], kept[0][1]], [got[0][0], got[0][1]])]
    ppermute x46 -> x48, starting transfers between devices: 46.5 us -> 42.7 us  [swap(): return lax.ppermute(value, axis, [(i, i ^ bit) for i in range(size)])]
  transfers between devices with their start and end apart: 47 -> 49, of which waited for: 18 -> 16; matrix products, arithmetic and copies ran while one was open for 14% -> 9% of each run, Pallas kernels for 22% -> 44%
where the time goes in v3:
time: 575 us; the launch traced here: 569 us
  Pallas kernels  345 us (60%)
  waiting for transfers between devices  90.4 us (16%)
  local copies, waits for them, and re-layouts  62.4 us (11%)
  starting transfers between devices  42.8 us (7%)
  between operations  15 us (3%)
  other arithmetic  12.8 us (2%)
    ppermute x48, waiting for transfers between devices, swap(): return lax.ppermute(value, axis, [(i, i ^ bit) for i in range(size)])  90.4 us
    pallas_call x16, Pallas kernels, add_split(): pl.pallas_call(functools.partial(add_split_kernel, parts=parts, merged=me...  72.2 us
    pallas_call x2, Pallas kernels, attention_backward(): pl.pallas_call(functools.partial(attention_backward_kernel, tile=tile), g...  47.2 us
    pallas_call x2, Pallas kernels, ffn_forward(): pl.pallas_call(functools.partial(ffn_forward_kernel, chunk=chunk), grid=(...  45.8 us
    pallas_call x2, Pallas kernels, ffn_backward(): pl.pallas_call(functools.partial(ffn_backward_kernel, chunk=chunk), grid=...  44.4 us
    pallas_call x2, Pallas kernels, attention_forward(): pl.pallas_call(functools.partial(attention_forward_kernel, tile=tile), gr...  43.2 us
    ppermute x48, starting transfers between devices, swap(): return lax.ppermute(value, axis, [(i, i ^ bit) for i in range(size)])  42.7 us
    pallas_call x4, Pallas kernels, weight_grad(): pl.pallas_call(functools.partial(weight_grad_kernel, dp_count=dp_count),...  41.4 us
  transfers between devices with their start and end apart: 49, of which 16 were waited for; matrix products, arithmetic and copies ran while one was open for 9% of the time, Pallas kernels for 44%

profile of v3, /device:TPU:0, one launch (start us, length us, event | category | flops | bytes accessed | tf_op | source)
XLA Modules:
  0.0 568.6 jit_solution(4960357228249754067)
XLA Ops:
  14.6 8.8 %slice_bitcast_fusion = (bf16[3072,768]{1,0:T(8,128)(2,1)}, bf16[3072,768]{1,0:T(8,128)(2,1)}) fusion(bf16[2,3072,768]{2,1,0:T(8,128)(2,1)} %param.25), kind=kLoop, calls=%fused_computation | loop fusion | bytes 18874368 | tf_op jit(solution)/shard_map/squeeze | solution.py:656
  39.2 7.0 %collective-permute-done.5 = f32[2,2,192]{2,1,0:T(2,128)S(1)} collective-permute-done((f32[2,2,192]{2,1,0:T(2,128)S(1)}, f32[2,2,192]{2,1,0:T(2,128)S(1)}, u32[]{:S(2)}, u32[]{:S(2)}) %collective-permute-start.5) | collective-permute-done | bytes 3104 | tf_op jit(solution)/shard_map/ppermute | solution.py:530
  47.3 26.4 %collective-permute-done.2 = bf16[3,768,192]{1,2,0:T(8,128)(2,1)S(1)} collective-permute-done((bf16[3,768,192]{1,2,0:T(8,128)(2,1)}, bf16[3,768,192]{1,2,0:T(8,128)(2,1)S(1)}, u32[]{:S(2)}, u32[]{:S(2)}) %collective-permute-start.2) | collective-permute-done | bytes 884768 | tf_op jit(solution)/shard_map/ppermute | solution.py:530
  86.7 21.4 %attention_forward.2 = (bf16[1024,768]{1,0:T(8,128)(2,1)}, bf16[1024,768]{1,0:T(8,128)(2,1)}, bf16[1024,768]{1,0:T(8,128)(2,1)}, bf16[24,512,512]{2,1,0:T(8,128)(2,1)}, bf16[1024,768]{1,0:T(8,128)(2,1)}) custom-call(bf16[1024,768]{1,0:T(8,128)(2,1)} %x_ref.4, bf16[3,768,768]{2,1,0:T(8,128)(2,1)} %pad_maximum_fusion.1.w_ref, ...), custom_call_target="tpu_custom_call" | custom-call | tf_op jit(solution)/shard_map/attention_forward/pallas_call | solution.py:344
  108.1 23.0 %ffn_forward.2 = (f32[1024,768]{1,0:T(8,128)}, bf16[1024,768]{1,0:T(8,128)(2,1)}, bf16[1024,3072]{1,0:T(8,128)(2,1)}, bf16[1024,3072]{1,0:T(8,128)(2,1)}, f32[10...) custom-call(bf16[1024,768]{1,0:T(8,128)(2,1)} %get-tuple-element.208.o_ref, ...), custom_call_target="tpu_custom_call" | custom-call | tf_op jit(solution)/shard_map/ffn_forward/pallas_call | solution.py:85
  137.1 21.8 %attention_forward.3 = (bf16[1024,768]{1,0:T(8,128)(2,1)}, bf16[1024,768]{1,0:T(8,128)(2,1)}, bf16[1024,768]{1,0:T(8,128)(2,1)}, bf16[24,512,512]{2,1,0:T(8,128)(2,1)}, bf16[1024,768]{1,0:T(8,128)(2,1)}) custom-call(bf16[1024,768]{1,0:T(8,128)(2,1)} %get-tuple-element.244.x_ref, bf16[3,768,768]{2,1,0:T(8,128)(2,1)} %bitcast.147, ...), custom_call_target="tpu_custom_call" | custom-call | tf_op jit(solution)/shard_map/attention_forward/pallas_call | solution.py:344
  158.9 22.8 %ffn_forward.3 = (f32[1024,768]{1,0:T(8,128)}, bf16[1024,768]{1,0:T(8,128)(2,1)}, bf16[1024,3072]{1,0:T(8,128)(2,1)}, bf16[1024,3072]{1,0:T(8,128)(2,1)}, f32[10...) custom-call(bf16[1024,768]{1,0:T(8,128)(2,1)} %get-tuple-element.210.o_ref, f32[1024,768]{1,0:T(8,128)} %get-tuple-element.211.x_ref, ...), custom_call_target="tpu_custom_call" | custom-call | tf_op jit(solution)/shard_map/ffn_forward/pallas_call | solution.py:85
  181.7 21.9 %ffn_backward.2 = (bf16[1024,768]{1,0:T(8,128)(2,1)}, bf16[1024,3072]{1,0:T(8,128)(2,1)}, bf16[1024,768]{1,0:T(8,128)(2,1)}, bf16[1024,768]{1,0:T(8,128)(2,1)}, ...) custom-call(bf16[1024,768]{1,0:T(8,128)(2,1)} %gx_ref.1, f32[1024,768]{1,0:T(8,128)} %get-tuple-element.213.u2_ref, ...), custom_call_target="tpu_custom_call" | custom-call | tf_op jit(solution)/shard_map/ffn_backward/pallas_call | solution.py:150
  203.6 10.2 %weight_grad.4 = (bf16[2,2,4,96,768]{4,3,2,1,0:T(8,128)(2,1)}, bf16[2,2,4,96,768]{4,3,2,1,0:T(8,128)(2,1)}) custom-call(s32[1]{0:T(128)} %bitcast.26.bit_ref.core_ref, bf16[1024,768]{1,0:T(8,128)(2,1)} %get-tuple-element.222.a_ref, bf16[1024,3072]{1,0:T(8,128)(2,1)} %get-tuple-element.223.b_ref), custom_call_target="tpu_custom_call" | custom-call | tf_op jit(solution)/shard_map/weight_grad/pallas_call | solution.py:220
  213.9 10.5 %weight_grad.5 = (bf16[2,2,4,96,768]{4,3,2,1,0:T(8,128)(2,1)}, bf16[2,2,4,96,768]{4,3,2,1,0:T(8,128)(2,1)}) custom-call(s32[1]{0:T(128)} %bitcast.26.bit_ref.core_ref, bf16[1024,768]{1,0:T(8,128)(2,1)} %get-tuple-element.225.a_ref, bf16[1024,3072]{1,0:T(8,128)(2,1)} %get-tuple-element.226.b_ref), custom_call_target="tpu_custom_call" | custom-call | tf_op jit(solution)/shard_map/weight_grad/pallas_call | solution.py:220
  225.5 23.5 %attention_backward.2 = (bf16[1024,768]{1,0:T(8,128)(2,1)}, bf16[1024,768]{1,0:T(8,128)(2,1)}, bf16[1024,768]{1,0:T(8,128)(2,1)}, f32[8,768]{1,0:T(8,128)}) custom-call(bf16[1024,768]{1,0:T(8,128)(2,1)} %get-tuple-element.228.q_ref, bf16[1024,768]{1,0:T(8,128)(2,1)} %get-tuple-element.229.k_ref, bf16[1024,768]{1,0:T(8,128)(2,1)} %get-tuple-element.230.v_ref, ...), custom_call_target="tpu_custom_call" | custom-call | tf_op jit(solution)/shard_map/attention_backward/pallas_call | solution.py:405
  250.5 7.8 %add_split.16 = (bf16[8,96,768]{2,1,0:T(8,128)(2,1)}, bf16[8,96,768]{2,1,0:T(8,128)(2,1)}, bf16[8,96,768]{2,1,0:T(8,128)(2,1)}, bf16[8,96,768]{2,1,0:T(8,128)(2,1)}) custom-call(s32[2]{0:T(128)} %get-tuple-element.469.bits_ref, bf16[16,96,768]{2,1,0:T(8,128)(2,1)} %bitcast.160, bf16[16,96,768]{2,1,0:T(8,128)(2,1)} %bitcast.161, ...), custom_call_target="tpu_custom_call" | custom-call | tf_op jit(solution)/shard_map/add_split/pallas_call | solution.py:286
  260.4 14.6 %qkv_grads.2 = (bf16[2,2,4,96,384]{4,3,2,1,0:T(8,128)(2,1)}, bf16[2,2,4,96,384]{4,3,2,1,0:T(8,128)(2,1)}, bf16[2,2,4,96,384]{4,3,2,1,0:T(8,128)(2,1)}, bf16[2,2,4,96,384]{4,3,2,1,0:T(8,128)(2,1)}) custom-call(s32[1]{0:T(128)} %bitcast.26.bit_ref.core_ref, bf16[1024,768]{1,0:T(8,128)(2,1)} %get-tuple-element.244.x_ref, ...), custom_call_target="tpu_custom_call" | custom-call | tf_op jit(solution)/shard_map/qkv_grads/pallas_call | solution.py:488
  275.5 8.9 %input_grad.2.gx_ref = f32[1024,768]{1,0:T(8,128)} custom-call(f32[1024,768]{1,0:T(8,128)} %get-tuple-element.248.du_ref, bf16[1024,768]{1,0:T(8,128)(2,1)} %get-tuple-element.249.dq_ref, bf16[1024,768]{1,0:T(8,128)(2,1)} %get-tuple-element.245.dk_ref, bf16[1024,768]{1,0:T(8,128)(2,1)} %get-tuple-element.236.dv_ref, bf16[3,768,768]{2,1,0:T(8,128)(2,1)} %bitcast.148), custom_call_target="tpu_custom_call" | custom-call | tf_op jit(solution)/shard_map/input_grad/pallas_call | solution.py:512
  305.3 22.5 %ffn_backward.3 = (bf16[1024,768]{1,0:T(8,128)(2,1)}, bf16[1024,3072]{1,0:T(8,128)(2,1)}, bf16[1024,768]{1,0:T(8,128)(2,1)}, bf16[1024,768]{1,0:T(8,128)(2,1)}, ...) custom-call(f32[1024,768]{1,0:T(8,128)} %input_grad.2.gx_ref, f32[1024,768]{1,0:T(8,128)} %get-tuple-element.267.u2_ref, ...), custom_call_target="tpu_custom_call" | custom-call | tf_op jit(solution)/shard_map/ffn_backward/pallas_call | solution.py:150
  344.2 10.2 %weight_grad.6 = (bf16[2,2,4,96,768]{4,3,2,1,0:T(8,128)(2,1)}, bf16[2,2,4,96,768]{4,3,2,1,0:T(8,128)(2,1)}) custom-call(s32[1]{0:T(128)} %bitcast.26.bit_ref.core_ref, bf16[1024,768]{1,0:T(8,128)(2,1)} %get-tuple-element.296.a_ref, bf16[1024,3072]{1,0:T(8,128)(2,1)} %get-tuple-element.297.b_ref), custom_call_target="tpu_custom_call" | custom-call | tf_op jit(solution)/shard_map/weight_grad/pallas_call | solution.py:220
  354.4 10.4 %weight_grad.7 = (bf16[2,2,4,96,768]{4,3,2,1,0:T(8,128)(2,1)}, bf16[2,2,4,96,768]{4,3,2,1,0:T(8,128)(2,1)}) custom-call(s32[1]{0:T(128)} %bitcast.26.bit_ref.core_ref, bf16[1024,768]{1,0:T(8,128)(2,1)} %get-tuple-element.299.a_ref, bf16[1024,3072]{1,0:T(8,128)(2,1)} %get-tuple-element.300.b_ref), custom_call_target="tpu_custom_call" | custom-call | tf_op jit(solution)/shard_map/weight_grad/pallas_call | solution.py:220
  373.0 23.7 %attention_backward.3 = (bf16[1024,768]{1,0:T(8,128)(2,1)}, bf16[1024,768]{1,0:T(8,128)(2,1)}, bf16[1024,768]{1,0:T(8,128)(2,1)}, f32[8,768]{1,0:T(8,128)}) custom-call(bf16[1024,768]{1,0:T(8,128)(2,1)} %get-tuple-element.312.q_ref, bf16[1024,768]{1,0:T(8,128)(2,1)} %get-tuple-element.313.k_ref, bf16[1024,768]{1,0:T(8,128)(2,1)} %get-tuple-element.314.v_ref, ...), custom_call_target="tpu_custom_call" | custom-call | tf_op jit(solution)/shard_map/attention_backward/pallas_call | solution.py:405
  415.4 7.9 %add_split.24 = (bf16[8,96,768]{2,1,0:T(8,128)(2,1)}, bf16[8,96,768]{2,1,0:T(8,128)(2,1)}, bf16[8,96,768]{2,1,0:T(8,128)(2,1)}, bf16[8,96,768]{2,1,0:T(8,128)(2,1)}) custom-call(s32[2]{0:T(128)} %get-tuple-element.469.bits_ref, bf16[16,96,768]{2,1,0:T(8,128)(2,1)} %bitcast.156, bf16[16,96,768]{2,1,0:T(8,128)(2,1)} %bitcast.157, ...), custom_call_target="tpu_custom_call" | custom-call | tf_op jit(solution)/shard_map/add_split/pallas_call | solution.py:286
  426.1 24.3 %collective-permute-done.45 = f32[2,1,3072]{2,0,1:T(2,128)S(1)} collective-permute-done((f32[2,1,3072]{2,0,1:T(2,128)S(1)}, f32[2,1,3072]{2,0,1:T(2,128)S(1)}, u32[]{:S(2)}, u32[]{:S(2)}) %collective-permute-start.45) | collective-permute-done | bytes 24608 | tf_op jit(solution)/shard_map/ppermute | solution.py:530
  457.0 14.6 %qkv_grads.3 = (bf16[2,2,4,96,384]{4,3,2,1,0:T(8,128)(2,1)}, bf16[2,2,4,96,384]{4,3,2,1,0:T(8,128)(2,1)}, bf16[2,2,4,96,384]{4,3,2,1,0:T(8,128)(2,1)}, bf16[2,2,4,96,384]{4,3,2,1,0:T(8,128)(2,1)}) custom-call(s32[1]{0:T(128)} %bitcast.26.bit_ref.core_ref, bf16[1024,768]{1,0:T(8,128)(2,1)} %x_ref.4, bf16[1024,768]{1,0:T(8,128)(2,1)} %get-tuple-element.208.o_ref, ...), custom_call_target="tpu_custom_call" | custom-call | tf_op jit(solution)/shard_map/qkv_grads/pallas_call | solution.py:488
  473.3 8.6 %input_grad.3 = bf16[1024,768]{1,0:T(8,128)(2,1)} custom-call(f32[1024,768]{1,0:T(8,128)} %get-tuple-element.338.du_ref, bf16[1024,768]{1,0:T(8,128)(2,1)} %get-tuple-element.339.dq_ref, bf16[1024,768]{1,0:T(8,128)(2,1)} %get-tuple-element.335.dk_ref, bf16[1024,768]{1,0:T(8,128)(2,1)} %get-tuple-element.321.dv_ref, bf16[3,768,768]{2,1,0:T(8,128)(2,1)} %pad_maximum_fusion.1.w_ref), custom_call_target="tpu_custom_call" | custom-call | tf_op jit(solution)/shard_map/input_grad/pallas_call | solution.py:512
  512.7 6.7 %collective-permute-done.26.refs_1_ = bf16[8,96,384]{2,1,0:T(8,128)(2,1)S(1)} collective-permute-done((bf16[8,96,384]{2,1,0:T(8,128)(2,1)}, bf16[8,96,384]{2,1,0:T(8,128)(2,1)S(1)}, u32[]{:S(2)}, u32[]{:S(2)}) %collective-permute-start.26) | collective-permute-done | bytes 589856 | tf_op jit(solution)/shard_map/ppermute | solution.py:530
  539.8 6.7 %collective-permute-done.41 = bf16[2,1,96,768]{3,2,1,0:T(8,128)(2,1)S(1)} collective-permute-done((bf16[2,1,96,768]{3,2,1,0:T(8,128)(2,1)}, bf16[2,1,96,768]{3,2,1,0:T(8,128)(2,1)S(1)}, u32[]{:S(2)}, u32[]{:S(2)}) %collective-permute-start.41) | collective-permute-done | bytes 294944 | tf_op jit(solution)/shard_map/ppermute | solution.py:530
  (283 shorter events, 189.5 us)
Async XLA Ops:
  7.2 123.8 %all-gather.3.cloned.1.call-start = ((), (), s32[]{:S(2)}) async-start(), calls=%async_computation | async-start | bytes 4423680 | tf_op jit(solution)/shard_map/all_gather | solution.py:631
  7.8 31.4 %collective-permute-start.4 = (f32[2,2,192]{2,1,0:T(2,128)}, f32[2,2,192]{2,1,0:T(2,128)S(1)}, u32[]{:S(2)}, u32[]{:S(2)}) collective-permute-start(f32[2,2,192]{2,1,0:T(2,128)} %param.18), channel_id=1, source_target_pairs={{0,2},{1,3},{2,0},{3,1},{4,6},{5,7},{6,4},{7,5},{8,10},{9,11},{10,... | collective-permute-start | bytes 9224 | tf_op jit(solution)/shard_map/ppermute | solution.py:530
  13.4 32.8 %collective-permute-start = (bf16[3,768,192]{1,2,0:T(8,128)(2,1)}, bf16[3,768,192]{1,2,0:T(8,128)(2,1)}, u32[]{:S(2)}, u32[]{:S(2)}) collective-permute-start(bf16[3,768,192]{1,2,0:T(8,128)(2,1)} %get-tuple-element.413), channel_id=1, source_target_pairs={{0,1},{1,0},{2,3},{3,2},{4,5},{5,4},{6,7},{7,6},{8,9},{9,8},{10,11... | collective-permute-start | bytes 2654216 | tf_op jit(solution)/shard_map/ppermute | solution.py:530
  13.6 33.7 %collective-permute-start.1 = (bf16[3,768,192]{1,2,0:T(8,128)(2,1)}, bf16[3,768,192]{1,2,0:T(8,128)(2,1)}, u32[]{:S(2)}, u32[]{:S(2)}) collective-permute-start(bf16[3,768,192]{1,2,0:T(8,128)(2,1)} %get-tuple-element.413), channel_id=1, source_target_pairs={{0,2},{1,3},{2,0},{3,1},{4,6},{5,7},{6,4},{7,5},{8,10},{9,11},{10,... | collective-permute-start | bytes 2654216 | tf_op jit(solution)/shard_map/ppermute | solution.py:530
  46.2 27.4 %collective-permute-start.2 = (bf16[3,768,192]{1,2,0:T(8,128)(2,1)}, bf16[3,768,192]{1,2,0:T(8,128)(2,1)S(1)}, u32[]{:S(2)}, u32[]{:S(2)}) collective-permute-start(bf16[3,768,192]{1,2,0:T(8,128)(2,1)} %collective-permute-done), channel_id=1, source_target_pairs={{0,2},{1,3},{2,0},{3,1},{4,6},{5,7},{6,4},{7,5},{8,10},{9,11},{10,... | collective-permute-start | bytes 2654216 | tf_op jit(solution)/shard_map/ppermute | solution.py:530
  224.3 24.7 %collective-permute-start.7 = (bf16[2,2,4,96,768]{4,3,2,1,0:T(8,128)(2,1)}, bf16[2,2,4,96,768]{4,3,2,1,0:T(8,128)(2,1)}, u32[]{:S(2)}, u32[]{:S(2)}) collective-permute-start(bf16[2,2,4,96,768]{4,3,2,1,0:T(8,128)(2,1)} %get-tuple-element.235), channel_id=1, source_target_pairs={{0,1},{1,0},{2,3},{3,2},{4,5},{5,4},{6,7},{7,6},{8,9},{9,8},{10,11... | collective-permute-start | bytes 7077896 | tf_op jit(solution)/shard_map/ppermute | solution.py:530
  258.3 28.1 %collective-permute-start.10 = (bf16[8,96,768]{2,1,0:T(8,128)(2,1)}, bf16[8,96,768]{2,1,0:T(8,128)(2,1)S(1)}, u32[]{:S(2)}, u32[]{:S(2)}) collective-permute-start(bf16[8,96,768]{2,1,0:T(8,128)(2,1)} %get-tuple-element.254), channel_id=1, source_target_pairs={{0,2},{1,3},{2,0},{3,1},{4,6},{5,7},{6,4},{7,5},{8,10},{9,11},{10,... | collective-permute-start | bytes 3538952 | tf_op jit(solution)/shard_map/ppermute | solution.py:530
  258.6 27.9 %collective-permute-start.11 = (bf16[8,96,768]{2,1,0:T(8,128)(2,1)}, bf16[8,96,768]{2,1,0:T(8,128)(2,1)S(1)}, u32[]{:S(2)}, u32[]{:S(2)}) collective-permute-start(bf16[8,96,768]{2,1,0:T(8,128)(2,1)} %get-tuple-element.255), channel_id=1, source_target_pairs={{0,4},{4,0},{8,12},{12,8},{16,20},{20,16},{24,28},{28,24},{1,5},{5... | collective-permute-start | bytes 3538952 | tf_op jit(solution)/shard_map/ppermute | solution.py:530
  293.6 34.2 %collective-permute-start.14 = (bf16[4,96,768]{2,1,0:T(8,128)(2,1)}, bf16[4,96,768]{2,1,0:T(8,128)(2,1)S(1)}, u32[]{:S(2)}, u32[]{:S(2)}) collective-permute-start(bf16[4,96,768]{2,1,0:T(8,128)(2,1)} %get-tuple-element.276), channel_id=1, source_target_pairs={{0,4},{4,0},{8,12},{12,8},{16,20},{20,16},{24,28},{28,24},{1,5},{5... | collective-permute-start | bytes 1769480 | tf_op jit(solution)/shard_map/ppermute | solution.py:530
  295.1 32.7 %collective-permute-start.15 = (bf16[4,96,768]{2,1,0:T(8,128)(2,1)}, bf16[4,96,768]{2,1,0:T(8,128)(2,1)S(1)}, u32[]{:S(2)}, u32[]{:S(2)}) collective-permute-start(bf16[4,96,768]{2,1,0:T(8,128)(2,1)} %get-tuple-element.277), channel_id=1, source_target_pairs={{0,2},{1,3},{2,0},{3,1},{4,6},{5,7},{6,4},{7,5},{8,10},{9,11},{10,... | collective-permute-start | bytes 1769480 | tf_op jit(solution)/shard_map/ppermute | solution.py:530
  303.5 31.2 %collective-permute-start.12 = (bf16[8,96,384]{2,1,0:T(8,128)(2,1)}, bf16[8,96,384]{2,1,0:T(8,128)(2,1)S(1)}, u32[]{:S(2)}, u32[]{:S(2)}) collective-permute-start(bf16[8,96,384]{2,1,0:T(8,128)(2,1)} %get-tuple-element.273), channel_id=1, source_target_pairs={{0,2},{1,3},{2,0},{3,1},{4,6},{5,7},{6,4},{7,5},{8,10},{9,11},{10,... | collective-permute-start | bytes 1769480 | tf_op jit(solution)/shard_map/ppermute | solution.py:530
  304.1 30.6 %collective-permute-start.13 = (bf16[8,96,384]{2,1,0:T(8,128)(2,1)}, bf16[8,96,384]{2,1,0:T(8,128)(2,1)S(1)}, u32[]{:S(2)}, u32[]{:S(2)}) collective-permute-start(bf16[8,96,384]{2,1,0:T(8,128)(2,1)} %get-tuple-element.274), channel_id=1, source_target_pairs={{0,4},{4,0},{8,12},{12,8},{16,20},{20,16},{24,28},{28,24},{1,5},{5... | collective-permute-start | bytes 1769480 | tf_op jit(solution)/shard_map/ppermute | solution.py:530
  332.4 33.0 %collective-permute-start.18 = (bf16[2,2,96,768]{3,2,1,0:T(8,128)(2,1)}, bf16[2,2,96,768]{3,2,1,0:T(8,128)(2,1)S(1)}, u32[]{:S(2)}, u32[]{:S(2)}) collective-permute-start(bf16[2,2,96,768]{3,2,1,0:T(8,128)(2,1)} %get-tuple-element.291), channel_id=1, source_target_pairs={{0,8},{4,12},{8,0},{12,4},{16,24},{20,28},{24,16},{28,20},{1,9},{5... | collective-permute-start | bytes 1769480 | tf_op jit(solution)/shard_map/ppermute | solution.py:530
  340.5 28.7 %collective-permute-start.16 = (bf16[4,96,384]{2,1,0:T(8,128)(2,1)}, bf16[4,96,384]{2,1,0:T(8,128)(2,1)S(1)}, u32[]{:S(2)}, u32[]{:S(2)}) collective-permute-start(bf16[4,96,384]{2,1,0:T(8,128)(2,1)} %get-tuple-element.288), channel_id=1, source_target_pairs={{0,4},{4,0},{8,12},{12,8},{16,20},{20,16},{24,28},{28,24},{1,5},{5... | collective-permute-start | bytes 884744 | tf_op jit(solution)/shard_map/ppermute | solution.py:530
  342.0 27.2 %collective-permute-start.17 = (bf16[4,96,384]{2,1,0:T(8,128)(2,1)}, bf16[4,96,384]{2,1,0:T(8,128)(2,1)S(1)}, u32[]{:S(2)}, u32[]{:S(2)}) collective-permute-start(bf16[4,96,384]{2,1,0:T(8,128)(2,1)} %get-tuple-element.290), channel_id=1, source_target_pairs={{0,2},{1,3},{2,0},{3,1},{4,6},{5,7},{6,4},{7,5},{8,10},{9,11},{10,... | collective-permute-start | bytes 884744 | tf_op jit(solution)/shard_map/ppermute | solution.py:530
  364.9 48.4 %collective-permute-start.19 = (bf16[2,2,4,96,768]{4,3,2,1,0:T(8,128)(2,1)}, bf16[2,2,4,96,768]{4,3,2,1,0:T(8,128)(2,1)S(1)}, u32[]{:S(2)}, u32[]{:S(2)}) collective-permute-start(bf16[2,2,4,96,768]{4,3,2,1,0:T(8,128)(2,1)} %get-tuple-element.318), channel_id=1, source_target_pairs={{0,1},{1,0},{2,3},{3,2},{4,5},{5,4},{6,7},{7,6},{8,9},{9,8},{10,11... | collective-permute-start | bytes 7077896 | tf_op jit(solution)/shard_map/ppermute | solution.py:530
  364.9 48.4 %collective-permute-start.20 = (bf16[2,2,4,96,768]{4,3,2,1,0:T(8,128)(2,1)S(1)}, bf16[2,2,4,96,768]{4,3,2,1,0:T(8,128)(2,1)S(1)}, u32[]{:S(2)}, u32[]{:S(2)}) collective-permute-start(bf16[2,2,4,96,768]{4,3,2,1,0:T(8,128)(2,1)S(1)} %copy-done.43), channel_id=1, source_target_pairs={{0,1},{1,0},{2,3},{3,2},{4,5},{5,4},{6,7},{7,6},{8,9},{9,8},{10,11... | collective-permute-start | bytes 7077896 | tf_op jit(solution)/shard_map/ppermute | solution.py:530
  399.5 25.0 %collective-permute-start.44 = (f32[2,1,3072]{2,0,1:T(2,128)S(1)}, f32[2,1,3072]{2,0,1:T(2,128)S(1)}, u32[]{:S(2)}, u32[]{:S(2)}) collective-permute-start(f32[2,1,3072]{2,0,1:T(2,128)S(1)} %fusion.1), channel_id=1, source_target_pairs={{0,2},{1,3},{2,0},{3,1},{4,6},{5,7},{6,4},{7,5},{8,10},{9,11},{10,... | collective-permute-start | bytes 73736 | tf_op jit(solution)/shard_map/ppermute | solution.py:530
  407.1 43.9 %collective-permute-start.39 = (f32[2,8,768]{2,1,0:T(8,128)S(1)}, f32[2,8,768]{2,1,0:T(8,128)S(1)}, u32[]{:S(2)}, u32[]{:S(2)}) collective-permute-start(f32[2,8,768]{2,1,0:T(8,128)S(1)} %add.122), channel_id=1, source_target_pairs={{0,8},{4,12},{8,0},{12,4},{16,24},{20,28},{24,16},{28,20},{1,9},{5... | collective-permute-start | bytes 147464 | tf_op jit(solution)/shard_map/ppermute | solution.py:530
  423.3 58.7 %collective-permute-start.24 = (bf16[8,96,768]{2,1,0:T(8,128)(2,1)}, bf16[8,96,768]{2,1,0:T(8,128)(2,1)S(1)}, u32[]{:S(2)}, u32[]{:S(2)}) collective-permute-start(bf16[8,96,768]{2,1,0:T(8,128)(2,1)} %get-tuple-element.344), channel_id=1, source_target_pairs={{0,2},{1,3},{2,0},{3,1},{4,6},{5,7},{6,4},{7,5},{8,10},{9,11},{10,... | collective-permute-start | bytes 3538952 | tf_op jit(solution)/shard_map/ppermute | solution.py:530
  424.0 58.0 %collective-permute-start.25 = (bf16[8,96,768]{2,1,0:T(8,128)(2,1)}, bf16[8,96,768]{2,1,0:T(8,128)(2,1)S(1)}, u32[]{:S(2)}, u32[]{:S(2)}) collective-permute-start(bf16[8,96,768]{2,1,0:T(8,128)(2,1)} %get-tuple-element.345), channel_id=1, source_target_pairs={{0,4},{4,0},{8,12},{12,8},{16,20},{20,16},{24,28},{28,24},{1,5},{5... | collective-permute-start | bytes 3538952 | tf_op jit(solution)/shard_map/ppermute | solution.py:530
  424.5 25.9 %collective-permute-start.45 = (f32[2,1,3072]{2,0,1:T(2,128)S(1)}, f32[2,1,3072]{2,0,1:T(2,128)S(1)}, u32[]{:S(2)}, u32[]{:S(2)}) collective-permute-start(f32[2,1,3072]{2,0,1:T(2,128)S(1)} %fusion.13), channel_id=1, source_target_pairs={{0,4},{4,0},{8,12},{12,8},{16,20},{20,16},{24,28},{28,24},{1,5},{5... | collective-permute-start | bytes 73736 | tf_op jit(solution)/shard_map/ppermute | solution.py:530
  471.7 26.2 %collective-permute-start.22 = (bf16[2,2,4,96,384]{4,3,2,1,0:T(8,128)(2,1)}, bf16[2,2,4,96,384]{4,3,2,1,0:T(8,128)(2,1)S(1)}, u32[]{:S(2)}, u32[]{:S(2)}) collective-permute-start(bf16[2,2,4,96,384]{4,3,2,1,0:T(8,128)(2,1)} %get-tuple-element.341), channel_id=1, source_target_pairs={{0,1},{1,0},{2,3},{3,2},{4,5},{5,4},{6,7},{7,6},{8,9},{9,8},{10,11... | collective-permute-start | bytes 3538952 | tf_op jit(solution)/shard_map/ppermute | solution.py:530
  471.7 26.3 %collective-permute-start.23 = (bf16[2,2,4,96,384]{4,3,2,1,0:T(8,128)(2,1)}, bf16[2,2,4,96,384]{4,3,2,1,0:T(8,128)(2,1)S(1)}, u32[]{:S(2)}, u32[]{:S(2)}) collective-permute-start(bf16[2,2,4,96,384]{4,3,2,1,0:T(8,128)(2,1)} %get-tuple-element.342), channel_id=1, source_target_pairs={{0,1},{1,0},{2,3},{3,2},{4,5},{5,4},{6,7},{7,6},{8,9},{9,8},{10,11... | collective-permute-start | bytes 3538952 | tf_op jit(solution)/shard_map/ppermute | solution.py:530
  (75 other events, 739.0 us)
Sparse Core Ops, SparseCore 0:
  14.0 48.5 all-gather.2

commit v4 on v1

v4 whole, which is shorter than its diff:
```python
import functools
import math

import jax
import jax.numpy as jnp
from jax import lax
from jax.experimental import pallas as pl
from jax.experimental.pallas import tpu as pltpu
from jax.sharding import PartitionSpec as P

HD = 64
EPSILON = 1e-06
LOW = jnp.bfloat16
WIDE = jnp.float32
VMEM_BYTES = 58 << 20
ROOT_HALF = 0.7071067811865476
INV_ROOT_TAU = 0.3989422804014327
FAR = -1e30


def row_stats(values):
    centre = jnp.mean(values, axis=-1, keepdims=True)
    centred = values - centre
    spread = jnp.mean(centred * centred, axis=-1, keepdims=True)
    inverse = lax.rsqrt(spread + EPSILON)
    return centred * inverse, inverse


def norm_backward(upstream, xhat, inverse, gain):
    scaled = upstream * gain
    first = jnp.mean(scaled, axis=-1, keepdims=True)
    second = jnp.mean(scaled * xhat, axis=-1, keepdims=True)
    return (scaled - first - xhat * second) * inverse


def column_sum(values):
    return jnp.sum(values, axis=0, keepdims=True)


def dot_nn(left, right):
    return jnp.dot(left, right, preferred_element_type=WIDE)


def dot_nt(left, right):
    return lax.dot_general(left, right, (((1,), (1,)), ((), ())), preferred_element_type=WIDE)


def dot_tn(left, right):
    return lax.dot_general(left, right, (((0,), (0,)), ((), ())), preferred_element_type=WIDE)


def gelu_pair(z):
    cdf = 0.5 + 0.5 * lax.erf(z * ROOT_HALF)
    return z * cdf, cdf + z * (jnp.exp(z * z * -0.5) * INV_ROOT_TAU)


def pick(mask, values):
    return jnp.where(mask, values, jnp.zeros_like(values))


def head_masks(width):
    lanes = lax.broadcasted_iota(jnp.int32, (1, width), 1) // HD
    return [lanes == head for head in range(width // HD)]


def params():
    return pltpu.CompilerParams(vmem_limit_bytes=VMEM_BYTES)


def whole(array):
    return pl.BlockSpec(array.shape, lambda *ids: (0,) * array.ndim, pipeline_mode=pl.Buffered(1))


def in_place():
    return pl.BlockSpec(memory_space=pl.ANY)


def in_hbm():
    return pl.BlockSpec(memory_space=pltpu.HBM)


def shape_of(shape, kind):
    return jax.ShapeDtypeStruct(shape, kind)


def cost(flops, out_shape, operands):
    made = out_shape if isinstance(out_shape, (list, tuple)) else [out_shape]
    moved = sum(math.prod(v.shape) * jnp.dtype(v.dtype).itemsize for v in [*made, *operands])
    return pl.CostEstimate(flops=flops, bytes_accessed=moved, transcendentals=0)


def stored(shape, kind):
    return pltpu.HBM(shape, kind)


def call(kernel, name, grid, in_specs, out_specs, out_shape, scratch, scalars, operands, alias=None, flops=0):
    return pl.pallas_call(
        kernel,
        grid_spec=pltpu.PrefetchScalarGridSpec(
            num_scalar_prefetch=len(scalars),
            grid=grid,
            in_specs=in_specs,
            out_specs=out_specs,
            scratch_shapes=scratch,
        ),
        out_shape=out_shape,
        compiler_params=params(),
        input_output_aliases=alias or {},
        cost_estimate=cost(flops, out_shape, operands),
        name=name,
    )(*scalars, *operands)


def mask_kernel(base_ref, lengths_ref, bias_ref):
    slots, rows, _ = bias_ref.shape
    across = lax.broadcasted_iota(jnp.int32, (8, rows), 1)
    down = lax.broadcasted_iota(jnp.int32, (rows, 128), 0)
    for slot in range(slots):
        reach = jnp.int32(0)
        seg_across = jnp.zeros((8, rows), jnp.int32)
        seg_down = jnp.zeros((rows, 128), jnp.int32)
        for k in range(lengths_ref.shape[1]):
            reach = reach + lengths_ref[base_ref[0] + slot, k]
            seg_across += (across >= reach).astype(jnp.int32)
            seg_down += (down >= reach).astype(jnp.int32)
        inside = seg_down[:, 0:1] == seg_across[0:1, :]
        bias_ref[slot] = jnp.where(inside, 0.0, FAR)


def mask_bias(lengths, base, slots, slot_rows):
    smem = pl.BlockSpec(memory_space=pltpu.SMEM)
    return pl.pallas_call(
        mask_kernel,
        in_specs=[smem, smem],
        out_shape=shape_of((slots, slot_rows, slot_rows), WIDE),
        compiler_params=params(),
        name="mask_bias",
    )(base, lengths)


def attention_forward_kernel(
    x_ref, wa_ref, wb_ref, b_ref, bias_ref, *refs, aliased, tile
):
    mixed_ref, p_ref, s_ref = refs[2 * aliased :]
    rows, part = x_ref.shape[0], wa_ref.shape[0] // 3
    x = x_ref[...]
    masks = head_masks(part)

    def work(w_ref):
        q = ((dot_nt(x, w_ref[:part]) + b_ref[0]).astype(LOW) * HD**-0.5).astype(LOW)
        k = dot_nt(x, w_ref[part : 2 * part]).astype(LOW)
        v = (dot_nt(x, w_ref[2 * part :]) + b_ref[1]).astype(LOW)
        mixed_ref[0] = q
        mixed_ref[1] = k
        mixed_ref[2] = v
        total = None
        for head, mask in enumerate(masks):
            s_ref[head] = dot_nt(pick(mask, q), k)
            for start in range(0, rows, tile):
                at = slice(start, start + tile)
                s = s_ref[head, at] + bias_ref[at]
                e = jnp.exp(s - jnp.max(s, axis=1, keepdims=True))
                p_ref[head, at] = (e * (1.0 / jnp.sum(e, axis=1, keepdims=True))).astype(LOW)
            made = dot_nn(p_ref[head], pick(mask, v))
            total = made if total is None else total + made
        mixed_ref[3] = total.astype(LOW)

    for block, w_ref in enumerate((wa_ref, wb_ref)):

        @pl.when(pl.program_id(1) == block)
        def _():
            work(w_ref)


def attention_forward(x, wa, wb, qv_bias, bias, first, before, tile=64):
    rows, width = x.shape
    slots, slot_rows, _ = bias.shape
    part = wa.shape[0] // 3
    heads = part // HD
    aliased = int(before is not None)
    mixed = shape_of((4, 4, rows, part), LOW)
    probs = shape_of((4, slots, heads, slot_rows, slot_rows), LOW)
    return call(
        functools.partial(attention_forward_kernel, aliased=aliased, tile=tile),
        "attention_forward",
        (slots, 2),
        [
            pl.BlockSpec((slot_rows, width), lambda s, b: (s, 0)),
            whole(wa),
            whole(wb),
            pl.BlockSpec((None, 2, 1, part), lambda s, b: (b, 0, 0, 0)),
            pl.BlockSpec((None, slot_rows, slot_rows), lambda s, b: (s, 0, 0)),
        ]
        + [in_place(), in_place()] * aliased,
        [
            pl.BlockSpec((None, 4, slot_rows, part), lambda s, b: (first + b, 0, s, 0)),
            pl.BlockSpec(
                (None, None, heads, slot_rows, slot_rows), lambda s, b: (first + b, s, 0, 0, 0)
            ),
        ],
        [mixed, probs],
        [pltpu.VMEM((heads, slot_rows, slot_rows), WIDE)],
        [],
        [x, wa, wb, qv_bias, bias, *(before or ())],
        alias={5: 0, 6: 1} if aliased else None,
        flops=12 * rows * width * part + 16 * heads * rows * slot_rows * 256,
    )


def row_tiles(rows, tile):
    return [pl.ds(start, tile) for start in range(0, rows, tile)]


def ffn_forward_kernel(own_ref, mixed_hbm, x_hbm, wo_hbm, wu_ref, wd_ref, bu_ref, small_ref,
                       u1_hbm, hr_hbm, gr_hbm, gp_hbm, u2_hbm, low_hbm,
                       o_ref, x_ref, wo_ref, u1_ref, hr_ref, gr_ref, gp_ref, u2_ref, low_ref, in_sems, out_sems, g_sems,
                       *, layer, tile, renorm):
    step, steps = pl.program_id(0), pl.num_programs(0)
    part = o_ref.shape[2]
    tiles = row_tiles(x_ref.shape[0], tile)
    wo_copy = pltpu.make_async_copy(wo_hbm.at[layer], wo_ref, in_sems.at[0, 0])
    loads, first_out, last_out = [], [], []
    for t, at in enumerate(tiles):
        loads.append(
            [
                pltpu.make_async_copy(mixed_hbm.at[:, 3, at], o_ref.at[:, at], in_sems.at[1, t]),
                pltpu.make_async_copy(x_hbm.at[at], x_ref.at[at], in_sems.at[2, t]),
            ]
        )
        first_out.append(
            [
                pltpu.make_async_copy(u1_ref.at[at], u1_hbm.at[at], out_sems.at[0, t]),
                pltpu.make_async_copy(hr_ref.at[at], hr_hbm.at[at], out_sems.at[1, t]),
            ]
        )
        last_out.append(
            [
                pltpu.make_async_copy(u2_ref.at[at], u2_hbm.at[at], out_sems.at[2, t]),
                pltpu.make_async_copy(low_ref.at[at], low_hbm.at[at], out_sems.at[3, t]),
            ]
        )

    def g_out(chunk, slot):
        return [
            pltpu.make_async_copy(gr_ref.at[slot], gr_hbm.at[chunk], g_sems.at[0, slot]),
            pltpu.make_async_copy(gp_ref.at[slot], gp_hbm.at[chunk], g_sems.at[1, slot]),
        ]

    @pl.when(step == 0)
    def _():
        wo_copy.start()
        for pair in loads:
            for copy in pair:
                copy.start()
        wo_copy.wait()
        for t, at in enumerate(tiles):
            for copy in loads[t]:
                copy.wait()
            residual = x_ref[at].astype(WIDE)
            if renorm:
                residual = row_stats(residual)[0] * small_ref[6:7] + small_ref[7:8]
            u1 = residual + small_ref[0:1]
            for block in range(4):
                rows = pl.ds(pl.multiple_of((own_ref[0] ^ block) * part, 16), part)
                u1 = u1 + dot_nn(o_ref[block, at], wo_ref[rows, :])
            u1_ref[at] = u1
            normed = row_stats(u1)[0] * small_ref[1:2] + small_ref[2:3]
            hr_ref[at] = normed.astype(LOW)
            u2_ref[at] = normed + small_ref[3:4]
            for copy in first_out[t]:
                copy.start()

    slot = step % 2

    @pl.when(step >= 2)
    def _():
        for copy in g_out(step - 2, slot):
            copy.wait()

    z = dot_nn(hr_ref[...], wu_ref[...]) + bu_ref[...]
    g, slope = gelu_pair(z)
    gr = g.astype(LOW)
    gr_ref[slot] = gr
    gp_ref[slot] = slope.astype(LOW)
    for copy in g_out(step, slot):
        copy.start()
    u2_ref[...] += dot_nn(gr, wd_ref[...])

    @pl.when(step == steps - 1)
    def _():
        for t, at in enumerate(tiles):
            total = u2_ref[at]
            low_ref[at] = (row_stats(total)[0] * small_ref[4:5] + small_ref[5:6]).astype(LOW)
            for copy in last_out[t]:
                copy.start()
        for copy in [*g_out(step - 1, 1 - slot), *g_out(step, slot)]:
            copy.wait()
        for pair in first_out + last_out:
            for copy in pair:
                copy.wait()


def ffn_forward(own, mixed, x, wo, wu, wd, bu, small, layer, renorm, tile=512):
    _, _, rows, part = mixed.shape
    width, hidden = wu.shape[1:]
    chunks = hidden // width
    fixed = lambda v: pl.BlockSpec(v.shape, lambda i, o: (0,) * v.ndim)
    sems = lambda *shape: pltpu.SemaphoreType.DMA(shape)
    return call(
        functools.partial(ffn_forward_kernel, layer=layer, tile=tile, renorm=renorm),
        "ffn_forward",
        (chunks,),
        [
            in_place(),
            in_place(),
            in_place(),
            pl.BlockSpec((None, width, width), lambda i, o: (layer, 0, i)),
            pl.BlockSpec((None, width, width), lambda i, o: (layer, i, 0)),
            pl.BlockSpec((None, 1, width), lambda i, o: (i, 0, 0)),
            fixed(small),
        ],
        [in_place()] * 6,
        [
            shape_of((rows, width), WIDE),
            shape_of((rows, width), LOW),
            shape_of((chunks, rows, width), LOW),
            shape_of((chunks, rows, width), LOW),
            shape_of((rows, width), WIDE),
            shape_of((rows, width), LOW),
        ],
        [
            pltpu.VMEM((4, rows, part), LOW),
            pltpu.VMEM((rows, width), x.dtype),
            pltpu.VMEM((width, width), LOW),
            pltpu.VMEM((rows, width), WIDE),
            pltpu.VMEM((rows, width), LOW),
            pltpu.VMEM((2, rows, width), LOW),
            pltpu.VMEM((2, rows, width), LOW),
            pltpu.VMEM((rows, width), WIDE),
            pltpu.VMEM((rows, width), LOW),
            sems(3, rows // tile),
            sems(4, rows // tile),
            sems(2, 2),
        ],
        [own],
        [mixed, x, wo, wu, wd, bu, small],
        flops=6 * rows * width * (width + 2 * hidden),
    )


def reversed_bits(value, count):
    made = 0
    for bit in range(count):
        made = made | (((value >> bit) & 1) << (count - 1 - bit))
    return made


def each_chunk(made, dp_count):
    rows = made.shape[0] // dp_count
    for dp in range(dp_count):
        yield dp, made[dp * rows : (dp + 1) * rows]


def place(dp, own_dp, dp_count):
    away = dp ^ own_dp
    return away & 1, reversed_bits(away >> 1, dp_count.bit_length() - 2)


def ffn_backward_kernel(own_ref, gx_hbm, u2_hbm, u1_hbm, gp_hbm, hr_hbm, gr_hbm, wo_hbm, wu_ref, wd_ref, gain_ref,
                        da_hbm, do_hbm, du_hbm, sums_ref, zsum_ref, send_ref, keep_ref,
                        gx_ref, u2_ref, u1_ref, gp_ref, hr_ref, gr_ref, wo_ref, acc_ref, df_ref, dz_ref, da_ref, do_ref,
                        in_sems, out_sems, g_sems, *, layer, tile, dp_count):
    step, steps = pl.program_id(0), pl.num_programs(0)
    own, own_dp = own_ref[0], own_ref[1]
    part = do_ref.shape[2]
    tiles = row_tiles(gx_ref.shape[0], tile)
    count = len(tiles)
    loads, last_out = [], []
    for t, at in enumerate(tiles):
        loads.append(
            [
                pltpu.make_async_copy(gx_hbm.at[at], gx_ref.at[at], in_sems.at[0, t]),
                pltpu.make_async_copy(u2_hbm.at[at], u2_ref.at[at], in_sems.at[1, t]),
            ]
        )
        last_out.append(
            [
                pltpu.make_async_copy(u2_ref.at[at], du_hbm.at[at], out_sems.at[0, t]),
                pltpu.make_async_copy(da_ref.at[:, at], da_hbm.at[:, at], out_sems.at[1, t]),
                pltpu.make_async_copy(do_ref.at[:, at], do_hbm.at[:, at], out_sems.at[2, t]),
            ]
        )
    hr_copy = pltpu.make_async_copy(hr_hbm, hr_ref, in_sems.at[2, 0])
    u1_copy = pltpu.make_async_copy(u1_hbm, u1_ref, in_sems.at[2, 1])
    wo_copy = pltpu.make_async_copy(wo_hbm.at[layer], wo_ref, in_sems.at[2, 2])

    def streams(at_step):
        slot, head = at_step % 2, own ^ head_order(at_step)
        return (
            pltpu.make_async_copy(gp_hbm.at[head], gp_ref.at[slot], g_sems.at[0, slot]),
            pltpu.make_async_copy(gr_hbm.at[head], gr_ref.at[slot], g_sems.at[1, slot]),
        )

    slot = step % 2
    gp_copy, gr_copy = streams(step)

    @pl.when(step == 0)
    def _():
        for pair in loads:
            for copy in pair:
                copy.start()

        gp_copy.start()
        hr_copy.start()
        gr_copy.start()

    @pl.when(step < steps - 1)
    def _():
        for copy in streams(step + 1):
            copy.start()

    @pl.when(step == 1)
    def _():
        u1_copy.start()
        wo_copy.start()

    @pl.when(step == 0)
    def _():
        sums_ref[...] = jnp.zeros_like(sums_ref)
        for t, at in enumerate(tiles):
            for copy in loads[t]:
                copy.wait()
            gx = gx_ref[at].astype(WIDE)
            xhat, inverse = row_stats(u2_ref[at])
            sums_ref[0:1] += column_sum(gx * xhat)
            sums_ref[1:2] += column_sum(gx)
            gv = norm_backward(gx, xhat, inverse, gain_ref[1:2])
            df = gv.astype(LOW)
            df_ref[at] = df
            sums_ref[2:3] += column_sum(df.astype(WIDE))
            acc_ref[at] = gv

    dg = dot_nt(df_ref[...], wd_ref[...])
    gp_copy.wait()
    dz = (dg * gp_ref[slot].astype(WIDE)).astype(LOW)
    dz_ref[...] = dz
    zsum_ref[...] = column_sum(dz.astype(WIDE))
    acc_ref[...] += dot_nt(dz_ref[...], wu_ref[...])

    @pl.when(step == 0)
    def _():
        hr_copy.wait()

    up = dot_tn(hr_ref[...], dz_ref[...]).astype(LOW)
    gr_copy.wait()
    down = dot_tn(df_ref[...], gr_ref[slot]).astype(LOW)
    for out, wanted in ((send_ref, step < 2), (keep_ref, step >= 2)):

        @pl.when(wanted)
        def _():
            for which, made in enumerate((up, down)):
                for dp, chunk in each_chunk(made, dp_count):
                    out[(which, *place(dp, own_dp, dp_count))] = chunk

    @pl.when(step == steps - 1)
    def _():
        u1_copy.wait()
        wo_copy.wait()
        for t, at in enumerate(tiles):
            total = acc_ref[at]
            xhat, inverse = row_stats(u1_ref[at])
            sums_ref[3:4] += column_sum(total * xhat)
            sums_ref[4:5] += column_sum(total)
            du = norm_backward(total, xhat, inverse, gain_ref[0:1])
            u2_ref[at] = du
            da = du.astype(LOW)
            for block in range(4):
                da_ref[block, at] = da[:, block * part : (block + 1) * part]
            sums_ref[5:6] += column_sum(da.astype(WIDE))
            for block in range(4):
                rows = pl.ds(pl.multiple_of((own ^ block) * part, 16), part)
                do_ref[block, at] = dot_nt(da, wo_ref[rows, :]).astype(LOW)
            for copy in last_out[t]:
                copy.start()
        for several in last_out:
            for copy in several:
                copy.wait()


def head_order(step):
    return jnp.where(step < 2, 1 + 2 * step, 2 * (step - 2))


def ffn_backward(own, gx, u2, u1, gp, hr, gr, wo, wu, wd, gains, layer, dp_count, tile=512):
    rows, width = gx.shape
    chunks = gp.shape[0]
    part = width // 4
    chunk_rows = width // dp_count
    rest = dp_count // 2
    fixed = lambda s: pl.BlockSpec(s.shape, lambda i, o: (0,) * len(s.shape))
    head = lambda i, o: o[0] ^ head_order(i)
    block = (2, None, 2, rest, chunk_rows, width)
    sums = shape_of((8, width), WIDE)
    grads = stored((2, 2, 2, rest, chunk_rows, width), LOW)
    sems = lambda *shape: pltpu.SemaphoreType.DMA(shape)
    low = lambda *shape: pltpu.VMEM(shape, LOW)
    wide = lambda *shape: pltpu.VMEM(shape, WIDE)
    return call(
        functools.partial(ffn_backward_kernel, layer=layer, tile=tile, dp_count=dp_count),
        "ffn_backward",
        (chunks,),
        [in_place()] * 7
        + [
            pl.BlockSpec((None, width, width), lambda i, o: (layer, 0, head(i, o))),
            pl.BlockSpec((None, width, width), lambda i, o: (layer, head(i, o), 0)),
            fixed(gains),
        ],
        [
            in_place(),
            in_place(),
            in_place(),
            fixed(sums),
            pl.BlockSpec((None, 1, width), lambda i, o: (head(i, o), 0, 0)),
            pl.BlockSpec(block, lambda i, o: (0, jnp.minimum(i, 1), 0, 0, 0, 0)),
            pl.BlockSpec(block, lambda i, o: (0, jnp.maximum(i - 2, 0), 0, 0, 0, 0)),
        ],
        [
            shape_of((4, rows, part), LOW),
            shape_of((4, rows, part), LOW),
            shape_of((rows, width), WIDE),
            sums,
            shape_of((chunks, 1, width), WIDE),
            grads,
            grads,
        ],
        [
            pltpu.VMEM((rows, width), gx.dtype),
            wide(rows, width),
            wide(rows, width),
            low(2, rows, width),
            low(rows, width),
            low(2, rows, width),
            low(width, width),
            wide(rows, width),
            low(rows, width),
            low(rows, width),
            low(4, rows, part),
            low(4, rows, part),
            sems(3, max(rows // tile, 3)),
            sems(3, rows // tile),
            sems(2, 2),
        ],
        [own],
        [gx, u2, u1, gp, hr, gr, wo, wu, wd, gains],
        flops=4 * rows * width * (width + 4 * chunks * width),
    )


def split_rows(made, got_ref, own_dp, dp_count, send_ref, keep_ref):
    for dp, chunk in each_chunk(made, dp_count):
        away, rest = place(dp, own_dp, dp_count)
        summed = (chunk + got_ref[away, rest].astype(WIDE)).astype(LOW)

        @pl.when(away == 1)
        def _():
            send_ref[rest] = summed

        @pl.when(away == 0)
        def _():
            keep_ref[rest] = summed


def add_rows(made, got_ref, own_dp, dp_count, out_ref):
    for dp, chunk in each_chunk(made, dp_count):
        at = place(dp, own_dp, dp_count)
        out_ref[at] = (chunk + got_ref[at].astype(WIDE)).astype(LOW)


def core_add_kernel(kept_ref, got_ref, up_send, up_keep, down_send, down_keep):
    step = pl.program_id(0)

    def summed(at):
        return (kept_ref[at].astype(WIDE) + got_ref[at].astype(WIDE)).astype(LOW)

    @pl.when(step < 2)
    def _():
        up_keep[...] = summed(0)
        up_send[...] = summed(1)

    for out, wanted in ((down_send, 2), (down_keep, 3)):

        @pl.when(step == wanted)
        def _():
            out[0] = summed(0)
            out[1] = summed(1)


def core_add(kept, got):
    _, _, _, rest, chunk_rows, width = kept.shape

    def at(i):
        return (i // 2, jnp.where(i < 2, i, 3 - i), 0, 0, 0, 0)

    block = pl.BlockSpec((None, None, 2, rest, chunk_rows, width), at)
    up = pl.BlockSpec((None, rest, chunk_rows, width), lambda i: (jnp.minimum(i, 1), 0, 0, 0))
    down = pl.BlockSpec((2, rest, chunk_rows, width), lambda i: (0, 0, 0, 0))
    made = stored((2, rest, chunk_rows, width), LOW)
    return call(
        core_add_kernel, "core_add", (4,), [block, block], [up, up, down, down], [made] * 4, [], [], [kept, got]
    )


def attention_backward_kernel(own_ref, mixed_ref, do_ref, p_ref, x_ref, o_ref, da_ref, wa_ref, wb_ref, gx_ref, *refs,
                              dp_count, tile, keep):
    if keep:
        got_ref, *refs = refs
    out_ref, sums_ref, *refs = refs
    grads = refs[: 4 if keep else 1]
    t_ref, ds_ref, parts_ref, xt_ref, ot_ref, acc_ref = refs[4 if keep else 1 :]
    slot, block = pl.program_id(0), pl.program_id(1)
    last = pl.num_programs(0) - 1
    own, own_dp = own_ref[0], own_ref[1]
    rows, part = mixed_ref.shape[1:]

    @pl.when((slot == 0) & (block == 0))
    def _():
        xt_ref[...] = x_ref[...].T
        for r in range(4):
            ot_ref[pl.ds(pl.multiple_of((own ^ r) * part, 16), part), :] = o_ref[r].T
        sums_ref[...] = jnp.zeros_like(sums_ref)

    dq = dk = dv = None
    for head, mask in enumerate(head_masks(part)):
        do = pick(mask, do_ref[...])
        t_ref[head] = dot_nt(do, mixed_ref[2])
        for start in range(0, rows, tile):
            at = slice(start, start + tile)
            p = p_ref[head, at].astype(WIDE)
            dp = t_ref[head, at]
            share = jnp.sum(p * dp, axis=1, keepdims=True)
            ds_ref[head, at] = (p * (dp - share)).astype(LOW)
        made = (
            dot_nn(ds_ref[head], pick(mask, mixed_ref[1])),
            dot_tn(ds_ref[head], pick(mask, mixed_ref[0])),
            dot_tn(p_ref[head], do),
        )
        dq, dk, dv = made if dq is None else (dq + made[0], dk + made[1], dv + made[2])
    dq = (dq * HD**-0.5).astype(LOW)
    dk = dk.astype(LOW)
    dv = dv.astype(LOW)
    sums_ref[block, 0:1] += column_sum(dq.astype(WIDE))
    sums_ref[block, 1:2] += column_sum(dv.astype(WIDE))
    joined = jnp.concatenate([dq, dk, dv], axis=1)
    parts_ref[block, pl.ds(pl.multiple_of(slot * rows, rows), rows), :] = joined
    weights = jnp.where(block == 0, wa_ref[...], wb_ref[...])
    passed = dot_nn(joined, weights)

    @pl.when(block == 0)
    def _():
        acc_ref[...] = gx_ref[...] + passed

    @pl.when(block == 1)
    def _():
        out_ref[...] = (acc_ref[...] + passed).astype(out_ref.dtype)

    @pl.when(slot == last)
    def _():
        first = dot_nn(xt_ref[...], parts_ref[block])
        second = dot_nn(ot_ref[...], da_ref[...])
        made = jnp.concatenate([first, second], axis=1)
        if not keep:
            for dp, chunk in each_chunk(made.astype(LOW), dp_count):
                grads[0][place(dp, own_dp, dp_count)] = chunk
            return
        half = made.shape[1] // 2
        a_send, a_keep, b_send, b_keep = grads
        got = [got_ref.at[:, :, :, :half], got_ref.at[:, :, :, half:]]
        for where_to, wanted in ((a_keep, 0), (a_send, 1)):

            @pl.when(block == wanted)
            def _():
                add_rows(made[:, :half], got[0], own_dp, dp_count, where_to)

        split_rows(made[:, half:], got[1], own_dp, dp_count, b_send, b_keep)


def attention_backward(own, mixed, do, probs, x, da, wa, wb, gx, got, dp_count, out_type, tile=64):
    rows, width = x.shape
    part = mixed.shape[3]
    _, slots, heads, slot_rows, _ = probs.shape
    chunk_rows, rest = width // dp_count, dp_count // 2
    keep = got is not None
    away = 0 if keep else 1
    block_of = lambda b: 2 * b + away
    row = pl.BlockSpec((slot_rows, width), lambda s, b, o: (s, 0))
    last = slots - 1
    late = lambda s, b: jnp.where(s == last, b, 0)
    in_specs = [
        pl.BlockSpec((None, 3, slot_rows, part), lambda s, b, o: (block_of(b), 0, s, 0)),
        pl.BlockSpec((None, slot_rows, part), lambda s, b, o: (block_of(b), s, 0)),
        pl.BlockSpec(
            (None, None, heads, slot_rows, slot_rows), lambda s, b, o: (block_of(b), s, 0, 0, 0)
        ),
        whole(x),
        pl.BlockSpec((4, None, rows, part), lambda s, b, o: (0, 3, 0, 0), pipeline_mode=pl.Buffered(1)),
        pl.BlockSpec((None, rows, part), lambda s, b, o: (o[0] ^ block_of(late(s, b)), 0, 0)),
        whole(wa),
        whole(wb),
        row,
    ]
    operands = [mixed, do, probs, x, mixed, da, wa, wb, gx]
    sums = shape_of((2, 8, part), WIDE)
    out_specs = [row, pl.BlockSpec(sums.shape, lambda s, b, o: (0, 0, 0))]
    out_shape = [shape_of((rows, width), out_type), sums]
    whole_block = lambda w: pl.BlockSpec((2, rest, chunk_rows, w), lambda s, b, o: (0, 0, 0, 0))
    if keep:
        in_specs.append(
            pl.BlockSpec(
                (None, 2, rest, chunk_rows, width), lambda s, b, o: (late(s, b), 0, 0, 0, 0)
            )
        )
        operands.append(got)
        half = width // 2
        b_block = pl.BlockSpec(
            (None, rest, chunk_rows, half), lambda s, b, o: (late(s, b), 0, 0, 0)
        )
        out_specs += [whole_block(half)] * 2 + [b_block] * 2
        out_shape += [stored((2, rest, chunk_rows, half), LOW)] * 4
    else:
        out_specs.append(
            pl.BlockSpec(
                (None, 2, rest, chunk_rows, width), lambda s, b, o: (late(s, b), 0, 0, 0, 0)
            )
        )
        out_shape.append(stored((2, 2, rest, chunk_rows, width), LOW))
    return call(
        functools.partial(attention_backward_kernel, dp_count=dp_count, tile=tile, keep=keep),
        "attention_backward",
        (slots, 2),
        in_specs,
        out_specs,
        out_shape,
        [
            pltpu.VMEM((heads, slot_rows, slot_rows), WIDE),
            pltpu.VMEM((heads, slot_rows, slot_rows), LOW),
            pltpu.VMEM((2, rows, 3 * part), LOW),
            pltpu.VMEM((width, rows), LOW),
            pltpu.VMEM((width, rows), LOW),
            pltpu.VMEM((slot_rows, width), WIDE),
        ],
        [own],
        operands,
        flops=36 * heads * rows * slot_rows * 256,
    )


def bits_of(axis):
    size = lax.axis_size(axis)
    return [1 << bit for bit in range(size.bit_length() - 1)]


def swap(value, axis, bit):
    size = lax.axis_size(axis)
    return lax.ppermute(value, axis, [(i, i ^ bit) for i in range(size)])


def add_split_kernel(*refs, merge_in, merge_out):
    inputs = 2 if merge_in else 4
    outputs = 2 if merge_out else 4
    ins, outs = refs[:inputs], refs[inputs : inputs + outputs]
    kept_ref, got_ref, send_ref, keep_ref, in_sems, out_sems = refs[inputs + outputs :]
    half = send_ref.shape[1]
    loads, stores = [], []
    for part in range(2):
        kept, got = (ins[0].at[part], ins[1].at[part]) if merge_in else ins[2 * part : 2 * part + 2]
        send, keep = (
            (outs[0].at[part], outs[1].at[part]) if merge_out else outs[2 * part : 2 * part + 2]
        )
        loads.append(
            [
                pltpu.make_async_copy(kept, kept_ref.at[part], in_sems.at[part, 0]),
                pltpu.make_async_copy(got, got_ref.at[part], in_sems.at[part, 1]),
            ]
        )
        stores.append(
            [
                pltpu.make_async_copy(send_ref.at[part], send, out_sems.at[part, 0]),
                pltpu.make_async_copy(keep_ref.at[part], keep, out_sems.at[part, 1]),
            ]
        )
    for copies in loads:
        for copy in copies:
            copy.start()
    for part in range(2):
        for copy in loads[part]:
            copy.wait()
        for out, at in ((send_ref, slice(half, None)), (keep_ref, slice(None, half))):
            out[part] = (kept_ref[part, at].astype(WIDE) + got_ref[part, at].astype(WIDE)).astype(LOW)
        for copy in stores[part]:
            copy.start()
    for copies in stores:
        for copy in copies:
            copy.wait()


def add_split(ins, merge_in, merge_out):
    size, rows, columns = ins[0].shape[-3:]
    half = (size // 2, rows, columns)
    out_shape = [stored((2, *half), LOW)] * 2 if merge_out else [stored(half, LOW)] * 4
    return pl.pallas_call(
        functools.partial(add_split_kernel, merge_in=merge_in, merge_out=merge_out),
        in_specs=[in_hbm()] * len(ins),
        out_specs=[in_hbm()] * len(out_shape),
        out_shape=out_shape,
        scratch_shapes=[
            pltpu.VMEM((2, size, rows, columns), LOW),
            pltpu.VMEM((2, size, rows, columns), LOW),
            pltpu.VMEM((2, *half), LOW),
            pltpu.VMEM((2, *half), LOW),
            pltpu.SemaphoreType.DMA((2, 2)),
            pltpu.SemaphoreType.DMA((2, 2)),
        ],
        compiler_params=params(),
        cost_estimate=cost(0, out_shape, ins),
        name="add_split",
    )(*ins)


class Summing:
    def __init__(self, a_send, a_keep, b_send, b_keep):
        head, dp = bits_of("head"), bits_of("dp")
        self.stages = [(("dp", dp[0]), ("head", head[1]))] + [(("dp", bit),) for bit in dp[1:]]
        self.at = 0
        self.kept = [a_keep, b_keep]
        self.got = [swap(a_send, "head", head[1]), swap(b_send, "dp", dp[0])]

    def busy(self):
        return self.at < len(self.stages)

    def step(self, after):
        stage = self.stages[self.at]
        merge_in, merge_out = len(self.kept) == 1, len(stage) == 1
        ins = [v for pair in zip(self.kept, self.got) for v in pair]
        lead = 1 if merge_in else 0
        ins = [v.reshape(*v.shape[:lead], -1, *v.shape[-2:]) for v in ins]
        ins, _ = lax.optimization_barrier((ins, after))
        outs = add_split(ins, merge_in, merge_out)
        if merge_out:
            self.got, self.kept = [swap(outs[0], *stage[0])], [outs[1]]
        else:
            self.got = [swap(outs[0], *stage[0]), swap(outs[2], *stage[1])]
            self.kept = [outs[1], outs[3]]
        self.at += 1
        return outs[-1]

    def finish(self):
        kept, got = self.kept[0], self.got[0]
        return (kept.astype(WIDE) + got.astype(WIDE)).reshape(2, *kept.shape[-2:])


def ordered(after, *values):
    values, _ = lax.optimization_barrier((values, after))
    return values


def near_blocks(block):
    low, high = bits_of("head")
    return block, swap(block, "head", low), swap(block, "head", high)


def gathered_pairs(block):
    own, near, far = near_blocks(block)
    return jnp.stack([own, near]), jnp.stack([far, swap(far, "head", bits_of("head")[0])])


def on_device(
    tokens,
    seq_lengths,
    qkv_weight,
    qv_bias,
    out_weight,
    out_bias,
    norm1_gain,
    norm1_shift,
    up_weight,
    up_bias,
    down_weight,
    down_bias,
    norm2_gain,
    norm2_shift,
    out_grad,
):
    head_count, dp_count = lax.axis_size("head"), lax.axis_size("dp")
    head_index, dp_index = lax.axis_index("head"), lax.axis_index("dp")
    own = jnp.stack([head_index, dp_index]).astype(jnp.int32)
    local_rows, width = tokens.shape
    slot_rows = local_rows * head_count // seq_lengths.shape[0]
    slots = local_rows // slot_rows
    layers = qkv_weight.shape[0]
    part = width // head_count
    turned = jnp.swapaxes(qkv_weight, 2, 3).reshape(layers, 3 * part, width)
    near_bias, far_bias = gathered_pairs(qv_bias[:, :, None])
    weights = [near_blocks(turned[0])]
    base = (head_index * slots).astype(jnp.int32).reshape(1)
    bias = mask_bias(seq_lengths, base, slots, slot_rows)
    up_rows = up_bias.reshape(layers, -1, 1, width)
    rounded, residual = tokens, tokens
    kept = []
    for layer in range(layers):
        before = max(layer - 1, 0)
        small = jnp.stack(
            [
                out_bias[layer],
                norm1_gain[layer],
                norm1_shift[layer],
                down_bias[layer],
                norm2_gain[layer],
                norm2_shift[layer],
                norm2_gain[before],
                norm2_shift[before],
            ]
        )
        own_w, near_w, far_w = weights[layer]
        near = attention_forward(rounded, own_w, near_w, near_bias[:, layer], bias, 0, None)
        (far_w, far_b) = ordered(near[0], far_w, far_bias[:, layer])
        both_w = swap(far_w, "head", bits_of("head")[0])
        if layer + 1 < layers:
            (later,) = ordered(near[0], turned[layer + 1])
            weights.append(near_blocks(later))
        mixed, probs = attention_forward(rounded, far_w, both_w, far_b, bias, 2, near)
        w = (own_w, near_w, far_w, both_w)
        weights[layer] = w
        u1, hr, gr, slope, u2, low = ffn_forward(
            own,
            mixed,
            residual,
            out_weight,
            up_weight,
            down_weight,
            up_rows[layer],
            small,
            layer,
            layer > 0,
        )
        kept.append((rounded, mixed, probs, u1, hr, gr, slope, u2))
        rounded, residual = low, u2
    out_state = rounded
    grad_state = out_grad
    small_sums = [None] * layers
    hidden_sums = [None] * layers
    ffn_groups, wide_groups = [None] * layers, [None] * layers
    running = []

    def advance(after, groups=None):
        for group in running if groups is None else groups:
            if group.busy():
                after = group.step(after)
        return after

    for layer in reversed(range(layers)):
        rounded, mixed, probs, u1, hr, gr, slope, u2 = kept[layer]
        w = weights[layer]
        gains = jnp.stack([norm1_gain[layer], norm2_gain[layer]])
        da, do, du, sums, zsums, sent, ffn_kept = ffn_backward(
            own,
            grad_state,
            u2,
            u1,
            slope,
            hr,
            gr,
            out_weight,
            up_weight,
            down_weight,
            gains,
            layer,
            dp_count,
        )
        low_bit = bits_of("head")[0]
        early = bool(running)
        token = advance(do)
        if early:
            (sent,) = ordered(token, sent)
        got = swap(sent, "head", low_bit)

        def sum_ffn(after):
            values = ordered(after, ffn_kept, got)
            up_send, up_keep, down_send, down_keep = core_add(*values)
            ffn_groups[layer] = Summing(down_send, down_keep, up_send, up_keep)
            running.insert(0, ffn_groups[layer])
            return down_keep

        if early:
            token = sum_ffn(token)
        (do, du) = ordered(token, do, du)
        half_grad, away_sums, sent = attention_backward(
            own, mixed, do, probs, rounded, da, w[1], w[3], du, None, dp_count, WIDE
        )
        if early:
            token = advance(half_grad, running[:1])
            (sent,) = ordered(token, sent)
            wide_got = swap(sent, "head", low_bit)
        else:
            wide_got = swap(sent, "head", low_bit)
            token = sum_ffn(half_grad)
        (half_grad, do) = ordered(token, half_grad, do)
        grad_state, own_sums, *parts = attention_backward(
            own,
            mixed,
            do,
            probs,
            rounded,
            da,
            w[0],
            w[2],
            half_grad,
            wide_got,
            dp_count,
            WIDE if layer else LOW,
        )
        wide_groups[layer] = Summing(*parts)
        token = advance(grad_state) if layer else grad_state
        if layer:
            (grad_state,) = ordered(token, grad_state)
        running.append(wide_groups[layer])
        blocks = [own_sums[0], away_sums[0], own_sums[1], away_sums[1]]
        stacked = jnp.stack(blocks)[:, :2]
        qv_sums = jnp.concatenate(
            [
                lax.dynamic_index_in_dim(stacked, head_index ^ head, 0, keepdims=False)
                for head in range(head_count)
            ],
            axis=1,
        )
        small_sums[layer] = jnp.concatenate([sums[:6], qv_sums, zsums[:, 0]])
    small_sum = jnp.stack(small_sums)
    spread = [("head", bits_of("head")[0])] + [("dp", bit) for bit in bits_of("dp")[1:]]
    spread += [("dp", bits_of("dp")[0]), ("head", bits_of("head")[1])]
    while any(group.busy() for group in running) or spread:
        if spread:
            small_sum = small_sum + swap(small_sum, *spread.pop(0))
        token = advance(token)
    ffn_sums = [group.finish() for group in ffn_groups]
    wide_sums = [group.finish() for group in wide_groups]
    wide = [
        [both[half, :, at * part : (at + 1) * part] for half in range(2) for at in range(2)]
        for both in wide_sums
    ]
    return (
        out_state,
        grad_state,
        jnp.stack([jnp.stack(w[:3]) for w in wide]),
        small_sum[:, 6:8],
        jnp.stack([w[3] for w in wide]),
        small_sum[:, 5],
        small_sum[:, 3],
        small_sum[:, 4],
        jnp.stack([both[1] for both in ffn_sums]),
        small_sum[:, 8:].reshape(layers, -1),
        jnp.stack([both[0].T for both in ffn_sums]),
        small_sum[:, 2],
        small_sum[:, 0],
        small_sum[:, 1],
    )


def solution(mesh):
    in_specs = (
        P(("dp", "head"), None),
        P("dp", None),
        P(None, None, None, "head"),
        P(None, None, "head"),
        P(),
        P(),
        P(),
        P(),
        P(),
        P(),
        P(),
        P(),
        P(),
        P(),
        P(("dp", "head"), None),
    )
    out_specs = (
        P(("dp", "head"), None),
        P(("dp", "head"), None),
        P(None, None, "dp", "head"),
        P(),
        P(None, "dp", "head"),
        P(),
        P(),
        P(),
        P(None, "dp", "head"),
        P(),
        P(None, "head", "dp"),
        P(),
        P(),
        P(),
    )
    return jax.shard_map(
        on_device, mesh=mesh, in_specs=in_specs, out_specs=out_specs, check_vma=False
    )
```

time: 1060 us -> 500 us (0.47)
  matrix products: 349 us -> 0 us
  Pallas kernels: 0 us -> 345 us
  local copies, waits for them, and re-layouts: 291 us -> 27.5 us
  waiting for transfers between devices: 324 us -> 75.2 us
  other arithmetic: 61.2 us -> 8.03 us
  starting transfers between devices: 0.2 us -> 38.9 us
  between operations: 16.1 us -> 1.8 us
    dot_general x64 -> x0, matrix products: 349 us -> none  [the longest x2 77.9 us: on_device(): jnp.dot(normed_low, up_weight[layer], preferred_element_type=jnp.float32)]
    pallas_call x0 -> x27, Pallas kernels: none -> 345 us  [the longest x14 311 us: call(): pl.pallas_call(kernel, grid_spec=pltpu.PrefetchScalarGridSpec(num_scalar_...]
    reduce_scatter x2 -> x0, waiting for transfers between devices: 319 us -> none  [on_device(): lax.psum_scatter(packed, ('dp', 'head'), scatter_dimension=0, tiled=True)[0]]
    reshape x37 -> x0, local copies, waits for them, and re-layouts: 109 us -> none  [the longest x12 64.6 us: chunked(): grad.reshape(dp_count, rows // dp_count, head_count, columns // head_count)]
    ppermute x0 -> x42, waiting for transfers between devices: none -> 75.2 us  [swap(): return lax.ppermute(value, axis, [(i, i ^ bit) for i in range(size)])]
    while x64 -> x0, local copies, waits for them, and re-layouts: 39.9 us -> none  [the longest x8 18.4 us: on_device(): lax.map(slot_forward, (queries, keys_in, values_in, segments))]
    ppermute x0 -> x42, starting transfers between devices: none -> 38.9 us  [swap(): return lax.ppermute(value, axis, [(i, i ^ bit) for i in range(size)])]
    transpose x13 -> x0, local copies, waits for them, and re-layouts: 37.9 us -> none  [the longest x12 36.8 us: chunked(): jnp.transpose(split, (0, 2, 1, 3)).reshape(dp_count * head_count, -1, rows)]
  transfers between devices with their start and end apart: 5 -> 42, of which waited for: 3 -> 15; matrix products, arithmetic and copies ran while one was open for 24% -> 3% of each run, Pallas kernels for 0% -> 49%
where the time goes in v4:
time: 500 us; the launch traced here: 496 us
  Pallas kernels  345 us (69%)
  waiting for transfers between devices  75.2 us (15%)
  starting transfers between devices  38.9 us (8%)
  local copies, waits for them, and re-layouts  27.5 us (6%)
  other arithmetic  8.03 us (2%)
    pallas_call x14, Pallas kernels, call(): pl.pallas_call(kernel, grid_spec=pltpu.PrefetchScalarGridSpec(num_scalar_...  311 us
    ppermute x42, waiting for transfers between devices, swap(): return lax.ppermute(value, axis, [(i, i ^ bit) for i in range(size)])  75.2 us
    ppermute x42, starting transfers between devices, swap(): return lax.ppermute(value, axis, [(i, i ^ bit) for i in range(size)])  38.9 us
    pallas_call x12, Pallas kernels, add_split(): pl.pallas_call(functools.partial(add_split_kernel, merge_in=merge_in, mer...  29.6 us
    unnamed x112, local copies, waits for them, and re-layouts  22.2 us
  transfers between devices with their start and end apart: 42, of which 15 were waited for; matrix products, arithmetic and copies ran while one was open for 3% of the time, Pallas kernels for 49%

profile of v4, /device:TPU:0, one launch (start us, length us, event | category | flops | bytes accessed | tf_op | source)
XLA Modules:
  0.0 496.5 jit_solution(14651807727250151398)
XLA Ops:
  6.0 4.4 mask_bias.1.bias_ref
  10.4 15.3 %collective-permute-done.1 = f32[2,2,1,192]{3,2,1,0:T(1,128)S(1)} collective-permute-done((f32[2,2,1,192]{3,2,1,0:T(1,128)S(1)}, f32[2,2,1,192]{3,2,1,0:T(1,128)S(1)}, u32[]{:S(2)}, u32[]{:S(2)}) %collective-permute-start.1) | collective-permute-done | bytes 3104 | tf_op jit(solution)/shard_map/ppermute | solution.py:764
  27.5 14.5 %attention_forward.4 = (bf16[4,4,1024,192]{3,2,1,0:T(8,128)(2,1)}, bf16[4,2,3,512,512]{4,3,2,1,0:T(8,128)(2,1)}) custom-call(bf16[1024,768]{1,0:T(8,128)(2,1)} %x_ref.7, bf16[576,768]{1,0:T(8,128)(2,1)} %bitcast.122, bf16[576,768]{1,0:T(8,128)(2,1)} %collective-permute-done.3.wb_ref.wa_ref, f32[2,2,1,192]{3,2,1,0:T(1,128)} %get-tuple-element.357.b_ref, ...), custom_call_target="tpu_custom_call" | custom-call | flops 8254390272 | bytes 24316928 | tf_op jit(solution)/shard_map/attention_forward/pallas_call | solution.py:97
  46.9 14.3 %attention_forward.5 = (bf16[4,4,1024,192]{3,2,1,0:T(8,128)(2,1)}, bf16[4,2,3,512,512]{4,3,2,1,0:T(8,128)(2,1)}) custom-call(bf16[1024,768]{1,0:T(8,128)(2,1)} %x_ref.7, bf16[576,768]{1,0:T(8,128)(2,1)} %copy-done.42, bf16[576,768]{1,0:T(8,128)(2,1)} %copy-done.43, ...), custom_call_target="tpu_custom_call", output_to_operand_aliasing={{0}: (5, {}), {1}: (6, {})} | custom-call | flops 8254390272 | bytes 43191296 | tf_op jit(solution)/shard_map/attention_forward/pallas_call | solution.py:97
  61.1 25.1 %ffn_forward.2 = (f32[1024,768]{1,0:T(8,128)}, bf16[1024,768]{1,0:T(8,128)(2,1)}, bf16[4,1024,768]{2,1,0:T(8,128)(2,1)}, bf16[4,1024,768]{2,1,0:T(8,128)(2,1)}, ...) custom-call(s32[2]{0:T(128)} %pad_add_fusion.own_ref, ...), custom_call_target="tpu_custom_call" | custom-call | flops 32614907904 | bytes 51154944 | tf_op jit(solution)/shard_map/ffn_forward/pallas_call | solution.py:97
  87.1 14.6 %attention_forward.6 = (bf16[4,4,1024,192]{3,2,1,0:T(8,128)(2,1)}, bf16[4,2,3,512,512]{4,3,2,1,0:T(8,128)(2,1)}) custom-call(bf16[1024,768]{1,0:T(8,128)(2,1)} %get-tuple-element.171.x_ref, bf16[576,768]{1,0:T(8,128)(2,1)} %bitcast.126, bf16[576,768]{1,0:T(8,128)(2,1)} %copy-done.44, f32[2,2,1,192]{3,2,1,0:T(1,128)} %get-tuple-element.356.b_ref, ...), custom_call_target="tpu_custom_call" | custom-call | flops 8254390272 | bytes 24316928 | tf_op jit(solution)/shard_map/attention_forward/pallas_call | solution.py:97
  105.6 14.3 %attention_forward.7 = (bf16[4,4,1024,192]{3,2,1,0:T(8,128)(2,1)}, bf16[4,2,3,512,512]{4,3,2,1,0:T(8,128)(2,1)}) custom-call(bf16[1024,768]{1,0:T(8,128)(2,1)} %get-tuple-element.171.x_ref, bf16[576,768]{1,0:T(8,128)(2,1)} %collective-permute-done.6.wa_ref.wb_ref, bf16[576,768]{1,0:T(8,128)(2,1)} %copy-done.45, ...), custom_call_target="tpu_custom_call", output_to_operand_aliasing={{0}: (5, {}), {1}: (6, {})} | custom-call | flops 8254390272 | bytes 43191296 | tf_op jit(solution)/shard_map/attention_forward/pallas_call | solution.py:97
  119.8 25.2 %ffn_forward.3 = (f32[1024,768]{1,0:T(8,128)}, bf16[1024,768]{1,0:T(8,128)(2,1)}, bf16[4,1024,768]{2,1,0:T(8,128)(2,1)}, bf16[4,1024,768]{2,1,0:T(8,128)(2,1)}, ...) custom-call(s32[2]{0:T(128)} %pad_add_fusion.own_ref, ...), custom_call_target="tpu_custom_call" | custom-call | flops 32614907904 | bytes 52727808 | tf_op jit(solution)/shard_map/ffn_forward/pallas_call | solution.py:97
  145.0 44.6 %ffn_backward.2 = (bf16[4,1024,192]{2,1,0:T(8,128)(2,1)}, bf16[4,1024,192]{2,1,0:T(8,128)(2,1)}, f32[1024,768]{1,0:T(8,128)}, f32[8,768]{1,0:T(8,128)}, f32[4,1,...) custom-call(s32[2]{0:T(128)} %pad_add_fusion.own_ref, ...), custom_call_target="tpu_custom_call" | custom-call | flops 41070624768 | bytes 59025408 | tf_op jit(solution)/shard_map/ffn_backward/pallas_call | solution.py:97
  190.0 24.7 %attention_backward.4 = (f32[1024,768]{1,0:T(8,128)}, f32[2,8,192]{2,1,0:T(8,128)}, bf16[2,2,4,96,768]{4,3,2,1,0:T(8,128)(2,1)}) custom-call(s32[2]{0:T(128)} %pad_add_fusion.own_ref, bf16[4,4,1024,192]{3,2,1,0:T(8,128)(2,1)} %get-tuple-element.177.mixed_hbm.mixed_ref.o_ref, bf16[4,1024,192]{2,1,0:T(8,128)(2,1)} %get-tuple-element.197.do_ref, ...), custom_call_target="tpu_custom_call" | custom-call | flops 14495514624 | bytes 40316928 | tf_op jit(solution)/shard_map/attention_backward/pallas_call | solution.py:97
  217.0 6.9 %core_add.2 = (bf16[2,4,96,768]{3,2,1,0:T(8,128)(2,1)}, bf16[2,4,96,768]{3,2,1,0:T(8,128)(2,1)}, bf16[2,4,96,768]{3,2,1,0:T(8,128)(2,1)}, bf16[2,4,96,768]{3,2,1,0:T(8,128)(2,1)}) custom-call(bf16[2,2,2,4,96,768]{5,4,3,2,1,0:T(8,128)(2,1)} %get-tuple-element.194.kept_ref, bf16[2,2,2,4,96,768]{5,4,3,2,1,0:T(8,128)(2,1)} %copy-done), custom_call_target="tpu_custom_call" | custom-call | bytes 14155776 | tf_op jit(solution)/shard_map/core_add/pallas_call | solution.py:97
  226.0 25.6 %attention_backward.5 = (f32[1024,768]{1,0:T(8,128)}, f32[2,8,192]{2,1,0:T(8,128)}, bf16[2,4,96,384]{3,2,1,0:T(8,128)(2,1)}, bf16[2,4,96,384]{3,2,1,0:T(8,128)(2...) custom-call(s32[2]{0:T(128)} %pad_add_fusion.own_ref, ...), custom_call_target="tpu_custom_call" | custom-call | flops 14495514624 | bytes 42676224 | tf_op jit(solution)/shard_map/attention_backward/pallas_call | solution.py:97
  255.0 3.6 add_split.12
  260.8 44.5 %ffn_backward.3 = (bf16[4,1024,192]{2,1,0:T(8,128)(2,1)}, bf16[4,1024,192]{2,1,0:T(8,128)(2,1)}, f32[1024,768]{1,0:T(8,128)}, f32[8,768]{1,0:T(8,128)}, f32[4,1,...) custom-call(s32[2]{0:T(128)} %pad_add_fusion.own_ref, ...), custom_call_target="tpu_custom_call" | custom-call | flops 41070624768 | bytes 60598272 | tf_op jit(solution)/shard_map/ffn_backward/pallas_call | solution.py:97
  312.6 8.1 %collective-permute-done.17.got_ref = bf16[2,2,2,4,96,768]{5,4,3,2,1,0:T(8,128)(2,1)S(1)} collective-permute-done((bf16[2,2,2,4,96,768]{5,4,3,2,1,0:T(8,128)(2,1)}, bf16[2,2,2,4,96,768]{5,4,3,2,1,0:T(8,128)(2,1)S(1)}, u32[]{:S(2)}, u32[]{:S(2)}) %collective-permute-start.17) | collective-permute-done | bytes 4718624 | tf_op jit(solution)/shard_map/ppermute | solution.py:764
  322.9 7.1 %core_add.3 = (bf16[2,4,96,768]{3,2,1,0:T(8,128)(2,1)}, bf16[2,4,96,768]{3,2,1,0:T(8,128)(2,1)}, bf16[2,4,96,768]{3,2,1,0:T(8,128)(2,1)}, bf16[2,4,96,768]{3,2,1,0:T(8,128)(2,1)}) custom-call(bf16[2,2,2,4,96,768]{5,4,3,2,1,0:T(8,128)(2,1)} %get-tuple-element.236.kept_ref, bf16[2,2,2,4,96,768]{5,4,3,2,1,0:T(8,128)(2,1)} %copy-done.1), custom_call_target="tpu_custom_call" | custom-call | bytes 14155776 | tf_op jit(solution)/shard_map/core_add/pallas_call | solution.py:97
  332.0 24.2 %attention_backward.6 = (f32[1024,768]{1,0:T(8,128)}, f32[2,8,192]{2,1,0:T(8,128)}, bf16[2,2,4,96,768]{4,3,2,1,0:T(8,128)(2,1)}) custom-call(s32[2]{0:T(128)} %pad_add_fusion.own_ref, bf16[4,4,1024,192]{3,2,1,0:T(8,128)(2,1)} %get-tuple-element.170.mixed_hbm.mixed_ref.o_ref, bf16[4,1024,192]{2,1,0:T(8,128)(2,1)} %get-tuple-element.252.do_ref, ...), custom_call_target="tpu_custom_call" | custom-call | flops 14495514624 | bytes 40316928 | tf_op jit(solution)/shard_map/attention_backward/pallas_call | solution.py:97
  360.5 3.7 add_split.15
  369.0 25.4 %attention_backward.7 = (bf16[1024,768]{1,0:T(8,128)(2,1)}, f32[2,8,192]{2,1,0:T(8,128)}, bf16[2,4,96,384]{3,2,1,0:T(8,128)(2,1)}, bf16[2,4,96,384]{3,2,1,0:T(8,...) custom-call(s32[2]{0:T(128)} %pad_add_fusion.own_ref, ...), custom_call_target="tpu_custom_call" | custom-call | flops 14495514624 | bytes 41103360 | tf_op jit(solution)/shard_map/attention_backward/pallas_call | solution.py:97
  415.4 10.6 %collective-permute-done.37 = f32[2,12,768]{2,1,0:T(8,128)S(1)} collective-permute-done((f32[2,12,768]{2,1,0:T(8,128)S(1)}, f32[2,12,768]{2,1,0:T(8,128)S(1)}, u32[]{:S(2)}, u32[]{:S(2)}) %collective-permute-start.37) | collective-permute-done | bytes 73760 | tf_op jit(solution)/shard_map/ppermute | solution.py:764
  429.2 14.1 %collective-permute-done.38 = f32[2,12,768]{2,1,0:T(8,128)S(1)} collective-permute-done((f32[2,12,768]{2,1,0:T(8,128)S(1)}, f32[2,12,768]{2,1,0:T(8,128)S(1)}, u32[]{:S(2)}, u32[]{:S(2)}) %collective-permute-start.38) | collective-permute-done | bytes 73760 | tf_op jit(solution)/shard_map/ppermute | solution.py:764
  475.2 3.6 collective-permute-done.40
  479.0 4.7 collective-permute-done.32.refs_1_
  488.4 6.0 %collective-permute-done.33 = bf16[2,1,96,384]{3,2,1,0:T(8,128)(2,1)S(1)} collective-permute-done((bf16[2,1,96,384]{3,2,1,0:T(8,128)(2,1)}, bf16[2,1,96,384]{3,2,1,0:T(8,128)(2,1)S(1)}, u32[]{:S(2)}, u32[]{:S(2)}) %collective-permute-start.33) | collective-permute-done | bytes 147488 | tf_op jit(solution)/shard_map/ppermute | solution.py:764
  (245 shorter events, 109.4 us)
Async XLA Ops:
  2.3 25.2 %collective-permute-start.3 = (bf16[576,768]{1,0:T(8,128)(2,1)S(1)}, bf16[576,768]{1,0:T(8,128)(2,1)}, u32[]{:S(2)}, u32[]{:S(2)}) collective-permute-start(bf16[576,768]{1,0:T(8,128)(2,1)S(1)} %bitcast.120), channel_id=1, source_target_pairs={{0,1},{1,0},{2,3},{3,2},{4,5},{5,4},{6,7},{7,6},{8,9},{9,8},{10,11... | collective-permute-start | bytes 2654216 | tf_op jit(solution)/shard_map/ppermute | solution.py:764
  2.8 39.2 %collective-permute-start = (bf16[576,768]{1,0:T(8,128)(2,1)S(1)}, bf16[576,768]{1,0:T(8,128)(2,1)S(1)}, u32[]{:S(2)}, u32[]{:S(2)}) collective-permute-start(bf16[576,768]{1,0:T(8,128)(2,1)S(1)} %bitcast.121), channel_id=1, source_target_pairs={{0,2},{1,3},{2,0},{3,1},{4,6},{5,7},{6,4},{7,5},{8,10},{9,11},{10,... | collective-permute-start | bytes 2654216 | tf_op jit(solution)/shard_map/ppermute | solution.py:764
  5.4 20.3 %collective-permute-start.4 = (f32[2,2,1,192]{3,2,1,0:T(1,128)S(1)}, f32[2,2,1,192]{3,2,1,0:T(1,128)S(1)}, u32[]{:S(2)}, u32[]{:S(2)}) collective-permute-start(f32[2,2,1,192]{3,2,1,0:T(1,128)S(1)} %broadcast_in_dim.3), channel_id=1, source_target_pairs={{0,1},{1,0},{2,3},{3,2},{4,5},{5,4},{6,7},{7,6},{8,9},{9,8},{10,11... | collective-permute-start | bytes 9224 | tf_op jit(solution)/shard_map/ppermute | solution.py:764
  5.6 20.2 %collective-permute-start.1 = (f32[2,2,1,192]{3,2,1,0:T(1,128)S(1)}, f32[2,2,1,192]{3,2,1,0:T(1,128)S(1)}, u32[]{:S(2)}, u32[]{:S(2)}) collective-permute-start(f32[2,2,1,192]{3,2,1,0:T(1,128)S(1)} %broadcast_in_dim.3), channel_id=1, source_target_pairs={{0,2},{1,3},{2,0},{3,1},{4,6},{5,7},{6,4},{7,5},{8,10},{9,11},{10,... | collective-permute-start | bytes 9224 | tf_op jit(solution)/shard_map/ppermute | solution.py:764
  44.1 57.7 %collective-permute-start.6 = (bf16[576,768]{1,0:T(8,128)(2,1)S(1)}, bf16[576,768]{1,0:T(8,128)(2,1)}, u32[]{:S(2)}, u32[]{:S(2)}) collective-permute-start(bf16[576,768]{1,0:T(8,128)(2,1)S(1)} %bitcast.124), channel_id=1, source_target_pairs={{0,2},{1,3},{2,0},{3,1},{4,6},{5,7},{6,4},{7,5},{8,10},{9,11},{10,... | collective-permute-start | bytes 2654216 | tf_op jit(solution)/shard_map/ppermute | solution.py:764
  45.9 40.3 %collective-permute-start.7 = (bf16[576,768]{1,0:T(8,128)(2,1)S(1)}, bf16[576,768]{1,0:T(8,128)(2,1)S(1)}, u32[]{:S(2)}, u32[]{:S(2)}) collective-permute-start(bf16[576,768]{1,0:T(8,128)(2,1)S(1)} %bitcast.125), channel_id=1, source_target_pairs={{0,1},{1,0},{2,3},{3,2},{4,5},{5,4},{6,7},{7,6},{8,9},{9,8},{10,11... | collective-permute-start | bytes 2654216 | tf_op jit(solution)/shard_map/ppermute | solution.py:764
  189.6 25.3 %collective-permute-start.9 = (bf16[2,2,2,4,96,768]{5,4,3,2,1,0:T(8,128)(2,1)}, bf16[2,2,2,4,96,768]{5,4,3,2,1,0:T(8,128)(2,1)S(1)}, u32[]{:S(2)}, u32[]{:S(2)}) collective-permute-start(bf16[2,2,2,4,96,768]{5,4,3,2,1,0:T(8,128)(2,1)} %get-tuple-element.193), channel_id=1, source_target_pairs={{0,1},{1,0},{2,3},{3,2},{4,5},{5,4},{6,7},{7,6},{8,9},{9,8},{10,11... | collective-permute-start | bytes 14155784 | tf_op jit(solution)/shard_map/ppermute | solution.py:764
  223.9 29.8 %collective-permute-start.11 = (bf16[2,4,96,768]{3,2,1,0:T(8,128)(2,1)}, bf16[2,4,96,768]{3,2,1,0:T(8,128)(2,1)S(1)}, u32[]{:S(2)}, u32[]{:S(2)}) collective-permute-start(bf16[2,4,96,768]{3,2,1,0:T(8,128)(2,1)} %get-tuple-element.201), channel_id=1, source_target_pairs={{0,2},{1,3},{2,0},{3,1},{4,6},{5,7},{6,4},{7,5},{8,10},{9,11},{10,... | collective-permute-start | bytes 3538952 | tf_op jit(solution)/shard_map/ppermute | solution.py:764
  224.2 29.5 %collective-permute-start.12 = (bf16[2,4,96,768]{3,2,1,0:T(8,128)(2,1)}, bf16[2,4,96,768]{3,2,1,0:T(8,128)(2,1)S(1)}, u32[]{:S(2)}, u32[]{:S(2)}) collective-permute-start(bf16[2,4,96,768]{3,2,1,0:T(8,128)(2,1)} %get-tuple-element.203), channel_id=1, source_target_pairs={{0,4},{4,0},{8,12},{12,8},{16,20},{20,16},{24,28},{28,24},{1,5},{5... | collective-permute-start | bytes 3538952 | tf_op jit(solution)/shard_map/ppermute | solution.py:764
  251.6 57.3 %collective-permute-start.13 = (bf16[2,4,96,384]{3,2,1,0:T(8,128)(2,1)}, bf16[2,4,96,384]{3,2,1,0:T(8,128)(2,1)S(1)}, u32[]{:S(2)}, u32[]{:S(2)}) collective-permute-start(bf16[2,4,96,384]{3,2,1,0:T(8,128)(2,1)} %get-tuple-element.219), channel_id=1, source_target_pairs={{0,2},{1,3},{2,0},{3,1},{4,6},{5,7},{6,4},{7,5},{8,10},{9,11},{10,... | collective-permute-start | bytes 1769480 | tf_op jit(solution)/shard_map/ppermute | solution.py:764
  253.2 55.8 %collective-permute-start.14 = (bf16[2,4,96,384]{3,2,1,0:T(8,128)(2,1)}, bf16[2,4,96,384]{3,2,1,0:T(8,128)(2,1)S(1)}, u32[]{:S(2)}, u32[]{:S(2)}) collective-permute-start(bf16[2,4,96,384]{3,2,1,0:T(8,128)(2,1)} %get-tuple-element.221), channel_id=1, source_target_pairs={{0,4},{4,0},{8,12},{12,8},{16,20},{20,16},{24,28},{28,24},{1,5},{5... | collective-permute-start | bytes 1769480 | tf_op jit(solution)/shard_map/ppermute | solution.py:764
  258.6 46.6 %collective-permute-start.15 = (bf16[4,96,768]{2,1,0:T(8,128)(2,1)}, bf16[4,96,768]{2,1,0:T(8,128)(2,1)S(1)}, u32[]{:S(2)}, u32[]{:S(2)}) collective-permute-start(bf16[4,96,768]{2,1,0:T(8,128)(2,1)} %get-tuple-element.223), channel_id=1, source_target_pairs={{0,4},{4,0},{8,12},{12,8},{16,20},{20,16},{24,28},{28,24},{1,5},{5... | collective-permute-start | bytes 1769480 | tf_op jit(solution)/shard_map/ppermute | solution.py:764
  260.2 45.0 %collective-permute-start.16 = (bf16[4,96,768]{2,1,0:T(8,128)(2,1)}, bf16[4,96,768]{2,1,0:T(8,128)(2,1)S(1)}, u32[]{:S(2)}, u32[]{:S(2)}) collective-permute-start(bf16[4,96,768]{2,1,0:T(8,128)(2,1)} %get-tuple-element.224), channel_id=1, source_target_pairs={{0,2},{1,3},{2,0},{3,1},{4,6},{5,7},{6,4},{7,5},{8,10},{9,11},{10,... | collective-permute-start | bytes 1769480 | tf_op jit(solution)/shard_map/ppermute | solution.py:764
  330.0 28.2 %collective-permute-start.18 = (bf16[2,4,96,768]{3,2,1,0:T(8,128)(2,1)}, bf16[2,4,96,768]{3,2,1,0:T(8,128)(2,1)S(1)}, u32[]{:S(2)}, u32[]{:S(2)}) collective-permute-start(bf16[2,4,96,768]{3,2,1,0:T(8,128)(2,1)} %get-tuple-element.244), channel_id=1, source_target_pairs={{0,2},{1,3},{2,0},{3,1},{4,6},{5,7},{6,4},{7,5},{8,10},{9,11},{10,... | collective-permute-start | bytes 3538952 | tf_op jit(solution)/shard_map/ppermute | solution.py:764
  331.5 27.9 %collective-permute-start.19 = (bf16[2,4,96,768]{3,2,1,0:T(8,128)(2,1)}, bf16[2,4,96,768]{3,2,1,0:T(8,128)(2,1)S(1)}, u32[]{:S(2)}, u32[]{:S(2)}) collective-permute-start(bf16[2,4,96,768]{3,2,1,0:T(8,128)(2,1)} %get-tuple-element.246), channel_id=1, source_target_pairs={{0,4},{4,0},{8,12},{12,8},{16,20},{20,16},{24,28},{28,24},{1,5},{5... | collective-permute-start | bytes 3538952 | tf_op jit(solution)/shard_map/ppermute | solution.py:764
  364.6 38.5 %collective-permute-start.25 = (bf16[2,2,96,768]{3,2,1,0:T(8,128)(2,1)S(1)}, bf16[2,2,96,768]{3,2,1,0:T(8,128)(2,1)S(1)}, u32[]{:S(2)}, u32[]{:S(2)}) collective-permute-start(bf16[2,2,96,768]{3,2,1,0:T(8,128)(2,1)S(1)} %copy-done.46), channel_id=1, source_target_pairs={{0,8},{4,12},{8,0},{12,4},{16,24},{20,28},{24,16},{28,20},{1,9},{5... | collective-permute-start | bytes 1769480 | tf_op jit(solution)/shard_map/ppermute | solution.py:764
  366.3 32.6 %collective-permute-start.26 = (bf16[4,96,768]{2,1,0:T(8,128)(2,1)}, bf16[4,96,768]{2,1,0:T(8,128)(2,1)S(1)}, u32[]{:S(2)}, u32[]{:S(2)}) collective-permute-start(bf16[4,96,768]{2,1,0:T(8,128)(2,1)} %get-tuple-element.266), channel_id=1, source_target_pairs={{0,4},{4,0},{8,12},{12,8},{16,20},{20,16},{24,28},{28,24},{1,5},{5... | collective-permute-start | bytes 1769480 | tf_op jit(solution)/shard_map/ppermute | solution.py:764
  366.8 32.8 %collective-permute-start.27 = (bf16[4,96,768]{2,1,0:T(8,128)(2,1)}, bf16[4,96,768]{2,1,0:T(8,128)(2,1)S(1)}, u32[]{:S(2)}, u32[]{:S(2)}) collective-permute-start(bf16[4,96,768]{2,1,0:T(8,128)(2,1)} %get-tuple-element.267), channel_id=1, source_target_pairs={{0,2},{1,3},{2,0},{3,1},{4,6},{5,7},{6,4},{7,5},{8,10},{9,11},{10,... | collective-permute-start | bytes 1769480 | tf_op jit(solution)/shard_map/ppermute | solution.py:764
  406.0 21.5 %collective-permute-start.41 = (bf16[2,1,96,768]{3,2,1,0:T(8,128)(2,1)}, bf16[2,1,96,768]{3,2,1,0:T(8,128)(2,1)S(1)}, u32[]{:S(2)}, u32[]{:S(2)}) collective-permute-start(bf16[2,1,96,768]{3,2,1,0:T(8,128)(2,1)} %get-tuple-element.317), channel_id=1, source_target_pairs={{0,16},{4,20},{8,24},{12,28},{16,0},{20,4},{24,8},{28,12},{1,17},{... | collective-permute-start | bytes 884744 | tf_op jit(solution)/shard_map/ppermute | solution.py:764
  408.7 17.4 %collective-permute-start.37 = (f32[2,12,768]{2,1,0:T(8,128)S(1)}, f32[2,12,768]{2,1,0:T(8,128)S(1)}, u32[]{:S(2)}, u32[]{:S(2)}) collective-permute-start(f32[2,12,768]{2,1,0:T(8,128)S(1)} %fusion.22), channel_id=1, source_target_pairs={{0,16},{4,20},{8,24},{12,28},{16,0},{20,4},{24,8},{28,12},{1,17},{... | collective-permute-start | bytes 221192 | tf_op jit(solution)/shard_map/ppermute | solution.py:764
  411.9 45.0 %collective-permute-start.30 = (bf16[2,2,96,384]{3,2,1,0:T(8,128)(2,1)}, bf16[2,2,96,384]{3,2,1,0:T(8,128)(2,1)S(1)}, u32[]{:S(2)}, u32[]{:S(2)}) collective-permute-start(bf16[2,2,96,384]{3,2,1,0:T(8,128)(2,1)} %get-tuple-element.289), channel_id=1, source_target_pairs={{0,8},{4,12},{8,0},{12,4},{16,24},{20,28},{24,16},{28,20},{1,9},{5... | collective-permute-start | bytes 884744 | tf_op jit(solution)/shard_map/ppermute | solution.py:764
  412.6 41.5 %collective-permute-start.31 = (bf16[2,2,96,768]{3,2,1,0:T(8,128)(2,1)S(1)}, bf16[2,2,96,768]{3,2,1,0:T(8,128)(2,1)S(1)}, u32[]{:S(2)}, u32[]{:S(2)}) collective-permute-start(bf16[2,2,96,768]{3,2,1,0:T(8,128)(2,1)S(1)} %copy-done.49), channel_id=1, source_target_pairs={{0,8},{4,12},{8,0},{12,4},{16,24},{20,28},{24,16},{28,20},{1,9},{5... | collective-permute-start | bytes 1769480 | tf_op jit(solution)/shard_map/ppermute | solution.py:764
  414.0 36.4 %collective-permute-start.21 = (bf16[2,4,96,384]{3,2,1,0:T(8,128)(2,1)S(1)}, bf16[2,4,96,384]{3,2,1,0:T(8,128)(2,1)S(1)}, u32[]{:S(2)}, u32[]{:S(2)}) collective-permute-start(bf16[2,4,96,384]{3,2,1,0:T(8,128)(2,1)S(1)} %copy-done.48), channel_id=1, source_target_pairs={{0,2},{1,3},{2,0},{3,1},{4,6},{5,7},{6,4},{7,5},{8,10},{9,11},{10,... | collective-permute-start | bytes 1769480 | tf_op jit(solution)/shard_map/ppermute | solution.py:764
  426.0 24.4 %collective-permute-start.22 = (bf16[2,4,96,384]{3,2,1,0:T(8,128)(2,1)S(1)}, bf16[2,4,96,384]{3,2,1,0:T(8,128)(2,1)S(1)}, u32[]{:S(2)}, u32[]{:S(2)}) collective-permute-start(bf16[2,4,96,384]{3,2,1,0:T(8,128)(2,1)S(1)} %copy-done.47), channel_id=1, source_target_pairs={{0,4},{4,0},{8,12},{12,8},{16,20},{20,16},{24,28},{28,24},{1,5},{5... | collective-permute-start | bytes 1769480 | tf_op jit(solution)/shard_map/ppermute | solution.py:764
  (69 other events, 477.3 us)

commit v5 on v4

--- a/solution.py
+++ b/solution.py
@@ -93,7 +93,7 @@
     return pltpu.HBM(shape, kind)
 
 
-def call(kernel, name, grid, in_specs, out_specs, out_shape, scratch, scalars, operands, alias=None, flops=0):
+def call(kernel, name, grid, in_specs, out_specs, out_shape, scratch, scalars, operands, alias=None, flops=0, vmem=VMEM_BYTES):
     return pl.pallas_call(
         kernel,
         grid_spec=pltpu.PrefetchScalarGridSpec(
@@ -104,7 +104,7 @@
             scratch_shapes=scratch,
         ),
         out_shape=out_shape,
-        compiler_params=params(),
+        compiler_params=pltpu.CompilerParams(vmem_limit_bytes=vmem),
         input_output_aliases=alias or {},
         cost_estimate=cost(flops, out_shape, operands),
         name=name,
@@ -579,8 +579,10 @@
 def core_add_kernel(kept_ref, got_ref, up_send, up_keep, down_send, down_keep):
     step = pl.program_id(0)
 
+    which, away = step // 2, jnp.where(step < 2, step, 3 - step)
+
     def summed(at):
-        return (kept_ref[at].astype(WIDE) + got_ref[at].astype(WIDE)).astype(LOW)
+        return (kept_ref[at].astype(WIDE) + got_ref[which, away, at].astype(WIDE)).astype(LOW)
 
     @pl.when(step < 2)
     def _():
@@ -606,7 +608,16 @@
     down = pl.BlockSpec((2, rest, chunk_rows, width), lambda i: (0, 0, 0, 0))
     made = stored((2, rest, chunk_rows, width), LOW)
     return call(
-        core_add_kernel, "core_add", (4,), [block, block], [up, up, down, down], [made] * 4, [], [], [kept, got]
+        core_add_kernel,
+        "core_add",
+        (4,),
+        [block, pl.BlockSpec(memory_space=pltpu.VMEM)],
+        [up, up, down, down],
+        [made] * 4,
+        [],
+        [],
+        [kept, got],
+        vmem=24 << 20,
     )
 
 
@@ -768,35 +779,29 @@
     inputs = 2 if merge_in else 4
     outputs = 2 if merge_out else 4
     ins, outs = refs[:inputs], refs[inputs : inputs + outputs]
-    kept_ref, got_ref, send_ref, keep_ref, in_sems, out_sems = refs[inputs + outputs :]
+    kept_ref, send_ref, keep_ref, in_sems, out_sems = refs[inputs + outputs :]
     half = send_ref.shape[1]
-    loads, stores = [], []
+    loads, got, stores = [], [], []
     for part in range(2):
-        kept, got = (ins[0].at[part], ins[1].at[part]) if merge_in else ins[2 * part : 2 * part + 2]
+        kept, came = (ins[0].at[part], ins[1].at[part]) if merge_in else ins[2 * part : 2 * part + 2]
         send, keep = (
             (outs[0].at[part], outs[1].at[part]) if merge_out else outs[2 * part : 2 * part + 2]
         )
-        loads.append(
-            [
-                pltpu.make_async_copy(kept, kept_ref.at[part], in_sems.at[part, 0]),
-                pltpu.make_async_copy(got, got_ref.at[part], in_sems.at[part, 1]),
-            ]
-        )
+        got.append(came)
+        loads.append(pltpu.make_async_copy(kept, kept_ref.at[part], in_sems.at[part]))
         stores.append(
             [
                 pltpu.make_async_copy(send_ref.at[part], send, out_sems.at[part, 0]),
                 pltpu.make_async_copy(keep_ref.at[part], keep, out_sems.at[part, 1]),
             ]
         )
-    for copies in loads:
-        for copy in copies:
-            copy.start()
+    for copy in loads:
+        copy.start()
     for part in range(2):
-        for copy in loads[part]:
-            copy.wait()
-        for out, at in ((send_ref, slice(half, None)), (keep_ref, slice(None, half))):
-            out[part] = (kept_ref[part, at].astype(WIDE) + got_ref[part, at].astype(WIDE)).astype(LOW)
-        for copy in stores[part]:
+        loads[part].wait()
+        for at, (out, copy) in enumerate(zip((send_ref, keep_ref), stores[part])):
+            rows = pl.ds(half * (1 - at), half)
+            out[part] = (kept_ref[part, rows].astype(WIDE) + got[part][rows].astype(WIDE)).astype(LOW)
             copy.start()
     for copies in stores:
         for copy in copies:
@@ -809,18 +814,17 @@
     out_shape = [stored((2, *half), LOW)] * 2 if merge_out else [stored(half, LOW)] * 4
     return pl.pallas_call(
         functools.partial(add_split_kernel, merge_in=merge_in, merge_out=merge_out),
-        in_specs=[in_hbm()] * len(ins),
+        in_specs=[in_hbm(), pl.BlockSpec(memory_space=pltpu.VMEM)] * (len(ins) // 2),
         out_specs=[in_hbm()] * len(out_shape),
         out_shape=out_shape,
         scratch_shapes=[
             pltpu.VMEM((2, size, rows, columns), LOW),
-            pltpu.VMEM((2, size, rows, columns), LOW),
             pltpu.VMEM((2, *half), LOW),
             pltpu.VMEM((2, *half), LOW),
-            pltpu.SemaphoreType.DMA((2, 2)),
+            pltpu.SemaphoreType.DMA((2,)),
             pltpu.SemaphoreType.DMA((2, 2)),
         ],
-        compiler_params=params(),
+        compiler_params=pltpu.CompilerParams(vmem_limit_bytes=16 << 20),
         cost_estimate=cost(0, out_shape, ins),
         name="add_split",
     )(*ins)
@@ -853,9 +857,70 @@
         self.at += 1
         return outs[-1]
 
-    def finish(self):
-        kept, got = self.kept[0], self.got[0]
-        return (kept.astype(WIDE) + got.astype(WIDE)).reshape(2, *kept.shape[-2:])
+
+def last_sums_kernel(*refs, layers):
+    ins, outs = refs[: 4 * layers + 2], refs[4 * layers + 2 :]
+    qkv, qv, out_w, out_b, gain1, shift1, up_w, up_b, down_w, down_b, gain2, shift2 = outs
+    part = out_w.shape[2]
+    width = down_b.shape[1]
+    rows = ins[-2][...] + ins[-1][...]
+    for layer in range(layers):
+        ffn_kept, ffn_got, wide_kept, wide_got = ins[4 * layer : 4 * layer + 4]
+        down_w[layer] = ffn_kept[0, 0].astype(WIDE) + ffn_got[0, 0].astype(WIDE)
+        up_w[layer] = ffn_kept[1, 0].astype(WIDE) + ffn_got[1, 0].astype(WIDE)
+        for half in range(2):
+            both = wide_kept[half, 0].astype(WIDE) + wide_got[half, 0].astype(WIDE)
+            for at in range(2):
+                which = 2 * half + at
+                block = both[:, at * part : (at + 1) * part]
+                if which < 3:
+                    qkv[layer, which] = block
+                else:
+                    out_w[layer] = block
+        for row, out in enumerate((gain2, shift2, down_b, gain1, shift1, out_b)):
+            out[layer : layer + 1] = rows[layer, row : row + 1]
+        qv[layer] = rows[layer, 6:8]
+        for row in range(up_b.shape[1] // width):
+            at = slice(row * width, (row + 1) * width)
+            up_b[layer : layer + 1, at] = rows[layer, 8 + row : 9 + row]
+
+
+def last_sums(groups, small, passing):
+    layers, _, width = small.shape
+    ins, specs = [], []
+    for group in groups:
+        ins += [group.kept[0], group.got[0]]
+    ins = [v.reshape(2, 1, *v.shape[-2:]) for v in ins] + [small, passing]
+    rows, part = ins[0].shape[2], ins[2].shape[3] // 2
+    hidden = (small.shape[1] - 8) * width
+    shapes = [
+        (layers, 3, rows, part),
+        (layers, 2, width),
+        (layers, rows, part),
+        (layers, width),
+        (layers, width),
+        (layers, width),
+        (layers, rows, width),
+        (layers, hidden),
+        (layers, rows, width),
+        (layers, width),
+        (layers, width),
+        (layers, width),
+    ]
+    spec = lambda shape: pl.BlockSpec(shape, lambda i: (0,) * len(shape))
+    specs = [spec(v.shape) for v in ins]
+    return call(
+        functools.partial(last_sums_kernel, layers=layers),
+        "last_sums",
+        (1,),
+        specs,
+        [spec(shape) for shape in shapes],
+        [shape_of(shape, WIDE) for shape in shapes],
+        [],
+        [],
+        ins,
+        vmem=24 << 20,
+    )
 
 
 def ordered(after, *values):
@@ -997,7 +1062,7 @@
             own, mixed, do, probs, rounded, da, w[1], w[3], du, None, dp_count, WIDE
         )
         if early:
-            token = advance(half_grad, running[:1])
+            token = advance(half_grad)
             (sent,) = ordered(token, sent)
             wide_got = swap(sent, "head", low_bit)
         else:
@@ -1036,31 +1101,33 @@
     small_sum = jnp.stack(small_sums)
     spread = [("head", bits_of("head")[0])] + [("dp", bit) for bit in bits_of("dp")[1:]]
     spread += [("dp", bits_of("dp")[0]), ("head", bits_of("head")[1])]
+    passing = swap(small_sum, *spread.pop(0))
     while any(group.busy() for group in running) or spread:
+        token = advance(token)
         if spread:
-            small_sum = small_sum + swap(small_sum, *spread.pop(0))
-        token = advance(token)
-    ffn_sums = [group.finish() for group in ffn_groups]
-    wide_sums = [group.finish() for group in wide_groups]
-    wide = [
-        [both[half, :, at * part : (at + 1) * part] for half in range(2) for at in range(2)]
-        for both in wide_sums
-    ]
+            (small_sum, passing) = ordered(token, small_sum, passing)
+            small_sum = small_sum + passing
+            token = small_sum
+            passing = swap(small_sum, *spread.pop(0))
+    groups = [group for pair in zip(ffn_groups, wide_groups) for group in pair]
+    qkv, qv, out_w, out_b, gain1, shift1, up_w, up_b, down_w, down_b, gain2, shift2 = last_sums(
+        groups, small_sum, passing
+    )
     return (
         out_state,
         grad_state,
-        jnp.stack([jnp.stack(w[:3]) for w in wide]),
-        small_sum[:, 6:8],
-        jnp.stack([w[3] for w in wide]),
-        small_sum[:, 5],
-        small_sum[:, 3],
-        small_sum[:, 4],
-        jnp.stack([both[1] for both in ffn_sums]),
-        small_sum[:, 8:].reshape(layers, -1),
-        jnp.stack([both[0].T for both in ffn_sums]),
-        small_sum[:, 2],
-        small_sum[:, 0],
-        small_sum[:, 1],
+        qkv,
+        qv,
+        out_w,
+        out_b,
+        gain1,
+        shift1,
+        up_w,
+        up_b,
+        jnp.swapaxes(down_w, 1, 2),
+        down_b,
+        gain2,
+        shift2,
     )
 
 

time: 500 us -> 464 us (0.928); the launches traced: 496 us -> 455 us
  local copies, waits for them, and re-layouts: 27.5 us -> 11.8 us
  Pallas kernels: 345 us -> 330 us
  other arithmetic: 8.03 us -> 2.65 us
    unnamed x112 -> x108, local copies, waits for them, and re-layouts: 22.2 us -> 8.18 us
    pallas_call x12, Pallas kernels: 29.6 us -> 16.6 us  [add_split(): pl.pallas_call(functools.partial(add_split_kernel, merge_in=merge_in, mer...]
    pallas_call x14 -> x15, Pallas kernels: 311 us -> 309 us  [call(): pl.pallas_call(kernel, grid_spec=pltpu.PrefetchScalarGridSpec(num_scalar_...]
  transfers between devices with their start and end apart: 42 -> 42, of which waited for: 15 -> 17; matrix products, arithmetic and copies ran while one was open for 3% -> 1% of each run, Pallas kernels for 49% -> 53%
where the time goes in v5:
time: 464 us; the launch traced here: 455 us
  Pallas kernels  330 us (71%)
  waiting for transfers between devices  71.6 us (15%)
  starting transfers between devices  37.4 us (8%)
  local copies, waits for them, and re-layouts  11.8 us (3%)
    pallas_call x15, Pallas kernels, call(): pl.pallas_call(kernel, grid_spec=pltpu.PrefetchScalarGridSpec(num_scalar_...  309 us
    ppermute x42, waiting for transfers between devices, swap(): return lax.ppermute(value, axis, [(i, i ^ bit) for i in range(size)])  71.6 us
    ppermute x42, starting transfers between devices, swap(): return lax.ppermute(value, axis, [(i, i ^ bit) for i in range(size)])  37.4 us
    pallas_call x12, Pallas kernels, add_split(): pl.pallas_call(functools.partial(add_split_kernel, merge_in=merge_in, mer...  16.6 us
  transfers between devices with their start and end apart: 42, of which 17 were waited for; matrix products, arithmetic and copies ran while one was open for 1% of the time, Pallas kernels for 53%

profile of v5, /device:TPU:0, one launch (start us, length us, event | category | flops | bytes accessed | tf_op | source)
XLA Modules:
  0.0 455.4 jit_solution(16366814634961458591)
XLA Ops:
  6.0 4.4 mask_bias.1.bias_ref
  10.4 15.3 %collective-permute-done.1 = f32[2,2,1,192]{3,2,1,0:T(1,128)S(1)} collective-permute-done((f32[2,2,1,192]{3,2,1,0:T(1,128)S(1)}, f32[2,2,1,192]{3,2,1,0:T(1,128)S(1)}, u32[]{:S(2)}, u32[]{:S(2)}) %collective-permute-start.1) | collective-permute-done | bytes 3104 | tf_op jit(solution)/shard_map/ppermute | solution.py:775
  27.5 14.8 %attention_forward.4 = (bf16[4,4,1024,192]{3,2,1,0:T(8,128)(2,1)}, bf16[4,2,3,512,512]{4,3,2,1,0:T(8,128)(2,1)}) custom-call(bf16[1024,768]{1,0:T(8,128)(2,1)} %x_ref.7, bf16[576,768]{1,0:T(8,128)(2,1)} %bitcast.85, bf16[576,768]{1,0:T(8,128)(2,1)} %collective-permute-done.3.wb_ref.wa_ref, f32[2,2,1,192]{3,2,1,0:T(1,128)} %get-tuple-element.379.b_ref, ...), custom_call_target="tpu_custom_call" | custom-call | flops 8254390272 | bytes 24316928 | tf_op jit(solution)/shard_map/attention_forward/pallas_call | solution.py:97
  47.2 14.3 %attention_forward.5 = (bf16[4,4,1024,192]{3,2,1,0:T(8,128)(2,1)}, bf16[4,2,3,512,512]{4,3,2,1,0:T(8,128)(2,1)}) custom-call(bf16[1024,768]{1,0:T(8,128)(2,1)} %x_ref.7, bf16[576,768]{1,0:T(8,128)(2,1)} %copy-done.44, bf16[576,768]{1,0:T(8,128)(2,1)} %copy-done.45, ...), custom_call_target="tpu_custom_call", output_to_operand_aliasing={{0}: (5, {}), {1}: (6, {})} | custom-call | flops 8254390272 | bytes 43191296 | tf_op jit(solution)/shard_map/attention_forward/pallas_call | solution.py:97
  61.5 25.0 %ffn_forward.2 = (f32[1024,768]{1,0:T(8,128)}, bf16[1024,768]{1,0:T(8,128)(2,1)}, bf16[4,1024,768]{2,1,0:T(8,128)(2,1)}, bf16[4,1024,768]{2,1,0:T(8,128)(2,1)}, ...) custom-call(s32[2]{0:T(128)} %pad_add_fusion.own_ref, ...), custom_call_target="tpu_custom_call" | custom-call | flops 32614907904 | bytes 51154944 | tf_op jit(solution)/shard_map/ffn_forward/pallas_call | solution.py:97
  87.5 14.4 %attention_forward.6 = (bf16[4,4,1024,192]{3,2,1,0:T(8,128)(2,1)}, bf16[4,2,3,512,512]{4,3,2,1,0:T(8,128)(2,1)}) custom-call(bf16[1024,768]{1,0:T(8,128)(2,1)} %get-tuple-element.191.x_ref, bf16[576,768]{1,0:T(8,128)(2,1)} %bitcast.89, bf16[576,768]{1,0:T(8,128)(2,1)} %copy-done.46, f32[2,2,1,192]{3,2,1,0:T(1,128)} %get-tuple-element.378.b_ref, ...), custom_call_target="tpu_custom_call" | custom-call | flops 8254390272 | bytes 24316928 | tf_op jit(solution)/shard_map/attention_forward/pallas_call | solution.py:97
  105.7 14.3 %attention_forward.7 = (bf16[4,4,1024,192]{3,2,1,0:T(8,128)(2,1)}, bf16[4,2,3,512,512]{4,3,2,1,0:T(8,128)(2,1)}) custom-call(bf16[1024,768]{1,0:T(8,128)(2,1)} %get-tuple-element.191.x_ref, bf16[576,768]{1,0:T(8,128)(2,1)} %collective-permute-done.6.wa_ref.wb_ref, bf16[576,768]{1,0:T(8,128)(2,1)} %copy-done.47, ...), custom_call_target="tpu_custom_call", output_to_operand_aliasing={{0}: (5, {}), {1}: (6, {})} | custom-call | flops 8254390272 | bytes 43191296 | tf_op jit(solution)/shard_map/attention_forward/pallas_call | solution.py:97
  119.9 25.2 %ffn_forward.3 = (f32[1024,768]{1,0:T(8,128)}, bf16[1024,768]{1,0:T(8,128)(2,1)}, bf16[4,1024,768]{2,1,0:T(8,128)(2,1)}, bf16[4,1024,768]{2,1,0:T(8,128)(2,1)}, ...) custom-call(s32[2]{0:T(128)} %pad_add_fusion.own_ref, ...), custom_call_target="tpu_custom_call" | custom-call | flops 32614907904 | bytes 52727808 | tf_op jit(solution)/shard_map/ffn_forward/pallas_call | solution.py:97
  145.1 44.8 %ffn_backward.2 = (bf16[4,1024,192]{2,1,0:T(8,128)(2,1)}, bf16[4,1024,192]{2,1,0:T(8,128)(2,1)}, f32[1024,768]{1,0:T(8,128)}, f32[8,768]{1,0:T(8,128)}, f32[4,1,...) custom-call(s32[2]{0:T(128)} %pad_add_fusion.own_ref, ...), custom_call_target="tpu_custom_call" | custom-call | flops 41070624768 | bytes 59025408 | tf_op jit(solution)/shard_map/ffn_backward/pallas_call | solution.py:97
  190.4 25.0 %attention_backward.4 = (f32[1024,768]{1,0:T(8,128)}, f32[2,8,192]{2,1,0:T(8,128)}, bf16[2,2,4,96,768]{4,3,2,1,0:T(8,128)(2,1)}) custom-call(s32[2]{0:T(128)} %pad_add_fusion.own_ref, bf16[4,4,1024,192]{3,2,1,0:T(8,128)(2,1)} %get-tuple-element.197.mixed_hbm.mixed_ref.o_ref, bf16[4,1024,192]{2,1,0:T(8,128)(2,1)} %get-tuple-element.217.do_ref, ...), custom_call_target="tpu_custom_call" | custom-call | flops 14495514624 | bytes 40316928 | tf_op jit(solution)/shard_map/attention_backward/pallas_call | solution.py:97
  215.5 6.1 %core_add.2 = (bf16[2,4,96,768]{3,2,1,0:T(8,128)(2,1)}, bf16[2,4,96,768]{3,2,1,0:T(8,128)(2,1)}, bf16[2,4,96,768]{3,2,1,0:T(8,128)(2,1)}, bf16[2,4,96,768]{3,2,1,0:T(8,128)(2,1)}) custom-call(bf16[2,2,2,4,96,768]{5,4,3,2,1,0:T(8,128)(2,1)S(1)} %bitcast.65, bf16[2,2,2,4,96,768]{5,4,3,2,1,0:T(8,128)(2,1)} %collective-permute-done.9.got_ref), custom_call_target="tpu_custom_call" | custom-call | bytes 14155776 | tf_op jit(solution)/shard_map/core_add/pallas_call | solution.py:97
  223.7 25.7 %attention_backward.5 = (f32[1024,768]{1,0:T(8,128)}, f32[2,8,192]{2,1,0:T(8,128)}, bf16[2,4,96,384]{3,2,1,0:T(8,128)(2,1)}, bf16[2,4,96,384]{3,2,1,0:T(8,128)(2...) custom-call(s32[2]{0:T(128)} %pad_add_fusion.own_ref, ...), custom_call_target="tpu_custom_call" | custom-call | flops 14495514624 | bytes 42676224 | tf_op jit(solution)/shard_map/attention_backward/pallas_call | solution.py:97
  255.7 44.7 %ffn_backward.3 = (bf16[4,1024,192]{2,1,0:T(8,128)(2,1)}, bf16[4,1024,192]{2,1,0:T(8,128)(2,1)}, f32[1024,768]{1,0:T(8,128)}, f32[8,768]{1,0:T(8,128)}, f32[4,1,...) custom-call(s32[2]{0:T(128)} %pad_add_fusion.own_ref, ...), custom_call_target="tpu_custom_call" | custom-call | flops 41070624768 | bytes 60598272 | tf_op jit(solution)/shard_map/ffn_backward/pallas_call | solution.py:97
  307.5 4.3 collective-permute-done.17.got_ref
  311.9 3.7 core_add.3
  317.7 24.4 %attention_backward.6 = (f32[1024,768]{1,0:T(8,128)}, f32[2,8,192]{2,1,0:T(8,128)}, bf16[2,2,4,96,768]{4,3,2,1,0:T(8,128)(2,1)}) custom-call(s32[2]{0:T(128)} %pad_add_fusion.own_ref, bf16[4,4,1024,192]{3,2,1,0:T(8,128)(2,1)} %get-tuple-element.190.mixed_hbm.mixed_ref.o_ref, bf16[4,1024,192]{2,1,0:T(8,128)(2,1)} %get-tuple-element.284.do_ref, ...), custom_call_target="tpu_custom_call" | custom-call | flops 14495514624 | bytes 40316928 | tf_op jit(solution)/shard_map/attention_backward/pallas_call | solution.py:97
  355.6 25.4 %attention_backward.7 = (bf16[1024,768]{1,0:T(8,128)(2,1)}, f32[2,8,192]{2,1,0:T(8,128)}, bf16[2,4,96,384]{3,2,1,0:T(8,128)(2,1)}, bf16[2,4,96,384]{3,2,1,0:T(8,...) custom-call(s32[2]{0:T(128)} %pad_add_fusion.own_ref, ...), custom_call_target="tpu_custom_call" | custom-call | flops 14495514624 | bytes 41103360 | tf_op jit(solution)/shard_map/attention_backward/pallas_call | solution.py:97
  386.6 10.1 %collective-permute-done.28 = bf16[2,4,96,384]{3,2,1,0:T(8,128)(2,1)S(1)} collective-permute-done((bf16[2,4,96,384]{3,2,1,0:T(8,128)(2,1)}, bf16[2,4,96,384]{3,2,1,0:T(8,128)(2,1)S(1)}, u32[]{:S(2)}, u32[]{:S(2)}) %collective-permute-start.28) | collective-permute-done | bytes 589856 | tf_op jit(solution)/shard_map/ppermute | solution.py:775
  403.1 3.5 collective-permute-done.32.refs_1_
  412.0 2.6 collective-permute-start.37
  414.9 12.5 %collective-permute-done.35 = f32[2,12,768]{2,1,0:T(8,128)S(1)} collective-permute-done((f32[2,12,768]{2,1,0:T(8,128)S(1)}, f32[2,12,768]{2,1,0:T(8,128)S(1)}, u32[]{:S(2)}, u32[]{:S(2)}) %collective-permute-start.35) | collective-permute-done | bytes 73760 | tf_op jit(solution)/shard_map/ppermute | solution.py:775
  429.6 12.9 %collective-permute-done.39 = f32[2,12,768]{2,1,0:T(8,128)S(1)} collective-permute-done((f32[2,12,768]{2,1,0:T(8,128)S(1)}, f32[2,12,768]{2,1,0:T(8,128)S(1)}, u32[]{:S(2)}, u32[]{:S(2)}) %collective-permute-start.39) | collective-permute-done | bytes 73760 | tf_op jit(solution)/shard_map/ppermute | solution.py:775
  443.8 2.9 collective-permute-start.36
  448.4 2.9 collective-permute-done.38.refs_7_
  (226 shorter events, 74.6 us)
Async XLA Ops:
  2.3 25.2 %collective-permute-start.3 = (bf16[576,768]{1,0:T(8,128)(2,1)S(1)}, bf16[576,768]{1,0:T(8,128)(2,1)}, u32[]{:S(2)}, u32[]{:S(2)}) collective-permute-start(bf16[576,768]{1,0:T(8,128)(2,1)S(1)} %bitcast.83), channel_id=1, source_target_pairs={{0,1},{1,0},{2,3},{3,2},{4,5},{5,4},{6,7},{7,6},{8,9},{9,8},{10,11... | collective-permute-start | bytes 2654216 | tf_op jit(solution)/shard_map/ppermute | solution.py:775
  2.8 39.5 %collective-permute-start = (bf16[576,768]{1,0:T(8,128)(2,1)S(1)}, bf16[576,768]{1,0:T(8,128)(2,1)S(1)}, u32[]{:S(2)}, u32[]{:S(2)}) collective-permute-start(bf16[576,768]{1,0:T(8,128)(2,1)S(1)} %bitcast.84), channel_id=1, source_target_pairs={{0,2},{1,3},{2,0},{3,1},{4,6},{5,7},{6,4},{7,5},{8,10},{9,11},{10,... | collective-permute-start | bytes 2654216 | tf_op jit(solution)/shard_map/ppermute | solution.py:775
  5.4 20.3 %collective-permute-start.4 = (f32[2,2,1,192]{3,2,1,0:T(1,128)S(1)}, f32[2,2,1,192]{3,2,1,0:T(1,128)S(1)}, u32[]{:S(2)}, u32[]{:S(2)}) collective-permute-start(f32[2,2,1,192]{3,2,1,0:T(1,128)S(1)} %broadcast_in_dim.3), channel_id=1, source_target_pairs={{0,1},{1,0},{2,3},{3,2},{4,5},{5,4},{6,7},{7,6},{8,9},{9,8},{10,11... | collective-permute-start | bytes 9224 | tf_op jit(solution)/shard_map/ppermute | solution.py:775
  5.6 20.2 %collective-permute-start.1 = (f32[2,2,1,192]{3,2,1,0:T(1,128)S(1)}, f32[2,2,1,192]{3,2,1,0:T(1,128)S(1)}, u32[]{:S(2)}, u32[]{:S(2)}) collective-permute-start(f32[2,2,1,192]{3,2,1,0:T(1,128)S(1)} %broadcast_in_dim.3), channel_id=1, source_target_pairs={{0,2},{1,3},{2,0},{3,1},{4,6},{5,7},{6,4},{7,5},{8,10},{9,11},{10,... | collective-permute-start | bytes 9224 | tf_op jit(solution)/shard_map/ppermute | solution.py:775
  44.5 57.4 %collective-permute-start.6 = (bf16[576,768]{1,0:T(8,128)(2,1)S(1)}, bf16[576,768]{1,0:T(8,128)(2,1)}, u32[]{:S(2)}, u32[]{:S(2)}) collective-permute-start(bf16[576,768]{1,0:T(8,128)(2,1)S(1)} %bitcast.87), channel_id=1, source_target_pairs={{0,2},{1,3},{2,0},{3,1},{4,6},{5,7},{6,4},{7,5},{8,10},{9,11},{10,... | collective-permute-start | bytes 2654216 | tf_op jit(solution)/shard_map/ppermute | solution.py:775
  46.2 40.3 %collective-permute-start.7 = (bf16[576,768]{1,0:T(8,128)(2,1)S(1)}, bf16[576,768]{1,0:T(8,128)(2,1)S(1)}, u32[]{:S(2)}, u32[]{:S(2)}) collective-permute-start(bf16[576,768]{1,0:T(8,128)(2,1)S(1)} %bitcast.88), channel_id=1, source_target_pairs={{0,1},{1,0},{2,3},{3,2},{4,5},{5,4},{6,7},{7,6},{8,9},{9,8},{10,11... | collective-permute-start | bytes 2654216 | tf_op jit(solution)/shard_map/ppermute | solution.py:775
  189.9 25.6 %collective-permute-start.9 = (bf16[2,2,2,4,96,768]{5,4,3,2,1,0:T(8,128)(2,1)}, bf16[2,2,2,4,96,768]{5,4,3,2,1,0:T(8,128)(2,1)}, u32[]{:S(2)}, u32[]{:S(2)}) collective-permute-start(bf16[2,2,2,4,96,768]{5,4,3,2,1,0:T(8,128)(2,1)} %get-tuple-element.213), channel_id=1, source_target_pairs={{0,1},{1,0},{2,3},{3,2},{4,5},{5,4},{6,7},{7,6},{8,9},{9,8},{10,11... | collective-permute-start | bytes 14155784 | tf_op jit(solution)/shard_map/ppermute | solution.py:775
  221.6 29.9 %collective-permute-start.11 = (bf16[2,4,96,768]{3,2,1,0:T(8,128)(2,1)}, bf16[2,4,96,768]{3,2,1,0:T(8,128)(2,1)S(1)}, u32[]{:S(2)}, u32[]{:S(2)}) collective-permute-start(bf16[2,4,96,768]{3,2,1,0:T(8,128)(2,1)} %get-tuple-element.221), channel_id=1, source_target_pairs={{0,2},{1,3},{2,0},{3,1},{4,6},{5,7},{6,4},{7,5},{8,10},{9,11},{10,... | collective-permute-start | bytes 3538952 | tf_op jit(solution)/shard_map/ppermute | solution.py:775
  221.9 29.7 %collective-permute-start.12 = (bf16[2,4,96,768]{3,2,1,0:T(8,128)(2,1)}, bf16[2,4,96,768]{3,2,1,0:T(8,128)(2,1)S(1)}, u32[]{:S(2)}, u32[]{:S(2)}) collective-permute-start(bf16[2,4,96,768]{3,2,1,0:T(8,128)(2,1)} %get-tuple-element.223), channel_id=1, source_target_pairs={{0,4},{4,0},{8,12},{12,8},{16,20},{20,16},{24,28},{28,24},{1,5},{5... | collective-permute-start | bytes 3538952 | tf_op jit(solution)/shard_map/ppermute | solution.py:775
  249.3 52.5 %collective-permute-start.13 = (bf16[2,4,96,384]{3,2,1,0:T(8,128)(2,1)}, bf16[2,4,96,384]{3,2,1,0:T(8,128)(2,1)S(1)}, u32[]{:S(2)}, u32[]{:S(2)}) collective-permute-start(bf16[2,4,96,384]{3,2,1,0:T(8,128)(2,1)} %get-tuple-element.239), channel_id=1, source_target_pairs={{0,2},{1,3},{2,0},{3,1},{4,6},{5,7},{6,4},{7,5},{8,10},{9,11},{10,... | collective-permute-start | bytes 1769480 | tf_op jit(solution)/shard_map/ppermute | solution.py:775
  250.9 50.9 %collective-permute-start.14 = (bf16[2,4,96,384]{3,2,1,0:T(8,128)(2,1)}, bf16[2,4,96,384]{3,2,1,0:T(8,128)(2,1)S(1)}, u32[]{:S(2)}, u32[]{:S(2)}) collective-permute-start(bf16[2,4,96,384]{3,2,1,0:T(8,128)(2,1)} %get-tuple-element.241), channel_id=1, source_target_pairs={{0,4},{4,0},{8,12},{12,8},{16,20},{20,16},{24,28},{28,24},{1,5},{5... | collective-permute-start | bytes 1769480 | tf_op jit(solution)/shard_map/ppermute | solution.py:775
  253.7 46.7 %collective-permute-start.15 = (bf16[4,96,768]{2,1,0:T(8,128)(2,1)}, bf16[4,96,768]{2,1,0:T(8,128)(2,1)S(1)}, u32[]{:S(2)}, u32[]{:S(2)}) collective-permute-start(bf16[4,96,768]{2,1,0:T(8,128)(2,1)} %get-tuple-element.243), channel_id=1, source_target_pairs={{0,4},{4,0},{8,12},{12,8},{16,20},{20,16},{24,28},{28,24},{1,5},{5... | collective-permute-start | bytes 1769480 | tf_op jit(solution)/shard_map/ppermute | solution.py:775
  255.2 45.2 %collective-permute-start.16 = (bf16[4,96,768]{2,1,0:T(8,128)(2,1)}, bf16[4,96,768]{2,1,0:T(8,128)(2,1)S(1)}, u32[]{:S(2)}, u32[]{:S(2)}) collective-permute-start(bf16[4,96,768]{2,1,0:T(8,128)(2,1)} %get-tuple-element.244), channel_id=1, source_target_pairs={{0,2},{1,3},{2,0},{3,1},{4,6},{5,7},{6,4},{7,5},{8,10},{9,11},{10,... | collective-permute-start | bytes 1769480 | tf_op jit(solution)/shard_map/ppermute | solution.py:775
  303.7 44.6 %collective-permute-start.18 = (bf16[4,96,384]{2,1,0:T(8,128)(2,1)}, bf16[4,96,384]{2,1,0:T(8,128)(2,1)S(1)}, u32[]{:S(2)}, u32[]{:S(2)}) collective-permute-start(bf16[4,96,384]{2,1,0:T(8,128)(2,1)} %get-tuple-element.265), channel_id=1, source_target_pairs={{0,4},{4,0},{8,12},{12,8},{16,20},{20,16},{24,28},{28,24},{1,5},{5... | collective-permute-start | bytes 884744 | tf_op jit(solution)/shard_map/ppermute | solution.py:775
  304.2 44.1 %collective-permute-start.19 = (bf16[4,96,384]{2,1,0:T(8,128)(2,1)}, bf16[4,96,384]{2,1,0:T(8,128)(2,1)S(1)}, u32[]{:S(2)}, u32[]{:S(2)}) collective-permute-start(bf16[4,96,384]{2,1,0:T(8,128)(2,1)} %get-tuple-element.266), channel_id=1, source_target_pairs={{0,2},{1,3},{2,0},{3,1},{4,6},{5,7},{6,4},{7,5},{8,10},{9,11},{10,... | collective-permute-start | bytes 884744 | tf_op jit(solution)/shard_map/ppermute | solution.py:775
  305.9 41.3 %collective-permute-start.20 = (bf16[2,2,96,768]{3,2,1,0:T(8,128)(2,1)}, bf16[2,2,96,768]{3,2,1,0:T(8,128)(2,1)S(1)}, u32[]{:S(2)}, u32[]{:S(2)}) collective-permute-start(bf16[2,2,96,768]{3,2,1,0:T(8,128)(2,1)} %get-tuple-element.267), channel_id=1, source_target_pairs={{0,8},{4,12},{8,0},{12,4},{16,24},{20,28},{24,16},{28,20},{1,9},{5... | collective-permute-start | bytes 1769480 | tf_op jit(solution)/shard_map/ppermute | solution.py:775
  315.6 28.2 %collective-permute-start.21 = (bf16[2,4,96,768]{3,2,1,0:T(8,128)(2,1)}, bf16[2,4,96,768]{3,2,1,0:T(8,128)(2,1)S(1)}, u32[]{:S(2)}, u32[]{:S(2)}) collective-permute-start(bf16[2,4,96,768]{3,2,1,0:T(8,128)(2,1)} %get-tuple-element.268), channel_id=1, source_target_pairs={{0,2},{1,3},{2,0},{3,1},{4,6},{5,7},{6,4},{7,5},{8,10},{9,11},{10,... | collective-permute-start | bytes 3538952 | tf_op jit(solution)/shard_map/ppermute | solution.py:775
  317.1 27.9 %collective-permute-start.22 = (bf16[2,4,96,768]{3,2,1,0:T(8,128)(2,1)}, bf16[2,4,96,768]{3,2,1,0:T(8,128)(2,1)S(1)}, u32[]{:S(2)}, u32[]{:S(2)}) collective-permute-start(bf16[2,4,96,768]{3,2,1,0:T(8,128)(2,1)} %get-tuple-element.270), channel_id=1, source_target_pairs={{0,4},{4,0},{8,12},{12,8},{16,20},{20,16},{24,28},{28,24},{1,5},{5... | collective-permute-start | bytes 3538952 | tf_op jit(solution)/shard_map/ppermute | solution.py:775
  349.7 32.6 %collective-permute-start.24 = (bf16[4,96,768]{2,1,0:T(8,128)(2,1)}, bf16[4,96,768]{2,1,0:T(8,128)(2,1)S(1)}, u32[]{:S(2)}, u32[]{:S(2)}) collective-permute-start(bf16[4,96,768]{2,1,0:T(8,128)(2,1)} %get-tuple-element.290), channel_id=1, source_target_pairs={{0,4},{4,0},{8,12},{12,8},{16,20},{20,16},{24,28},{28,24},{1,5},{5... | collective-permute-start | bytes 1769480 | tf_op jit(solution)/shard_map/ppermute | solution.py:775
  350.4 31.9 %collective-permute-start.25 = (bf16[4,96,768]{2,1,0:T(8,128)(2,1)S(1)}, bf16[4,96,768]{2,1,0:T(8,128)(2,1)S(1)}, u32[]{:S(2)}, u32[]{:S(2)}) collective-permute-start(bf16[4,96,768]{2,1,0:T(8,128)(2,1)S(1)} %copy-done.48), channel_id=1, source_target_pairs={{0,2},{1,3},{2,0},{3,1},{4,6},{5,7},{6,4},{7,5},{8,10},{9,11},{10,... | collective-permute-start | bytes 1769480 | tf_op jit(solution)/shard_map/ppermute | solution.py:775
  350.8 34.6 %collective-permute-start.30 = (bf16[2,2,96,384]{3,2,1,0:T(8,128)(2,1)}, bf16[2,2,96,384]{3,2,1,0:T(8,128)(2,1)S(1)}, u32[]{:S(2)}, u32[]{:S(2)}) collective-permute-start(bf16[2,2,96,384]{3,2,1,0:T(8,128)(2,1)} %get-tuple-element.310), channel_id=1, source_target_pairs={{0,8},{4,12},{8,0},{12,4},{16,24},{20,28},{24,16},{28,20},{1,9},{5... | collective-permute-start | bytes 884744 | tf_op jit(solution)/shard_map/ppermute | solution.py:775
  383.7 18.3 %collective-permute-start.26 = (bf16[2,2,96,768]{3,2,1,0:T(8,128)(2,1)}, bf16[2,2,96,768]{3,2,1,0:T(8,128)(2,1)S(1)}, u32[]{:S(2)}, u32[]{:S(2)}) collective-permute-start(bf16[2,2,96,768]{3,2,1,0:T(8,128)(2,1)} %get-tuple-element.297), channel_id=1, source_target_pairs={{0,8},{4,12},{8,0},{12,4},{16,24},{20,28},{24,16},{28,20},{1,9},{5... | collective-permute-start | bytes 1769480 | tf_op jit(solution)/shard_map/ppermute | solution.py:775
  412.0 36.4 %collective-permute-start.37 = (bf16[2,1,96,768]{3,2,1,0:T(8,128)(2,1)S(1)}, bf16[2,1,96,768]{3,2,1,0:T(8,128)(2,1)S(1)}, u32[]{:S(2)}, u32[]{:S(2)}) collective-permute-start(bf16[2,1,96,768]{3,2,1,0:T(8,128)(2,1)S(1)} %copy-done.49), channel_id=1, source_target_pairs={{0,16},{4,20},{8,24},{12,28},{16,0},{20,4},{24,8},{28,12},{1,17},{... | collective-permute-start | bytes 884744 | tf_op jit(solution)/shard_map/ppermute | solution.py:775
  414.6 36.7 %collective-permute-start.31 = (bf16[2,1,96,768]{3,2,1,0:T(8,128)(2,1)}, bf16[2,1,96,768]{3,2,1,0:T(8,128)(2,1)S(1)}, u32[]{:S(2)}, u32[]{:S(2)}) collective-permute-start(bf16[2,1,96,768]{3,2,1,0:T(8,128)(2,1)} %get-tuple-element.324), channel_id=1, source_target_pairs={{0,16},{4,20},{8,24},{12,28},{16,0},{20,4},{24,8},{28,12},{1,17},{... | collective-permute-start | bytes 884744 | tf_op jit(solution)/shard_map/ppermute | solution.py:775
  (71 other events, 1069.2 us)

commit v6 on v5

--- a/solution.py
+++ b/solution.py
@@ -84,6 +84,8 @@
 
 
 def cost(flops, out_shape, operands):
+    if not flops:
+        return pl.CostEstimate(flops=0, bytes_accessed=0, transcendentals=0)
     made = out_shape if isinstance(out_shape, (list, tuple)) else [out_shape]
     moved = sum(math.prod(v.shape) * jnp.dtype(v.dtype).itemsize for v in [*made, *operands])
     return pl.CostEstimate(flops=flops, bytes_accessed=moved, transcendentals=0)
@@ -138,60 +140,63 @@
     )(base, lengths)
 
 
-def attention_forward_kernel(
-    x_ref, wa_ref, wb_ref, b_ref, bias_ref, *refs, aliased, tile
-):
-    mixed_ref, p_ref, s_ref = refs[2 * aliased :]
-    rows, part = x_ref.shape[0], wa_ref.shape[0] // 3
+def attention_forward_kernel(x_ref, b_ref, bias_ref, *refs, blocks, aliased, tile):
+    sources = refs[:blocks]
+    mixed_ref, p_ref, s_ref, w_ref, sems = refs[blocks + 2 * aliased :]
+    rows, part = x_ref.shape[0], w_ref.shape[1] // 3
+    slot, block = pl.program_id(0), pl.program_id(1)
+    copies = [pltpu.make_async_copy(w, w_ref.at[b], sems.at[b]) for b, w in enumerate(sources)]
+
+    @pl.when((slot == 0) & (block == 0))
+    def _():
+        for copy in copies:
+            copy.start()
+
+    for b, copy in enumerate(copies):
+
+        @pl.when((slot == 0) & (block == b))
+        def _():
+            copy.wait()
+
     x = x_ref[...]
-    masks = head_masks(part)
-
-    def work(w_ref):
-        q = ((dot_nt(x, w_ref[:part]) + b_ref[0]).astype(LOW) * HD**-0.5).astype(LOW)
-        k = dot_nt(x, w_ref[part : 2 * part]).astype(LOW)
-        v = (dot_nt(x, w_ref[2 * part :]) + b_ref[1]).astype(LOW)
-        mixed_ref[0] = q
-        mixed_ref[1] = k
-        mixed_ref[2] = v
-        total = None
-        for head, mask in enumerate(masks):
-            s_ref[head] = dot_nt(pick(mask, q), k)
-            for start in range(0, rows, tile):
-                at = slice(start, start + tile)
-                s = s_ref[head, at] + bias_ref[at]
-                e = jnp.exp(s - jnp.max(s, axis=1, keepdims=True))
-                p_ref[head, at] = (e * (1.0 / jnp.sum(e, axis=1, keepdims=True))).astype(LOW)
-            made = dot_nn(p_ref[head], pick(mask, v))
-            total = made if total is None else total + made
-        mixed_ref[3] = total.astype(LOW)
-
-    for block, w_ref in enumerate((wa_ref, wb_ref)):
-
-        @pl.when(pl.program_id(1) == block)
-        def _():
-            work(w_ref)
-
-
-def attention_forward(x, wa, wb, qv_bias, bias, first, before, tile=64):
+    q = ((dot_nt(x, w_ref[block, :part]) + b_ref[0]).astype(LOW) * HD**-0.5).astype(LOW)
+    k = dot_nt(x, w_ref[block, part : 2 * part]).astype(LOW)
+    v = (dot_nt(x, w_ref[block, 2 * part :]) + b_ref[1]).astype(LOW)
+    mixed_ref[0] = q
+    mixed_ref[1] = k
+    mixed_ref[2] = v
+    total = None
+    for head, mask in enumerate(head_masks(part)):
+        s_ref[head] = dot_nt(pick(mask, q), k)
+        for start in range(0, rows, tile):
+            at = slice(start, start + tile)
+            s = s_ref[head, at] + bias_ref[at]
+            e = jnp.exp(s - jnp.max(s, axis=1, keepdims=True))
+            p_ref[head, at] = (e * (1.0 / jnp.sum(e, axis=1, keepdims=True))).astype(LOW)
+        made = dot_nn(p_ref[head], pick(mask, v))
+        total = made if total is None else total + made
+    mixed_ref[3] = total.astype(LOW)
+
+
+def attention_forward(x, sources, qv_bias, bias, first, before, tile=64):
     rows, width = x.shape
     slots, slot_rows, _ = bias.shape
-    part = wa.shape[0] // 3
+    blocks = len(sources)
+    part = sources[0].shape[0] // 3
     heads = part // HD
     aliased = int(before is not None)
     mixed = shape_of((4, 4, rows, part), LOW)
     probs = shape_of((4, slots, heads, slot_rows, slot_rows), LOW)
     return call(
-        functools.partial(attention_forward_kernel, aliased=aliased, tile=tile),
+        functools.partial(attention_forward_kernel, blocks=blocks, aliased=aliased, tile=tile),
         "attention_forward",
-        (slots, 2),
+        (slots, blocks),
         [
             pl.BlockSpec((slot_rows, width), lambda s, b: (s, 0)),
-            whole(wa),
-            whole(wb),
             pl.BlockSpec((None, 2, 1, part), lambda s, b: (b, 0, 0, 0)),
             pl.BlockSpec((None, slot_rows, slot_rows), lambda s, b: (s, 0, 0)),
         ]
-        + [in_place(), in_place()] * aliased,
+        + [in_place()] * (blocks + 2 * aliased),
         [
             pl.BlockSpec((None, 4, slot_rows, part), lambda s, b: (first + b, 0, s, 0)),
             pl.BlockSpec(
@@ -199,11 +204,15 @@
             ),
         ],
         [mixed, probs],
-        [pltpu.VMEM((heads, slot_rows, slot_rows), WIDE)],
+        [
+            pltpu.VMEM((heads, slot_rows, slot_rows), WIDE),
+            pltpu.VMEM((blocks, 3 * part, width), LOW),
+            pltpu.SemaphoreType.DMA((blocks,)),
+        ],
         [],
-        [x, wa, wb, qv_bias, bias, *(before or ())],
-        alias={5: 0, 6: 1} if aliased else None,
-        flops=12 * rows * width * part + 16 * heads * rows * slot_rows * 256,
+        [x, qv_bias, bias, *sources, *(before or ())],
+        alias={3 + blocks: 0, 4 + blocks: 1} if aliased else None,
+        flops=blocks * (6 * rows * width * part + 8 * heads * rows * slot_rows * 256),
     )
 
 
@@ -775,10 +784,11 @@
     return lax.ppermute(value, axis, [(i, i ^ bit) for i in range(size)])
 
 
-def add_split_kernel(*refs, merge_in, merge_out):
+def add_split_kernel(*refs, merge_in, merge_out, extra):
     inputs = 2 if merge_in else 4
     outputs = 2 if merge_out else 4
-    ins, outs = refs[:inputs], refs[inputs : inputs + outputs]
+    ins, refs = refs[:inputs], refs[extra:]
+    outs = refs[inputs : inputs + outputs]
     kept_ref, send_ref, keep_ref, in_sems, out_sems = refs[inputs + outputs :]
     half = send_ref.shape[1]
     loads, got, stores = [], [], []
@@ -808,13 +818,16 @@
             copy.wait()
 
 
-def add_split(ins, merge_in, merge_out):
+def add_split(ins, merge_in, merge_out, arrived):
     size, rows, columns = ins[0].shape[-3:]
     half = (size // 2, rows, columns)
     out_shape = [stored((2, *half), LOW)] * 2 if merge_out else [stored(half, LOW)] * 4
     return pl.pallas_call(
-        functools.partial(add_split_kernel, merge_in=merge_in, merge_out=merge_out),
-        in_specs=[in_hbm(), pl.BlockSpec(memory_space=pltpu.VMEM)] * (len(ins) // 2),
+        functools.partial(
+            add_split_kernel, merge_in=merge_in, merge_out=merge_out, extra=len(arrived)
+        ),
+        in_specs=[in_hbm(), pl.BlockSpec(memory_space=pltpu.VMEM)] * (len(ins) // 2)
+        + [in_place()] * len(arrived),
         out_specs=[in_hbm()] * len(out_shape),
         out_shape=out_shape,
         scratch_shapes=[
@@ -825,9 +838,9 @@
             pltpu.SemaphoreType.DMA((2, 2)),
         ],
         compiler_params=pltpu.CompilerParams(vmem_limit_bytes=16 << 20),
-        cost_estimate=cost(0, out_shape, ins),
+        cost_estimate=pl.CostEstimate(flops=0, bytes_accessed=0, transcendentals=0),
         name="add_split",
-    )(*ins)
+    )(*ins, *arrived)
 
 
 class Summing:
@@ -835,20 +848,21 @@
         head, dp = bits_of("head"), bits_of("dp")
         self.stages = [(("dp", dp[0]), ("head", head[1]))] + [(("dp", bit),) for bit in dp[1:]]
         self.at = 0
+        self.settled = False
         self.kept = [a_keep, b_keep]
         self.got = [swap(a_send, "head", head[1]), swap(b_send, "dp", dp[0])]
 
     def busy(self):
         return self.at < len(self.stages)
 
-    def step(self, after):
+    def step(self, after, arrived=()):
         stage = self.stages[self.at]
         merge_in, merge_out = len(self.kept) == 1, len(stage) == 1
         ins = [v for pair in zip(self.kept, self.got) for v in pair]
         lead = 1 if merge_in else 0
         ins = [v.reshape(*v.shape[:lead], -1, *v.shape[-2:]) for v in ins]
         ins, _ = lax.optimization_barrier((ins, after))
-        outs = add_split(ins, merge_in, merge_out)
+        outs = add_split(ins, merge_in, merge_out, arrived)
         if merge_out:
             self.got, self.kept = [swap(outs[0], *stage[0])], [outs[1]]
         else:
@@ -928,13 +942,15 @@
     return values
 
 
-def near_blocks(block):
+def near_blocks(block, after):
     low, high = bits_of("head")
-    return block, swap(block, "head", low), swap(block, "head", high)
-
-
-def gathered_pairs(block):
-    own, near, far = near_blocks(block)
+    near = swap(block, "head", low)
+    (later,) = ordered((after, near), block)
+    return block, near, swap(later, "head", high)
+
+
+def gathered_pairs(block, after):
+    own, near, far = near_blocks(block, after)
     return jnp.stack([own, near]), jnp.stack([far, swap(far, "head", bits_of("head")[0])])
 
 
@@ -964,10 +980,10 @@
     layers = qkv_weight.shape[0]
     part = width // head_count
     turned = jnp.swapaxes(qkv_weight, 2, 3).reshape(layers, 3 * part, width)
-    near_bias, far_bias = gathered_pairs(qv_bias[:, :, None])
-    weights = [near_blocks(turned[0])]
     base = (head_index * slots).astype(jnp.int32).reshape(1)
     bias = mask_bias(seq_lengths, base, slots, slot_rows)
+    weights = [near_blocks(turned[0], base)]
+    near_bias, far_bias = gathered_pairs(qv_bias[:, :, None], base)
     up_rows = up_bias.reshape(layers, -1, 1, width)
     rounded, residual = tokens, tokens
     kept = []
@@ -986,15 +1002,23 @@
             ]
         )
         own_w, near_w, far_w = weights[layer]
-        near = attention_forward(rounded, own_w, near_w, near_bias[:, layer], bias, 0, None)
-        (far_w, far_b) = ordered(near[0], far_w, far_bias[:, layer])
-        both_w = swap(far_w, "head", bits_of("head")[0])
-        if layer + 1 < layers:
-            (later,) = ordered(near[0], turned[layer + 1])
-            weights.append(near_blocks(later))
-        mixed, probs = attention_forward(rounded, far_w, both_w, far_b, bias, 2, near)
-        w = (own_w, near_w, far_w, both_w)
-        weights[layer] = w
+        if layer == 0:
+            near = attention_forward(rounded, (own_w, near_w), near_bias[:, layer], bias, 0, None)
+            (far_w, far_b) = ordered(near[0], far_w, far_bias[:, layer])
+            both_w = swap(far_w, "head", bits_of("head")[0])
+            for other in range(1, layers):
+                (later,) = ordered(near[0], turned[other])
+                weights.append(near_blocks(later, near[0]))
+            mixed, probs = attention_forward(rounded, (far_w, both_w), far_b, bias, 2, near)
+            (far_ws,) = ordered(mixed, [w[2] for w in weights[1:]])
+            both_ws = [swap(w, "head", bits_of("head")[0]) for w in far_ws]
+        else:
+            both_w = both_ws[layer - 1]
+            all_bias = jnp.concatenate([near_bias[:, layer], far_bias[:, layer]])
+            mixed, probs = attention_forward(
+                rounded, (own_w, near_w, far_w, both_w), all_bias, bias, 0, None
+            )
+        weights[layer] = w = (own_w, near_w, far_w, both_w)
         u1, hr, gr, slope, u2, low = ffn_forward(
             own,
             mixed,
@@ -1016,10 +1040,16 @@
     ffn_groups, wide_groups = [None] * layers, [None] * layers
     running = []
 
-    def advance(after, groups=None):
-        for group in running if groups is None else groups:
+    def advance(after):
+        arrived = []
+        for group in running:
+            if not group.busy() and not group.settled:
+                arrived += group.got
+                group.settled = True
+        for group in running:
             if group.busy():
-                after = group.step(after)
+                after = group.step(after, arrived)
+                arrived = []
         return after
 
     for layer in reversed(range(layers)):
@@ -1099,16 +1129,20 @@
         )
         small_sums[layer] = jnp.concatenate([sums[:6], qv_sums, zsums[:, 0]])
     small_sum = jnp.stack(small_sums)
-    spread = [("head", bits_of("head")[0])] + [("dp", bit) for bit in bits_of("dp")[1:]]
-    spread += [("dp", bits_of("dp")[0]), ("head", bits_of("head")[1])]
-    passing = swap(small_sum, *spread.pop(0))
-    while any(group.busy() for group in running) or spread:
-        token = advance(token)
-        if spread:
-            (small_sum, passing) = ordered(token, small_sum, passing)
-            small_sum = small_sum + passing
+    near, far = bits_of("head")
+    waiting = [[("head", near)], [("dp", 1)], [("head", far)], [("dp", 2 * k) for k in range(1, dp_count // 2)]]
+    passing = [swap(small_sum, *one) for one in waiting.pop(0)]
+    while any(not group.settled for group in running) or waiting:
+        if any(group.busy() for group in running):
+            token = advance(token)
+        elif not waiting:
+            break
+        if waiting:
+            small_sum, passing = ordered(token, small_sum, passing)
+            small_sum = sum(passing, small_sum)
             token = small_sum
-            passing = swap(small_sum, *spread.pop(0))
+            passing = [swap(small_sum, *one) for one in waiting.pop(0)]
+    small_sum, passing = sum(passing[:-1], small_sum), passing[-1]
     groups = [group for pair in zip(ffn_groups, wide_groups) for group in pair]
     qkv, qv, out_w, out_b, gain1, shift1, up_w, up_b, down_w, down_b, gain2, shift2 = last_sums(
         groups, small_sum, passing

time: 464 us -> 444 us (0.957)
  waiting for transfers between devices: 71.6 us -> 49.2 us
  starting transfers between devices: 37.4 us -> 44.1 us
    ppermute x42 -> x43, waiting for transfers between devices: 71.6 us -> 49.2 us  [swap(): return lax.ppermute(value, axis, [(i, i ^ bit) for i in range(size)])]
    ppermute x42 -> x43, starting transfers between devices: 37.4 us -> 44.1 us  [swap(): return lax.ppermute(value, axis, [(i, i ^ bit) for i in range(size)])]
    pallas_call x15 -> x14, Pallas kernels: 309 us -> 307 us  [call(): pl.pallas_call(kernel, grid_spec=pltpu.PrefetchScalarGridSpec(num_scalar_...]
  transfers between devices with their start and end apart: 42 -> 43, of which waited for: 17 -> 16; matrix products, arithmetic and copies ran while one was open for 1% -> 2% of each run, Pallas kernels for 53% -> 52%
where the time goes in v6:
time: 444 us; the launch traced here: 437 us
  Pallas kernels  327 us (74%)
  waiting for transfers between devices  49.2 us (11%)
  starting transfers between devices  44.1 us (10%)
  local copies, waits for them, and re-layouts  11.6 us (3%)
    pallas_call x14, Pallas kernels, call(): pl.pallas_call(kernel, grid_spec=pltpu.PrefetchScalarGridSpec(num_scalar_...  307 us
    ppermute x43, waiting for transfers between devices, swap(): return lax.ppermute(value, axis, [(i, i ^ bit) for i in range(size)])  49.2 us
    ppermute x43, starting transfers between devices, swap(): return lax.ppermute(value, axis, [(i, i ^ bit) for i in range(size)])  44.1 us
    pallas_call x12, Pallas kernels, add_split(): pl.pallas_call(functools.partial(add_split_kernel, merge_in=merge_in, mer...  16.3 us
  transfers between devices with their start and end apart: 43, of which 16 were waited for; matrix products, arithmetic and copies ran while one was open for 2% of the time, Pallas kernels for 52%

profile of v6, /device:TPU:0, one launch (start us, length us, event | category | flops | bytes accessed | tf_op | source)
XLA Modules:
  0.0 437.5 jit_solution(871573021294877374)
XLA Ops:
  4.6 4.4 %mask_bias.1.bias_ref = f32[2,512,512]{2,1,0:T(8,128)} custom-call(s32[1]{0:T(128)} %bitcast.4.base_ref, s32[8,32]{1,0:T(8,128)} %lengths_ref.1), custom_call_target="tpu_custom_call" | custom-call | tf_op jit(solution)/shard_map/mask_bias/pallas_call | solution.py:134
  16.6 14.7 %attention_forward.3 = (bf16[4,4,1024,192]{3,2,1,0:T(8,128)(2,1)}, bf16[4,2,3,512,512]{4,3,2,1,0:T(8,128)(2,1)}) custom-call(bf16[1024,768]{1,0:T(8,128)(2,1)} %x_ref.7, f32[2,2,1,192]{3,2,1,0:T(1,128)} %get-tuple-element.375.b_ref, f32[2,512,512]{2,1,0:T(8,128)} %mask_bias.1.bias_ref, bf16[576,768]{1,0:T(8,128)(2,1)} %bitcast.85, bf16[576,768]{1,0:T(8,128)(2,1)} %copy-done.45), custom_call_target="tpu_custom_call" | custom-call | flops 8254390272 | bytes 24316928 | tf_op jit(solution)/shard_map/attention_forward/pallas_call | solution.py:99
  32.2 4.7 %collective-permute-done.1.refs_0_.wb_ref = bf16[576,768]{1,0:T(8,128)(2,1)S(1)} collective-permute-done((bf16[576,768]{1,0:T(8,128)(2,1)S(1)}, bf16[576,768]{1,0:T(8,128)(2,1)S(1)}, u32[]{:S(2)}, u32[]{:S(2)}) %collective-permute-start.1) | collective-permute-done | bytes 884768 | tf_op jit(solution)/shard_map/ppermute | solution.py:784
  41.6 14.7 %attention_forward.4 = (bf16[4,4,1024,192]{3,2,1,0:T(8,128)(2,1)}, bf16[4,2,3,512,512]{4,3,2,1,0:T(8,128)(2,1)}) custom-call(bf16[1024,768]{1,0:T(8,128)(2,1)} %x_ref.7, f32[2,2,1,192]{3,2,1,0:T(1,128)} %get-tuple-element.187.b_ref, f32[2,512,512]{2,1,0:T(8,128)} %mask_bias.1.bias_ref, ...), custom_call_target="tpu_custom_call", output_to_operand_aliasing={{0}: (5, {}), {1}: (6, {})} | custom-call | flops 8254390272 | bytes 43191296 | tf_op jit(solution)/shard_map/attention_forward/pallas_call | solution.py:99
  56.3 4.0 collective-permute-done.7.refs_2_.wb_ref
  60.3 25.1 %ffn_forward.2 = (f32[1024,768]{1,0:T(8,128)}, bf16[1024,768]{1,0:T(8,128)(2,1)}, bf16[4,1024,768]{2,1,0:T(8,128)(2,1)}, bf16[4,1024,768]{2,1,0:T(8,128)(2,1)}, ...) custom-call(s32[2]{0:T(128)} %pad_add_fusion.own_ref, ...), custom_call_target="tpu_custom_call" | custom-call | flops 32614907904 | bytes 51154944 | tf_op jit(solution)/shard_map/ffn_forward/pallas_call | solution.py:99
  86.3 25.3 %attention_forward.5 = (bf16[4,4,1024,192]{3,2,1,0:T(8,128)(2,1)}, bf16[4,2,3,512,512]{4,3,2,1,0:T(8,128)(2,1)}) custom-call(bf16[1024,768]{1,0:T(8,128)(2,1)} %get-tuple-element.191.x_ref, f32[4,2,1,192]{3,2,1,0:T(1,128)} %pad_maximum_fusion.7.b_ref, f32[2,512,512]{2,1,0:T(8,128)} %mask_bias.1.bias_ref, bf16[576,768]{1,0:T(8,128)(2,1)} %bitcast.89, ...), custom_call_target="tpu_custom_call" | custom-call | flops 16508780544 | bytes 26089472 | tf_op jit(solution)/shard_map/attention_forward/pallas_call | solution.py:99
  111.7 25.6 %ffn_forward.3 = (f32[1024,768]{1,0:T(8,128)}, bf16[1024,768]{1,0:T(8,128)(2,1)}, bf16[4,1024,768]{2,1,0:T(8,128)(2,1)}, bf16[4,1024,768]{2,1,0:T(8,128)(2,1)}, ...) custom-call(s32[2]{0:T(128)} %pad_add_fusion.own_ref, ...), custom_call_target="tpu_custom_call" | custom-call | flops 32614907904 | bytes 52727808 | tf_op jit(solution)/shard_map/ffn_forward/pallas_call | solution.py:99
  137.3 44.6 %ffn_backward.2 = (bf16[4,1024,192]{2,1,0:T(8,128)(2,1)}, bf16[4,1024,192]{2,1,0:T(8,128)(2,1)}, f32[1024,768]{1,0:T(8,128)}, f32[8,768]{1,0:T(8,128)}, f32[4,1,...) custom-call(s32[2]{0:T(128)} %pad_add_fusion.own_ref, ...), custom_call_target="tpu_custom_call" | custom-call | flops 41070624768 | bytes 59025408 | tf_op jit(solution)/shard_map/ffn_backward/pallas_call | solution.py:99
  182.5 25.0 %attention_backward.4 = (f32[1024,768]{1,0:T(8,128)}, f32[2,8,192]{2,1,0:T(8,128)}, bf16[2,2,4,96,768]{4,3,2,1,0:T(8,128)(2,1)}) custom-call(s32[2]{0:T(128)} %pad_add_fusion.own_ref, bf16[4,4,1024,192]{3,2,1,0:T(8,128)(2,1)} %get-tuple-element.195.mixed_hbm.mixed_ref.o_ref, bf16[4,1024,192]{2,1,0:T(8,128)(2,1)} %get-tuple-element.215.do_ref, ...), custom_call_target="tpu_custom_call" | custom-call | flops 14495514624 | bytes 40316928 | tf_op jit(solution)/shard_map/attention_backward/pallas_call | solution.py:99
  207.5 6.1 %core_add.2 = (bf16[2,4,96,768]{3,2,1,0:T(8,128)(2,1)}, bf16[2,4,96,768]{3,2,1,0:T(8,128)(2,1)}, bf16[2,4,96,768]{3,2,1,0:T(8,128)(2,1)}, bf16[2,4,96,768]{3,2,1,0:T(8,128)(2,1)}) custom-call(bf16[2,2,2,4,96,768]{5,4,3,2,1,0:T(8,128)(2,1)S(1)} %bitcast.65, bf16[2,2,2,4,96,768]{5,4,3,2,1,0:T(8,128)(2,1)} %collective-permute-done.9.got_ref), custom_call_target="tpu_custom_call" | custom-call | tf_op jit(solution)/shard_map/core_add/pallas_call | solution.py:99
  216.9 25.9 %attention_backward.5 = (f32[1024,768]{1,0:T(8,128)}, f32[2,8,192]{2,1,0:T(8,128)}, bf16[2,4,96,384]{3,2,1,0:T(8,128)(2,1)}, bf16[2,4,96,384]{3,2,1,0:T(8,128)(2...) custom-call(s32[2]{0:T(128)} %pad_add_fusion.own_ref, ...), custom_call_target="tpu_custom_call" | custom-call | flops 14495514624 | bytes 42676224 | tf_op jit(solution)/shard_map/attention_backward/pallas_call | solution.py:99
  249.1 44.7 %ffn_backward.3 = (bf16[4,1024,192]{2,1,0:T(8,128)(2,1)}, bf16[4,1024,192]{2,1,0:T(8,128)(2,1)}, f32[1024,768]{1,0:T(8,128)}, f32[8,768]{1,0:T(8,128)}, f32[4,1,...) custom-call(s32[2]{0:T(128)} %pad_add_fusion.own_ref, ...), custom_call_target="tpu_custom_call" | custom-call | flops 41070624768 | bytes 60598272 | tf_op jit(solution)/shard_map/ffn_backward/pallas_call | solution.py:99
  299.8 5.3 %collective-permute-done.17.got_ref = bf16[2,2,2,4,96,768]{5,4,3,2,1,0:T(8,128)(2,1)S(1)} collective-permute-done((bf16[2,2,2,4,96,768]{5,4,3,2,1,0:T(8,128)(2,1)}, bf16[2,2,2,4,96,768]{5,4,3,2,1,0:T(8,128)(2,1)S(1)}, u32[]{:S(2)}, u32[]{:S(2)}) %collective-permute-start.17) | collective-permute-done | bytes 4718624 | tf_op jit(solution)/shard_map/ppermute | solution.py:784
  305.1 3.7 core_add.3
  309.7 24.4 %attention_backward.6 = (f32[1024,768]{1,0:T(8,128)}, f32[2,8,192]{2,1,0:T(8,128)}, bf16[2,2,4,96,768]{4,3,2,1,0:T(8,128)(2,1)}) custom-call(s32[2]{0:T(128)} %pad_add_fusion.own_ref, bf16[4,4,1024,192]{3,2,1,0:T(8,128)(2,1)} %get-tuple-element.190.mixed_hbm.mixed_ref.o_ref, bf16[4,1024,192]{2,1,0:T(8,128)(2,1)} %get-tuple-element.282.do_ref, ...), custom_call_target="tpu_custom_call" | custom-call | flops 14495514624 | bytes 40316928 | tf_op jit(solution)/shard_map/attention_backward/pallas_call | solution.py:99
  334.0 2.9 collective-permute-done.21
  349.7 25.4 %attention_backward.7 = (bf16[1024,768]{1,0:T(8,128)(2,1)}, f32[2,8,192]{2,1,0:T(8,128)}, bf16[2,4,96,384]{3,2,1,0:T(8,128)(2,1)}, bf16[2,4,96,384]{3,2,1,0:T(8,...) custom-call(s32[2]{0:T(128)} %pad_add_fusion.own_ref, ...), custom_call_target="tpu_custom_call" | custom-call | flops 14495514624 | bytes 41103360 | tf_op jit(solution)/shard_map/attention_backward/pallas_call | solution.py:99
  382.4 7.6 %collective-permute-done.29 = bf16[2,4,96,384]{3,2,1,0:T(8,128)(2,1)S(1)} collective-permute-done((bf16[2,4,96,384]{3,2,1,0:T(8,128)(2,1)}, bf16[2,4,96,384]{3,2,1,0:T(8,128)(2,1)S(1)}, u32[]{:S(2)}, u32[]{:S(2)}) %collective-permute-start.29) | collective-permute-done | bytes 589856 | tf_op jit(solution)/shard_map/ppermute | solution.py:784
  404.4 2.8 collective-permute-start.33
  408.6 3.2 collective-permute-done.37
  412.5 3.4 collective-permute-done.36.refs_1_
  421.0 2.8 collective-permute-start.40
  425.2 7.0 %collective-permute-done.41 = f32[2,12,768]{2,1,0:T(8,128)S(1)} collective-permute-done((f32[2,12,768]{2,1,0:T(8,128)S(1)}, f32[2,12,768]{2,1,0:T(8,128)S(1)}, u32[]{:S(2)}, u32[]{:S(2)}) %collective-permute-start.41) | collective-permute-done | bytes 73760 | tf_op jit(solution)/shard_map/ppermute | solution.py:784
  (228 shorter events, 82.4 us)
Async XLA Ops:
  14.5 17.1 %collective-permute-start.4 = (f32[2,2,1,192]{3,2,1,0:T(1,128)S(1)}, f32[2,2,1,192]{3,2,1,0:T(1,128)S(1)}, u32[]{:S(2)}, u32[]{:S(2)}) collective-permute-start(f32[2,2,1,192]{3,2,1,0:T(1,128)S(1)} %collective-permute-done.3), channel_id=1, source_target_pairs={{0,1},{1,0},{2,3},{3,2},{4,5},{5,4},{6,7},{7,6},{8,9},{9,8},{10,11... | collective-permute-start | bytes 9224 | tf_op jit(solution)/shard_map/ppermute | solution.py:784
  14.6 22.3 %collective-permute-start.1 = (bf16[576,768]{1,0:T(8,128)(2,1)S(1)}, bf16[576,768]{1,0:T(8,128)(2,1)S(1)}, u32[]{:S(2)}, u32[]{:S(2)}) collective-permute-start(bf16[576,768]{1,0:T(8,128)(2,1)S(1)} %bitcast.84), channel_id=1, source_target_pairs={{0,2},{1,3},{2,0},{3,1},{4,6},{5,7},{6,4},{7,5},{8,10},{9,11},{10,... | collective-permute-start | bytes 2654216 | tf_op jit(solution)/shard_map/ppermute | solution.py:784
  38.2 22.0 %collective-permute-start.7 = (bf16[576,768]{1,0:T(8,128)(2,1)S(1)}, bf16[576,768]{1,0:T(8,128)(2,1)S(1)}, u32[]{:S(2)}, u32[]{:S(2)}) collective-permute-start(bf16[576,768]{1,0:T(8,128)(2,1)S(1)} %bitcast.88), channel_id=1, source_target_pairs={{0,2},{1,3},{2,0},{3,1},{4,6},{5,7},{6,4},{7,5},{8,10},{9,11},{10,... | collective-permute-start | bytes 2654216 | tf_op jit(solution)/shard_map/ppermute | solution.py:784
  60.3 25.1 %collective-permute-start.8 = (bf16[576,768]{1,0:T(8,128)(2,1)S(1)}, bf16[576,768]{1,0:T(8,128)(2,1)S(1)}, u32[]{:S(2)}, u32[]{:S(2)}) collective-permute-start(bf16[576,768]{1,0:T(8,128)(2,1)S(1)} %collective-permute-done.7.refs_2_.wb_ref), channel_id=1, source_target_pairs={{0,1},{1,0},{2,3},{3,2},{4,5},{5,4},{6,7},{7,6},{8,9},{9,8},{10,11... | collective-permute-start | bytes 2654216 | tf_op jit(solution)/shard_map/ppermute | solution.py:784
  181.9 25.6 %collective-permute-start.9 = (bf16[2,2,2,4,96,768]{5,4,3,2,1,0:T(8,128)(2,1)}, bf16[2,2,2,4,96,768]{5,4,3,2,1,0:T(8,128)(2,1)}, u32[]{:S(2)}, u32[]{:S(2)}) collective-permute-start(bf16[2,2,2,4,96,768]{5,4,3,2,1,0:T(8,128)(2,1)} %get-tuple-element.211), channel_id=1, source_target_pairs={{0,1},{1,0},{2,3},{3,2},{4,5},{5,4},{6,7},{7,6},{8,9},{9,8},{10,11... | collective-permute-start | bytes 14155784 | tf_op jit(solution)/shard_map/ppermute | solution.py:784
  213.6 30.1 %collective-permute-start.11 = (bf16[2,4,96,768]{3,2,1,0:T(8,128)(2,1)}, bf16[2,4,96,768]{3,2,1,0:T(8,128)(2,1)S(1)}, u32[]{:S(2)}, u32[]{:S(2)}) collective-permute-start(bf16[2,4,96,768]{3,2,1,0:T(8,128)(2,1)} %get-tuple-element.219), channel_id=1, source_target_pairs={{0,2},{1,3},{2,0},{3,1},{4,6},{5,7},{6,4},{7,5},{8,10},{9,11},{10,... | collective-permute-start | bytes 3538952 | tf_op jit(solution)/shard_map/ppermute | solution.py:784
  215.4 28.4 %collective-permute-start.12 = (bf16[2,4,96,768]{3,2,1,0:T(8,128)(2,1)}, bf16[2,4,96,768]{3,2,1,0:T(8,128)(2,1)S(1)}, u32[]{:S(2)}, u32[]{:S(2)}) collective-permute-start(bf16[2,4,96,768]{3,2,1,0:T(8,128)(2,1)} %get-tuple-element.221), channel_id=1, source_target_pairs={{0,4},{4,0},{8,12},{12,8},{16,20},{20,16},{24,28},{28,24},{1,5},{5... | collective-permute-start | bytes 3538952 | tf_op jit(solution)/shard_map/ppermute | solution.py:784
  242.7 52.5 %collective-permute-start.13 = (bf16[2,4,96,384]{3,2,1,0:T(8,128)(2,1)}, bf16[2,4,96,384]{3,2,1,0:T(8,128)(2,1)S(1)}, u32[]{:S(2)}, u32[]{:S(2)}) collective-permute-start(bf16[2,4,96,384]{3,2,1,0:T(8,128)(2,1)} %get-tuple-element.237), channel_id=1, source_target_pairs={{0,2},{1,3},{2,0},{3,1},{4,6},{5,7},{6,4},{7,5},{8,10},{9,11},{10,... | collective-permute-start | bytes 1769480 | tf_op jit(solution)/shard_map/ppermute | solution.py:784
  243.4 51.9 %collective-permute-start.14 = (bf16[2,4,96,384]{3,2,1,0:T(8,128)(2,1)}, bf16[2,4,96,384]{3,2,1,0:T(8,128)(2,1)S(1)}, u32[]{:S(2)}, u32[]{:S(2)}) collective-permute-start(bf16[2,4,96,384]{3,2,1,0:T(8,128)(2,1)} %get-tuple-element.239), channel_id=1, source_target_pairs={{0,4},{4,0},{8,12},{12,8},{16,20},{20,16},{24,28},{28,24},{1,5},{5... | collective-permute-start | bytes 1769480 | tf_op jit(solution)/shard_map/ppermute | solution.py:784
  245.9 47.9 %collective-permute-start.15 = (bf16[4,96,768]{2,1,0:T(8,128)(2,1)}, bf16[4,96,768]{2,1,0:T(8,128)(2,1)S(1)}, u32[]{:S(2)}, u32[]{:S(2)}) collective-permute-start(bf16[4,96,768]{2,1,0:T(8,128)(2,1)} %get-tuple-element.241), channel_id=1, source_target_pairs={{0,4},{4,0},{8,12},{12,8},{16,20},{20,16},{24,28},{28,24},{1,5},{5... | collective-permute-start | bytes 1769480 | tf_op jit(solution)/shard_map/ppermute | solution.py:784
  247.7 46.2 %collective-permute-start.16 = (bf16[4,96,768]{2,1,0:T(8,128)(2,1)}, bf16[4,96,768]{2,1,0:T(8,128)(2,1)S(1)}, u32[]{:S(2)}, u32[]{:S(2)}) collective-permute-start(bf16[4,96,768]{2,1,0:T(8,128)(2,1)} %get-tuple-element.242), channel_id=1, source_target_pairs={{0,2},{1,3},{2,0},{3,1},{4,6},{5,7},{6,4},{7,5},{8,10},{9,11},{10,... | collective-permute-start | bytes 1769480 | tf_op jit(solution)/shard_map/ppermute | solution.py:784
  297.0 43.6 %collective-permute-start.18 = (bf16[4,96,384]{2,1,0:T(8,128)(2,1)}, bf16[4,96,384]{2,1,0:T(8,128)(2,1)S(1)}, u32[]{:S(2)}, u32[]{:S(2)}) collective-permute-start(bf16[4,96,384]{2,1,0:T(8,128)(2,1)} %get-tuple-element.263), channel_id=1, source_target_pairs={{0,4},{4,0},{8,12},{12,8},{16,20},{20,16},{24,28},{28,24},{1,5},{5... | collective-permute-start | bytes 884744 | tf_op jit(solution)/shard_map/ppermute | solution.py:784
  297.6 42.9 %collective-permute-start.19 = (bf16[4,96,384]{2,1,0:T(8,128)(2,1)}, bf16[4,96,384]{2,1,0:T(8,128)(2,1)S(1)}, u32[]{:S(2)}, u32[]{:S(2)}) collective-permute-start(bf16[4,96,384]{2,1,0:T(8,128)(2,1)} %get-tuple-element.264), channel_id=1, source_target_pairs={{0,2},{1,3},{2,0},{3,1},{4,6},{5,7},{6,4},{7,5},{8,10},{9,11},{10,... | collective-permute-start | bytes 884744 | tf_op jit(solution)/shard_map/ppermute | solution.py:784
  297.9 41.5 %collective-permute-start.20 = (bf16[2,2,96,768]{3,2,1,0:T(8,128)(2,1)}, bf16[2,2,96,768]{3,2,1,0:T(8,128)(2,1)S(1)}, u32[]{:S(2)}, u32[]{:S(2)}) collective-permute-start(bf16[2,2,96,768]{3,2,1,0:T(8,128)(2,1)} %get-tuple-element.265), channel_id=1, source_target_pairs={{0,8},{4,12},{8,0},{12,4},{16,24},{20,28},{24,16},{28,20},{1,9},{5... | collective-permute-start | bytes 1769480 | tf_op jit(solution)/shard_map/ppermute | solution.py:784
  308.8 28.2 %collective-permute-start.21 = (bf16[2,4,96,768]{3,2,1,0:T(8,128)(2,1)}, bf16[2,4,96,768]{3,2,1,0:T(8,128)(2,1)S(1)}, u32[]{:S(2)}, u32[]{:S(2)}) collective-permute-start(bf16[2,4,96,768]{3,2,1,0:T(8,128)(2,1)} %get-tuple-element.266), channel_id=1, source_target_pairs={{0,2},{1,3},{2,0},{3,1},{4,6},{5,7},{6,4},{7,5},{8,10},{9,11},{10,... | collective-permute-start | bytes 3538952 | tf_op jit(solution)/shard_map/ppermute | solution.py:784
  309.3 27.9 %collective-permute-start.22 = (bf16[2,4,96,768]{3,2,1,0:T(8,128)(2,1)}, bf16[2,4,96,768]{3,2,1,0:T(8,128)(2,1)S(1)}, u32[]{:S(2)}, u32[]{:S(2)}) collective-permute-start(bf16[2,4,96,768]{3,2,1,0:T(8,128)(2,1)} %get-tuple-element.268), channel_id=1, source_target_pairs={{0,4},{4,0},{8,12},{12,8},{16,20},{20,16},{24,28},{28,24},{1,5},{5... | collective-permute-start | bytes 3538952 | tf_op jit(solution)/shard_map/ppermute | solution.py:784
  342.0 33.8 %collective-permute-start.24 = (bf16[4,96,768]{2,1,0:T(8,128)(2,1)}, bf16[4,96,768]{2,1,0:T(8,128)(2,1)S(1)}, u32[]{:S(2)}, u32[]{:S(2)}) collective-permute-start(bf16[4,96,768]{2,1,0:T(8,128)(2,1)} %get-tuple-element.288), channel_id=1, source_target_pairs={{0,4},{4,0},{8,12},{12,8},{16,20},{20,16},{24,28},{28,24},{1,5},{5... | collective-permute-start | bytes 1769480 | tf_op jit(solution)/shard_map/ppermute | solution.py:784
  342.4 34.8 %collective-permute-start.25 = (bf16[4,96,768]{2,1,0:T(8,128)(2,1)S(1)}, bf16[4,96,768]{2,1,0:T(8,128)(2,1)S(1)}, u32[]{:S(2)}, u32[]{:S(2)}) collective-permute-start(bf16[4,96,768]{2,1,0:T(8,128)(2,1)S(1)} %copy-done.50), channel_id=1, source_target_pairs={{0,2},{1,3},{2,0},{3,1},{4,6},{5,7},{6,4},{7,5},{8,10},{9,11},{10,... | collective-permute-start | bytes 1769480 | tf_op jit(solution)/shard_map/ppermute | solution.py:784
  344.1 33.1 %collective-permute-start.26 = (bf16[2,1,96,768]{3,2,1,0:T(8,128)(2,1)}, bf16[2,1,96,768]{3,2,1,0:T(8,128)(2,1)S(1)}, u32[]{:S(2)}, u32[]{:S(2)}) collective-permute-start(bf16[2,1,96,768]{3,2,1,0:T(8,128)(2,1)} %get-tuple-element.294), channel_id=1, source_target_pairs={{0,16},{4,20},{8,24},{12,28},{16,0},{20,4},{24,8},{28,12},{1,17},{... | collective-permute-start | bytes 884744 | tf_op jit(solution)/shard_map/ppermute | solution.py:784
  346.7 32.4 %collective-permute-start.31 = (bf16[2,2,96,384]{3,2,1,0:T(8,128)(2,1)}, bf16[2,2,96,384]{3,2,1,0:T(8,128)(2,1)S(1)}, u32[]{:S(2)}, u32[]{:S(2)}) collective-permute-start(bf16[2,2,96,384]{3,2,1,0:T(8,128)(2,1)} %get-tuple-element.309), channel_id=1, source_target_pairs={{0,8},{4,12},{8,0},{12,4},{16,24},{20,28},{24,16},{28,20},{1,9},{5... | collective-permute-start | bytes 884744 | tf_op jit(solution)/shard_map/ppermute | solution.py:784
  375.2 14.8 %collective-permute-start.29 = (bf16[2,4,96,384]{3,2,1,0:T(8,128)(2,1)}, bf16[2,4,96,384]{3,2,1,0:T(8,128)(2,1)S(1)}, u32[]{:S(2)}, u32[]{:S(2)}) collective-permute-start(bf16[2,4,96,384]{3,2,1,0:T(8,128)(2,1)} %get-tuple-element.306), channel_id=1, source_target_pairs={{0,2},{1,3},{2,0},{3,1},{4,6},{5,7},{6,4},{7,5},{8,10},{9,11},{10,... | collective-permute-start | bytes 1769480 | tf_op jit(solution)/shard_map/ppermute | solution.py:784
  375.8 14.5 %collective-permute-start.30 = (bf16[2,4,96,384]{3,2,1,0:T(8,128)(2,1)}, bf16[2,4,96,384]{3,2,1,0:T(8,128)(2,1)S(1)}, u32[]{:S(2)}, u32[]{:S(2)}) collective-permute-start(bf16[2,4,96,384]{3,2,1,0:T(8,128)(2,1)} %get-tuple-element.308), channel_id=1, source_target_pairs={{0,4},{4,0},{8,12},{12,8},{16,20},{20,16},{24,28},{28,24},{1,5},{5... | collective-permute-start | bytes 1769480 | tf_op jit(solution)/shard_map/ppermute | solution.py:784
  378.6 17.5 %collective-permute-start.27 = (bf16[2,2,96,768]{3,2,1,0:T(8,128)(2,1)}, bf16[2,2,96,768]{3,2,1,0:T(8,128)(2,1)S(1)}, u32[]{:S(2)}, u32[]{:S(2)}) collective-permute-start(bf16[2,2,96,768]{3,2,1,0:T(8,128)(2,1)} %get-tuple-element.296), channel_id=1, source_target_pairs={{0,8},{4,12},{8,0},{12,4},{16,24},{20,28},{24,16},{28,20},{1,9},{5... | collective-permute-start | bytes 1769480 | tf_op jit(solution)/shard_map/ppermute | solution.py:784
  380.3 15.8 %collective-permute-start.32 = (bf16[2,1,96,384]{3,2,1,0:T(8,128)(2,1)}, bf16[2,1,96,384]{3,2,1,0:T(8,128)(2,1)S(1)}, u32[]{:S(2)}, u32[]{:S(2)}) collective-permute-start(bf16[2,1,96,384]{3,2,1,0:T(8,128)(2,1)} %get-tuple-element.322), channel_id=1, source_target_pairs={{0,16},{4,20},{8,24},{12,28},{16,0},{20,4},{24,8},{28,12},{1,17},{... | collective-permute-start | bytes 442376 | tf_op jit(solution)/shard_map/ppermute | solution.py:784
  (72 other events, 964.6 us)

commit v7 on v6

--- a/solution.py
+++ b/solution.py
@@ -364,10 +364,14 @@
     return made
 
 
-def each_chunk(made, dp_count):
-    rows = made.shape[0] // dp_count
-    for dp in range(dp_count):
-        yield dp, made[dp * rows : (dp + 1) * rows]
+def row_halves(depth):
+    return [(half, slice(half * depth // 2, (half + 1) * depth // 2)) for half in range(2)]
+
+
+def each_chunk(made, count, half):
+    rows = made.shape[0] // count
+    for dp in range(count):
+        yield half * count + dp, made[dp * rows : (dp + 1) * rows]
 
 
 def place(dp, own_dp, dp_count):
@@ -449,27 +453,31 @@
             sums_ref[2:3] += column_sum(df.astype(WIDE))
             acc_ref[at] = gv
 
-    dg = dot_nt(df_ref[...], wd_ref[...])
     gp_copy.wait()
-    dz = (dg * gp_ref[slot].astype(WIDE)).astype(LOW)
-    dz_ref[...] = dz
-    zsum_ref[...] = column_sum(dz.astype(WIDE))
-    acc_ref[...] += dot_nt(dz_ref[...], wu_ref[...])
+    zsum = jnp.zeros(zsum_ref.shape, WIDE)
+    for start in range(0, dz_ref.shape[0], 256):
+        at = slice(start, start + 256)
+        dg = dot_nt(df_ref[at], wd_ref[...])
+        dz = (dg * gp_ref[slot, at].astype(WIDE)).astype(LOW)
+        dz_ref[at] = dz
+        zsum = zsum + column_sum(dz.astype(WIDE))
+        acc_ref[at] += dot_nt(dz, wu_ref[...])
+    zsum_ref[...] = zsum
 
     @pl.when(step == 0)
     def _():
         hr_copy.wait()
 
-    up = dot_tn(hr_ref[...], dz_ref[...]).astype(LOW)
     gr_copy.wait()
-    down = dot_tn(df_ref[...], gr_ref[slot]).astype(LOW)
     for out, wanted in ((send_ref, step < 2), (keep_ref, step >= 2)):
 
         @pl.when(wanted)
         def _():
-            for which, made in enumerate((up, down)):
-                for dp, chunk in each_chunk(made, dp_count):
-                    out[(which, *place(dp, own_dp, dp_count))] = chunk
+            for which, (a, b) in enumerate(((hr_ref, dz_ref[...]), (df_ref, gr_ref[slot]))):
+                for first, rows in row_halves(hr_ref.shape[1]):
+                    made = dot_tn(a[:, rows], b).astype(LOW)
+                    for dp, chunk in each_chunk(made, dp_count // 2, first):
+                        out[(which, *place(dp, own_dp, dp_count))] = chunk
 
     @pl.when(step == steps - 1)
     def _():
@@ -565,8 +573,8 @@
     )
 
 
-def split_rows(made, got_ref, own_dp, dp_count, send_ref, keep_ref):
-    for dp, chunk in each_chunk(made, dp_count):
+def split_rows(made, half, got_ref, own_dp, dp_count, send_ref, keep_ref):
+    for dp, chunk in each_chunk(made, dp_count // 2, half):
         away, rest = place(dp, own_dp, dp_count)
         summed = (chunk + got_ref[away, rest].astype(WIDE)).astype(LOW)
 
@@ -579,8 +587,8 @@
             keep_ref[rest] = summed
 
 
-def add_rows(made, got_ref, own_dp, dp_count, out_ref):
-    for dp, chunk in each_chunk(made, dp_count):
+def add_rows(made, half, got_ref, own_dp, dp_count, out_ref):
+    for dp, chunk in each_chunk(made, dp_count // 2, half):
         at = place(dp, own_dp, dp_count)
         out_ref[at] = (chunk + got_ref[at].astype(WIDE)).astype(LOW)
 
@@ -685,23 +693,24 @@
 
     @pl.when(slot == last)
     def _():
-        first = dot_nn(xt_ref[...], parts_ref[block])
-        second = dot_nn(ot_ref[...], da_ref[...])
-        made = jnp.concatenate([first, second], axis=1)
-        if not keep:
-            for dp, chunk in each_chunk(made.astype(LOW), dp_count):
-                grads[0][place(dp, own_dp, dp_count)] = chunk
-            return
-        half = made.shape[1] // 2
-        a_send, a_keep, b_send, b_keep = grads
-        got = [got_ref.at[:, :, :, :half], got_ref.at[:, :, :, half:]]
-        for where_to, wanted in ((a_keep, 0), (a_send, 1)):
-
-            @pl.when(block == wanted)
-            def _():
-                add_rows(made[:, :half], got[0], own_dp, dp_count, where_to)
-
-        split_rows(made[:, half:], got[1], own_dp, dp_count, b_send, b_keep)
+        for half, rows in row_halves(xt_ref.shape[0]):
+            first = dot_nn(xt_ref[rows, :], parts_ref[block])
+            second = dot_nn(ot_ref[rows, :], da_ref[...])
+            made = jnp.concatenate([first, second], axis=1)
+            if not keep:
+                for dp, chunk in each_chunk(made.astype(LOW), dp_count // 2, half):
+                    grads[0][place(dp, own_dp, dp_count)] = chunk
+                continue
+            cut = made.shape[1] // 2
+            a_send, a_keep, b_send, b_keep = grads
+            got = [got_ref.at[:, :, :, :cut], got_ref.at[:, :, :, cut:]]
+            for where_to, wanted in ((a_keep, 0), (a_send, 1)):
+
+                @pl.when(block == wanted)
+                def _():
+                    add_rows(made[:, :cut], half, got[0], own_dp, dp_count, where_to)
+
+            split_rows(made[:, cut:], half, got[1], own_dp, dp_count, b_send, b_keep)
 
 
 def attention_backward(own, mixed, do, probs, x, da, wa, wb, gx, got, dp_count, out_type, tile=64):

time: 444 us -> 429 us (0.966)
  Pallas kernels: 327 us -> 312 us
    pallas_call x14, Pallas kernels: 307 us -> 291 us  [call(): pl.pallas_call(kernel, grid_spec=pltpu.PrefetchScalarGridSpec(num_scalar_...]
where the time goes in v7:
time: 429 us; the launch traced here: 422 us
  Pallas kernels  312 us (73%)
  waiting for transfers between devices  49.1 us (11%)
  starting transfers between devices  44.2 us (10%)
  local copies, waits for them, and re-layouts  11.6 us (3%)
    pallas_call x14, Pallas kernels, call(): pl.pallas_call(kernel, grid_spec=pltpu.PrefetchScalarGridSpec(num_scalar_...  291 us
    ppermute x43, waiting for transfers between devices, swap(): return lax.ppermute(value, axis, [(i, i ^ bit) for i in range(size)])  49.1 us
    ppermute x43, starting transfers between devices, swap(): return lax.ppermute(value, axis, [(i, i ^ bit) for i in range(size)])  44.2 us
    pallas_call x12, Pallas kernels, add_split(): pl.pallas_call(functools.partial(add_split_kernel, merge_in=merge_in, mer...  16.2 us
  transfers between devices with their start and end apart: 43, of which 16 were waited for; matrix products, arithmetic and copies ran while one was open for 2% of the time, Pallas kernels for 52%

profile of v7, /device:TPU:0, one launch (start us, length us, event | category | flops | bytes accessed | tf_op | source)
XLA Modules:
  0.0 422.2 jit_solution(9274350577344260365)
XLA Ops:
  4.6 4.4 %mask_bias.1.bias_ref = f32[2,512,512]{2,1,0:T(8,128)} custom-call(s32[1]{0:T(128)} %bitcast.4.base_ref, s32[8,32]{1,0:T(8,128)} %lengths_ref.1), custom_call_target="tpu_custom_call" | custom-call | tf_op jit(solution)/shard_map/mask_bias/pallas_call | solution.py:134
  16.6 14.7 %attention_forward.3 = (bf16[4,4,1024,192]{3,2,1,0:T(8,128)(2,1)}, bf16[4,2,3,512,512]{4,3,2,1,0:T(8,128)(2,1)}) custom-call(bf16[1024,768]{1,0:T(8,128)(2,1)} %x_ref.7, f32[2,2,1,192]{3,2,1,0:T(1,128)} %get-tuple-element.375.b_ref, f32[2,512,512]{2,1,0:T(8,128)} %mask_bias.1.bias_ref, bf16[576,768]{1,0:T(8,128)(2,1)} %bitcast.85, bf16[576,768]{1,0:T(8,128)(2,1)} %copy-done.45), custom_call_target="tpu_custom_call" | custom-call | flops 8254390272 | bytes 24316928 | tf_op jit(solution)/shard_map/attention_forward/pallas_call | solution.py:99
  32.2 4.7 %collective-permute-done.1.refs_0_.wb_ref = bf16[576,768]{1,0:T(8,128)(2,1)S(1)} collective-permute-done((bf16[576,768]{1,0:T(8,128)(2,1)S(1)}, bf16[576,768]{1,0:T(8,128)(2,1)S(1)}, u32[]{:S(2)}, u32[]{:S(2)}) %collective-permute-start.1) | collective-permute-done | bytes 884768 | tf_op jit(solution)/shard_map/ppermute | solution.py:793
  41.6 14.7 %attention_forward.4 = (bf16[4,4,1024,192]{3,2,1,0:T(8,128)(2,1)}, bf16[4,2,3,512,512]{4,3,2,1,0:T(8,128)(2,1)}) custom-call(bf16[1024,768]{1,0:T(8,128)(2,1)} %x_ref.7, f32[2,2,1,192]{3,2,1,0:T(1,128)} %get-tuple-element.187.b_ref, f32[2,512,512]{2,1,0:T(8,128)} %mask_bias.1.bias_ref, ...), custom_call_target="tpu_custom_call", output_to_operand_aliasing={{0}: (5, {}), {1}: (6, {})} | custom-call | flops 8254390272 | bytes 43191296 | tf_op jit(solution)/shard_map/attention_forward/pallas_call | solution.py:99
  56.3 4.0 collective-permute-done.7.refs_2_.wb_ref
  60.3 25.1 %ffn_forward.2 = (f32[1024,768]{1,0:T(8,128)}, bf16[1024,768]{1,0:T(8,128)(2,1)}, bf16[4,1024,768]{2,1,0:T(8,128)(2,1)}, bf16[4,1024,768]{2,1,0:T(8,128)(2,1)}, ...) custom-call(s32[2]{0:T(128)} %pad_add_fusion.own_ref, ...), custom_call_target="tpu_custom_call" | custom-call | flops 32614907904 | bytes 51154944 | tf_op jit(solution)/shard_map/ffn_forward/pallas_call | solution.py:99
  86.3 25.3 %attention_forward.5 = (bf16[4,4,1024,192]{3,2,1,0:T(8,128)(2,1)}, bf16[4,2,3,512,512]{4,3,2,1,0:T(8,128)(2,1)}) custom-call(bf16[1024,768]{1,0:T(8,128)(2,1)} %get-tuple-element.191.x_ref, f32[4,2,1,192]{3,2,1,0:T(1,128)} %pad_maximum_fusion.7.b_ref, f32[2,512,512]{2,1,0:T(8,128)} %mask_bias.1.bias_ref, bf16[576,768]{1,0:T(8,128)(2,1)} %bitcast.89, ...), custom_call_target="tpu_custom_call" | custom-call | flops 16508780544 | bytes 26089472 | tf_op jit(solution)/shard_map/attention_forward/pallas_call | solution.py:99
  111.7 25.6 %ffn_forward.3 = (f32[1024,768]{1,0:T(8,128)}, bf16[1024,768]{1,0:T(8,128)(2,1)}, bf16[4,1024,768]{2,1,0:T(8,128)(2,1)}, bf16[4,1024,768]{2,1,0:T(8,128)(2,1)}, ...) custom-call(s32[2]{0:T(128)} %pad_add_fusion.own_ref, ...), custom_call_target="tpu_custom_call" | custom-call | flops 32614907904 | bytes 52727808 | tf_op jit(solution)/shard_map/ffn_forward/pallas_call | solution.py:99
  137.3 36.7 %ffn_backward.2 = (bf16[4,1024,192]{2,1,0:T(8,128)(2,1)}, bf16[4,1024,192]{2,1,0:T(8,128)(2,1)}, f32[1024,768]{1,0:T(8,128)}, f32[8,768]{1,0:T(8,128)}, f32[4,1,...) custom-call(s32[2]{0:T(128)} %pad_add_fusion.own_ref, ...), custom_call_target="tpu_custom_call" | custom-call | flops 41070624768 | bytes 59025408 | tf_op jit(solution)/shard_map/ffn_backward/pallas_call | solution.py:99
  174.6 24.8 %attention_backward.4 = (f32[1024,768]{1,0:T(8,128)}, f32[2,8,192]{2,1,0:T(8,128)}, bf16[2,2,4,96,768]{4,3,2,1,0:T(8,128)(2,1)}) custom-call(s32[2]{0:T(128)} %pad_add_fusion.own_ref, bf16[4,4,1024,192]{3,2,1,0:T(8,128)(2,1)} %get-tuple-element.195.mixed_hbm.mixed_ref.o_ref, bf16[4,1024,192]{2,1,0:T(8,128)(2,1)} %get-tuple-element.215.do_ref, ...), custom_call_target="tpu_custom_call" | custom-call | flops 14495514624 | bytes 40316928 | tf_op jit(solution)/shard_map/attention_backward/pallas_call | solution.py:99
  199.5 6.1 %core_add.2 = (bf16[2,4,96,768]{3,2,1,0:T(8,128)(2,1)}, bf16[2,4,96,768]{3,2,1,0:T(8,128)(2,1)}, bf16[2,4,96,768]{3,2,1,0:T(8,128)(2,1)}, bf16[2,4,96,768]{3,2,1,0:T(8,128)(2,1)}) custom-call(bf16[2,2,2,4,96,768]{5,4,3,2,1,0:T(8,128)(2,1)S(1)} %bitcast.65, bf16[2,2,2,4,96,768]{5,4,3,2,1,0:T(8,128)(2,1)} %collective-permute-done.9.got_ref), custom_call_target="tpu_custom_call" | custom-call | tf_op jit(solution)/shard_map/core_add/pallas_call | solution.py:99
  208.9 26.0 %attention_backward.5 = (f32[1024,768]{1,0:T(8,128)}, f32[2,8,192]{2,1,0:T(8,128)}, bf16[2,4,96,384]{3,2,1,0:T(8,128)(2,1)}, bf16[2,4,96,384]{3,2,1,0:T(8,128)(2...) custom-call(s32[2]{0:T(128)} %pad_add_fusion.own_ref, ...), custom_call_target="tpu_custom_call" | custom-call | flops 14495514624 | bytes 42676224 | tf_op jit(solution)/shard_map/attention_backward/pallas_call | solution.py:99
  241.2 36.8 %ffn_backward.3 = (bf16[4,1024,192]{2,1,0:T(8,128)(2,1)}, bf16[4,1024,192]{2,1,0:T(8,128)(2,1)}, f32[1024,768]{1,0:T(8,128)}, f32[8,768]{1,0:T(8,128)}, f32[4,1,...) custom-call(s32[2]{0:T(128)} %pad_add_fusion.own_ref, ...), custom_call_target="tpu_custom_call" | custom-call | flops 41070624768 | bytes 60598272 | tf_op jit(solution)/shard_map/ffn_backward/pallas_call | solution.py:99
  283.8 5.3 %collective-permute-done.17.got_ref = bf16[2,2,2,4,96,768]{5,4,3,2,1,0:T(8,128)(2,1)S(1)} collective-permute-done((bf16[2,2,2,4,96,768]{5,4,3,2,1,0:T(8,128)(2,1)}, bf16[2,2,2,4,96,768]{5,4,3,2,1,0:T(8,128)(2,1)S(1)}, u32[]{:S(2)}, u32[]{:S(2)}) %collective-permute-start.17) | collective-permute-done | bytes 4718624 | tf_op jit(solution)/shard_map/ppermute | solution.py:793
  289.1 3.7 core_add.3
  293.7 24.4 %attention_backward.6 = (f32[1024,768]{1,0:T(8,128)}, f32[2,8,192]{2,1,0:T(8,128)}, bf16[2,2,4,96,768]{4,3,2,1,0:T(8,128)(2,1)}) custom-call(s32[2]{0:T(128)} %pad_add_fusion.own_ref, bf16[4,4,1024,192]{3,2,1,0:T(8,128)(2,1)} %get-tuple-element.190.mixed_hbm.mixed_ref.o_ref, bf16[4,1024,192]{2,1,0:T(8,128)(2,1)} %get-tuple-element.282.do_ref, ...), custom_call_target="tpu_custom_call" | custom-call | flops 14495514624 | bytes 40316928 | tf_op jit(solution)/shard_map/attention_backward/pallas_call | solution.py:99
  318.1 2.9 collective-permute-done.21
  333.7 25.9 %attention_backward.7 = (bf16[1024,768]{1,0:T(8,128)(2,1)}, f32[2,8,192]{2,1,0:T(8,128)}, bf16[2,4,96,384]{3,2,1,0:T(8,128)(2,1)}, bf16[2,4,96,384]{3,2,1,0:T(8,...) custom-call(s32[2]{0:T(128)} %pad_add_fusion.own_ref, ...), custom_call_target="tpu_custom_call" | custom-call | flops 14495514624 | bytes 41103360 | tf_op jit(solution)/shard_map/attention_backward/pallas_call | solution.py:99
  367.0 7.6 %collective-permute-done.29 = bf16[2,4,96,384]{3,2,1,0:T(8,128)(2,1)S(1)} collective-permute-done((bf16[2,4,96,384]{3,2,1,0:T(8,128)(2,1)}, bf16[2,4,96,384]{3,2,1,0:T(8,128)(2,1)S(1)}, u32[]{:S(2)}, u32[]{:S(2)}) %collective-permute-start.29) | collective-permute-done | bytes 589856 | tf_op jit(solution)/shard_map/ppermute | solution.py:793
  388.9 2.9 collective-permute-start.33
  393.2 3.2 collective-permute-done.37
  397.1 3.4 collective-permute-done.36.refs_1_
  405.5 2.8 collective-permute-start.40
  409.8 7.0 %collective-permute-done.41 = f32[2,12,768]{2,1,0:T(8,128)S(1)} collective-permute-done((f32[2,12,768]{2,1,0:T(8,128)S(1)}, f32[2,12,768]{2,1,0:T(8,128)S(1)}, u32[]{:S(2)}, u32[]{:S(2)}) %collective-permute-start.41) | collective-permute-done | bytes 73760 | tf_op jit(solution)/shard_map/ppermute | solution.py:793
  (228 shorter events, 82.3 us)
Async XLA Ops:
  14.5 17.1 %collective-permute-start.4 = (f32[2,2,1,192]{3,2,1,0:T(1,128)S(1)}, f32[2,2,1,192]{3,2,1,0:T(1,128)S(1)}, u32[]{:S(2)}, u32[]{:S(2)}) collective-permute-start(f32[2,2,1,192]{3,2,1,0:T(1,128)S(1)} %collective-permute-done.3), channel_id=1, source_target_pairs={{0,1},{1,0},{2,3},{3,2},{4,5},{5,4},{6,7},{7,6},{8,9},{9,8},{10,11... | collective-permute-start | bytes 9224 | tf_op jit(solution)/shard_map/ppermute | solution.py:793
  14.6 22.3 %collective-permute-start.1 = (bf16[576,768]{1,0:T(8,128)(2,1)S(1)}, bf16[576,768]{1,0:T(8,128)(2,1)S(1)}, u32[]{:S(2)}, u32[]{:S(2)}) collective-permute-start(bf16[576,768]{1,0:T(8,128)(2,1)S(1)} %bitcast.84), channel_id=1, source_target_pairs={{0,2},{1,3},{2,0},{3,1},{4,6},{5,7},{6,4},{7,5},{8,10},{9,11},{10,... | collective-permute-start | bytes 2654216 | tf_op jit(solution)/shard_map/ppermute | solution.py:793
  38.2 22.0 %collective-permute-start.7 = (bf16[576,768]{1,0:T(8,128)(2,1)S(1)}, bf16[576,768]{1,0:T(8,128)(2,1)S(1)}, u32[]{:S(2)}, u32[]{:S(2)}) collective-permute-start(bf16[576,768]{1,0:T(8,128)(2,1)S(1)} %bitcast.88), channel_id=1, source_target_pairs={{0,2},{1,3},{2,0},{3,1},{4,6},{5,7},{6,4},{7,5},{8,10},{9,11},{10,... | collective-permute-start | bytes 2654216 | tf_op jit(solution)/shard_map/ppermute | solution.py:793
  60.3 25.1 %collective-permute-start.8 = (bf16[576,768]{1,0:T(8,128)(2,1)S(1)}, bf16[576,768]{1,0:T(8,128)(2,1)S(1)}, u32[]{:S(2)}, u32[]{:S(2)}) collective-permute-start(bf16[576,768]{1,0:T(8,128)(2,1)S(1)} %collective-permute-done.7.refs_2_.wb_ref), channel_id=1, source_target_pairs={{0,1},{1,0},{2,3},{3,2},{4,5},{5,4},{6,7},{7,6},{8,9},{9,8},{10,11... | collective-permute-start | bytes 2654216 | tf_op jit(solution)/shard_map/ppermute | solution.py:793
  174.0 25.5 %collective-permute-start.9 = (bf16[2,2,2,4,96,768]{5,4,3,2,1,0:T(8,128)(2,1)}, bf16[2,2,2,4,96,768]{5,4,3,2,1,0:T(8,128)(2,1)}, u32[]{:S(2)}, u32[]{:S(2)}) collective-permute-start(bf16[2,2,2,4,96,768]{5,4,3,2,1,0:T(8,128)(2,1)} %get-tuple-element.211), channel_id=1, source_target_pairs={{0,1},{1,0},{2,3},{3,2},{4,5},{5,4},{6,7},{7,6},{8,9},{9,8},{10,11... | collective-permute-start | bytes 14155784 | tf_op jit(solution)/shard_map/ppermute | solution.py:793
  205.6 30.2 %collective-permute-start.11 = (bf16[2,4,96,768]{3,2,1,0:T(8,128)(2,1)}, bf16[2,4,96,768]{3,2,1,0:T(8,128)(2,1)S(1)}, u32[]{:S(2)}, u32[]{:S(2)}) collective-permute-start(bf16[2,4,96,768]{3,2,1,0:T(8,128)(2,1)} %get-tuple-element.219), channel_id=1, source_target_pairs={{0,2},{1,3},{2,0},{3,1},{4,6},{5,7},{6,4},{7,5},{8,10},{9,11},{10,... | collective-permute-start | bytes 3538952 | tf_op jit(solution)/shard_map/ppermute | solution.py:793
  207.3 28.5 %collective-permute-start.12 = (bf16[2,4,96,768]{3,2,1,0:T(8,128)(2,1)}, bf16[2,4,96,768]{3,2,1,0:T(8,128)(2,1)S(1)}, u32[]{:S(2)}, u32[]{:S(2)}) collective-permute-start(bf16[2,4,96,768]{3,2,1,0:T(8,128)(2,1)} %get-tuple-element.221), channel_id=1, source_target_pairs={{0,4},{4,0},{8,12},{12,8},{16,20},{20,16},{24,28},{28,24},{1,5},{5... | collective-permute-start | bytes 3538952 | tf_op jit(solution)/shard_map/ppermute | solution.py:793
  234.8 44.6 %collective-permute-start.13 = (bf16[2,4,96,384]{3,2,1,0:T(8,128)(2,1)}, bf16[2,4,96,384]{3,2,1,0:T(8,128)(2,1)S(1)}, u32[]{:S(2)}, u32[]{:S(2)}) collective-permute-start(bf16[2,4,96,384]{3,2,1,0:T(8,128)(2,1)} %get-tuple-element.237), channel_id=1, source_target_pairs={{0,2},{1,3},{2,0},{3,1},{4,6},{5,7},{6,4},{7,5},{8,10},{9,11},{10,... | collective-permute-start | bytes 1769480 | tf_op jit(solution)/shard_map/ppermute | solution.py:793
  235.4 44.0 %collective-permute-start.14 = (bf16[2,4,96,384]{3,2,1,0:T(8,128)(2,1)}, bf16[2,4,96,384]{3,2,1,0:T(8,128)(2,1)S(1)}, u32[]{:S(2)}, u32[]{:S(2)}) collective-permute-start(bf16[2,4,96,384]{3,2,1,0:T(8,128)(2,1)} %get-tuple-element.239), channel_id=1, source_target_pairs={{0,4},{4,0},{8,12},{12,8},{16,20},{20,16},{24,28},{28,24},{1,5},{5... | collective-permute-start | bytes 1769480 | tf_op jit(solution)/shard_map/ppermute | solution.py:793
  238.0 40.0 %collective-permute-start.15 = (bf16[4,96,768]{2,1,0:T(8,128)(2,1)}, bf16[4,96,768]{2,1,0:T(8,128)(2,1)S(1)}, u32[]{:S(2)}, u32[]{:S(2)}) collective-permute-start(bf16[4,96,768]{2,1,0:T(8,128)(2,1)} %get-tuple-element.241), channel_id=1, source_target_pairs={{0,4},{4,0},{8,12},{12,8},{16,20},{20,16},{24,28},{28,24},{1,5},{5... | collective-permute-start | bytes 1769480 | tf_op jit(solution)/shard_map/ppermute | solution.py:793
  239.7 38.3 %collective-permute-start.16 = (bf16[4,96,768]{2,1,0:T(8,128)(2,1)}, bf16[4,96,768]{2,1,0:T(8,128)(2,1)S(1)}, u32[]{:S(2)}, u32[]{:S(2)}) collective-permute-start(bf16[4,96,768]{2,1,0:T(8,128)(2,1)} %get-tuple-element.242), channel_id=1, source_target_pairs={{0,2},{1,3},{2,0},{3,1},{4,6},{5,7},{6,4},{7,5},{8,10},{9,11},{10,... | collective-permute-start | bytes 1769480 | tf_op jit(solution)/shard_map/ppermute | solution.py:793
  281.0 43.6 %collective-permute-start.18 = (bf16[4,96,384]{2,1,0:T(8,128)(2,1)}, bf16[4,96,384]{2,1,0:T(8,128)(2,1)S(1)}, u32[]{:S(2)}, u32[]{:S(2)}) collective-permute-start(bf16[4,96,384]{2,1,0:T(8,128)(2,1)} %get-tuple-element.263), channel_id=1, source_target_pairs={{0,4},{4,0},{8,12},{12,8},{16,20},{20,16},{24,28},{28,24},{1,5},{5... | collective-permute-start | bytes 884744 | tf_op jit(solution)/shard_map/ppermute | solution.py:793
  281.7 42.9 %collective-permute-start.19 = (bf16[4,96,384]{2,1,0:T(8,128)(2,1)}, bf16[4,96,384]{2,1,0:T(8,128)(2,1)S(1)}, u32[]{:S(2)}, u32[]{:S(2)}) collective-permute-start(bf16[4,96,384]{2,1,0:T(8,128)(2,1)} %get-tuple-element.264), channel_id=1, source_target_pairs={{0,2},{1,3},{2,0},{3,1},{4,6},{5,7},{6,4},{7,5},{8,10},{9,11},{10,... | collective-permute-start | bytes 884744 | tf_op jit(solution)/shard_map/ppermute | solution.py:793
  281.9 41.5 %collective-permute-start.20 = (bf16[2,2,96,768]{3,2,1,0:T(8,128)(2,1)}, bf16[2,2,96,768]{3,2,1,0:T(8,128)(2,1)S(1)}, u32[]{:S(2)}, u32[]{:S(2)}) collective-permute-start(bf16[2,2,96,768]{3,2,1,0:T(8,128)(2,1)} %get-tuple-element.265), channel_id=1, source_target_pairs={{0,8},{4,12},{8,0},{12,4},{16,24},{20,28},{24,16},{28,20},{1,9},{5... | collective-permute-start | bytes 1769480 | tf_op jit(solution)/shard_map/ppermute | solution.py:793
  292.8 28.2 %collective-permute-start.21 = (bf16[2,4,96,768]{3,2,1,0:T(8,128)(2,1)}, bf16[2,4,96,768]{3,2,1,0:T(8,128)(2,1)S(1)}, u32[]{:S(2)}, u32[]{:S(2)}) collective-permute-start(bf16[2,4,96,768]{3,2,1,0:T(8,128)(2,1)} %get-tuple-element.266), channel_id=1, source_target_pairs={{0,2},{1,3},{2,0},{3,1},{4,6},{5,7},{6,4},{7,5},{8,10},{9,11},{10,... | collective-permute-start | bytes 3538952 | tf_op jit(solution)/shard_map/ppermute | solution.py:793
  293.3 27.9 %collective-permute-start.22 = (bf16[2,4,96,768]{3,2,1,0:T(8,128)(2,1)}, bf16[2,4,96,768]{3,2,1,0:T(8,128)(2,1)S(1)}, u32[]{:S(2)}, u32[]{:S(2)}) collective-permute-start(bf16[2,4,96,768]{3,2,1,0:T(8,128)(2,1)} %get-tuple-element.268), channel_id=1, source_target_pairs={{0,4},{4,0},{8,12},{12,8},{16,20},{20,16},{24,28},{28,24},{1,5},{5... | collective-permute-start | bytes 3538952 | tf_op jit(solution)/shard_map/ppermute | solution.py:793
  325.9 34.4 %collective-permute-start.24 = (bf16[4,96,768]{2,1,0:T(8,128)(2,1)}, bf16[4,96,768]{2,1,0:T(8,128)(2,1)S(1)}, u32[]{:S(2)}, u32[]{:S(2)}) collective-permute-start(bf16[4,96,768]{2,1,0:T(8,128)(2,1)} %get-tuple-element.288), channel_id=1, source_target_pairs={{0,4},{4,0},{8,12},{12,8},{16,20},{20,16},{24,28},{28,24},{1,5},{5... | collective-permute-start | bytes 1769480 | tf_op jit(solution)/shard_map/ppermute | solution.py:793
  326.4 35.3 %collective-permute-start.25 = (bf16[4,96,768]{2,1,0:T(8,128)(2,1)S(1)}, bf16[4,96,768]{2,1,0:T(8,128)(2,1)S(1)}, u32[]{:S(2)}, u32[]{:S(2)}) collective-permute-start(bf16[4,96,768]{2,1,0:T(8,128)(2,1)S(1)} %copy-done.50), channel_id=1, source_target_pairs={{0,2},{1,3},{2,0},{3,1},{4,6},{5,7},{6,4},{7,5},{8,10},{9,11},{10,... | collective-permute-start | bytes 1769480 | tf_op jit(solution)/shard_map/ppermute | solution.py:793
  328.1 33.6 %collective-permute-start.26 = (bf16[2,1,96,768]{3,2,1,0:T(8,128)(2,1)}, bf16[2,1,96,768]{3,2,1,0:T(8,128)(2,1)S(1)}, u32[]{:S(2)}, u32[]{:S(2)}) collective-permute-start(bf16[2,1,96,768]{3,2,1,0:T(8,128)(2,1)} %get-tuple-element.294), channel_id=1, source_target_pairs={{0,16},{4,20},{8,24},{12,28},{16,0},{20,4},{24,8},{28,12},{1,17},{... | collective-permute-start | bytes 884744 | tf_op jit(solution)/shard_map/ppermute | solution.py:793
  330.7 32.9 %collective-permute-start.31 = (bf16[2,2,96,384]{3,2,1,0:T(8,128)(2,1)}, bf16[2,2,96,384]{3,2,1,0:T(8,128)(2,1)S(1)}, u32[]{:S(2)}, u32[]{:S(2)}) collective-permute-start(bf16[2,2,96,384]{3,2,1,0:T(8,128)(2,1)} %get-tuple-element.309), channel_id=1, source_target_pairs={{0,8},{4,12},{8,0},{12,4},{16,24},{20,28},{24,16},{28,20},{1,9},{5... | collective-permute-start | bytes 884744 | tf_op jit(solution)/shard_map/ppermute | solution.py:793
  359.7 14.8 %collective-permute-start.29 = (bf16[2,4,96,384]{3,2,1,0:T(8,128)(2,1)}, bf16[2,4,96,384]{3,2,1,0:T(8,128)(2,1)S(1)}, u32[]{:S(2)}, u32[]{:S(2)}) collective-permute-start(bf16[2,4,96,384]{3,2,1,0:T(8,128)(2,1)} %get-tuple-element.306), channel_id=1, source_target_pairs={{0,2},{1,3},{2,0},{3,1},{4,6},{5,7},{6,4},{7,5},{8,10},{9,11},{10,... | collective-permute-start | bytes 1769480 | tf_op jit(solution)/shard_map/ppermute | solution.py:793
  360.3 14.5 %collective-permute-start.30 = (bf16[2,4,96,384]{3,2,1,0:T(8,128)(2,1)}, bf16[2,4,96,384]{3,2,1,0:T(8,128)(2,1)S(1)}, u32[]{:S(2)}, u32[]{:S(2)}) collective-permute-start(bf16[2,4,96,384]{3,2,1,0:T(8,128)(2,1)} %get-tuple-element.308), channel_id=1, source_target_pairs={{0,4},{4,0},{8,12},{12,8},{16,20},{20,16},{24,28},{28,24},{1,5},{5... | collective-permute-start | bytes 1769480 | tf_op jit(solution)/shard_map/ppermute | solution.py:793
  363.1 17.5 %collective-permute-start.27 = (bf16[2,2,96,768]{3,2,1,0:T(8,128)(2,1)}, bf16[2,2,96,768]{3,2,1,0:T(8,128)(2,1)S(1)}, u32[]{:S(2)}, u32[]{:S(2)}) collective-permute-start(bf16[2,2,96,768]{3,2,1,0:T(8,128)(2,1)} %get-tuple-element.296), channel_id=1, source_target_pairs={{0,8},{4,12},{8,0},{12,4},{16,24},{20,28},{24,16},{28,20},{1,9},{5... | collective-permute-start | bytes 1769480 | tf_op jit(solution)/shard_map/ppermute | solution.py:793
  364.8 15.8 %collective-permute-start.32 = (bf16[2,1,96,384]{3,2,1,0:T(8,128)(2,1)}, bf16[2,1,96,384]{3,2,1,0:T(8,128)(2,1)S(1)}, u32[]{:S(2)}, u32[]{:S(2)}) collective-permute-start(bf16[2,1,96,384]{3,2,1,0:T(8,128)(2,1)} %get-tuple-element.322), channel_id=1, source_target_pairs={{0,16},{4,20},{8,24},{12,28},{16,0},{20,4},{24,8},{28,12},{1,17},{... | collective-permute-start | bytes 442376 | tf_op jit(solution)/shard_map/ppermute | solution.py:793
  (72 other events, 934.3 us)

commit v8 on v7

--- a/solution.py
+++ b/solution.py
@@ -73,6 +73,10 @@
 
 def in_place():
     return pl.BlockSpec(memory_space=pl.ANY)
+
+
+def in_vmem():
+    return pl.BlockSpec(memory_space=pltpu.VMEM)
 
 
 def in_hbm():
@@ -793,21 +797,25 @@
     return lax.ppermute(value, axis, [(i, i ^ bit) for i in range(size)])
 
 
-def add_split_kernel(*refs, merge_in, merge_out, extra):
+def add_split_kernel(*refs, merge_in, merge_out, extra, late):
     inputs = 2 if merge_in else 4
     outputs = 2 if merge_out else 4
     ins, refs = refs[:inputs], refs[extra:]
     outs = refs[inputs : inputs + outputs]
     kept_ref, send_ref, keep_ref, in_sems, out_sems = refs[inputs + outputs :]
     half = send_ref.shape[1]
-    loads, got, stores = [], [], []
+    own, loads, got, stores = [], [], [], []
     for part in range(2):
         kept, came = (ins[0].at[part], ins[1].at[part]) if merge_in else ins[2 * part : 2 * part + 2]
         send, keep = (
             (outs[0].at[part], outs[1].at[part]) if merge_out else outs[2 * part : 2 * part + 2]
         )
         got.append(came)
-        loads.append(pltpu.make_async_copy(kept, kept_ref.at[part], in_sems.at[part]))
+        if late:
+            own.append(kept)
+        else:
+            own.append(kept_ref.at[part])
+            loads.append(pltpu.make_async_copy(kept, kept_ref.at[part], in_sems.at[part]))
         stores.append(
             [
                 pltpu.make_async_copy(send_ref.at[part], send, out_sems.at[part, 0]),
@@ -817,25 +825,30 @@
     for copy in loads:
         copy.start()
     for part in range(2):
-        loads[part].wait()
+        if loads:
+            loads[part].wait()
         for at, (out, copy) in enumerate(zip((send_ref, keep_ref), stores[part])):
             rows = pl.ds(half * (1 - at), half)
-            out[part] = (kept_ref[part, rows].astype(WIDE) + got[part][rows].astype(WIDE)).astype(LOW)
+            out[part] = (own[part][rows].astype(WIDE) + got[part][rows].astype(WIDE)).astype(LOW)
             copy.start()
     for copies in stores:
         for copy in copies:
             copy.wait()
 
 
-def add_split(ins, merge_in, merge_out, arrived):
+def add_split(ins, merge_in, merge_out, arrived, late):
     size, rows, columns = ins[0].shape[-3:]
     half = (size // 2, rows, columns)
     out_shape = [stored((2, *half), LOW)] * 2 if merge_out else [stored(half, LOW)] * 4
     return pl.pallas_call(
         functools.partial(
-            add_split_kernel, merge_in=merge_in, merge_out=merge_out, extra=len(arrived)
+            add_split_kernel,
+            merge_in=merge_in,
+            merge_out=merge_out,
+            extra=len(arrived),
+            late=late,
         ),
-        in_specs=[in_hbm(), pl.BlockSpec(memory_space=pltpu.VMEM)] * (len(ins) // 2)
+        in_specs=[in_vmem() if late else in_hbm(), in_vmem()] * (len(ins) // 2)
         + [in_place()] * len(arrived),
         out_specs=[in_hbm()] * len(out_shape),
         out_shape=out_shape,
@@ -864,14 +877,14 @@
     def busy(self):
         return self.at < len(self.stages)
 
-    def step(self, after, arrived=()):
+    def step(self, after, arrived=(), late=False):
         stage = self.stages[self.at]
         merge_in, merge_out = len(self.kept) == 1, len(stage) == 1
         ins = [v for pair in zip(self.kept, self.got) for v in pair]
         lead = 1 if merge_in else 0
         ins = [v.reshape(*v.shape[:lead], -1, *v.shape[-2:]) for v in ins]
         ins, _ = lax.optimization_barrier((ins, after))
-        outs = add_split(ins, merge_in, merge_out, arrived)
+        outs = add_split(ins, merge_in, merge_out, arrived, late)
         if merge_out:
             self.got, self.kept = [swap(outs[0], *stage[0])], [outs[1]]
         else:
@@ -1019,8 +1032,6 @@
                 (later,) = ordered(near[0], turned[other])
                 weights.append(near_blocks(later, near[0]))
             mixed, probs = attention_forward(rounded, (far_w, both_w), far_b, bias, 2, near)
-            (far_ws,) = ordered(mixed, [w[2] for w in weights[1:]])
-            both_ws = [swap(w, "head", bits_of("head")[0]) for w in far_ws]
         else:
             both_w = both_ws[layer - 1]
             all_bias = jnp.concatenate([near_bias[:, layer], far_bias[:, layer]])
@@ -1042,6 +1053,9 @@
         )
         kept.append((rounded, mixed, probs, u1, hr, gr, slope, u2))
         rounded, residual = low, u2
+        if layer == 0:
+            (far_ws,) = ordered(u2, [w[2] for w in weights[1:]])
+            both_ws = [swap(w, "head", bits_of("head")[0]) for w in far_ws]
     out_state = rounded
     grad_state = out_grad
     small_sums = [None] * layers
@@ -1049,7 +1063,7 @@
     ffn_groups, wide_groups = [None] * layers, [None] * layers
     running = []
 
-    def advance(after):
+    def advance(after, late=False):
         arrived = []
         for group in running:
             if not group.busy() and not group.settled:
@@ -1057,7 +1071,7 @@
                 group.settled = True
         for group in running:
             if group.busy():
-                after = group.step(after, arrived)
+                after = group.step(after, arrived, late)
                 arrived = []
         return after
 
@@ -1143,7 +1157,7 @@
     passing = [swap(small_sum, *one) for one in waiting.pop(0)]
     while any(not group.settled for group in running) or waiting:
         if any(group.busy() for group in running):
-            token = advance(token)
+            token = advance(token, True)
         elif not waiting:
             break
         if waiting:

time: 429 us -> 422 us (0.984)
  transfers between devices with their start and end apart: 43 -> 43, of which waited for: 16 -> 18; matrix products, arithmetic and copies ran while one was open for 2% -> 1% of each run, Pallas kernels for 52% -> 52%
where the time goes in v8:
time: 422 us; the launch traced here: 415 us
  Pallas kernels  310 us (73%)
  waiting for transfers between devices  48.6 us (12%)
  starting transfers between devices  41.1 us (10%)
  local copies, waits for them, and re-layouts  10.1 us (2%)
    pallas_call x14, Pallas kernels, call(): pl.pallas_call(kernel, grid_spec=pltpu.PrefetchScalarGridSpec(num_scalar_...  291 us
    ppermute x43, waiting for transfers between devices, swap(): return lax.ppermute(value, axis, [(i, i ^ bit) for i in range(size)])  48.6 us
    ppermute x43, starting transfers between devices, swap(): return lax.ppermute(value, axis, [(i, i ^ bit) for i in range(size)])  41.1 us
    pallas_call x12, Pallas kernels, add_split(): pl.pallas_call(functools.partial(add_split_kernel, merge_in=merge_in, mer...  14.7 us
  transfers between devices with their start and end apart: 43, of which 18 were waited for; matrix products, arithmetic and copies ran while one was open for 1% of the time, Pallas kernels for 52%

profile of v8, /device:TPU:0, one launch (start us, length us, event | category | flops | bytes accessed | tf_op | source)
XLA Modules:
  0.0 415.2 jit_solution(13955467005007152654)
XLA Ops:
  4.8 2.7 collective-permute-start.3
  7.5 4.4 %mask_bias.1.bias_ref = f32[2,512,512]{2,1,0:T(8,128)} custom-call(s32[1]{0:T(128)} %bitcast.4.base_ref, s32[8,32]{1,0:T(8,128)} %lengths_ref.1), custom_call_target="tpu_custom_call" | custom-call | tf_op jit(solution)/shard_map/mask_bias/pallas_call | solution.py:138
  13.7 14.7 %attention_forward.3 = (bf16[4,4,1024,192]{3,2,1,0:T(8,128)(2,1)}, bf16[4,2,3,512,512]{4,3,2,1,0:T(8,128)(2,1)}) custom-call(bf16[1024,768]{1,0:T(8,128)(2,1)} %x_ref.7, f32[2,2,1,192]{3,2,1,0:T(1,128)} %get-tuple-element.375.b_ref, f32[2,512,512]{2,1,0:T(8,128)} %mask_bias.1.bias_ref, bf16[576,768]{1,0:T(8,128)(2,1)} %bitcast.85, ...), custom_call_target="tpu_custom_call" | custom-call | flops 8254390272 | bytes 24316928 | tf_op jit(solution)/shard_map/attention_forward/pallas_call | solution.py:103
  28.6 6.0 %collective-permute-done.1.refs_0_.wb_ref = bf16[576,768]{1,0:T(8,128)(2,1)S(1)} collective-permute-done((bf16[576,768]{1,0:T(8,128)(2,1)S(1)}, bf16[576,768]{1,0:T(8,128)(2,1)S(1)}, u32[]{:S(2)}, u32[]{:S(2)}) %collective-permute-start.1) | collective-permute-done | bytes 884768 | tf_op jit(solution)/shard_map/ppermute | solution.py:797
  37.2 14.7 %attention_forward.4 = (bf16[4,4,1024,192]{3,2,1,0:T(8,128)(2,1)}, bf16[4,2,3,512,512]{4,3,2,1,0:T(8,128)(2,1)}) custom-call(bf16[1024,768]{1,0:T(8,128)(2,1)} %x_ref.7, f32[2,2,1,192]{3,2,1,0:T(1,128)} %get-tuple-element.187.b_ref, f32[2,512,512]{2,1,0:T(8,128)} %mask_bias.1.bias_ref, ...), custom_call_target="tpu_custom_call", output_to_operand_aliasing={{0}: (5, {}), {1}: (6, {})} | custom-call | flops 8254390272 | bytes 43191296 | tf_op jit(solution)/shard_map/attention_forward/pallas_call | solution.py:103
  51.9 25.1 %ffn_forward.2 = (f32[1024,768]{1,0:T(8,128)}, bf16[1024,768]{1,0:T(8,128)(2,1)}, bf16[4,1024,768]{2,1,0:T(8,128)(2,1)}, bf16[4,1024,768]{2,1,0:T(8,128)(2,1)}, ...) custom-call(s32[2]{0:T(128)} %pad_add_fusion.own_ref, ...), custom_call_target="tpu_custom_call" | custom-call | flops 32614907904 | bytes 51154944 | tf_op jit(solution)/shard_map/ffn_forward/pallas_call | solution.py:103
  80.5 25.3 %attention_forward.5 = (bf16[4,4,1024,192]{3,2,1,0:T(8,128)(2,1)}, bf16[4,2,3,512,512]{4,3,2,1,0:T(8,128)(2,1)}) custom-call(bf16[1024,768]{1,0:T(8,128)(2,1)} %get-tuple-element.191.x_ref, f32[4,2,1,192]{3,2,1,0:T(1,128)} %pad_maximum_fusion.7.b_ref, f32[2,512,512]{2,1,0:T(8,128)} %mask_bias.1.bias_ref, bf16[576,768]{1,0:T(8,128)(2,1)} %bitcast.89, ...), custom_call_target="tpu_custom_call" | custom-call | flops 16508780544 | bytes 26089472 | tf_op jit(solution)/shard_map/attention_forward/pallas_call | solution.py:103
  105.8 25.6 %ffn_forward.3 = (f32[1024,768]{1,0:T(8,128)}, bf16[1024,768]{1,0:T(8,128)(2,1)}, bf16[4,1024,768]{2,1,0:T(8,128)(2,1)}, bf16[4,1024,768]{2,1,0:T(8,128)(2,1)}, ...) custom-call(s32[2]{0:T(128)} %pad_add_fusion.own_ref, ...), custom_call_target="tpu_custom_call" | custom-call | flops 32614907904 | bytes 52727808 | tf_op jit(solution)/shard_map/ffn_forward/pallas_call | solution.py:103
  131.4 36.7 %ffn_backward.2 = (bf16[4,1024,192]{2,1,0:T(8,128)(2,1)}, bf16[4,1024,192]{2,1,0:T(8,128)(2,1)}, f32[1024,768]{1,0:T(8,128)}, f32[8,768]{1,0:T(8,128)}, f32[4,1,...) custom-call(s32[2]{0:T(128)} %pad_add_fusion.own_ref, ...), custom_call_target="tpu_custom_call" | custom-call | flops 41070624768 | bytes 59025408 | tf_op jit(solution)/shard_map/ffn_backward/pallas_call | solution.py:103
  168.3 24.8 %attention_backward.4 = (f32[1024,768]{1,0:T(8,128)}, f32[2,8,192]{2,1,0:T(8,128)}, bf16[2,2,4,96,768]{4,3,2,1,0:T(8,128)(2,1)}) custom-call(s32[2]{0:T(128)} %pad_add_fusion.own_ref, bf16[4,4,1024,192]{3,2,1,0:T(8,128)(2,1)} %get-tuple-element.196.mixed_hbm.mixed_ref.o_ref, bf16[4,1024,192]{2,1,0:T(8,128)(2,1)} %get-tuple-element.215.do_ref, ...), custom_call_target="tpu_custom_call" | custom-call | flops 14495514624 | bytes 40316928 | tf_op jit(solution)/shard_map/attention_backward/pallas_call | solution.py:103
  193.5 6.1 %core_add.2 = (bf16[2,4,96,768]{3,2,1,0:T(8,128)(2,1)}, bf16[2,4,96,768]{3,2,1,0:T(8,128)(2,1)}, bf16[2,4,96,768]{3,2,1,0:T(8,128)(2,1)}, bf16[2,4,96,768]{3,2,1,0:T(8,128)(2,1)}) custom-call(bf16[2,2,2,4,96,768]{5,4,3,2,1,0:T(8,128)(2,1)S(1)} %bitcast.65, bf16[2,2,2,4,96,768]{5,4,3,2,1,0:T(8,128)(2,1)} %collective-permute-done.9.got_ref), custom_call_target="tpu_custom_call" | custom-call | tf_op jit(solution)/shard_map/core_add/pallas_call | solution.py:103
  202.6 26.0 %attention_backward.5 = (f32[1024,768]{1,0:T(8,128)}, f32[2,8,192]{2,1,0:T(8,128)}, bf16[2,4,96,384]{3,2,1,0:T(8,128)(2,1)}, bf16[2,4,96,384]{3,2,1,0:T(8,128)(2...) custom-call(s32[2]{0:T(128)} %pad_add_fusion.own_ref, ...), custom_call_target="tpu_custom_call" | custom-call | flops 14495514624 | bytes 42676224 | tf_op jit(solution)/shard_map/attention_backward/pallas_call | solution.py:103
  235.0 36.7 %ffn_backward.3 = (bf16[4,1024,192]{2,1,0:T(8,128)(2,1)}, bf16[4,1024,192]{2,1,0:T(8,128)(2,1)}, f32[1024,768]{1,0:T(8,128)}, f32[8,768]{1,0:T(8,128)}, f32[4,1,...) custom-call(s32[2]{0:T(128)} %pad_add_fusion.own_ref, ...), custom_call_target="tpu_custom_call" | custom-call | flops 41070624768 | bytes 60598272 | tf_op jit(solution)/shard_map/ffn_backward/pallas_call | solution.py:103
  277.5 5.3 %collective-permute-done.17.got_ref = bf16[2,2,2,4,96,768]{5,4,3,2,1,0:T(8,128)(2,1)S(1)} collective-permute-done((bf16[2,2,2,4,96,768]{5,4,3,2,1,0:T(8,128)(2,1)}, bf16[2,2,2,4,96,768]{5,4,3,2,1,0:T(8,128)(2,1)S(1)}, u32[]{:S(2)}, u32[]{:S(2)}) %collective-permute-start.17) | collective-permute-done | bytes 4718624 | tf_op jit(solution)/shard_map/ppermute | solution.py:797
  282.8 3.7 core_add.3
  287.6 24.4 %attention_backward.6 = (f32[1024,768]{1,0:T(8,128)}, f32[2,8,192]{2,1,0:T(8,128)}, bf16[2,2,4,96,768]{4,3,2,1,0:T(8,128)(2,1)}) custom-call(s32[2]{0:T(128)} %pad_add_fusion.own_ref, bf16[4,4,1024,192]{3,2,1,0:T(8,128)(2,1)} %get-tuple-element.190.mixed_hbm.mixed_ref.o_ref, bf16[4,1024,192]{2,1,0:T(8,128)(2,1)} %get-tuple-element.282.do_ref, ...), custom_call_target="tpu_custom_call" | custom-call | flops 14495514624 | bytes 40316928 | tf_op jit(solution)/shard_map/attention_backward/pallas_call | solution.py:103
  312.0 2.7 collective-permute-done.21
  327.4 25.9 %attention_backward.7 = (bf16[1024,768]{1,0:T(8,128)(2,1)}, f32[2,8,192]{2,1,0:T(8,128)}, bf16[2,4,96,384]{3,2,1,0:T(8,128)(2,1)}, bf16[2,4,96,384]{3,2,1,0:T(8,...) custom-call(s32[2]{0:T(128)} %pad_add_fusion.own_ref, ...), custom_call_target="tpu_custom_call" | custom-call | flops 14495514624 | bytes 41103360 | tf_op jit(solution)/shard_map/attention_backward/pallas_call | solution.py:103
  360.0 8.2 %collective-permute-done.29 = bf16[2,4,96,384]{3,2,1,0:T(8,128)(2,1)S(1)} collective-permute-done((bf16[2,4,96,384]{3,2,1,0:T(8,128)(2,1)}, bf16[2,4,96,384]{3,2,1,0:T(8,128)(2,1)S(1)}, u32[]{:S(2)}, u32[]{:S(2)}) %collective-permute-start.29) | collective-permute-done | bytes 589856 | tf_op jit(solution)/shard_map/ppermute | solution.py:797
  382.2 2.9 collective-permute-start.33
  386.5 3.2 collective-permute-done.37
  390.4 3.4 collective-permute-done.36.refs_1_
  398.5 2.8 collective-permute-start.40
  402.7 7.0 %collective-permute-done.41 = f32[2,12,768]{2,1,0:T(8,128)S(1)} collective-permute-done((f32[2,12,768]{2,1,0:T(8,128)S(1)}, f32[2,12,768]{2,1,0:T(8,128)S(1)}, u32[]{:S(2)}, u32[]{:S(2)}) %collective-permute-start.41) | collective-permute-done | bytes 73760 | tf_op jit(solution)/shard_map/ppermute | solution.py:797
  (222 shorter events, 75.0 us)
Async XLA Ops:
  12.5 22.1 %collective-permute-start.1 = (bf16[576,768]{1,0:T(8,128)(2,1)S(1)}, bf16[576,768]{1,0:T(8,128)(2,1)S(1)}, u32[]{:S(2)}, u32[]{:S(2)}) collective-permute-start(bf16[576,768]{1,0:T(8,128)(2,1)S(1)} %bitcast.84), channel_id=1, source_target_pairs={{0,2},{1,3},{2,0},{3,1},{4,6},{5,7},{6,4},{7,5},{8,10},{9,11},{10,... | collective-permute-start | bytes 2654216 | tf_op jit(solution)/shard_map/ppermute | solution.py:797
  36.6 40.4 %collective-permute-start.7 = (bf16[576,768]{1,0:T(8,128)(2,1)S(1)}, bf16[576,768]{1,0:T(8,128)(2,1)S(1)}, u32[]{:S(2)}, u32[]{:S(2)}) collective-permute-start(bf16[576,768]{1,0:T(8,128)(2,1)S(1)} %bitcast.88), channel_id=1, source_target_pairs={{0,2},{1,3},{2,0},{3,1},{4,6},{5,7},{6,4},{7,5},{8,10},{9,11},{10,... | collective-permute-start | bytes 2654216 | tf_op jit(solution)/shard_map/ppermute | solution.py:797
  168.1 25.4 %collective-permute-start.9 = (bf16[2,2,2,4,96,768]{5,4,3,2,1,0:T(8,128)(2,1)}, bf16[2,2,2,4,96,768]{5,4,3,2,1,0:T(8,128)(2,1)}, u32[]{:S(2)}, u32[]{:S(2)}) collective-permute-start(bf16[2,2,2,4,96,768]{5,4,3,2,1,0:T(8,128)(2,1)} %get-tuple-element.211), channel_id=1, source_target_pairs={{0,1},{1,0},{2,3},{3,2},{4,5},{5,4},{6,7},{7,6},{8,9},{9,8},{10,11... | collective-permute-start | bytes 14155784 | tf_op jit(solution)/shard_map/ppermute | solution.py:797
  199.6 30.2 %collective-permute-start.11 = (bf16[2,4,96,768]{3,2,1,0:T(8,128)(2,1)}, bf16[2,4,96,768]{3,2,1,0:T(8,128)(2,1)S(1)}, u32[]{:S(2)}, u32[]{:S(2)}) collective-permute-start(bf16[2,4,96,768]{3,2,1,0:T(8,128)(2,1)} %get-tuple-element.219), channel_id=1, source_target_pairs={{0,2},{1,3},{2,0},{3,1},{4,6},{5,7},{6,4},{7,5},{8,10},{9,11},{10,... | collective-permute-start | bytes 3538952 | tf_op jit(solution)/shard_map/ppermute | solution.py:797
  201.1 28.7 %collective-permute-start.12 = (bf16[2,4,96,768]{3,2,1,0:T(8,128)(2,1)}, bf16[2,4,96,768]{3,2,1,0:T(8,128)(2,1)S(1)}, u32[]{:S(2)}, u32[]{:S(2)}) collective-permute-start(bf16[2,4,96,768]{3,2,1,0:T(8,128)(2,1)} %get-tuple-element.221), channel_id=1, source_target_pairs={{0,4},{4,0},{8,12},{12,8},{16,20},{20,16},{24,28},{28,24},{1,5},{5... | collective-permute-start | bytes 3538952 | tf_op jit(solution)/shard_map/ppermute | solution.py:797
  228.6 44.6 %collective-permute-start.13 = (bf16[2,4,96,384]{3,2,1,0:T(8,128)(2,1)}, bf16[2,4,96,384]{3,2,1,0:T(8,128)(2,1)S(1)}, u32[]{:S(2)}, u32[]{:S(2)}) collective-permute-start(bf16[2,4,96,384]{3,2,1,0:T(8,128)(2,1)} %get-tuple-element.237), channel_id=1, source_target_pairs={{0,2},{1,3},{2,0},{3,1},{4,6},{5,7},{6,4},{7,5},{8,10},{9,11},{10,... | collective-permute-start | bytes 1769480 | tf_op jit(solution)/shard_map/ppermute | solution.py:797
  229.2 44.0 %collective-permute-start.14 = (bf16[2,4,96,384]{3,2,1,0:T(8,128)(2,1)}, bf16[2,4,96,384]{3,2,1,0:T(8,128)(2,1)S(1)}, u32[]{:S(2)}, u32[]{:S(2)}) collective-permute-start(bf16[2,4,96,384]{3,2,1,0:T(8,128)(2,1)} %get-tuple-element.239), channel_id=1, source_target_pairs={{0,4},{4,0},{8,12},{12,8},{16,20},{20,16},{24,28},{28,24},{1,5},{5... | collective-permute-start | bytes 1769480 | tf_op jit(solution)/shard_map/ppermute | solution.py:797
  232.0 39.7 %collective-permute-start.15 = (bf16[4,96,768]{2,1,0:T(8,128)(2,1)}, bf16[4,96,768]{2,1,0:T(8,128)(2,1)S(1)}, u32[]{:S(2)}, u32[]{:S(2)}) collective-permute-start(bf16[4,96,768]{2,1,0:T(8,128)(2,1)} %get-tuple-element.241), channel_id=1, source_target_pairs={{0,4},{4,0},{8,12},{12,8},{16,20},{20,16},{24,28},{28,24},{1,5},{5... | collective-permute-start | bytes 1769480 | tf_op jit(solution)/shard_map/ppermute | solution.py:797
  233.5 38.2 %collective-permute-start.16 = (bf16[4,96,768]{2,1,0:T(8,128)(2,1)}, bf16[4,96,768]{2,1,0:T(8,128)(2,1)S(1)}, u32[]{:S(2)}, u32[]{:S(2)}) collective-permute-start(bf16[4,96,768]{2,1,0:T(8,128)(2,1)} %get-tuple-element.242), channel_id=1, source_target_pairs={{0,2},{1,3},{2,0},{3,1},{4,6},{5,7},{6,4},{7,5},{8,10},{9,11},{10,... | collective-permute-start | bytes 1769480 | tf_op jit(solution)/shard_map/ppermute | solution.py:797
  274.6 43.6 %collective-permute-start.18 = (bf16[4,96,384]{2,1,0:T(8,128)(2,1)}, bf16[4,96,384]{2,1,0:T(8,128)(2,1)S(1)}, u32[]{:S(2)}, u32[]{:S(2)}) collective-permute-start(bf16[4,96,384]{2,1,0:T(8,128)(2,1)} %get-tuple-element.263), channel_id=1, source_target_pairs={{0,4},{4,0},{8,12},{12,8},{16,20},{20,16},{24,28},{28,24},{1,5},{5... | collective-permute-start | bytes 884744 | tf_op jit(solution)/shard_map/ppermute | solution.py:797
  275.3 42.9 %collective-permute-start.19 = (bf16[4,96,384]{2,1,0:T(8,128)(2,1)}, bf16[4,96,384]{2,1,0:T(8,128)(2,1)S(1)}, u32[]{:S(2)}, u32[]{:S(2)}) collective-permute-start(bf16[4,96,384]{2,1,0:T(8,128)(2,1)} %get-tuple-element.264), channel_id=1, source_target_pairs={{0,2},{1,3},{2,0},{3,1},{4,6},{5,7},{6,4},{7,5},{8,10},{9,11},{10,... | collective-permute-start | bytes 884744 | tf_op jit(solution)/shard_map/ppermute | solution.py:797
  275.9 41.3 %collective-permute-start.20 = (bf16[2,2,96,768]{3,2,1,0:T(8,128)(2,1)}, bf16[2,2,96,768]{3,2,1,0:T(8,128)(2,1)S(1)}, u32[]{:S(2)}, u32[]{:S(2)}) collective-permute-start(bf16[2,2,96,768]{3,2,1,0:T(8,128)(2,1)} %get-tuple-element.265), channel_id=1, source_target_pairs={{0,8},{4,12},{8,0},{12,4},{16,24},{20,28},{24,16},{28,20},{1,9},{5... | collective-permute-start | bytes 1769480 | tf_op jit(solution)/shard_map/ppermute | solution.py:797
  286.5 28.2 %collective-permute-start.21 = (bf16[2,4,96,768]{3,2,1,0:T(8,128)(2,1)}, bf16[2,4,96,768]{3,2,1,0:T(8,128)(2,1)S(1)}, u32[]{:S(2)}, u32[]{:S(2)}) collective-permute-start(bf16[2,4,96,768]{3,2,1,0:T(8,128)(2,1)} %get-tuple-element.266), channel_id=1, source_target_pairs={{0,2},{1,3},{2,0},{3,1},{4,6},{5,7},{6,4},{7,5},{8,10},{9,11},{10,... | collective-permute-start | bytes 3538952 | tf_op jit(solution)/shard_map/ppermute | solution.py:797
  287.0 27.9 %collective-permute-start.22 = (bf16[2,4,96,768]{3,2,1,0:T(8,128)(2,1)}, bf16[2,4,96,768]{3,2,1,0:T(8,128)(2,1)S(1)}, u32[]{:S(2)}, u32[]{:S(2)}) collective-permute-start(bf16[2,4,96,768]{3,2,1,0:T(8,128)(2,1)} %get-tuple-element.268), channel_id=1, source_target_pairs={{0,4},{4,0},{8,12},{12,8},{16,20},{20,16},{24,28},{28,24},{1,5},{5... | collective-permute-start | bytes 3538952 | tf_op jit(solution)/shard_map/ppermute | solution.py:797
  319.6 34.4 %collective-permute-start.24 = (bf16[4,96,768]{2,1,0:T(8,128)(2,1)}, bf16[4,96,768]{2,1,0:T(8,128)(2,1)S(1)}, u32[]{:S(2)}, u32[]{:S(2)}) collective-permute-start(bf16[4,96,768]{2,1,0:T(8,128)(2,1)} %get-tuple-element.288), channel_id=1, source_target_pairs={{0,4},{4,0},{8,12},{12,8},{16,20},{20,16},{24,28},{28,24},{1,5},{5... | collective-permute-start | bytes 1769480 | tf_op jit(solution)/shard_map/ppermute | solution.py:797
  320.3 35.1 %collective-permute-start.25 = (bf16[4,96,768]{2,1,0:T(8,128)(2,1)S(1)}, bf16[4,96,768]{2,1,0:T(8,128)(2,1)S(1)}, u32[]{:S(2)}, u32[]{:S(2)}) collective-permute-start(bf16[4,96,768]{2,1,0:T(8,128)(2,1)S(1)} %copy-done.47), channel_id=1, source_target_pairs={{0,2},{1,3},{2,0},{3,1},{4,6},{5,7},{6,4},{7,5},{8,10},{9,11},{10,... | collective-permute-start | bytes 1769480 | tf_op jit(solution)/shard_map/ppermute | solution.py:797
  321.8 33.6 %collective-permute-start.26 = (bf16[2,1,96,768]{3,2,1,0:T(8,128)(2,1)}, bf16[2,1,96,768]{3,2,1,0:T(8,128)(2,1)S(1)}, u32[]{:S(2)}, u32[]{:S(2)}) collective-permute-start(bf16[2,1,96,768]{3,2,1,0:T(8,128)(2,1)} %get-tuple-element.294), channel_id=1, source_target_pairs={{0,16},{4,20},{8,24},{12,28},{16,0},{20,4},{24,8},{28,12},{1,17},{... | collective-permute-start | bytes 884744 | tf_op jit(solution)/shard_map/ppermute | solution.py:797
  324.4 32.7 %collective-permute-start.31 = (bf16[2,2,96,384]{3,2,1,0:T(8,128)(2,1)}, bf16[2,2,96,384]{3,2,1,0:T(8,128)(2,1)S(1)}, u32[]{:S(2)}, u32[]{:S(2)}) collective-permute-start(bf16[2,2,96,384]{3,2,1,0:T(8,128)(2,1)} %get-tuple-element.309), channel_id=1, source_target_pairs={{0,8},{4,12},{8,0},{12,4},{16,24},{20,28},{24,16},{28,20},{1,9},{5... | collective-permute-start | bytes 884744 | tf_op jit(solution)/shard_map/ppermute | solution.py:797
  353.3 14.8 %collective-permute-start.29 = (bf16[2,4,96,384]{3,2,1,0:T(8,128)(2,1)}, bf16[2,4,96,384]{3,2,1,0:T(8,128)(2,1)S(1)}, u32[]{:S(2)}, u32[]{:S(2)}) collective-permute-start(bf16[2,4,96,384]{3,2,1,0:T(8,128)(2,1)} %get-tuple-element.306), channel_id=1, source_target_pairs={{0,2},{1,3},{2,0},{3,1},{4,6},{5,7},{6,4},{7,5},{8,10},{9,11},{10,... | collective-permute-start | bytes 1769480 | tf_op jit(solution)/shard_map/ppermute | solution.py:797
  353.9 14.5 %collective-permute-start.30 = (bf16[2,4,96,384]{3,2,1,0:T(8,128)(2,1)}, bf16[2,4,96,384]{3,2,1,0:T(8,128)(2,1)S(1)}, u32[]{:S(2)}, u32[]{:S(2)}) collective-permute-start(bf16[2,4,96,384]{3,2,1,0:T(8,128)(2,1)} %get-tuple-element.308), channel_id=1, source_target_pairs={{0,4},{4,0},{8,12},{12,8},{16,20},{20,16},{24,28},{28,24},{1,5},{5... | collective-permute-start | bytes 1769480 | tf_op jit(solution)/shard_map/ppermute | solution.py:797
  356.5 17.5 %collective-permute-start.27 = (bf16[2,2,96,768]{3,2,1,0:T(8,128)(2,1)}, bf16[2,2,96,768]{3,2,1,0:T(8,128)(2,1)S(1)}, u32[]{:S(2)}, u32[]{:S(2)}) collective-permute-start(bf16[2,2,96,768]{3,2,1,0:T(8,128)(2,1)} %get-tuple-element.296), channel_id=1, source_target_pairs={{0,8},{4,12},{8,0},{12,4},{16,24},{20,28},{24,16},{28,20},{1,9},{5... | collective-permute-start | bytes 1769480 | tf_op jit(solution)/shard_map/ppermute | solution.py:797
  357.9 16.2 %collective-permute-start.32 = (bf16[2,1,96,384]{3,2,1,0:T(8,128)(2,1)}, bf16[2,1,96,384]{3,2,1,0:T(8,128)(2,1)S(1)}, u32[]{:S(2)}, u32[]{:S(2)}) collective-permute-start(bf16[2,1,96,384]{3,2,1,0:T(8,128)(2,1)} %get-tuple-element.322), channel_id=1, source_target_pairs={{0,16},{4,20},{8,24},{12,28},{16,0},{20,4},{24,8},{28,12},{1,17},{... | collective-permute-start | bytes 442376 | tf_op jit(solution)/shard_map/ppermute | solution.py:797
  380.9 12.9 %collective-permute-start.36 = (bf16[2,2,96,384]{3,2,1,0:T(8,128)(2,1)}, bf16[2,2,96,384]{3,2,1,0:T(8,128)(2,1)S(1)}, u32[]{:S(2)}, u32[]{:S(2)}) collective-permute-start(bf16[2,2,96,384]{3,2,1,0:T(8,128)(2,1)} %get-tuple-element.333), channel_id=1, source_target_pairs={{0,8},{4,12},{8,0},{12,4},{16,24},{20,28},{24,16},{28,20},{1,9},{5... | collective-permute-start | bytes 884744 | tf_op jit(solution)/shard_map/ppermute | solution.py:797
  382.2 14.1 %collective-permute-start.33 = (bf16[2,1,96,768]{3,2,1,0:T(8,128)(2,1)}, bf16[2,1,96,768]{3,2,1,0:T(8,128)(2,1)S(1)}, u32[]{:S(2)}, u32[]{:S(2)}) collective-permute-start(bf16[2,1,96,768]{3,2,1,0:T(8,128)(2,1)} %get-tuple-element.324), channel_id=1, source_target_pairs={{0,16},{4,20},{8,24},{12,28},{16,0},{20,4},{24,8},{28,12},{1,17},{... | collective-permute-start | bytes 884744 | tf_op jit(solution)/shard_map/ppermute | solution.py:797
  (69 other events, 875.8 us)

commit v9 on v8

--- a/solution.py
+++ b/solution.py
@@ -313,7 +313,7 @@
                 copy.wait()
 
 
-def ffn_forward(own, mixed, x, wo, wu, wd, bu, small, layer, renorm, tile=512):
+def ffn_forward(own, mixed, x, wo, wu, wd, bu, small, layer, renorm, tile=1024):
     _, _, rows, part = mixed.shape
     width, hidden = wu.shape[1:]
     chunks = hidden // width

time: 422 us -> 416 us (0.986)
  no operation moved by 1% of the time
where the time goes in v9:
time: 416 us; the launch traced here: 413 us
  Pallas kernels  309 us (74%)
  waiting for transfers between devices  48.4 us (12%)
  starting transfers between devices  41.1 us (10%)
  local copies, waits for them, and re-layouts  10.1 us (2%)
    pallas_call x14, Pallas kernels, call(): pl.pallas_call(kernel, grid_spec=pltpu.PrefetchScalarGridSpec(num_scalar_...  289 us
    ppermute x43, waiting for transfers between devices, swap(): return lax.ppermute(value, axis, [(i, i ^ bit) for i in range(size)])  48.4 us
    ppermute x43, starting transfers between devices, swap(): return lax.ppermute(value, axis, [(i, i ^ bit) for i in range(size)])  41.1 us
    pallas_call x12, Pallas kernels, add_split(): pl.pallas_call(functools.partial(add_split_kernel, merge_in=merge_in, mer...  14.7 us
  transfers between devices with their start and end apart: 43, of which 18 were waited for; matrix products, arithmetic and copies ran while one was open for 1% of the time, Pallas kernels for 52%

profile of v9, /device:TPU:0, one launch (start us, length us, event | category | flops | bytes accessed | tf_op | source)
XLA Modules:
  0.0 413.1 jit_solution(13613200397479456736)
XLA Ops:
  4.8 2.7 collective-permute-start.3
  7.5 4.4 %mask_bias.1.bias_ref = f32[2,512,512]{2,1,0:T(8,128)} custom-call(s32[1]{0:T(128)} %bitcast.4.base_ref, s32[8,32]{1,0:T(8,128)} %lengths_ref.1), custom_call_target="tpu_custom_call" | custom-call | tf_op jit(solution)/shard_map/mask_bias/pallas_call | solution.py:138
  13.7 15.0 %attention_forward.3 = (bf16[4,4,1024,192]{3,2,1,0:T(8,128)(2,1)}, bf16[4,2,3,512,512]{4,3,2,1,0:T(8,128)(2,1)}) custom-call(bf16[1024,768]{1,0:T(8,128)(2,1)} %x_ref.7, f32[2,2,1,192]{3,2,1,0:T(1,128)} %get-tuple-element.375.b_ref, f32[2,512,512]{2,1,0:T(8,128)} %mask_bias.1.bias_ref, bf16[576,768]{1,0:T(8,128)(2,1)} %bitcast.85, ...), custom_call_target="tpu_custom_call" | custom-call | flops 8254390272 | bytes 24316928 | tf_op jit(solution)/shard_map/attention_forward/pallas_call | solution.py:103
  28.9 5.7 %collective-permute-done.1.refs_0_.wb_ref = bf16[576,768]{1,0:T(8,128)(2,1)S(1)} collective-permute-done((bf16[576,768]{1,0:T(8,128)(2,1)S(1)}, bf16[576,768]{1,0:T(8,128)(2,1)S(1)}, u32[]{:S(2)}, u32[]{:S(2)}) %collective-permute-start.1) | collective-permute-done | bytes 884768 | tf_op jit(solution)/shard_map/ppermute | solution.py:797
  37.2 14.7 %attention_forward.4 = (bf16[4,4,1024,192]{3,2,1,0:T(8,128)(2,1)}, bf16[4,2,3,512,512]{4,3,2,1,0:T(8,128)(2,1)}) custom-call(bf16[1024,768]{1,0:T(8,128)(2,1)} %x_ref.7, f32[2,2,1,192]{3,2,1,0:T(1,128)} %get-tuple-element.187.b_ref, f32[2,512,512]{2,1,0:T(8,128)} %mask_bias.1.bias_ref, ...), custom_call_target="tpu_custom_call", output_to_operand_aliasing={{0}: (5, {}), {1}: (6, {})} | custom-call | flops 8254390272 | bytes 43191296 | tf_op jit(solution)/shard_map/attention_forward/pallas_call | solution.py:103
  51.9 23.7 %ffn_forward.2 = (f32[1024,768]{1,0:T(8,128)}, bf16[1024,768]{1,0:T(8,128)(2,1)}, bf16[4,1024,768]{2,1,0:T(8,128)(2,1)}, bf16[4,1024,768]{2,1,0:T(8,128)(2,1)}, ...) custom-call(s32[2]{0:T(128)} %pad_add_fusion.own_ref, ...), custom_call_target="tpu_custom_call" | custom-call | flops 32614907904 | bytes 51154944 | tf_op jit(solution)/shard_map/ffn_forward/pallas_call | solution.py:103
  79.1 25.8 %attention_forward.5 = (bf16[4,4,1024,192]{3,2,1,0:T(8,128)(2,1)}, bf16[4,2,3,512,512]{4,3,2,1,0:T(8,128)(2,1)}) custom-call(bf16[1024,768]{1,0:T(8,128)(2,1)} %get-tuple-element.191.x_ref, f32[4,2,1,192]{3,2,1,0:T(1,128)} %pad_maximum_fusion.7.b_ref, f32[2,512,512]{2,1,0:T(8,128)} %mask_bias.1.bias_ref, bf16[576,768]{1,0:T(8,128)(2,1)} %bitcast.89, ...), custom_call_target="tpu_custom_call" | custom-call | flops 16508780544 | bytes 26089472 | tf_op jit(solution)/shard_map/attention_forward/pallas_call | solution.py:103
  104.9 24.5 %ffn_forward.3 = (f32[1024,768]{1,0:T(8,128)}, bf16[1024,768]{1,0:T(8,128)(2,1)}, bf16[4,1024,768]{2,1,0:T(8,128)(2,1)}, bf16[4,1024,768]{2,1,0:T(8,128)(2,1)}, ...) custom-call(s32[2]{0:T(128)} %pad_add_fusion.own_ref, ...), custom_call_target="tpu_custom_call" | custom-call | flops 32614907904 | bytes 52727808 | tf_op jit(solution)/shard_map/ffn_forward/pallas_call | solution.py:103
  129.4 36.7 %ffn_backward.2 = (bf16[4,1024,192]{2,1,0:T(8,128)(2,1)}, bf16[4,1024,192]{2,1,0:T(8,128)(2,1)}, f32[1024,768]{1,0:T(8,128)}, f32[8,768]{1,0:T(8,128)}, f32[4,1,...) custom-call(s32[2]{0:T(128)} %pad_add_fusion.own_ref, ...), custom_call_target="tpu_custom_call" | custom-call | flops 41070624768 | bytes 59025408 | tf_op jit(solution)/shard_map/ffn_backward/pallas_call | solution.py:103
  166.3 24.8 %attention_backward.4 = (f32[1024,768]{1,0:T(8,128)}, f32[2,8,192]{2,1,0:T(8,128)}, bf16[2,2,4,96,768]{4,3,2,1,0:T(8,128)(2,1)}) custom-call(s32[2]{0:T(128)} %pad_add_fusion.own_ref, bf16[4,4,1024,192]{3,2,1,0:T(8,128)(2,1)} %get-tuple-element.196.mixed_hbm.mixed_ref.o_ref, bf16[4,1024,192]{2,1,0:T(8,128)(2,1)} %get-tuple-element.215.do_ref, ...), custom_call_target="tpu_custom_call" | custom-call | flops 14495514624 | bytes 40316928 | tf_op jit(solution)/shard_map/attention_backward/pallas_call | solution.py:103
  191.5 6.1 %core_add.2 = (bf16[2,4,96,768]{3,2,1,0:T(8,128)(2,1)}, bf16[2,4,96,768]{3,2,1,0:T(8,128)(2,1)}, bf16[2,4,96,768]{3,2,1,0:T(8,128)(2,1)}, bf16[2,4,96,768]{3,2,1,0:T(8,128)(2,1)}) custom-call(bf16[2,2,2,4,96,768]{5,4,3,2,1,0:T(8,128)(2,1)S(1)} %bitcast.65, bf16[2,2,2,4,96,768]{5,4,3,2,1,0:T(8,128)(2,1)} %collective-permute-done.9.got_ref), custom_call_target="tpu_custom_call" | custom-call | tf_op jit(solution)/shard_map/core_add/pallas_call | solution.py:103
  200.7 26.0 %attention_backward.5 = (f32[1024,768]{1,0:T(8,128)}, f32[2,8,192]{2,1,0:T(8,128)}, bf16[2,4,96,384]{3,2,1,0:T(8,128)(2,1)}, bf16[2,4,96,384]{3,2,1,0:T(8,128)(2...) custom-call(s32[2]{0:T(128)} %pad_add_fusion.own_ref, ...), custom_call_target="tpu_custom_call" | custom-call | flops 14495514624 | bytes 42676224 | tf_op jit(solution)/shard_map/attention_backward/pallas_call | solution.py:103
  233.0 36.7 %ffn_backward.3 = (bf16[4,1024,192]{2,1,0:T(8,128)(2,1)}, bf16[4,1024,192]{2,1,0:T(8,128)(2,1)}, f32[1024,768]{1,0:T(8,128)}, f32[8,768]{1,0:T(8,128)}, f32[4,1,...) custom-call(s32[2]{0:T(128)} %pad_add_fusion.own_ref, ...), custom_call_target="tpu_custom_call" | custom-call | flops 41070624768 | bytes 60598272 | tf_op jit(solution)/shard_map/ffn_backward/pallas_call | solution.py:103
  275.5 5.3 %collective-permute-done.17.got_ref = bf16[2,2,2,4,96,768]{5,4,3,2,1,0:T(8,128)(2,1)S(1)} collective-permute-done((bf16[2,2,2,4,96,768]{5,4,3,2,1,0:T(8,128)(2,1)}, bf16[2,2,2,4,96,768]{5,4,3,2,1,0:T(8,128)(2,1)S(1)}, u32[]{:S(2)}, u32[]{:S(2)}) %collective-permute-start.17) | collective-permute-done | bytes 4718624 | tf_op jit(solution)/shard_map/ppermute | solution.py:797
  280.8 3.7 core_add.3
  285.7 24.4 %attention_backward.6 = (f32[1024,768]{1,0:T(8,128)}, f32[2,8,192]{2,1,0:T(8,128)}, bf16[2,2,4,96,768]{4,3,2,1,0:T(8,128)(2,1)}) custom-call(s32[2]{0:T(128)} %pad_add_fusion.own_ref, bf16[4,4,1024,192]{3,2,1,0:T(8,128)(2,1)} %get-tuple-element.190.mixed_hbm.mixed_ref.o_ref, bf16[4,1024,192]{2,1,0:T(8,128)(2,1)} %get-tuple-element.282.do_ref, ...), custom_call_target="tpu_custom_call" | custom-call | flops 14495514624 | bytes 40316928 | tf_op jit(solution)/shard_map/attention_backward/pallas_call | solution.py:103
  310.0 2.7 collective-permute-done.21
  325.4 25.9 %attention_backward.7 = (bf16[1024,768]{1,0:T(8,128)(2,1)}, f32[2,8,192]{2,1,0:T(8,128)}, bf16[2,4,96,384]{3,2,1,0:T(8,128)(2,1)}, bf16[2,4,96,384]{3,2,1,0:T(8,...) custom-call(s32[2]{0:T(128)} %pad_add_fusion.own_ref, ...), custom_call_target="tpu_custom_call" | custom-call | flops 14495514624 | bytes 41103360 | tf_op jit(solution)/shard_map/attention_backward/pallas_call | solution.py:103
  358.0 8.2 %collective-permute-done.29 = bf16[2,4,96,384]{3,2,1,0:T(8,128)(2,1)S(1)} collective-permute-done((bf16[2,4,96,384]{3,2,1,0:T(8,128)(2,1)}, bf16[2,4,96,384]{3,2,1,0:T(8,128)(2,1)S(1)}, u32[]{:S(2)}, u32[]{:S(2)}) %collective-permute-start.29) | collective-permute-done | bytes 589856 | tf_op jit(solution)/shard_map/ppermute | solution.py:797
  380.2 2.9 collective-permute-start.33
  384.5 3.2 collective-permute-done.37
  388.4 3.4 collective-permute-done.36.refs_1_
  396.5 2.8 collective-permute-start.40
  400.8 7.1 %collective-permute-done.41 = f32[2,12,768]{2,1,0:T(8,128)S(1)} collective-permute-done((f32[2,12,768]{2,1,0:T(8,128)S(1)}, f32[2,12,768]{2,1,0:T(8,128)S(1)}, u32[]{:S(2)}, u32[]{:S(2)}) %collective-permute-start.41) | collective-permute-done | bytes 73760 | tf_op jit(solution)/shard_map/ppermute | solution.py:797
  (222 shorter events, 75.0 us)
Async XLA Ops:
  12.5 22.1 %collective-permute-start.1 = (bf16[576,768]{1,0:T(8,128)(2,1)S(1)}, bf16[576,768]{1,0:T(8,128)(2,1)S(1)}, u32[]{:S(2)}, u32[]{:S(2)}) collective-permute-start(bf16[576,768]{1,0:T(8,128)(2,1)S(1)} %bitcast.84), channel_id=1, source_target_pairs={{0,2},{1,3},{2,0},{3,1},{4,6},{5,7},{6,4},{7,5},{8,10},{9,11},{10,... | collective-permute-start | bytes 2654216 | tf_op jit(solution)/shard_map/ppermute | solution.py:797
  36.6 39.0 %collective-permute-start.7 = (bf16[576,768]{1,0:T(8,128)(2,1)S(1)}, bf16[576,768]{1,0:T(8,128)(2,1)S(1)}, u32[]{:S(2)}, u32[]{:S(2)}) collective-permute-start(bf16[576,768]{1,0:T(8,128)(2,1)S(1)} %bitcast.88), channel_id=1, source_target_pairs={{0,2},{1,3},{2,0},{3,1},{4,6},{5,7},{6,4},{7,5},{8,10},{9,11},{10,... | collective-permute-start | bytes 2654216 | tf_op jit(solution)/shard_map/ppermute | solution.py:797
  166.1 25.4 %collective-permute-start.9 = (bf16[2,2,2,4,96,768]{5,4,3,2,1,0:T(8,128)(2,1)}, bf16[2,2,2,4,96,768]{5,4,3,2,1,0:T(8,128)(2,1)}, u32[]{:S(2)}, u32[]{:S(2)}) collective-permute-start(bf16[2,2,2,4,96,768]{5,4,3,2,1,0:T(8,128)(2,1)} %get-tuple-element.211), channel_id=1, source_target_pairs={{0,1},{1,0},{2,3},{3,2},{4,5},{5,4},{6,7},{7,6},{8,9},{9,8},{10,11... | collective-permute-start | bytes 14155784 | tf_op jit(solution)/shard_map/ppermute | solution.py:797
  197.6 30.2 %collective-permute-start.11 = (bf16[2,4,96,768]{3,2,1,0:T(8,128)(2,1)}, bf16[2,4,96,768]{3,2,1,0:T(8,128)(2,1)S(1)}, u32[]{:S(2)}, u32[]{:S(2)}) collective-permute-start(bf16[2,4,96,768]{3,2,1,0:T(8,128)(2,1)} %get-tuple-element.219), channel_id=1, source_target_pairs={{0,2},{1,3},{2,0},{3,1},{4,6},{5,7},{6,4},{7,5},{8,10},{9,11},{10,... | collective-permute-start | bytes 3538952 | tf_op jit(solution)/shard_map/ppermute | solution.py:797
  199.1 28.7 %collective-permute-start.12 = (bf16[2,4,96,768]{3,2,1,0:T(8,128)(2,1)}, bf16[2,4,96,768]{3,2,1,0:T(8,128)(2,1)S(1)}, u32[]{:S(2)}, u32[]{:S(2)}) collective-permute-start(bf16[2,4,96,768]{3,2,1,0:T(8,128)(2,1)} %get-tuple-element.221), channel_id=1, source_target_pairs={{0,4},{4,0},{8,12},{12,8},{16,20},{20,16},{24,28},{28,24},{1,5},{5... | collective-permute-start | bytes 3538952 | tf_op jit(solution)/shard_map/ppermute | solution.py:797
  226.6 44.6 %collective-permute-start.13 = (bf16[2,4,96,384]{3,2,1,0:T(8,128)(2,1)}, bf16[2,4,96,384]{3,2,1,0:T(8,128)(2,1)S(1)}, u32[]{:S(2)}, u32[]{:S(2)}) collective-permute-start(bf16[2,4,96,384]{3,2,1,0:T(8,128)(2,1)} %get-tuple-element.237), channel_id=1, source_target_pairs={{0,2},{1,3},{2,0},{3,1},{4,6},{5,7},{6,4},{7,5},{8,10},{9,11},{10,... | collective-permute-start | bytes 1769480 | tf_op jit(solution)/shard_map/ppermute | solution.py:797
  227.2 44.0 %collective-permute-start.14 = (bf16[2,4,96,384]{3,2,1,0:T(8,128)(2,1)}, bf16[2,4,96,384]{3,2,1,0:T(8,128)(2,1)S(1)}, u32[]{:S(2)}, u32[]{:S(2)}) collective-permute-start(bf16[2,4,96,384]{3,2,1,0:T(8,128)(2,1)} %get-tuple-element.239), channel_id=1, source_target_pairs={{0,4},{4,0},{8,12},{12,8},{16,20},{20,16},{24,28},{28,24},{1,5},{5... | collective-permute-start | bytes 1769480 | tf_op jit(solution)/shard_map/ppermute | solution.py:797
  230.1 39.7 %collective-permute-start.15 = (bf16[4,96,768]{2,1,0:T(8,128)(2,1)}, bf16[4,96,768]{2,1,0:T(8,128)(2,1)S(1)}, u32[]{:S(2)}, u32[]{:S(2)}) collective-permute-start(bf16[4,96,768]{2,1,0:T(8,128)(2,1)} %get-tuple-element.241), channel_id=1, source_target_pairs={{0,4},{4,0},{8,12},{12,8},{16,20},{20,16},{24,28},{28,24},{1,5},{5... | collective-permute-start | bytes 1769480 | tf_op jit(solution)/shard_map/ppermute | solution.py:797
  231.5 38.2 %collective-permute-start.16 = (bf16[4,96,768]{2,1,0:T(8,128)(2,1)}, bf16[4,96,768]{2,1,0:T(8,128)(2,1)S(1)}, u32[]{:S(2)}, u32[]{:S(2)}) collective-permute-start(bf16[4,96,768]{2,1,0:T(8,128)(2,1)} %get-tuple-element.242), channel_id=1, source_target_pairs={{0,2},{1,3},{2,0},{3,1},{4,6},{5,7},{6,4},{7,5},{8,10},{9,11},{10,... | collective-permute-start | bytes 1769480 | tf_op jit(solution)/shard_map/ppermute | solution.py:797
  272.7 43.6 %collective-permute-start.18 = (bf16[4,96,384]{2,1,0:T(8,128)(2,1)}, bf16[4,96,384]{2,1,0:T(8,128)(2,1)S(1)}, u32[]{:S(2)}, u32[]{:S(2)}) collective-permute-start(bf16[4,96,384]{2,1,0:T(8,128)(2,1)} %get-tuple-element.263), channel_id=1, source_target_pairs={{0,4},{4,0},{8,12},{12,8},{16,20},{20,16},{24,28},{28,24},{1,5},{5... | collective-permute-start | bytes 884744 | tf_op jit(solution)/shard_map/ppermute | solution.py:797
  273.4 42.9 %collective-permute-start.19 = (bf16[4,96,384]{2,1,0:T(8,128)(2,1)}, bf16[4,96,384]{2,1,0:T(8,128)(2,1)S(1)}, u32[]{:S(2)}, u32[]{:S(2)}) collective-permute-start(bf16[4,96,384]{2,1,0:T(8,128)(2,1)} %get-tuple-element.264), channel_id=1, source_target_pairs={{0,2},{1,3},{2,0},{3,1},{4,6},{5,7},{6,4},{7,5},{8,10},{9,11},{10,... | collective-permute-start | bytes 884744 | tf_op jit(solution)/shard_map/ppermute | solution.py:797
  273.9 41.3 %collective-permute-start.20 = (bf16[2,2,96,768]{3,2,1,0:T(8,128)(2,1)}, bf16[2,2,96,768]{3,2,1,0:T(8,128)(2,1)S(1)}, u32[]{:S(2)}, u32[]{:S(2)}) collective-permute-start(bf16[2,2,96,768]{3,2,1,0:T(8,128)(2,1)} %get-tuple-element.265), channel_id=1, source_target_pairs={{0,8},{4,12},{8,0},{12,4},{16,24},{20,28},{24,16},{28,20},{1,9},{5... | collective-permute-start | bytes 1769480 | tf_op jit(solution)/shard_map/ppermute | solution.py:797
  284.5 28.2 %collective-permute-start.21 = (bf16[2,4,96,768]{3,2,1,0:T(8,128)(2,1)}, bf16[2,4,96,768]{3,2,1,0:T(8,128)(2,1)S(1)}, u32[]{:S(2)}, u32[]{:S(2)}) collective-permute-start(bf16[2,4,96,768]{3,2,1,0:T(8,128)(2,1)} %get-tuple-element.266), channel_id=1, source_target_pairs={{0,2},{1,3},{2,0},{3,1},{4,6},{5,7},{6,4},{7,5},{8,10},{9,11},{10,... | collective-permute-start | bytes 3538952 | tf_op jit(solution)/shard_map/ppermute | solution.py:797
  285.1 27.9 %collective-permute-start.22 = (bf16[2,4,96,768]{3,2,1,0:T(8,128)(2,1)}, bf16[2,4,96,768]{3,2,1,0:T(8,128)(2,1)S(1)}, u32[]{:S(2)}, u32[]{:S(2)}) collective-permute-start(bf16[2,4,96,768]{3,2,1,0:T(8,128)(2,1)} %get-tuple-element.268), channel_id=1, source_target_pairs={{0,4},{4,0},{8,12},{12,8},{16,20},{20,16},{24,28},{28,24},{1,5},{5... | collective-permute-start | bytes 3538952 | tf_op jit(solution)/shard_map/ppermute | solution.py:797
  317.6 34.4 %collective-permute-start.24 = (bf16[4,96,768]{2,1,0:T(8,128)(2,1)}, bf16[4,96,768]{2,1,0:T(8,128)(2,1)S(1)}, u32[]{:S(2)}, u32[]{:S(2)}) collective-permute-start(bf16[4,96,768]{2,1,0:T(8,128)(2,1)} %get-tuple-element.288), channel_id=1, source_target_pairs={{0,4},{4,0},{8,12},{12,8},{16,20},{20,16},{24,28},{28,24},{1,5},{5... | collective-permute-start | bytes 1769480 | tf_op jit(solution)/shard_map/ppermute | solution.py:797
  318.3 35.1 %collective-permute-start.25 = (bf16[4,96,768]{2,1,0:T(8,128)(2,1)S(1)}, bf16[4,96,768]{2,1,0:T(8,128)(2,1)S(1)}, u32[]{:S(2)}, u32[]{:S(2)}) collective-permute-start(bf16[4,96,768]{2,1,0:T(8,128)(2,1)S(1)} %copy-done.47), channel_id=1, source_target_pairs={{0,2},{1,3},{2,0},{3,1},{4,6},{5,7},{6,4},{7,5},{8,10},{9,11},{10,... | collective-permute-start | bytes 1769480 | tf_op jit(solution)/shard_map/ppermute | solution.py:797
  319.8 33.6 %collective-permute-start.26 = (bf16[2,1,96,768]{3,2,1,0:T(8,128)(2,1)}, bf16[2,1,96,768]{3,2,1,0:T(8,128)(2,1)S(1)}, u32[]{:S(2)}, u32[]{:S(2)}) collective-permute-start(bf16[2,1,96,768]{3,2,1,0:T(8,128)(2,1)} %get-tuple-element.294), channel_id=1, source_target_pairs={{0,16},{4,20},{8,24},{12,28},{16,0},{20,4},{24,8},{28,12},{1,17},{... | collective-permute-start | bytes 884744 | tf_op jit(solution)/shard_map/ppermute | solution.py:797
  322.4 32.7 %collective-permute-start.31 = (bf16[2,2,96,384]{3,2,1,0:T(8,128)(2,1)}, bf16[2,2,96,384]{3,2,1,0:T(8,128)(2,1)S(1)}, u32[]{:S(2)}, u32[]{:S(2)}) collective-permute-start(bf16[2,2,96,384]{3,2,1,0:T(8,128)(2,1)} %get-tuple-element.309), channel_id=1, source_target_pairs={{0,8},{4,12},{8,0},{12,4},{16,24},{20,28},{24,16},{28,20},{1,9},{5... | collective-permute-start | bytes 884744 | tf_op jit(solution)/shard_map/ppermute | solution.py:797
  351.4 14.8 %collective-permute-start.29 = (bf16[2,4,96,384]{3,2,1,0:T(8,128)(2,1)}, bf16[2,4,96,384]{3,2,1,0:T(8,128)(2,1)S(1)}, u32[]{:S(2)}, u32[]{:S(2)}) collective-permute-start(bf16[2,4,96,384]{3,2,1,0:T(8,128)(2,1)} %get-tuple-element.306), channel_id=1, source_target_pairs={{0,2},{1,3},{2,0},{3,1},{4,6},{5,7},{6,4},{7,5},{8,10},{9,11},{10,... | collective-permute-start | bytes 1769480 | tf_op jit(solution)/shard_map/ppermute | solution.py:797
  352.0 14.5 %collective-permute-start.30 = (bf16[2,4,96,384]{3,2,1,0:T(8,128)(2,1)}, bf16[2,4,96,384]{3,2,1,0:T(8,128)(2,1)S(1)}, u32[]{:S(2)}, u32[]{:S(2)}) collective-permute-start(bf16[2,4,96,384]{3,2,1,0:T(8,128)(2,1)} %get-tuple-element.308), channel_id=1, source_target_pairs={{0,4},{4,0},{8,12},{12,8},{16,20},{20,16},{24,28},{28,24},{1,5},{5... | collective-permute-start | bytes 1769480 | tf_op jit(solution)/shard_map/ppermute | solution.py:797
  354.6 17.5 %collective-permute-start.27 = (bf16[2,2,96,768]{3,2,1,0:T(8,128)(2,1)}, bf16[2,2,96,768]{3,2,1,0:T(8,128)(2,1)S(1)}, u32[]{:S(2)}, u32[]{:S(2)}) collective-permute-start(bf16[2,2,96,768]{3,2,1,0:T(8,128)(2,1)} %get-tuple-element.296), channel_id=1, source_target_pairs={{0,8},{4,12},{8,0},{12,4},{16,24},{20,28},{24,16},{28,20},{1,9},{5... | collective-permute-start | bytes 1769480 | tf_op jit(solution)/shard_map/ppermute | solution.py:797
  355.9 16.2 %collective-permute-start.32 = (bf16[2,1,96,384]{3,2,1,0:T(8,128)(2,1)}, bf16[2,1,96,384]{3,2,1,0:T(8,128)(2,1)S(1)}, u32[]{:S(2)}, u32[]{:S(2)}) collective-permute-start(bf16[2,1,96,384]{3,2,1,0:T(8,128)(2,1)} %get-tuple-element.322), channel_id=1, source_target_pairs={{0,16},{4,20},{8,24},{12,28},{16,0},{20,4},{24,8},{28,12},{1,17},{... | collective-permute-start | bytes 442376 | tf_op jit(solution)/shard_map/ppermute | solution.py:797
  378.9 12.9 %collective-permute-start.36 = (bf16[2,2,96,384]{3,2,1,0:T(8,128)(2,1)}, bf16[2,2,96,384]{3,2,1,0:T(8,128)(2,1)S(1)}, u32[]{:S(2)}, u32[]{:S(2)}) collective-permute-start(bf16[2,2,96,384]{3,2,1,0:T(8,128)(2,1)} %get-tuple-element.333), channel_id=1, source_target_pairs={{0,8},{4,12},{8,0},{12,4},{16,24},{20,28},{24,16},{28,20},{1,9},{5... | collective-permute-start | bytes 884744 | tf_op jit(solution)/shard_map/ppermute | solution.py:797
  380.2 14.1 %collective-permute-start.33 = (bf16[2,1,96,768]{3,2,1,0:T(8,128)(2,1)}, bf16[2,1,96,768]{3,2,1,0:T(8,128)(2,1)S(1)}, u32[]{:S(2)}, u32[]{:S(2)}) collective-permute-start(bf16[2,1,96,768]{3,2,1,0:T(8,128)(2,1)} %get-tuple-element.324), channel_id=1, source_target_pairs={{0,16},{4,20},{8,24},{12,28},{16,0},{20,4},{24,8},{28,12},{1,17},{... | collective-permute-start | bytes 884744 | tf_op jit(solution)/shard_map/ppermute | solution.py:797
  (69 other events, 875.7 us)
